TPU v7x, 32 devices: a whole 2x2x4 slice. The times are simulated.
32 devices in a mesh: dp: 8 (over y, x, core), tensor: 4 (over z).
Axes of the slice: x: 2, y: 2, z: 4, core: 2. Of those that a mesh axis runs over, the one named last changes fastest.
Arguments:
- tokens: bfloat16 [9216, 2048], P(('dp', 'tensor')), may hold values from -6 to 6
- segment_ids: int32 [8, 1152], P('dp'), may hold values from 0 to 2, as said below
- attn_gain: bfloat16 [1, 2048], P(None, 'dp'), may hold values from 0.5 to 1.5
- q_weight: bfloat16 [1, 2048, 2048], P(None, 'dp', 'tensor'), may hold values from -0.125 to 0.125
- key_matrix: bfloat16 [1, 2048, 1024], P(None, 'dp', 'tensor'), may hold values from -0.125 to 0.125
- value_matrix: bfloat16 [1, 2048, 1024], P(None, 'dp', 'tensor'), may hold values from -0.125 to 0.125
- o_weight: bfloat16 [1, 2048, 2048], P(None, 'dp', 'tensor'), may hold values from -0.75 to 0.75
- q_gain: bfloat16 [1, 128], P(None, 'dp'), may hold values from 0.25 to 1.75
- k_gain: bfloat16 [1, 128], P(None, 'dp'), may hold values from 0.25 to 1.75
- mlp_gain: bfloat16 [1, 2048], P(None, 'dp'), may hold values from 0.5 to 1.5
- gate_weight: bfloat16 [1, 2048, 6144], P(None, 'dp', 'tensor'), may hold values from -0.125 to 0.125
- up_weight: bfloat16 [1, 2048, 6144], P(None, 'dp', 'tensor'), may hold values from -0.125 to 0.125
- down_weight: bfloat16 [1, 2048, 6144], P(None, 'dp', 'tensor'), may hold values from -0.078125 to 0.078125
- cotangent: bfloat16 [9216, 2048], P(('dp', 'tensor')), may hold values from -6 to 6
Outputs:
- activations: bfloat16 [9216, 2048], P(('dp', 'tensor'))
- input_grad: float32 [9216, 2048], P(('dp', 'tensor'))
- attn_gain_grad: float32 [1, 2048], P(None, 'dp')
- q_weight_grad: float32 [1, 2048, 2048], P(None, 'dp', 'tensor')
- k_weight_grad: float32 [1, 2048, 1024], P(None, 'dp', 'tensor')
- v_weight_grad: float32 [1, 2048, 1024], P(None, 'dp', 'tensor')
- o_weight_grad: float32 [1, 2048, 2048], P(None, 'dp', 'tensor')
- q_gain_grad: float32 [1, 128], P(None, 'dp')
- k_gain_grad: float32 [1, 128], P(None, 'dp')
- mlp_gain_grad: float32 [1, 2048], P(None, 'dp')
- gate_weight_grad: float32 [1, 2048, 6144], P(None, 'dp', 'tensor')
- up_weight_grad: float32 [1, 2048, 6144], P(None, 'dp', 'tensor')
- down_weight_grad: float32 [1, 2048, 6144], P(None, 'dp', 'tensor')
Inputs may be any that keep to these rules, and one draw needn't show every extreme that they name: `segment_ids`: in each group the numbers never fall, each of the 3 sequences has one token or more, and one sequence of each group has exactly 1024 tokens.
All inputs are finite; a program needn't handle non-finite values.
Results may differ from a plain program's by a relative error of at most 0.02.
Values may be sent and summed in bfloat16 or wider, within the bound.
A program may use at most 192 MiB of HBM per device.

v0:
```python
import jax
import jax.numpy as jnp
from jax import lax
from jax.sharding import PartitionSpec as P

HEAD_WIDTH = 128
DECODER_LAYERS = 1
NSEQ = 3
QBLOCK = 576


EPS = 1e-06
THETA = 1000000.0


def rms_scale(values, gain):
    return values * lax.rsqrt(jnp.mean(values * values, axis=-1, keepdims=True) + EPS) * gain


def rotate(values, cosine, sine_table):
    half_size = values.shape[-1] // 2
    turned = jnp.concatenate([-values[..., half_size:], values[..., :half_size]], axis=-1)
    return values * cosine + turned * sine_table


def swiglu(gate_raw, up_raw):
    return jax.nn.silu(gate_raw) * up_raw


def rotary_tables(sequence_labels):
    grouped_rows = sequence_labels.shape[0]
    row_index = jnp.arange(grouped_rows, dtype=jnp.int32)
    labels = jnp.arange(NSEQ, dtype=jnp.int32)
    starts = jnp.sum((sequence_labels[None, :] < labels[:, None]).astype(jnp.int32), axis=1)
    first_row = jnp.sum(
        jnp.where(sequence_labels[:, None] == labels[None, :], starts[None, :], 0), axis=1
    )
    position = (row_index - first_row).astype(jnp.float32)
    frequency = THETA ** (-(jnp.arange(HEAD_WIDTH // 2, dtype=jnp.float32) * (2.0 / HEAD_WIDTH)))
    angles = position[:, None] * frequency[None, :]
    cosine = jnp.concatenate([jnp.cos(angles), jnp.cos(angles)], axis=1)[:, None, :]
    sine_table = jnp.concatenate([jnp.sin(angles), jnp.sin(angles)], axis=1)[:, None, :]
    return (cosine, sine_table)


def contract_rows(left, right):
    return lax.dot_general(
        left, right, (((0,), (0,)), ((), ())), preferred_element_type=jnp.float32
    )


def contract_cols(left, right):
    return lax.dot_general(
        left, right, (((1,), (1,)), ((), ())), preferred_element_type=jnp.float32
    )


def block_items(queries, sequence_labels):
    grouped_rows, kv_heads, repeat, head_size = queries.shape
    blocks = grouped_rows // QBLOCK
    columns = jnp.arange(grouped_rows, dtype=jnp.int32)
    return (
        (
            queries.reshape(blocks, QBLOCK, kv_heads, repeat, head_size),
            sequence_labels.reshape(blocks, QBLOCK),
            columns.reshape(blocks, QBLOCK),
        ),
        columns,
    )


def attend_forward(queries, key_reduced, value_reduced, sequence_labels):
    grouped_rows, kv_heads, repeat, head_size = queries.shape
    score_scale = HEAD_WIDTH ** (-0.5)
    items, columns = block_items(queries, sequence_labels)

    def one_block(block_item):
        q_block, id_block, row_block = block_item
        allowed = (id_block[:, None] == sequence_labels[None, :]) & (
            columns[None, :] <= row_block[:, None]
        )
        scores = (
            jnp.einsum("qgrd,kgd->grqk", q_block, key_reduced, preferred_element_type=jnp.float32)
            * score_scale
        )
        weights = jnp.where(allowed[None, None], jnp.exp(scores), 0.0)
        totals = jnp.sum(weights, axis=-1, keepdims=True)
        shares = (weights / totals).astype(jnp.bfloat16)
        attention_result = jnp.einsum(
            "grqk,kgd->qgrd", shares, value_reduced, preferred_element_type=jnp.float32
        )
        return (attention_result.astype(jnp.bfloat16), totals)

    attention_result, totals = lax.map(one_block, items)
    return (attention_result.reshape(grouped_rows, kv_heads * repeat * head_size), totals)


def attend_backward(queries, key_reduced, value_reduced, sequence_labels, totals, out_grad):
    grouped_rows, kv_heads, repeat, head_size = queries.shape
    score_scale = HEAD_WIDTH ** (-0.5)
    items, columns = block_items(queries, sequence_labels)
    grad_blocks = out_grad.reshape(grouped_rows // QBLOCK, QBLOCK, kv_heads, repeat, head_size)

    def one_block(running, block_item):
        key_grad, value_grad = running
        q_block, id_block, row_block, total_block, grad_block = block_item
        allowed = (id_block[:, None] == sequence_labels[None, :]) & (
            columns[None, :] <= row_block[:, None]
        )
        scores = (
            jnp.einsum("qgrd,kgd->grqk", q_block, key_reduced, preferred_element_type=jnp.float32)
            * score_scale
        )
        shares = jnp.where(allowed[None, None], jnp.exp(scores), 0.0) / total_block
        low_shares = shares.astype(jnp.bfloat16)
        share_grad = jnp.einsum(
            "qgrd,kgd->grqk", grad_block, value_reduced, preferred_element_type=jnp.float32
        )
        row_inner = jnp.sum(shares * share_grad, axis=-1, keepdims=True)
        score_grad = (shares * (share_grad - row_inner)).astype(jnp.bfloat16)
        query_grad = (
            jnp.einsum(
                "grqk,kgd->qgrd", score_grad, key_reduced, preferred_element_type=jnp.float32
            )
            * score_scale
        )
        key_grad = (
            key_grad
            + jnp.einsum("grqk,qgrd->kgd", score_grad, q_block, preferred_element_type=jnp.float32)
            * score_scale
        )
        value_grad = value_grad + jnp.einsum(
            "grqk,qgrd->kgd", low_shares, grad_block, preferred_element_type=jnp.float32
        )
        return ((key_grad, value_grad), query_grad)

    zero_keys = jnp.zeros(key_reduced.shape, jnp.float32)
    (key_grad, value_grad), query_grad = lax.scan(
        one_block, (zero_keys, zero_keys), items + (totals, grad_blocks)
    )
    return (query_grad.reshape(grouped_rows, kv_heads * repeat, head_size), key_grad, value_grad)


def gather_attention(
    layer_index, attn_gain, q_weight, key_matrix, value_matrix, o_weight, q_gain, k_gain
):
    return (
        lax.all_gather(attn_gain[layer_index], "dp", axis=0, tiled=True),
        lax.all_gather(q_weight[layer_index], "dp", axis=0, tiled=True),
        lax.all_gather(key_matrix[layer_index], "dp", axis=0, tiled=True),
        lax.all_gather(value_matrix[layer_index], "dp", axis=0, tiled=True),
        lax.all_gather(o_weight[layer_index], "dp", axis=0, tiled=True),
        lax.all_gather(q_gain[layer_index], "dp", axis=0, tiled=True),
        lax.all_gather(k_gain[layer_index], "dp", axis=0, tiled=True),
    )


def gather_feedforward(layer_index, mlp_gain, gate_weight, up_weight, down_weight):
    return (
        lax.all_gather(mlp_gain[layer_index], "dp", axis=0, tiled=True),
        lax.all_gather(gate_weight[layer_index], "dp", axis=0, tiled=True),
        lax.all_gather(up_weight[layer_index], "dp", axis=0, tiled=True),
        lax.all_gather(down_weight[layer_index], "dp", axis=0, tiled=True),
    )


def attention_forward(stream, attn_parts, sequence_labels, cosine, sine_table):
    norm_gain, q_full, k_full, v_full, o_full, q_scale, k_scale = attn_parts
    norm_result = rms_scale(stream, norm_gain.astype(jnp.float32)).astype(jnp.bfloat16)
    gathered = lax.all_gather(norm_result, "tensor", axis=0, tiled=True)
    grouped_rows = gathered.shape[0]
    head_count = q_full.shape[1] // HEAD_WIDTH
    kv_heads = k_full.shape[1] // HEAD_WIDTH
    queries = jnp.dot(gathered, q_full, preferred_element_type=jnp.float32).reshape(
        grouped_rows, head_count, HEAD_WIDTH
    )
    key_unrotated = jnp.dot(gathered, k_full, preferred_element_type=jnp.float32).reshape(
        grouped_rows, kv_heads, HEAD_WIDTH
    )
    value_reduced = (
        jnp.dot(gathered, v_full, preferred_element_type=jnp.float32)
        .reshape(grouped_rows, kv_heads, HEAD_WIDTH)
        .astype(jnp.bfloat16)
    )
    query_reduced = rotate(
        rms_scale(queries, q_scale.astype(jnp.float32)), cosine, sine_table
    ).astype(jnp.bfloat16)
    key_reduced = rotate(
        rms_scale(key_unrotated, k_scale.astype(jnp.float32)), cosine, sine_table
    ).astype(jnp.bfloat16)
    query_reduced = query_reduced.reshape(
        grouped_rows, kv_heads, head_count // kv_heads, HEAD_WIDTH
    )
    attention_result, totals = attend_forward(
        query_reduced, key_reduced, value_reduced, sequence_labels
    )
    branch = lax.psum_scatter(
        contract_cols(attention_result, o_full), "tensor", scatter_dimension=0, tiled=True
    )
    return (
        stream + branch,
        (
            gathered,
            queries,
            key_unrotated,
            query_reduced,
            key_reduced,
            value_reduced,
            attention_result,
            totals,
        ),
    )


def feedforward_forward(middle, mlp_parts):
    norm_gain, gate_full, up_full, down_full = mlp_parts
    norm_result = rms_scale(middle, norm_gain.astype(jnp.float32)).astype(jnp.bfloat16)
    gathered = lax.all_gather(norm_result, "tensor", axis=0, tiled=True)
    gate_raw = jnp.dot(gathered, gate_full, preferred_element_type=jnp.float32)
    up_raw = jnp.dot(gathered, up_full, preferred_element_type=jnp.float32)
    hidden = swiglu(gate_raw, up_raw).astype(jnp.bfloat16)
    branch = lax.psum_scatter(
        contract_cols(hidden, down_full).astype(jnp.bfloat16),
        "tensor",
        scatter_dimension=0,
        tiled=True,
    ).astype(jnp.float32)
    return (middle + branch, (gathered, gate_raw, up_raw, hidden))


def feedforward_backward(gradient, middle, mlp_parts, mlp_kept):
    norm_gain, gate_full, up_full, down_full = mlp_parts
    gathered, gate_raw, up_raw, hidden = mlp_kept
    grad_rows = lax.all_gather(gradient.astype(jnp.bfloat16), "tensor", axis=0, tiled=True)
    hidden_grad = jnp.dot(grad_rows, down_full, preferred_element_type=jnp.float32)
    down_grad = contract_rows(grad_rows, hidden)
    _, pull_back = jax.vjp(swiglu, gate_raw, up_raw)
    gate_grad, up_grad = pull_back(hidden_grad)
    gate_low = gate_grad.astype(jnp.bfloat16)
    up_low = up_grad.astype(jnp.bfloat16)
    gate_wgrad = contract_rows(gathered, gate_low)
    up_wgrad = contract_rows(gathered, up_low)
    normed_grad = lax.psum_scatter(
        contract_cols(gate_low, gate_full) + contract_cols(up_low, up_full),
        "tensor",
        scatter_dimension=0,
        tiled=True,
    )
    _, pull_norm = jax.vjp(rms_scale, middle, norm_gain.astype(jnp.float32))
    middle_grad, gain_grad = pull_norm(normed_grad)
    return (gradient + middle_grad, (gain_grad, gate_wgrad, up_wgrad, down_grad))


def attention_backward(
    gradient, stream, attn_parts, attn_kept, sequence_labels, cosine, sine_table
):
    norm_gain, q_full, k_full, v_full, o_full, q_scale, k_scale = attn_parts
    (
        gathered,
        queries,
        key_unrotated,
        query_reduced,
        key_reduced,
        value_reduced,
        attention_result,
        totals,
    ) = attn_kept
    grouped_rows, kv_heads, repeat, head_size = query_reduced.shape
    grad_rows = lax.all_gather(gradient.astype(jnp.bfloat16), "tensor", axis=0, tiled=True)
    out_grad = jnp.dot(grad_rows, o_full, preferred_element_type=jnp.float32).astype(jnp.bfloat16)
    o_wgrad = contract_rows(grad_rows, attention_result)
    query_grad, key_grad, value_grad = attend_backward(
        query_reduced,
        key_reduced,
        value_reduced,
        sequence_labels,
        totals,
        out_grad.reshape(grouped_rows, kv_heads, repeat, head_size),
    )

    def query_path(raw_values, scales):
        return rotate(rms_scale(raw_values, scales), cosine, sine_table)

    _, pull_query = jax.vjp(query_path, queries, q_scale.astype(jnp.float32))
    query_raw_grad, q_gain_grad = pull_query(query_grad)
    _, pull_key = jax.vjp(query_path, key_unrotated, k_scale.astype(jnp.float32))
    key_raw_grad, k_gain_grad = pull_key(key_grad)
    query_back = query_raw_grad.reshape(grouped_rows, -1).astype(jnp.bfloat16)
    key_back = key_raw_grad.reshape(grouped_rows, -1).astype(jnp.bfloat16)
    value_back = value_grad.reshape(grouped_rows, -1).astype(jnp.bfloat16)
    q_wgrad = contract_rows(gathered, query_back)
    k_wgrad = contract_rows(gathered, key_back)
    v_wgrad = contract_rows(gathered, value_back)
    normed_grad = lax.psum_scatter(
        (
            contract_cols(query_back, q_full)
            + contract_cols(key_back, k_full)
            + contract_cols(value_back, v_full)
        ).astype(jnp.bfloat16),
        "tensor",
        scatter_dimension=0,
        tiled=True,
    ).astype(jnp.float32)
    _, pull_norm = jax.vjp(rms_scale, stream, norm_gain.astype(jnp.float32))
    stream_grad, gain_grad = pull_norm(normed_grad)
    return (
        gradient + stream_grad,
        (gain_grad, q_wgrad, k_wgrad, v_wgrad, o_wgrad, q_gain_grad, k_gain_grad),
    )


def per_device(
    tokens,
    segment_ids,
    attn_gain,
    q_weight,
    key_matrix,
    value_matrix,
    o_weight,
    q_gain,
    k_gain,
    mlp_gain,
    gate_weight,
    up_weight,
    down_weight,
    cotangent,
):
    sequence_labels = segment_ids[0]
    cosine, sine_table = rotary_tables(sequence_labels)
    stream = tokens.astype(jnp.float32)
    layer_index = 0
    attn_parts = gather_attention(
        layer_index, attn_gain, q_weight, key_matrix, value_matrix, o_weight, q_gain, k_gain
    )
    middle, attn_kept = attention_forward(stream, attn_parts, sequence_labels, cosine, sine_table)
    mlp_parts = gather_feedforward(layer_index, mlp_gain, gate_weight, up_weight, down_weight)
    after_layer, mlp_kept = feedforward_forward(middle, mlp_parts)
    saved = [(stream, middle, attn_parts, attn_kept, mlp_parts, mlp_kept)]
    activations = after_layer.astype(jnp.bfloat16)
    gradient = cotangent.astype(jnp.float32)
    attn_owned = []
    mlp_owned = []
    for layer_index in reversed(range(DECODER_LAYERS)):
        stream_in, middle, attn_parts, attn_kept, mlp_parts, mlp_kept = saved[layer_index]
        gradient, local_mlp = feedforward_backward(gradient, middle, mlp_parts, mlp_kept)
        local_mlp = (
            lax.psum_scatter(
                local_mlp[0].astype(jnp.bfloat16), "dp", scatter_dimension=0, tiled=True
            ).astype(jnp.float32),
            lax.psum_scatter(
                local_mlp[1].astype(jnp.bfloat16), "dp", scatter_dimension=0, tiled=True
            ).astype(jnp.float32),
            lax.psum_scatter(
                local_mlp[2].astype(jnp.bfloat16), "dp", scatter_dimension=0, tiled=True
            ).astype(jnp.float32),
            lax.psum_scatter(
                local_mlp[3].astype(jnp.bfloat16), "dp", scatter_dimension=0, tiled=True
            ).astype(jnp.float32),
        )
        mlp_owned.insert(0, local_mlp)
        gradient, local_attn = attention_backward(
            gradient, stream_in, attn_parts, attn_kept, sequence_labels, cosine, sine_table
        )
        local_attn = (
            lax.psum_scatter(
                local_attn[0].astype(jnp.bfloat16), "dp", scatter_dimension=0, tiled=True
            ).astype(jnp.float32),
            lax.psum_scatter(
                local_attn[1].astype(jnp.bfloat16), "dp", scatter_dimension=0, tiled=True
            ).astype(jnp.float32),
            lax.psum_scatter(
                local_attn[2].astype(jnp.bfloat16), "dp", scatter_dimension=0, tiled=True
            ).astype(jnp.float32),
            lax.psum_scatter(
                local_attn[3].astype(jnp.bfloat16), "dp", scatter_dimension=0, tiled=True
            ).astype(jnp.float32),
            lax.psum_scatter(
                local_attn[4].astype(jnp.bfloat16), "dp", scatter_dimension=0, tiled=True
            ).astype(jnp.float32),
            lax.psum_scatter(
                local_attn[5].astype(jnp.bfloat16), "dp", scatter_dimension=0, tiled=True
            ).astype(jnp.float32),
            lax.psum_scatter(
                local_attn[6].astype(jnp.bfloat16), "dp", scatter_dimension=0, tiled=True
            ).astype(jnp.float32),
        )
        attn_owned.insert(0, local_attn)
    attn_stack = [jnp.stack([owned[member] for owned in attn_owned]) for member in range(7)]
    mlp_stack = [jnp.stack([owned[member] for owned in mlp_owned]) for member in range(4)]
    gain_totals = lax.psum((attn_stack[0], attn_stack[5], attn_stack[6], mlp_stack[0]), "tensor")
    return (
        activations,
        gradient,
        gain_totals[0],
        attn_stack[1],
        attn_stack[2],
        attn_stack[3],
        attn_stack[4],
        gain_totals[1],
        gain_totals[2],
        gain_totals[3],
        mlp_stack[1],
        mlp_stack[2],
        mlp_stack[3],
    )


def solution(mesh):
    placed = (
        P(("dp", "tensor"), None),
        P("dp", None),
        P(None, "dp"),
        P(None, "dp", "tensor"),
        P(None, "dp", "tensor"),
        P(None, "dp", "tensor"),
        P(None, "dp", "tensor"),
        P(None, "dp"),
        P(None, "dp"),
        P(None, "dp"),
        P(None, "dp", "tensor"),
        P(None, "dp", "tensor"),
        P(None, "dp", "tensor"),
        P(("dp", "tensor"), None),
    )
    return jax.shard_map(
        per_device,
        mesh=mesh,
        in_specs=placed,
        out_specs=(
            P(("dp", "tensor"), None),
            P(("dp", "tensor"), None),
            P(None, "dp"),
            P(None, "dp", "tensor"),
            P(None, "dp", "tensor"),
            P(None, "dp", "tensor"),
            P(None, "dp", "tensor"),
            P(None, "dp"),
            P(None, "dp"),
            P(None, "dp"),
            P(None, "dp", "tensor"),
            P(None, "dp", "tensor"),
            P(None, "dp", "tensor"),
        ),
        check_vma=False,
    )
```

profile of v0, /device:TPU:0, one launch (start us, length us, event | category | flops | bytes accessed | tf_op | source)
XLA Modules:
  0.0 1585.5 jit_solution(960862814224746702)
XLA Ops:
  8.0 10.6 all-gather
  21.4 2.6 fusion.67
  28.8 13.2 all-reduce.12
  47.2 80.4 %all-gather.23.cloned.1.call-done = bf16[1152,2048]{1,0:T(8,128)(2,1)} async-done(((bf16[288,2048]{1,0:T(8,128)(2,1)}), bf16[1152,2048]{1,0:T(8,128)(2,1)}) %all-gather.23.cloned.1.call-update) | async-done | bytes 4718608 | tf_op jit(solution)/shard_map/all_gather | solution.py:170
  127.7 4.2 convolution_convert_fusion.9
  132.2 19.2 %all-gather.33.cloned.1.call-done = bf16[1,2048,256]{2,1,0:T(8,128)(2,1)} async-done(((bf16[1,256,256]{2,1,0:T(8,128)(2,1)}), bf16[1,2048,256]{2,1,0:T(8,128)(2,1)}) %all-gather.33.cloned.1.call-update) | async-done | bytes 1048592 | tf_op jit(solution)/shard_map/all_gather | solution.py:150
  151.4 4.3 multiply_reduce_fusion.8
  157.4 23.5 %all-gather.31.cloned.1.call-done = bf16[1,2048,512]{2,1,0:T(8,128)(2,1)} async-done(((bf16[1,256,512]{2,1,0:T(8,128)(2,1)}), bf16[1,2048,512]{2,1,0:T(8,128)(2,1)}) %all-gather.31.cloned.1.call-update) | async-done | bytes 2097168 | tf_op jit(solution)/shard_map/all_gather | solution.py:149
  180.9 6.0 multiply_reduce_fusion.5
  189.7 2.6 copy.122
  192.3 3.2 reshape.379
  198.2 2.6 copy.144
  200.8 3.7 copy.145
  204.5 7.3 copy.143
  211.8 7.5 fusion.75
  219.4 19.3 %while.28 = (s32[]{:T(128)}, bf16[2,576,2,2,128]{4,3,2,1,0:T(2,128)(2,1)}, f32[2,2,2,576,1]{3,2,1,4,0:T(2,128)}, s32[2,576]{1,0:T(2,128)}, s32[1,1152]{1,0:T(1,1...) while((s32[]{:T(128)}, ...), condition=%wide.region_7.8_spmd.clone, body=%wide.region_5.7_spmd.clone.sunk | while | flops 1379817216 | bytes 36414712 | solution.py:94
  220.9 3.2 bitcast_reduce_fusion.2
  224.1 3.2 fusion.149
  230.5 3.2 bitcast_reduce_fusion.2
  233.7 3.2 fusion.149
  238.7 3.5 reshape.331
  242.3 7.1 fusion.77
  250.3 9.0 all-gather.7
  259.3 151.6 %reduce-scatter.12.cloned.1.call-done = f32[288,2048]{1,0:T(8,128)} async-done(((f32[1152,2048]{1,0:T(8,128)}), f32[288,2048]{1,0:T(8,128)}) %reduce-scatter.12.cloned.1.call-update) | async-done | bytes 2359312 | tf_op jit(solution)/shard_map/reduce_scatter | solution.py:197
  416.6 42.5 %all-gather.41.cloned.1.call-done = bf16[1,2048,1536]{2,1,0:T(8,128)(2,1)} async-done(((bf16[1,256,1536]{2,1,0:T(8,128)(2,1)}), bf16[1,2048,1536]{2,1,0:T(8,128)(2,1)}) %all-gather.41.cloned.1.call-update) | async-done | bytes 6291472 | tf_op jit(solution)/shard_map/all_gather | solution.py:162
  459.2 91.6 %all-gather.25.cloned.1.call-done = bf16[1152,2048]{1,0:T(8,128)(2,1)} async-done(((bf16[288,2048]{1,0:T(8,128)(2,1)}), bf16[1152,2048]{1,0:T(8,128)(2,1)}) %all-gather.25.cloned.1.call-update) | async-done | bytes 4718608 | tf_op jit(solution)/shard_map/all_gather | solution.py:218
  550.7 13.1 fusion.59
  563.8 32.7 %all-gather.39.cloned.1.call-done = bf16[1,2048,1536]{2,1,0:T(8,128)(2,1)} async-done(((bf16[1,256,1536]{2,1,0:T(8,128)(2,1)}), bf16[1,2048,1536]{2,1,0:T(8,128)(2,1)}) %all-gather.39.cloned.1.call-update) | async-done | bytes 6291472 | tf_op jit(solution)/shard_map/all_gather | solution.py:161
  596.5 12.9 fusion.63
  609.4 77.9 %all-gather.27.cloned.1.call-done = bf16[1152,2048]{1,0:T(8,128)(2,1)} async-done(((bf16[288,2048]{1,0:T(8,128)(2,1)}), bf16[1152,2048]{1,0:T(8,128)(2,1)}) %all-gather.27.cloned.1.call-update) | async-done | bytes 4718608 | tf_op jit(solution)/shard_map/all_gather | solution.py:234
  687.3 45.7 %all-gather.43.cloned.1.call-done = bf16[1,2048,1536]{2,1,0:T(8,128)(2,1)} async-done(((bf16[1,256,1536]{2,1,0:T(8,128)(2,1)}), bf16[1,2048,1536]{2,1,0:T(8,128)(2,1)}) %all-gather.43.cloned.1.call-update) | async-done | bytes 6291472 | tf_op jit(solution)/shard_map/all_gather | solution.py:163
  733.0 18.5 %multiply_convert_fusion = (bf16[1152,1536]{1,0:T(8,128)(2,1)S(1)}, bf16[1152,1536]{1,0:T(8,128)(2,1)}, bf16[1152,1536]{1,0:T(8,128)(2,1)}) fusion(f32[1152,1536]{1,0:T(8,128)} %fusion.63, f32[1152,1536]{1,0:T(8,128)} %fusion.59, bf16[1152,2048]{1,0:T(8,128)(2,1)} %all-gather.27.cloned.1.call-done, bf16[1,2048,1536]{2,1,0:T(8,128)(2,1)} %all-gather.43.cloned.1.call-done), kind=kOutput, calls=%fused_computation.69 | convolution fusion | flops 7276068864 | bytes 35782656 | tf_op jit(solution)/shard_map/dot_general | solution.py:235
  751.5 12.6 fusion.61
  764.1 13.7 convolution_add_fusion.2
  778.0 161.3 %reduce-scatter.16.cloned.1.call-done = f32[288,2048]{1,0:T(8,128)} async-done(((f32[1152,2048]{1,0:T(8,128)}), f32[288,2048]{1,0:T(8,128)}) %reduce-scatter.16.cloned.1.call-update) | async-done | bytes 2359312 | tf_op jit(solution)/shard_map/reduce_scatter | solution.py:243
  939.2 3.0 multiply_reduce_fusion
  944.7 13.0 fusion.54
  959.7 12.9 convolution_convert_fusion.1
  972.7 13.1 convolution_convert_fusion.2
  985.9 49.2 %all-gather.29.cloned.1.call-done = bf16[1152,2048]{1,0:T(8,128)(2,1)} async-done(((bf16[288,2048]{1,0:T(8,128)(2,1)}), bf16[1152,2048]{1,0:T(8,128)(2,1)}) %all-gather.29.cloned.1.call-update) | async-done | bytes 4718608 | tf_op jit(solution)/shard_map/all_gather | solution.py:269
  1035.1 6.7 convolution_convert_fusion.6
  1041.8 3.9 reshape_reshape.2
  1045.7 33.4 %while.29 = (s32[]{:T(128)}, f32[1152,2,128]{0,2,1:T(8,128)S(1)}, f32[1152,2,128]{0,2,1:T(8,128)S(1)}, f32[2,576,2,2,128]{4,1,0,3,2:T(8,128)}, bf16[2,576,2,2,12...) while((s32[]{:T(128)}, f32[1152,2,128]{0,2,1:T(8,128)S(1)}, ...), condition=%wide.region_15.16_spmd.clone, body=%wide.region_13.15_spmd.clone.sunk | while | flops 3425031936 | bytes 115827968 | solution.py:138
  1051.3 3.9 fusion.158
  1067.7 3.9 fusion.158
  1079.2 5.2 convolution_convert_fusion.7
  1089.8 4.9 convolution_convert_fusion.8
  1096.8 7.0 convolution_convert_fusion.4
  1108.0 4.3 convolution_convert_fusion.5
  1112.6 5.0 fusion.79
  1119.2 3.6 fusion.49
  1124.8 12.8 convolution_convert_fusion.3
  1141.8 21.6 %reduce-scatter.30.cloned.1.call-done = bf16[256,1536]{1,0:T(8,128)(2,1)} async-done(((bf16[2048,1536]{1,0:T(8,128)(2,1)}), bf16[256,1536]{1,0:T(8,128)(2,1)}) %reduce-scatter.30.cloned.1.call-update) | async-done | bytes 786448 | tf_op jit(solution)/shard_map/reduce_scatter | solution.py:353
  1165.9 62.6 %reduce-scatter.28.cloned.1.call-done = bf16[256,1536]{1,0:T(8,128)(2,1)} async-done(((bf16[2048,1536]{1,0:T(8,128)(2,1)}), bf16[256,1536]{1,0:T(8,128)(2,1)}) %reduce-scatter.28.cloned.1.call-update) | async-done | bytes 786448 | tf_op jit(solution)/shard_map/reduce_scatter | solution.py:350
  1230.9 36.6 %reduce-scatter.24.cloned.1.call-done = bf16[256,256]{1,0:T(8,128)(2,1)} async-done(((bf16[2048,256]{1,0:T(8,128)(2,1)}), bf16[256,256]{1,0:T(8,128)(2,1)}) %reduce-scatter.24.cloned.1.call-update) | async-done | bytes 131088 | tf_op jit(solution)/shard_map/reduce_scatter | solution.py:374
  1269.1 38.0 %reduce-scatter.22.cloned.1.call-done = bf16[256,256]{1,0:T(8,128)(2,1)} async-done(((bf16[2048,256]{1,0:T(8,128)(2,1)}), bf16[256,256]{1,0:T(8,128)(2,1)}) %reduce-scatter.22.cloned.1.call-update) | async-done | bytes 131088 | tf_op jit(solution)/shard_map/reduce_scatter | solution.py:371
  1308.7 42.8 %reduce-scatter.26.cloned.1.call-done = bf16[256,512]{1,0:T(8,128)(2,1)} async-done(((bf16[2048,512]{1,0:T(8,128)(2,1)}), bf16[256,512]{1,0:T(8,128)(2,1)}) %reduce-scatter.26.cloned.1.call-update) | async-done | bytes 262160 | tf_op jit(solution)/shard_map/reduce_scatter | solution.py:377
  1353.3 43.0 %reduce-scatter.20.cloned.1.call-done = bf16[256,512]{1,0:T(8,128)(2,1)} async-done(((bf16[2048,512]{1,0:T(8,128)(2,1)}), bf16[256,512]{1,0:T(8,128)(2,1)}) %reduce-scatter.20.cloned.1.call-update) | async-done | bytes 262160 | tf_op jit(solution)/shard_map/reduce_scatter | solution.py:368
  1398.1 85.8 %reduce-scatter.18.cloned.1.call-done = bf16[288,2048]{1,0:T(8,128)(2,1)} async-done(((bf16[1152,2048]{1,0:T(8,128)(2,1)}), bf16[288,2048]{1,0:T(8,128)(2,1)}) %reduce-scatter.18.cloned.1.call-update) | async-done | bytes 1179664 | tf_op jit(solution)/shard_map/reduce_scatter | solution.py:294
  1484.0 2.9 fusion.68
  1486.9 15.2 all-reduce.11
  1507.2 12.1 all-reduce.10
  1520.6 51.8 %reduce-scatter.14.cloned.1.call-done = bf16[288,2048]{1,0:T(8,128)(2,1)} async-done(((bf16[1152,2048]{1,0:T(8,128)(2,1)}), bf16[288,2048]{1,0:T(8,128)(2,1)}) %reduce-scatter.14.cloned.1.call-update) | async-done | bytes 1179664 | tf_op jit(solution)/shard_map/reduce_scatter | solution.py:222
  1572.4 5.8 fusion.71
  (292 shorter events, 99.1 us)
Async XLA Ops:
  7.2 40.1 %all-gather.35.cloned.1.call-start = ((), (), s32[]{:S(2)}) async-start(), calls=%async_computation.28 | async-start | bytes 1179648 | tf_op jit(solution)/shard_map/all_gather | solution.py:151
  7.9 119.8 %all-gather.23.cloned.1.call-start = ((), (), s32[]{:S(2)}) async-start(), calls=%async_computation.11 | async-start | bytes 5898240 | tf_op jit(solution)/shard_map/all_gather | solution.py:170
  18.5 2.3 copy-start.39
  20.7 5.3 copy-start.31
  20.7 6.3 copy-start.54
  20.7 7.5 copy-start.57
  20.8 7.8 copy-start.58
  24.0 127.4 %all-gather.33.cloned.1.call-start = ((), (), s32[]{:S(2)}) async-start(), calls=%async_computation.27 | async-start | bytes 1179648 | tf_op jit(solution)/shard_map/all_gather | solution.py:150
  24.7 156.2 %all-gather.31.cloned.1.call-start = ((), (), s32[]{:S(2)}) async-start(), calls=%async_computation.26 | async-start | bytes 2359296 | tf_op jit(solution)/shard_map/all_gather | solution.py:149
  25.3 217.0 %all-gather.37.cloned.1.call-start = ((), (), s32[]{:S(2)}) async-start(), calls=%async_computation.29 | async-start | bytes 2359296 | tf_op jit(solution)/shard_map/all_gather | solution.py:152
  25.9 385.0 %reduce-scatter.12.cloned.1.call-start = ((), (), s32[]{:S(2)}) async-start(), calls=%async_computation.12 | async-start | bytes 11796480 | tf_op jit(solution)/shard_map/reduce_scatter | solution.py:197
  42.5 113.7 %copy-start.51 = (f32[128]{0:T(128)}, f32[128]{0:T(128)S(1)}, u32[]{:S(2)}) copy-start(f32[128]{0:T(128)S(1)} %convert_element_type.213) | copy-start | bytes 1540
  43.6 112.6 %copy-start.16 = (f32[1152,128]{0,1:T(8,128)}, f32[1152,128]{0,1:T(8,128)S(1)}, u32[]{:S(2)}) copy-start(f32[1152,128]{0,1:T(8,128)S(1)} %pad_maximum_fusion.2) | copy-start | bytes 1769476
  43.7 112.5 %copy-start.18 = (f32[1152,128]{0,1:T(8,128)}, f32[1152,128]{0,1:T(8,128)S(1)}, u32[]{:S(2)}) copy-start(f32[1152,128]{0,1:T(8,128)S(1)} %pad_maximum_fusion.3) | copy-start | bytes 1769476
  186.9 8.6 copy-start.2
  224.1 3.3 copy-start.41
  224.1 3.3 copy-start.27
  233.7 3.3 copy-start.41
  233.7 3.3 copy-start.27
  238.7 10.7 copy-start.8
  238.7 10.7 copy-start.10
  238.7 10.7 copy-start.13
  238.7 10.7 copy-start.38
  242.3 7.1 copy-start.26
  249.4 161.5 %copy-start.6 = (bf16[288,2048]{1,0:T(8,128)(2,1)S(1)}, bf16[288,2048]{1,0:T(8,128)(2,1)}, u32[]{:S(2)}) copy-start(bf16[288,2048]{1,0:T(8,128)(2,1)} %param.18) | copy-start | bytes 3538948
  249.5 209.7 %all-gather.41.cloned.1.call-start = ((), (), s32[]{:S(2)}) async-start(), calls=%async_computation.31 | async-start | bytes 7077888 | tf_op jit(solution)/shard_map/all_gather | solution.py:162
  250.2 300.5 %all-gather.25.cloned.1.call-start = ((), (), s32[]{:S(2)}) async-start(), calls=%async_computation.13 | async-start | bytes 5898240 | tf_op jit(solution)/shard_map/all_gather | solution.py:218
  259.3 683.0 %copy-start.36 = (f32[1,2048]{1,0:T(1,128)}, f32[1,2048]{1,0:T(1,128)S(1)}, u32[]{:S(2)}) copy-start(f32[1,2048]{1,0:T(1,128)S(1)} %convert_element_type.211) | copy-start | bytes 24580
  413.0 529.3 %copy-start = (f32[288,2048]{1,0:T(8,128)}, f32[288,2048]{1,0:T(8,128)S(1)}, u32[]{:S(2)}) copy-start(f32[288,2048]{1,0:T(8,128)S(1)} %get-tuple-element.468) | copy-start | bytes 7077892
  413.0 529.2 %copy-start.45 = (f32[288]{0:T(512)}, f32[288]{0:T(512)S(1)}, u32[]{:S(2)}) copy-start(f32[288]{0:T(512)S(1)} %fusion.94) | copy-start | bytes 3460
  414.5 181.9 %all-gather.39.cloned.1.call-start = ((), (), s32[]{:S(2)}) async-start(), calls=%async_computation.30 | async-start | bytes 7077888 | tf_op jit(solution)/shard_map/all_gather | solution.py:161
  415.3 272.0 %all-gather.27.cloned.1.call-start = ((), (), s32[]{:S(2)}) async-start(), calls=%async_computation.15 | async-start | bytes 5898240 | tf_op jit(solution)/shard_map/all_gather | solution.py:234
  415.8 317.2 %all-gather.43.cloned.1.call-start = ((), (), s32[]{:S(2)}) async-start(), calls=%async_computation.32 | async-start | bytes 7077888 | tf_op jit(solution)/shard_map/all_gather | solution.py:163
  416.6 522.7 %reduce-scatter.16.cloned.1.call-start = ((), (), s32[]{:S(2)}) async-start(), calls=%async_computation.16 | async-start | bytes 11796480 | tf_op jit(solution)/shard_map/reduce_scatter | solution.py:243
  733.0 18.5 %copy-start.56 = (bf16[1,2048,1536]{2,1,0:T(8,128)(2,1)S(1)}, bf16[1,2048,1536]{2,1,0:T(8,128)(2,1)}, u32[]{:S(2)}) copy-start(bf16[1,2048,1536]{2,1,0:T(8,128)(2,1)} %all-gather.39.cloned.1.call-done) | copy-start | bytes 18874372
  751.5 12.6 copy-start.60
  777.9 164.9 %copy-start.15 = (bf16[288,2048]{1,0:T(8,128)(2,1)S(1)}, bf16[288,2048]{1,0:T(8,128)(2,1)}, u32[]{:S(2)}) copy-start(bf16[288,2048]{1,0:T(8,128)(2,1)} %param.31) | copy-start | bytes 3538948
  777.9 257.2 %all-gather.29.cloned.1.call-start = ((), (), s32[]{:S(2)}) async-start(), calls=%async_computation.17 | async-start | bytes 5898240 | tf_op jit(solution)/shard_map/all_gather | solution.py:269
  939.2 3.6 copy-start.12
  944.6 194.3 %reduce-scatter.32.cloned.1.call-start = ((), (), s32[]{:S(2)}) async-start(), calls=%async_computation.25 | async-start | bytes 7077888 | tf_op jit(solution)/shard_map/reduce_scatter | solution.py:356
  957.7 2.0 copy-start.61
  957.7 205.7 %reduce-scatter.30.cloned.1.call-start = ((), (), s32[]{:S(2)}) async-start(), calls=%async_computation.24 | async-start | bytes 7077888 | tf_op jit(solution)/shard_map/reduce_scatter | solution.py:353
  972.6 255.8 %reduce-scatter.28.cloned.1.call-start = ((), (), s32[]{:S(2)}) async-start(), calls=%async_computation.23 | async-start | bytes 7077888 | tf_op jit(solution)/shard_map/reduce_scatter | solution.py:350
  985.9 281.6 %reduce-scatter.24.cloned.1.call-start = ((), (), s32[]{:S(2)}) async-start(), calls=%async_computation.21 | async-start | bytes 1179648 | tf_op jit(solution)/shard_map/reduce_scatter | solution.py:374
  1041.8 3.9 copy-start.9
  1041.8 3.9 copy-start.11
  1041.8 3.9 copy-start.32
  1079.2 5.3 copy-start.20
  1079.2 5.3 copy-start.19
  1085.7 221.4 %reduce-scatter.22.cloned.1.call-start = ((), (), s32[]{:S(2)}) async-start(), calls=%async_computation.20 | async-start | bytes 1179648 | tf_op jit(solution)/shard_map/reduce_scatter | solution.py:371
  1086.4 2.3 copy-start.47
  1094.8 256.8 %reduce-scatter.26.cloned.1.call-start = ((), (), s32[]{:S(2)}) async-start(), calls=%async_computation.22 | async-start | bytes 2359296 | tf_op jit(solution)/shard_map/reduce_scatter | solution.py:377
  1103.9 292.5 %reduce-scatter.20.cloned.1.call-start = ((), (), s32[]{:S(2)}) async-start(), calls=%async_computation.19 | async-start | bytes 2359296 | tf_op jit(solution)/shard_map/reduce_scatter | solution.py:368
  1104.1 3.8 slice-start
  1105.8 2.2 slice-start.1
  1112.3 5.3 copy-start.23
  1112.3 5.3 copy-start.29
  1112.3 371.7 %reduce-scatter.18.cloned.1.call-start = ((), (), s32[]{:S(2)}) async-start(), calls=%async_computation.18 | async-start | bytes 5898240 | tf_op jit(solution)/shard_map/reduce_scatter | solution.py:294
  1122.8 2.0 copy-start.59
  1122.8 449.6 %reduce-scatter.14.cloned.1.call-start = ((), (), s32[]{:S(2)}) async-start(), calls=%async_computation.14 | async-start | bytes 5898240 | tf_op jit(solution)/shard_map/reduce_scatter | solution.py:222
  1165.9 318.1 %copy-start.7 = (bf16[288,2048]{1,0:T(8,128)(2,1)S(1)}, bf16[288,2048]{1,0:T(8,128)(2,1)}, u32[]{:S(2)}) copy-start(bf16[288,2048]{1,0:T(8,128)(2,1)} %param.18) | copy-start | bytes 3538948
  1165.9 318.1 %copy-start.40 = (f32[1,2048]{1,0:T(1,128)S(1)}, f32[1,2048]{1,0:T(1,128)}, u32[]{:S(2)}) copy-start(f32[1,2048]{1,0:T(1,128)} %copy-done.39) | copy-start | bytes 24580
  1230.9 341.5 %copy-start.1 = (f32[288,2048]{1,0:T(8,128)S(1)}, f32[288,2048]{1,0:T(8,128)}, u32[]{:S(2)}) copy-start(f32[288,2048]{1,0:T(8,128)} %copy-done) | copy-start | bytes 7077892
  1230.9 341.5 %copy-start.37 = (f32[1,2048]{1,0:T(1,128)S(1)}, f32[1,2048]{1,0:T(1,128)}, u32[]{:S(2)}) copy-start(f32[1,2048]{1,0:T(1,128)} %copy-done.36) | copy-start | bytes 24580
  (29 other events, 36.2 us)
Sparse Core Ops, SparseCore 0:
  9.9 26.1 all-gather.34
  38.2 89.4 all-gather.22
  129.6 21.7 all-gather.32
  153.1 27.7 all-gather.30
  182.7 27.7 all-gather.36
  249.6 161.2 reduce-scatter.11
  412.8 46.3 all-gather.40
  461.3 89.3 all-gather.24
  552.6 43.7 all-gather.38
  597.9 89.3 all-gather.26
  689.2 43.7 all-gather.42
  778.0 161.1 reduce-scatter.15
  944.7 90.3 all-gather.28
  1038.4 60.0 reduce-scatter.31
  1101.7 61.7 reduce-scatter.29
  1166.7 61.7 reduce-scatter.27
  1231.5 35.9 reduce-scatter.23
  1271.1 35.9 reduce-scatter.21
  1310.4 41.0 reduce-scatter.25
  1355.2 41.0 reduce-scatter.19
  1398.7 85.2 reduce-scatter.17
  1486.3 86.0 reduce-scatter.13
where the time goes:
time: 1600 us; the launch traced here: 1590 us
  waiting for transfers between devices  1160 us (72%)
  matrix products  215 us (13%)
  other arithmetic  69.3 us (4%)
  blocking collectives  59.9 us (4%)
  local copies, waits for them, and re-layouts  58.6 us (4%)
  between operations  17.5 us (1%)
    reduce_scatter x1, waiting for transfers between devices, feedforward_backward(): lax.psum_scatter(contract_cols(gate_low, gate_full) + contract_cols(up_lo...  161 us
    reduce_scatter x1, waiting for transfers between devices, attention_forward(): lax.psum_scatter(contract_cols(attention_result, o_full), 'tensor', scatt...  152 us
    all_gather x1, waiting for transfers between devices, feedforward_forward(): gathered = lax.all_gather(norm_result, 'tensor', axis=0, tiled=True)  91.6 us
    reduce_scatter x1, waiting for transfers between devices, attention_backward(): lax.psum_scatter((contract_cols(query_back, q_full) + contract_cols(key_b...  85.8 us
    all_gather x1, waiting for transfers between devices, attention_forward(): gathered = lax.all_gather(norm_result, 'tensor', axis=0, tiled=True)  80.4 us
    all_gather x1, waiting for transfers between devices, feedforward_backward(): lax.all_gather(gradient.astype(jnp.bfloat16), 'tensor', axis=0, tiled=True)  77.9 us
    reduce_scatter x1, waiting for transfers between devices, per_device(): lax.psum_scatter(local_mlp[1].astype(jnp.bfloat16), 'dp', scatter_dimensi...  62.6 us
    dot_general x7, matrix products, contract_rows(): lax.dot_general(left, right, (((0,), (0,)), ((), ())), preferred_element_...  60.5 us
  transfers between devices with their start and end apart: 22, of which 19 were waited for; matrix products, arithmetic and copies ran while one was open for 17% of the time, Pallas kernels for 0%

commit v1 on v0

v1 whole, which is shorter than its diff:
```python
import jax
import jax.numpy as jnp
from jax import lax
from jax.sharding import Mesh
from jax.sharding import PartitionSpec as P

HEAD_WIDTH = 128
DECODER_LAYERS = 1
NSEQ = 3
QBLOCK = 576


EPS = 1e-06
THETA = 1000000.0


def rms_scale(values, gain):
    return values * lax.rsqrt(jnp.mean(values * values, axis=-1, keepdims=True) + EPS) * gain


def rotate(values, cosine, sine_table):
    half_size = values.shape[-1] // 2
    turned = jnp.concatenate([-values[..., half_size:], values[..., :half_size]], axis=-1)
    return values * cosine + turned * sine_table


def swiglu(gate_raw, up_raw):
    return jax.nn.silu(gate_raw) * up_raw


def rotary_tables(sequence_labels, row_index):
    labels = jnp.arange(NSEQ, dtype=jnp.int32)
    starts = jnp.sum((sequence_labels[None, :] < labels[:, None]).astype(jnp.int32), axis=1)
    first_row = jnp.sum(
        jnp.where(sequence_labels[:, None] == labels[None, :], starts[None, :], 0), axis=1
    )
    position = (row_index - first_row).astype(jnp.float32)
    frequency = THETA ** (-(jnp.arange(HEAD_WIDTH // 2, dtype=jnp.float32) * (2.0 / HEAD_WIDTH)))
    angles = position[:, None] * frequency[None, :]
    cosine = jnp.concatenate([jnp.cos(angles), jnp.cos(angles)], axis=1)[:, None, :]
    sine_table = jnp.concatenate([jnp.sin(angles), jnp.sin(angles)], axis=1)[:, None, :]
    return (cosine, sine_table)


def contract_rows(left, right):
    return lax.dot_general(
        left, right, (((0,), (0,)), ((), ())), preferred_element_type=jnp.float32
    )


def contract_cols(left, right):
    return lax.dot_general(
        left, right, (((1,), (1,)), ((), ())), preferred_element_type=jnp.float32
    )


def block_items(queries, sequence_labels, columns):
    grouped_rows, kv_heads, repeat, head_size = queries.shape
    blocks = grouped_rows // QBLOCK
    return (
        (
            queries.reshape(blocks, QBLOCK, kv_heads, repeat, head_size),
            sequence_labels.reshape(blocks, QBLOCK),
            columns.reshape(blocks, QBLOCK),
        ),
        columns,
    )


def attend_forward(queries, key_reduced, value_reduced, sequence_labels, row_index):
    grouped_rows, kv_heads, repeat, head_size = queries.shape
    score_scale = HEAD_WIDTH ** (-0.5)
    items, columns = block_items(queries, sequence_labels, row_index)

    def one_block(block_item):
        q_block, id_block, row_block = block_item
        allowed = (id_block[:, None] == sequence_labels[None, :]) & (
            columns[None, :] <= row_block[:, None]
        )
        scores = (
            jnp.einsum("qgrd,kgd->grqk", q_block, key_reduced, preferred_element_type=jnp.float32)
            * score_scale
        )
        weights = jnp.where(allowed[None, None], jnp.exp(scores), 0.0)
        totals = jnp.sum(weights, axis=-1, keepdims=True)
        shares = (weights / totals).astype(jnp.bfloat16)
        attention_result = jnp.einsum(
            "grqk,kgd->qgrd", shares, value_reduced, preferred_element_type=jnp.float32
        )
        return (attention_result.astype(jnp.bfloat16), totals)

    attention_result, totals = lax.map(one_block, items)
    return (attention_result.reshape(grouped_rows, kv_heads * repeat * head_size), totals)


def attend_backward(
    queries, key_reduced, value_reduced, sequence_labels, row_index, totals, out_grad
):
    grouped_rows, kv_heads, repeat, head_size = queries.shape
    score_scale = HEAD_WIDTH ** (-0.5)
    items, columns = block_items(queries, sequence_labels, row_index)
    grad_blocks = out_grad.reshape(grouped_rows // QBLOCK, QBLOCK, kv_heads, repeat, head_size)

    def one_block(running, block_item):
        key_grad, value_grad = running
        q_block, id_block, row_block, total_block, grad_block = block_item
        allowed = (id_block[:, None] == sequence_labels[None, :]) & (
            columns[None, :] <= row_block[:, None]
        )
        scores = (
            jnp.einsum("qgrd,kgd->grqk", q_block, key_reduced, preferred_element_type=jnp.float32)
            * score_scale
        )
        shares = jnp.where(allowed[None, None], jnp.exp(scores), 0.0) / total_block
        low_shares = shares.astype(jnp.bfloat16)
        share_grad = jnp.einsum(
            "qgrd,kgd->grqk", grad_block, value_reduced, preferred_element_type=jnp.float32
        )
        row_inner = jnp.sum(shares * share_grad, axis=-1, keepdims=True)
        score_grad = (shares * (share_grad - row_inner)).astype(jnp.bfloat16)
        query_grad = (
            jnp.einsum(
                "grqk,kgd->qgrd", score_grad, key_reduced, preferred_element_type=jnp.float32
            )
            * score_scale
        )
        key_grad = (
            key_grad
            + jnp.einsum("grqk,qgrd->kgd", score_grad, q_block, preferred_element_type=jnp.float32)
            * score_scale
        )
        value_grad = value_grad + jnp.einsum(
            "grqk,qgrd->kgd", low_shares, grad_block, preferred_element_type=jnp.float32
        )
        return ((key_grad, value_grad), query_grad)

    zero_keys = jnp.zeros(key_reduced.shape, jnp.float32)
    (key_grad, value_grad), query_grad = lax.scan(
        one_block, (zero_keys, zero_keys), items + (totals, grad_blocks)
    )
    return (query_grad.reshape(grouped_rows, kv_heads * repeat, head_size), key_grad, value_grad)


def shift_perm(size, step):
    return [((place + step) % size, place) for place in range(size)]


def trade(values):
    return lax.ppermute(values, ("c", "h"), [(0, 0), (1, 2), (2, 1), (3, 3)])


def gather_tokens(own):
    places = lax.axis_size("l")
    parts = [own] + [lax.ppermute(own, "l", shift_perm(places, step)) for step in range(1, places)]
    half = jnp.concatenate(parts, axis=0)
    return jnp.concatenate([half, lax.ppermute(half, "c", shift_perm(2, 1))], axis=0)


def scatter_tokens(partial):
    places = lax.axis_size("l")
    half = partial.shape[0] // 2
    rows = half // places
    other = lax.ppermute(partial[half:].astype(jnp.bfloat16), "c", shift_perm(2, 1))
    total = partial[:half] + other.astype(jnp.float32)
    own = total[:rows]
    for step in range(1, places):
        sent = total[step * rows : (step + 1) * rows].astype(jnp.bfloat16)
        own = own + lax.ppermute(sent, "l", shift_perm(places, -step)).astype(jnp.float32)
    return own


def gather_weights(shard):
    core, upper = lax.axis_index("c"), lax.axis_index("h")
    far = lax.ppermute(shard, "h", shift_perm(2, 1))
    same = core == upper
    mine = jnp.where(same, shard, far)
    other = lax.ppermute(jnp.where(same, far, shard), "c", shift_perm(2, 1))
    rows = jnp.concatenate(
        [jnp.where(core == 0, mine, other), jnp.where(core == 0, other, mine)], axis=0
    )
    return lax.all_gather(rows, "d", axis=0, tiled=True)


def scatter_weights(partial):
    core, upper = lax.axis_index("c"), lax.axis_index("h")
    rows = lax.psum_scatter(partial.astype(jnp.bfloat16), "d", scatter_dimension=0, tiled=True)
    half = rows.shape[0] // 2
    first, second = rows[:half], rows[half:]
    mine = jnp.where(core == 0, first, second)
    other = lax.ppermute(jnp.where(core == 0, second, first), "c", shift_perm(2, 1))
    same = core == upper
    far = lax.ppermute(jnp.where(same, other, mine), "h", shift_perm(2, 1))
    return jnp.where(same, mine, other).astype(jnp.float32) + far.astype(jnp.float32)


def per_device(
    tokens,
    segment_ids,
    attn_gain,
    q_weight,
    key_matrix,
    value_matrix,
    o_weight,
    q_gain,
    k_gain,
    mlp_gain,
    gate_weight,
    up_weight,
    down_weight,
    cotangent,
):
    width = attn_gain.shape[1] * lax.axis_size("d") * 2
    own_rows = tokens.shape[0]
    places = lax.axis_size("l")
    core, place = lax.axis_index("c"), lax.axis_index("l")
    q_cols, kv_cols, ff_cols = q_weight.shape[2], key_matrix.shape[2], gate_weight.shape[2]

    tokens = trade(tokens)
    labels = trade(segment_ids)[0]
    attn_weights = gather_weights(
        jnp.concatenate([q_weight[0], key_matrix[0], value_matrix[0], o_weight[0]], axis=1)
    )
    mid_weights = gather_weights(jnp.concatenate([gate_weight[0], up_weight[0]], axis=1))
    down_full = gather_weights(down_weight[0])
    cotangent = trade(cotangent)

    gains = lax.all_gather(
        jnp.concatenate([attn_gain[0], mlp_gain[0], q_gain[0], k_gain[0]]), ("d", "c"), axis=0
    ).astype(jnp.float32)
    cut = attn_gain.shape[1]
    head_cut = q_gain.shape[1]
    attn_scale = gains[:, :cut].reshape(-1)
    mlp_scale = gains[:, cut : 2 * cut].reshape(-1)
    q_scale = gains[:, 2 * cut : 2 * cut + head_cut].reshape(-1)
    k_scale = gains[:, 2 * cut + head_cut :].reshape(-1)

    order = jnp.stack(
        [
            ((core + core_step) % 2) * places + (place + step) % places
            for core_step in range(2)
            for step in range(places)
        ]
    )
    row_index = (order[:, None] * own_rows + jnp.arange(own_rows, dtype=jnp.int32)[None, :]).reshape(-1)
    labels = labels.reshape(2 * places, own_rows)[order].reshape(-1)
    cosine, sine_table = rotary_tables(labels, row_index)

    stream = tokens.astype(jnp.float32)
    normed = gather_tokens(rms_scale(stream, attn_scale).astype(jnp.bfloat16))
    rows = normed.shape[0]
    head_count, kv_heads = q_cols // HEAD_WIDTH, kv_cols // HEAD_WIDTH
    q_full = attn_weights[:, :q_cols]
    k_full = attn_weights[:, q_cols : q_cols + kv_cols]
    v_full = attn_weights[:, q_cols + kv_cols : q_cols + 2 * kv_cols]
    o_full = attn_weights[:, q_cols + 2 * kv_cols :]
    queries = jnp.dot(normed, q_full, preferred_element_type=jnp.float32).reshape(
        rows, head_count, HEAD_WIDTH
    )
    keys = jnp.dot(normed, k_full, preferred_element_type=jnp.float32).reshape(
        rows, kv_heads, HEAD_WIDTH
    )
    value_reduced = (
        jnp.dot(normed, v_full, preferred_element_type=jnp.float32)
        .reshape(rows, kv_heads, HEAD_WIDTH)
        .astype(jnp.bfloat16)
    )
    query_reduced = rotate(rms_scale(queries, q_scale), cosine, sine_table).astype(jnp.bfloat16)
    key_reduced = rotate(rms_scale(keys, k_scale), cosine, sine_table).astype(jnp.bfloat16)
    query_reduced = query_reduced.reshape(rows, kv_heads, head_count // kv_heads, HEAD_WIDTH)
    attended, totals = attend_forward(
        query_reduced, key_reduced, value_reduced, labels, row_index
    )
    middle = stream + scatter_tokens(contract_cols(attended, o_full))

    normed_mid = gather_tokens(rms_scale(middle, mlp_scale).astype(jnp.bfloat16))
    gate_full, up_full = mid_weights[:, :ff_cols], mid_weights[:, ff_cols:]
    gate_raw = jnp.dot(normed_mid, gate_full, preferred_element_type=jnp.float32)
    up_raw = jnp.dot(normed_mid, up_full, preferred_element_type=jnp.float32)
    hidden = swiglu(gate_raw, up_raw).astype(jnp.bfloat16)
    branch = scatter_tokens(contract_cols(hidden, down_full))
    activations = trade((middle + branch).astype(jnp.bfloat16))

    grad_rows = gather_tokens(cotangent)
    gradient = cotangent.astype(jnp.float32)
    down_grad = scatter_weights(contract_rows(grad_rows, hidden))
    hidden_grad = jnp.dot(grad_rows, down_full, preferred_element_type=jnp.float32)
    _, pull_back = jax.vjp(swiglu, gate_raw, up_raw)
    gate_grad, up_grad = pull_back(hidden_grad)
    gate_low = gate_grad.astype(jnp.bfloat16)
    up_low = up_grad.astype(jnp.bfloat16)
    mid_grad = scatter_weights(
        jnp.concatenate(
            [
                contract_rows(normed_mid, gate_low).astype(jnp.bfloat16),
                contract_rows(normed_mid, up_low).astype(jnp.bfloat16),
            ],
            axis=1,
        )
    )
    normed_grad = scatter_tokens(
        contract_cols(gate_low, gate_full) + contract_cols(up_low, up_full)
    )
    _, pull_norm = jax.vjp(rms_scale, middle, mlp_scale)
    middle_grad, mlp_gain_grad = pull_norm(normed_grad)
    gradient = gradient + middle_grad

    grad_rows = gather_tokens(gradient.astype(jnp.bfloat16))
    out_grad = jnp.dot(grad_rows, o_full, preferred_element_type=jnp.float32).astype(jnp.bfloat16)
    o_wgrad = contract_rows(grad_rows, attended)
    query_grad, key_grad, value_grad = attend_backward(
        query_reduced,
        key_reduced,
        value_reduced,
        labels,
        row_index,
        totals,
        out_grad.reshape(query_reduced.shape),
    )

    def query_path(raw_values, scales):
        return rotate(rms_scale(raw_values, scales), cosine, sine_table)

    _, pull_query = jax.vjp(query_path, queries, q_scale)
    query_raw_grad, q_gain_grad = pull_query(query_grad)
    _, pull_key = jax.vjp(query_path, keys, k_scale)
    key_raw_grad, k_gain_grad = pull_key(key_grad)
    query_back = query_raw_grad.reshape(rows, -1).astype(jnp.bfloat16)
    key_back = key_raw_grad.reshape(rows, -1).astype(jnp.bfloat16)
    value_back = value_grad.reshape(rows, -1).astype(jnp.bfloat16)
    attn_grad = scatter_weights(
        jnp.concatenate(
            [
                contract_rows(normed, query_back).astype(jnp.bfloat16),
                contract_rows(normed, key_back).astype(jnp.bfloat16),
                contract_rows(normed, value_back).astype(jnp.bfloat16),
                o_wgrad.astype(jnp.bfloat16),
            ],
            axis=1,
        )
    )
    normed_grad = scatter_tokens(
        contract_cols(query_back, q_full)
        + contract_cols(key_back, k_full)
        + contract_cols(value_back, v_full)
    )
    _, pull_norm = jax.vjp(rms_scale, stream, attn_scale)
    stream_grad, attn_gain_grad = pull_norm(normed_grad)
    gradient = gradient + stream_grad
    moved = trade(gradient.astype(jnp.bfloat16))
    gradient = jnp.where(core == lax.axis_index("h"), gradient, moved.astype(jnp.float32))

    sums = lax.psum(
        jnp.concatenate([attn_gain_grad, mlp_gain_grad, q_gain_grad, k_gain_grad]),
        ("d", "c", "h", "l"),
    )
    row = lax.axis_index("d") * 2 + core

    def owned(start, whole, part):
        return lax.dynamic_slice(sums[start : start + whole], (row * part,), (part,))[None]

    return (
        activations,
        gradient,
        owned(0, width, cut),
        attn_grad[None, :, :q_cols],
        attn_grad[None, :, q_cols : q_cols + kv_cols],
        attn_grad[None, :, q_cols + kv_cols : q_cols + 2 * kv_cols],
        attn_grad[None, :, q_cols + 2 * kv_cols :],
        owned(2 * width, HEAD_WIDTH, head_cut),
        owned(2 * width + HEAD_WIDTH, HEAD_WIDTH, head_cut),
        owned(width, width, cut),
        mid_grad[None, :, :ff_cols],
        mid_grad[None, :, ff_cols:],
        down_grad[None],
    )


def solution(mesh):
    dp, tensor = mesh.shape["dp"], mesh.shape["tensor"]
    cut = Mesh(mesh.devices.reshape(dp // 2, 2, 2, tensor // 2), ("d", "c", "h", "l"))
    rows, cols = ("d", "c"), ("h", "l")
    tokens, labels = P(rows + cols, None), P(rows, None)
    gain, weight = P(None, rows), P(None, rows, cols)
    return jax.shard_map(
        per_device,
        mesh=cut,
        in_specs=(
            tokens,
            labels,
            gain,
            weight,
            weight,
            weight,
            weight,
            gain,
            gain,
            gain,
            weight,
            weight,
            weight,
            tokens,
        ),
        out_specs=(
            tokens,
            tokens,
            gain,
            weight,
            weight,
            weight,
            weight,
            gain,
            gain,
            gain,
            weight,
            weight,
            weight,
        ),
        check_vma=False,
    )
```

time: 1600 us -> 1070 us (0.67)
  waiting for transfers between devices: 1160 us -> 470 us
  local copies, waits for them, and re-layouts: 58.6 us -> 134 us
  starting transfers between devices: 1.14 us -> 55.5 us
  other arithmetic: 69.3 us -> 119 us
    reduce_scatter x11 -> x3, waiting for transfers between devices: 695 us -> 27.4 us  [scatter_weights(): lax.psum_scatter(partial.astype(jnp.bfloat16), 'd', scatter_dimension=0,...]
    all_gather x11 -> x3, waiting for transfers between devices: 463 us -> 0.02 us  [gather_weights(): return lax.all_gather(rows, 'd', axis=0, tiled=True)]
    ppermute x0 -> x33, waiting for transfers between devices: none -> 442 us  [the longest x4 126 us: scatter_tokens(): lax.ppermute(sent, 'l', shift_perm(places, -step)).astype(jnp.float32)]
    ppermute x0 -> x33, starting transfers between devices: none -> 54.9 us  [the longest x5 26.3 us: trade(): return lax.ppermute(values, ('c', 'h'), [(0, 0), (1, 2), (2, 1), (3, 3)])]
    concatenate x0 -> x13, other arithmetic: none -> 38.6 us  [the longest x1 15.3 us: per_device(): jnp.concatenate([contract_rows(normed_mid, gate_low).astype(jnp.bfloat16)...]
    unnamed x123 -> x210, local copies, waits for them, and re-layouts: 13.5 us -> 51.2 us
    psum x1, blocking collectives: 12.1 us -> 39.3 us  [per_device(): lax.psum(jnp.concatenate([attn_gain_grad, mlp_gain_grad, q_gain_grad, k_g...]
    all_gather x2 -> x0, blocking collectives: 19.5 us -> none  [the longest x1 10.6 us: gather_attention(): lax.all_gather(attn_gain[layer_index], 'dp', axis=0, tiled=True)]
  transfers between devices with their start and end apart: 22 -> 39, of which waited for: 19 -> 19; matrix products, arithmetic and copies ran while one was open for 17% -> 34% of each run, Pallas kernels for 0% -> 0%
where the time goes in v1:
time: 1070 us; the launch traced here: 1060 us
  waiting for transfers between devices  470 us (44%)
  matrix products  204 us (19%)
  local copies, waits for them, and re-layouts  134 us (13%)
  other arithmetic  119 us (11%)
  blocking collectives  65 us (6%)
  starting transfers between devices  55.5 us (5%)
  between operations  16.4 us (2%)
    ppermute x4, waiting for transfers between devices, scatter_tokens(): lax.ppermute(sent, 'l', shift_perm(places, -step)).astype(jnp.float32)  126 us
    ppermute x3, waiting for transfers between devices, gather_weights(): far = lax.ppermute(shard, 'h', shift_perm(2, 1))  122 us
    ppermute x3, waiting for transfers between devices, scatter_weights(): far = lax.ppermute(jnp.where(same, other, mine), 'h', shift_perm(2, 1))  113 us
    ppermute x4, waiting for transfers between devices, gather_tokens(): lax.ppermute(own, 'l', shift_perm(places, step))  74.4 us
    unnamed x210, local copies, waits for them, and re-layouts  51.2 us
    dot_general x7, matrix products, contract_rows(): lax.dot_general(left, right, (((0,), (0,)), ((), ())), preferred_element_...  50.7 us
    dot_general x7, matrix products, contract_cols(): lax.dot_general(left, right, (((1,), (1,)), ((), ())), preferred_element_...  46.3 us
    psum x1, blocking collectives, per_device(): lax.psum(jnp.concatenate([attn_gain_grad, mlp_gain_grad, q_gain_grad, k_g...  39.3 us
  transfers between devices with their start and end apart: 39, of which 19 were waited for; matrix products, arithmetic and copies ran while one was open for 34% of the time, Pallas kernels for 0%

profile of v1, /device:TPU:0, one launch (start us, length us, event | category | flops | bytes accessed | tf_op | source)
XLA Modules:
  0.0 1063.8 jit_solution(16250169278718028177)
XLA Ops:
  11.5 4.1 collective-permute-start.4
  15.6 34.4 %collective-permute-done.4 = bf16[256,1536]{0,1:T(8,128)(2,1)S(1)} collective-permute-done((bf16[256,1536]{0,1:T(8,128)(2,1)S(1)}, bf16[256,1536]{0,1:T(8,128)(2,1)S(1)}, u32[]{:S(2)}, u32[]{:S(2)}) %collective-permute-start.4) | collective-permute-done | bytes 786464 | tf_op jit(solution)/shard_map/ppermute | solution.py:174
  59.5 3.3 collective-permute-start.10
  64.4 25.7 %all-reduce.4 = bf16[4352]{0:T(1024)(128)(2,1)S(1)} all-reduce(bf16[4352]{0:T(1024)(128)(2,1)S(1)} %dynamic-update-slice), channel_id=2, replica_groups=mesh['d'=4,'c'=2,'h'=2,'l'=2] {'d','c'}, use_global_device_ids=true, to_apply=%add.4 | all-reduce | flops 4352 | bytes 17408
  102.3 51.4 %collective-permute-done.10 = bf16[256,3072]{0,1:T(8,128)(2,1)} collective-permute-done((bf16[256,3072]{0,1:T(8,128)(2,1)}, bf16[256,3072]{0,1:T(8,128)(2,1)}, u32[]{:S(2)}, u32[]{:S(2)}) %collective-permute-start.10) | collective-permute-done | bytes 1572896 | tf_op jit(solution)/shard_map/ppermute | solution.py:174
  155.6 9.9 collective-permute-done.2
  167.3 6.5 collective-permute-start.3
  180.8 3.5 multiply_reduce_fusion.8
  186.1 7.4 multiply_reduce_fusion.5
  200.7 3.8 copy.194
  204.5 5.0 copy.192
  210.8 7.0 fusion.70
  219.4 4.4 convolution_convert_fusion.8
  225.2 25.8 %while.28 = (s32[]{:T(128)}, bf16[2,576,2,2,128]{4,3,2,1,0:T(2,128)(2,1)S(1)}, f32[2,2,2,576,1]{3,2,1,4,0:T(2,128)}, s32[2,576]{1,0:T(2,128)}, s32[4,288]{1,0:T(...) while((s32[]{:T(128)}, ...), condition=%wide.region_7.8_spmd.clone, body=%wide.region_5.7_spmd.clone.sunk | while | flops 1379818368 | bytes 26884800 | solution.py:92
  230.6 3.1 bitcast_reduce_fusion.2
  233.7 3.1 fusion.140
  243.5 3.1 bitcast_reduce_fusion.2
  246.6 3.1 fusion.140
  252.1 15.6 %reshape.558 = bf16[1152,512]{1,0:T(8,128)(2,1)S(1)} reshape(bf16[2,576,2,2,128]{4,3,2,1,0:T(2,128)(2,1)} %copy-done.46) | data formatting | bytes 2359296 | tf_op jit(solution)/shard_map/reshape | solution.py:93
  267.7 4.6 fusion.72
  279.7 36.7 %collective-permute-done.12 = bf16[256,1536]{0,1:T(8,128)(2,1)S(1)} collective-permute-done((bf16[256,1536]{0,1:T(8,128)(2,1)S(1)}, bf16[256,1536]{0,1:T(8,128)(2,1)S(1)}, u32[]{:S(2)}, u32[]{:S(2)}) %collective-permute-start.12) | collective-permute-done | bytes 786464 | tf_op jit(solution)/shard_map/ppermute | solution.py:174
  316.6 10.4 collective-permute-start.17
  335.1 37.7 %collective-permute-done.7 = bf16[288,2048]{1,0:T(8,128)(2,1)} collective-permute-done((bf16[288,2048]{1,0:T(8,128)(2,1)}, bf16[288,2048]{1,0:T(8,128)(2,1)}, u32[]{:S(2)}, u32[]{:S(2)}) %collective-permute-start.7) | collective-permute-done | bytes 1179680 | tf_op jit(solution)/shard_map/ppermute | solution.py:168
  375.8 22.1 %collective-permute-done.18 = bf16[288,2048]{1,0:T(8,128)(2,1)S(1)} collective-permute-done((bf16[288,2048]{1,0:T(8,128)(2,1)}, bf16[288,2048]{1,0:T(8,128)(2,1)S(1)}, u32[]{:S(2)}, u32[]{:S(2)}) %collective-permute-start.18) | collective-permute-done | bytes 1179680 | tf_op jit(solution)/shard_map/ppermute | solution.py:154
  399.5 15.3 %collective-permute-done.8 = bf16[288,2048]{1,0:T(8,128)(2,1)S(1)} collective-permute-done((bf16[288,2048]{1,0:T(8,128)(2,1)S(1)}, bf16[288,2048]{1,0:T(8,128)(2,1)S(1)}, u32[]{:S(2)}, u32[]{:S(2)}) %collective-permute-start.8) | collective-permute-done | bytes 1179680 | tf_op jit(solution)/shard_map/ppermute | solution.py:154
  419.8 12.7 %fusion.52 = f32[1152,1536]{1,0:T(8,128)} fusion(bf16[2048,3072]{0,1:T(8,128)(2,1)} %all-gather.7.cloned.1.call-done, bf16[576,2048]{1,0:T(8,128)(2,1)} %collective-permute-done.9, bf16[288,2048]{1,0:T(8,128)(2,1)} %copy-done.51, bf16[288,2048]{1,0:T(8,128)(2,1)S(1)} %multiply_convert_fusion.2), kind=kOutput, calls=%fused_computation.75 | convolution fusion | flops 7261913088 | bytes 18087936 | tf_op jit(solution)/shard_map/dot_general | solution.py:278
  432.6 11.0 %fusion.56 = f32[1152,1536]{1,0:T(8,128)} fusion(bf16[2048,3072]{0,1:T(8,128)(2,1)S(1)} %copy-done.94, bf16[576,2048]{1,0:T(8,128)(2,1)} %collective-permute-done.9, bf16[288,2048]{1,0:T(8,128)(2,1)S(1)} %copy-done.52, bf16[288,2048]{1,0:T(8,128)(2,1)S(1)} %multiply_convert_fusion.2), kind=kOutput, calls=%fused_computation.79 | convolution fusion | flops 7261913088 | bytes 18087936 | tf_op jit(solution)/shard_map/dot_general | solution.py:277
  443.5 18.9 %multiply_convert_fusion = (bf16[1152,1536]{1,0:T(8,128)(2,1)}, bf16[1152,1536]{1,0:T(8,128)(2,1)}, bf16[1152,1536]{1,0:T(8,128)(2,1)}) fusion(f32[1152,1536]{1,0:T(8,128)} %fusion.56, f32[1152,1536]{1,0:T(8,128)} %fusion.52, bf16[1152,2048]{1,0:T(8,128)(2,1)} %copy-done.64, bf16[2048,1536]{0,1:T(8,128)(2,1)} %all-gather.9.cloned.1.call-done), kind=kOutput, calls=%fused_computation.69 | convolution fusion | flops 7276068864 | bytes 35782656 | tf_op jit(solution)/shard_map/dot_general | solution.py:286
  462.5 11.2 %fusion.54 = f32[1152,2048]{1,0:T(8,128)S(1)} fusion(bf16[1152,1536]{1,0:T(8,128)(2,1)} %get-tuple-element.461, bf16[2048,3072]{0,1:T(8,128)(2,1)} %all-gather.7.cloned.1.call-done), kind=kOutput, calls=%fused_computation.77 | convolution fusion | flops 7247757312 | bytes 19267584 | tf_op jit(solution)/shard_map/dot_general | solution.py:52
  473.7 10.9 %convolution_add_fusion.2 = f32[1152,2048]{1,0:T(8,128)S(1)} fusion(f32[1152,2048]{1,0:T(8,128)S(1)} %fusion.54, bf16[1152,1536]{1,0:T(8,128)(2,1)} %get-tuple-element.460, bf16[2048,3072]{0,1:T(8,128)(2,1)} %all-gather.7.cloned.1.call-done), kind=kOutput, calls=%fused_computation.62 | convolution fusion | flops 7250116608 | bytes 28704768 | tf_op jit(solution)/shard_map/dot_general | solution.py:52
  485.2 3.8 copy-done.29
  489.3 10.0 fusion.102
  499.9 3.1 slice_add_fusion.1
  506.5 25.5 %collective-permute-done.21 = bf16[288,2048]{1,0:T(8,128)(2,1)S(1)} collective-permute-done((bf16[288,2048]{1,0:T(8,128)(2,1)S(1)}, bf16[288,2048]{1,0:T(8,128)(2,1)S(1)}, u32[]{:S(2)}, u32[]{:S(2)}) %collective-permute-start.21) | collective-permute-done | bytes 1179680 | tf_op jit(solution)/shard_map/ppermute | solution.py:168
  533.4 23.3 %collective-permute-done.15 = bf16[288,2048]{1,0:T(8,128)(2,1)S(1)} collective-permute-done((bf16[288,2048]{1,0:T(8,128)(2,1)S(1)}, bf16[288,2048]{1,0:T(8,128)(2,1)S(1)}, u32[]{:S(2)}, u32[]{:S(2)}) %collective-permute-start.15) | collective-permute-done | bytes 1179680 | tf_op jit(solution)/shard_map/ppermute | solution.py:168
  556.7 4.4 fusion.95
  561.4 27.1 %collective-permute-done.22 = bf16[288,2048]{1,0:T(8,128)(2,1)S(1)} collective-permute-done((bf16[288,2048]{1,0:T(8,128)(2,1)S(1)}, bf16[288,2048]{1,0:T(8,128)(2,1)S(1)}, u32[]{:S(2)}, u32[]{:S(2)}) %collective-permute-start.22) | collective-permute-done | bytes 1179680 | tf_op jit(solution)/shard_map/ppermute | solution.py:154
  591.2 13.1 %convolution_convert_fusion = bf16[2048,1536]{0,1:T(8,128)(2,1)} fusion(bf16[1152,2048]{1,0:T(8,128)(2,1)} %copy-done.64, bf16[1152,1536]{1,0:T(8,128)(2,1)} %get-tuple-element.462), kind=kOutput, calls=%fused_computation.63 | convolution fusion | flops 7250903040 | bytes 14548992 | tf_op jit(solution)/shard_map/dot_general | solution.py:46
  604.4 6.3 convolution_convert_fusion.5
  610.7 3.8 reshape_reshape.5
  614.5 55.6 %while.29 = (s32[]{:T(128)}, f32[1152,2,128]{0,2,1:T(8,128)S(1)}, f32[1152,2,128]{0,2,1:T(8,128)S(1)}, f32[2,576,2,2,128]{4,1,0,3,2:T(8,128)}, bf16[2,576,2,2,12...) while((s32[]{:T(128)}, f32[1152,2,128]{0,2,1:T(8,128)S(1)}, ...), condition=%wide.region_12.13_spmd.clone, body=%wide.region_10.12_spmd.clone.sunk | while | flops 3425033216 | bytes 203141424 | solution.py:138
  622.2 4.0 fusion.148
  635.1 4.2 fusion.150
  649.7 4.0 fusion.148
  662.7 4.4 fusion.150
  670.1 3.3 copy.175
  681.6 3.2 convolution_convert_fusion.7
  684.8 3.4 convolution_convert_fusion.6
  688.2 4.7 convolution_convert_fusion.4
  693.4 5.0 convolution_convert_fusion.3
  698.5 12.4 %pad_maximum_fusion.1 = bf16[2048,1536]{0,1:T(8,128)(2,1)} fusion(bf16[2048,512]{0,1:T(8,128)(2,1)S(1)} %convolution_convert_fusion.4, bf16[2048,256]{0,1:T(8,128)(2,1)S(1)} %convolution_convert_fusion.6, bf16[2048,256]{0,1:T(8,128)(2,1)S(1)} %convolution_convert_fusion.7, bf16[2048,512]{0,1:T(8,128)(2,1)S(1)} %convolution_convert_fusion.3), kind=kLoop, calls=%fused_computation.73 | loop fusion | flops 25165824 | bytes 12582912 | tf_op jit(solution)/shard_map/concatenate | solution.py:331
  712.5 11.2 %convolution_convert_fusion.2 = bf16[2048,1536]{0,1:T(8,128)(2,1)S(1)} fusion(bf16[1152,1536]{1,0:T(8,128)(2,1)} %get-tuple-element.461, bf16[576,2048]{1,0:T(8,128)(2,1)} %collective-permute-done.9, bf16[288,2048]{1,0:T(8,128)(2,1)S(1)} %copy-done.53, bf16[288,2048]{1,0:T(8,128)(2,1)S(1)} %copy-done.31), kind=kOutput, calls=%fused_computation.65 | convolution fusion | flops 7265058816 | bytes 14548992 | tf_op jit(solution)/shard_map/dot_general | solution.py:46
  723.7 10.2 convolution_convert_fusion.1
  733.9 15.3 %pad_maximum_fusion = bf16[2048,3072]{0,1:T(8,128)(2,1)} fusion(bf16[2048,1536]{0,1:T(8,128)(2,1)S(1)} %convolution_convert_fusion.1, bf16[2048,1536]{0,1:T(8,128)(2,1)S(1)} %convolution_convert_fusion.2), kind=kLoop, calls=%fused_computation.58 | loop fusion | flops 25165824 | bytes 25165824 | tf_op jit(solution)/shard_map/concatenate | solution.py:292
  750.6 4.2 fusion.74
  770.4 39.9 %collective-permute-done.25 = bf16[288,2048]{1,0:T(8,128)(2,1)S(1)} collective-permute-done((bf16[288,2048]{1,0:T(8,128)(2,1)}, bf16[288,2048]{1,0:T(8,128)(2,1)S(1)}, u32[]{:S(2)}, u32[]{:S(2)}) %collective-permute-start.25) | collective-permute-done | bytes 1179680 | tf_op jit(solution)/shard_map/ppermute | solution.py:168
  810.4 3.6 fusion.61
  814.0 39.3 %psum.7 = f32[4352]{0:T(1024)S(1)} all-reduce(f32[4352]{0:T(1024)S(1)} %pad_maximum_fusion.20), channel_id=1, replica_groups=mesh['d'=4,'c'=2,'h'=2,'l'=2] {'d','c','h','l'}, use_global_device_ids=true, to_apply=%region_20.21 | all-reduce | flops 4352 | bytes 34816 | tf_op jit(solution)/shard_map/psum | solution.py:352
  855.3 4.6 fusion.93
  859.8 10.6 collective-permute-start.26
  877.6 27.4 %reduce-scatter.6.cloned.1.call-done = bf16[512,3072]{0,1:T(8,128)(2,1)} async-done(((bf16[2048,3072]{0,1:T(8,128)(2,1)}), bf16[512,3072]{0,1:T(8,128)(2,1)}) %reduce-scatter.6.cloned.1.call-update) | async-done | bytes 3145744 | tf_op jit(solution)/shard_map/reduce_scatter | solution.py:186
  920.6 79.5 %collective-permute-done.32 = bf16[256,1536]{0,1:T(8,128)(2,1)S(1)} collective-permute-done((bf16[256,1536]{0,1:T(8,128)(2,1)S(1)}, bf16[256,1536]{0,1:T(8,128)(2,1)S(1)}, u32[]{:S(2)}, u32[]{:S(2)}) %collective-permute-start.32) | collective-permute-done | bytes 786464 | tf_op jit(solution)/shard_map/ppermute | solution.py:192
  1004.6 12.4 %collective-permute-done.28 = bf16[256,1536]{0,1:T(8,128)(2,1)} collective-permute-done((bf16[256,1536]{0,1:T(8,128)(2,1)}, bf16[256,1536]{0,1:T(8,128)(2,1)}, u32[]{:S(2)}, u32[]{:S(2)}) %collective-permute-start.28) | collective-permute-done | bytes 786464 | tf_op jit(solution)/shard_map/ppermute | solution.py:192
  1029.6 20.6 %collective-permute-done.30 = bf16[256,3072]{0,1:T(8,128)(2,1)} collective-permute-done((bf16[256,3072]{0,1:T(8,128)(2,1)}, bf16[256,3072]{0,1:T(8,128)(2,1)}, u32[]{:S(2)}, u32[]{:S(2)}) %collective-permute-start.30) | collective-permute-done | bytes 1572896 | tf_op jit(solution)/shard_map/ppermute | solution.py:192
  (458 shorter events, 212.8 us)
Async XLA Ops:
  7.2 172.5 %all-gather.5.cloned.1.call-start = ((), (), s32[]{:S(2)}) async-start(), calls=%async_computation.3 | async-start | bytes 7864320 | tf_op jit(solution)/shard_map/all_gather | solution.py:181
  11.5 38.5 %collective-permute-start.4 = (bf16[256,1536]{0,1:T(8,128)(2,1)S(1)}, bf16[256,1536]{0,1:T(8,128)(2,1)S(1)}, u32[]{:S(2)}, u32[]{:S(2)}) collective-permute-start(bf16[256,1536]{0,1:T(8,128)(2,1)S(1)} %pad_maximum_fusion.15), channel_id=1, source_target_pairs={{2,0},{0,2},{3,1},{1,3},{6,4},{4,6},{7,5},{5,7},{10,8},{8,10},{11,... | collective-permute-start | bytes 2359304 | tf_op jit(solution)/shard_map/ppermute | solution.py:174
  50.2 2.4 collective-permute-start.5
  54.2 365.6 %all-gather.7.cloned.1.call-start = ((), (), s32[]{:S(2)}) async-start(), calls=%async_computation.4 | async-start | bytes 15728640 | tf_op jit(solution)/shard_map/all_gather | solution.py:181
  54.3 42.5 %collective-permute-start = (bf16[288,2048]{1,0:T(8,128)(2,1)}, bf16[288,2048]{1,0:T(8,128)(2,1)S(1)}, u32[]{:S(2)}, u32[]{:S(2)}) collective-permute-start(bf16[288,2048]{1,0:T(8,128)(2,1)} %param.18), channel_id=1, source_target_pairs={{0,0},{2,4},{4,2},{6,6},{1,1},{3,5},{5,3},{7,7},{8,8},{10,12},{12,... | collective-permute-start | bytes 3538952 | tf_op jit(solution)/shard_map/ppermute | solution.py:149
  56.3 38.7 %collective-permute-start.1 = (s32[1,1152]{1,0:T(1,128)}, s32[1,1152]{1,0:T(1,128)S(1)}, u32[]{:S(2)}, u32[]{:S(2)}) collective-permute-start(s32[1,1152]{1,0:T(1,128)} %param.19), channel_id=1, source_target_pairs={{0,0},{2,4},{4,2},{6,6},{1,1},{3,5},{5,3},{7,7},{8,8},{10,12},{12,... | collective-permute-start | bytes 13832 | tf_op jit(solution)/shard_map/ppermute | solution.py:149
  59.5 94.2 %collective-permute-start.10 = (bf16[256,3072]{0,1:T(8,128)(2,1)}, bf16[256,3072]{0,1:T(8,128)(2,1)}, u32[]{:S(2)}, u32[]{:S(2)}) collective-permute-start(bf16[256,3072]{0,1:T(8,128)(2,1)} %pad_maximum_fusion.13), channel_id=1, source_target_pairs={{2,0},{0,2},{3,1},{1,3},{6,4},{4,6},{7,5},{5,7},{10,8},{8,10},{11,... | collective-permute-start | bytes 4718600 | tf_op jit(solution)/shard_map/ppermute | solution.py:174
  97.1 58.4 %copy-start.82 = (f32[288]{0:T(512)}, f32[288]{0:T(512)S(1)}, u32[]{:S(2)}) copy-start(f32[288]{0:T(512)S(1)} %fusion.65) | copy-start | bytes 3460
  97.1 58.4 %copy-start.80 = (f32[288]{0:T(512)}, f32[288]{0:T(512)S(1)}, u32[]{:S(2)}) copy-start(f32[288]{0:T(512)S(1)} %fusion.88) | copy-start | bytes 3460
  97.4 68.1 %copy-start.32 = (bf16[288,2048]{1,0:T(8,128)(2,1)}, bf16[288,2048]{1,0:T(8,128)(2,1)S(1)}, u32[]{:S(2)}) copy-start(bf16[288,2048]{1,0:T(8,128)(2,1)S(1)} %fusion.60) | copy-start | bytes 3538948
  97.4 68.0 %collective-permute-start.2 = (bf16[288,2048]{1,0:T(8,128)(2,1)S(1)}, bf16[288,2048]{1,0:T(8,128)(2,1)S(1)}, u32[]{:S(2)}, u32[]{:S(2)}) collective-permute-start(bf16[288,2048]{1,0:T(8,128)(2,1)S(1)} %fusion.60), channel_id=1, source_target_pairs={{1,0},{0,1},{3,2},{2,3},{5,4},{4,5},{7,6},{6,7},{9,8},{8,9},{11,10... | collective-permute-start | bytes 3538952 | tf_op jit(solution)/shard_map/ppermute | solution.py:154
  155.5 20.9 %collective-permute-start.11 = (bf16[256,3072]{0,1:T(8,128)(2,1)S(1)}, bf16[256,3072]{0,1:T(8,128)(2,1)S(1)}, u32[]{:S(2)}, u32[]{:S(2)}) collective-permute-start(bf16[256,3072]{0,1:T(8,128)(2,1)S(1)} %broadcast_select_fusion.1), channel_id=1, source_target_pairs={{4,0},{0,4},{5,1},{1,5},{6,2},{2,6},{7,3},{3,7},{12,8},{8,12},{13,... | collective-permute-start | bytes 4718600 | tf_op jit(solution)/shard_map/ppermute | solution.py:177
  167.3 12.3 %collective-permute-start.3 = (bf16[576,2048]{1,0:T(8,128)(2,1)}, bf16[576,2048]{1,0:T(8,128)(2,1)}, u32[]{:S(2)}, u32[]{:S(2)}) collective-permute-start(bf16[576,2048]{1,0:T(8,128)(2,1)} %pad_maximum_fusion.6), channel_id=1, source_target_pairs={{4,0},{0,4},{5,1},{1,5},{6,2},{2,6},{7,3},{3,7},{12,8},{8,12},{13,... | collective-permute-start | bytes 7077896 | tf_op jit(solution)/shard_map/ppermute | solution.py:156
  176.3 9.0 copy-start.22
  176.4 9.0 copy-start.24
  179.2 264.3 %all-gather.9.cloned.1.call-start = ((), (), s32[]{:S(2)}) async-start(), calls=%async_computation.5 | async-start | bytes 7864320 | tf_op jit(solution)/shard_map/all_gather | solution.py:181
  252.0 20.3 %copy-start.12 = (bf16[1152,2,128]{2,0,1:T(8,128)(2,1)}, bf16[1152,2,128]{2,0,1:T(8,128)(2,1)S(1)}, u32[]{:S(2)}) copy-start(bf16[1152,2,128]{2,0,1:T(8,128)(2,1)S(1)} %get-tuple-element.774) | copy-start | bytes 1769476
  252.0 20.3 %copy-start.14 = (bf16[1152,2,128]{2,0,1:T(8,128)(2,1)}, bf16[1152,2,128]{2,0,1:T(8,128)(2,1)S(1)}, u32[]{:S(2)}) copy-start(bf16[1152,2,128]{2,0,1:T(8,128)(2,1)S(1)} %get-tuple-element.775) | copy-start | bytes 1769476
  252.0 20.3 %copy-start.16 = (bf16[2,576,2,2,128]{4,1,3,2,0:T(8,128)(2,1)}, bf16[2,576,2,2,128]{4,1,3,2,0:T(8,128)(2,1)S(1)}, u32[]{:S(2)}) copy-start(bf16[2,576,2,2,128]{4,1,3,2,0:T(8,128)(2,1)S(1)} %get-tuple-element.776) | copy-start | bytes 3538948
  252.0 20.3 %copy-start.58 = (s32[4,288]{1,0:T(4,128)}, s32[4,288]{1,0:T(4,128)S(1)}, u32[]{:S(2)}) copy-start(s32[4,288]{1,0:T(4,128)S(1)} %get-tuple-element.818) | copy-start | bytes 13828
  252.0 20.4 %copy-start.69 = (s32[2,576]{1,0:T(2,128)}, s32[2,576]{1,0:T(2,128)S(1)}, u32[]{:S(2)}) copy-start(s32[2,576]{1,0:T(2,128)S(1)} %get-tuple-element.827) | copy-start | bytes 13828
  276.7 50.3 %collective-permute-start.6 = (bf16[576,2048]{1,0:T(8,128)(2,1)}, bf16[576,2048]{1,0:T(8,128)(2,1)S(1)}, u32[]{:S(2)}, u32[]{:S(2)}) collective-permute-start(bf16[576,2048]{1,0:T(8,128)(2,1)} %slice.347), channel_id=1, source_target_pairs={{4,0},{0,4},{5,1},{1,5},{6,2},{2,6},{7,3},{3,7},{12,8},{8,12},{13,... | collective-permute-start | bytes 7077896 | tf_op jit(solution)/shard_map/ppermute | solution.py:163
  279.7 36.7 %collective-permute-start.12 = (bf16[256,1536]{0,1:T(8,128)(2,1)S(1)}, bf16[256,1536]{0,1:T(8,128)(2,1)S(1)}, u32[]{:S(2)}, u32[]{:S(2)}) collective-permute-start(bf16[256,1536]{0,1:T(8,128)(2,1)S(1)} %bitcast.247), channel_id=1, source_target_pairs={{2,0},{0,2},{3,1},{1,3},{6,4},{4,6},{7,5},{5,7},{10,8},{8,10},{11,... | collective-permute-start | bytes 2359304 | tf_op jit(solution)/shard_map/ppermute | solution.py:174
  316.5 14.9 %collective-permute-start.13 = (bf16[256,1536]{0,1:T(8,128)(2,1)S(1)}, bf16[256,1536]{0,1:T(8,128)(2,1)S(1)}, u32[]{:S(2)}, u32[]{:S(2)}) collective-permute-start(bf16[256,1536]{0,1:T(8,128)(2,1)S(1)} %broadcast_select_fusion.9), channel_id=1, source_target_pairs={{4,0},{0,4},{5,1},{1,5},{6,2},{2,6},{7,3},{3,7},{12,8},{8,12},{13,... | collective-permute-start | bytes 2359304 | tf_op jit(solution)/shard_map/ppermute | solution.py:177
  316.6 17.3 %collective-permute-start.17 = (bf16[288,2048]{1,0:T(8,128)(2,1)}, bf16[288,2048]{1,0:T(8,128)(2,1)}, u32[]{:S(2)}, u32[]{:S(2)}) collective-permute-start(bf16[288,2048]{1,0:T(8,128)(2,1)} %param.31), channel_id=1, source_target_pairs={{0,0},{2,4},{4,2},{6,6},{1,1},{3,5},{5,3},{7,7},{8,8},{10,12},{12,... | collective-permute-start | bytes 3538952 | tf_op jit(solution)/shard_map/ppermute | solution.py:149
  331.4 41.4 %collective-permute-start.7 = (bf16[288,2048]{1,0:T(8,128)(2,1)}, bf16[288,2048]{1,0:T(8,128)(2,1)}, u32[]{:S(2)}, u32[]{:S(2)}) collective-permute-start(bf16[288,2048]{1,0:T(8,128)(2,1)} %slice.351), channel_id=1, source_target_pairs={{1,0},{0,1},{3,2},{2,3},{5,4},{4,5},{7,6},{6,7},{9,8},{8,9},{11,10... | collective-permute-start | bytes 3538952 | tf_op jit(solution)/shard_map/ppermute | solution.py:168
  332.5 40.3 %copy-start.8 = (bf16[288,2048]{1,0:T(8,128)(2,1)S(1)}, bf16[288,2048]{1,0:T(8,128)(2,1)}, u32[]{:S(2)}) copy-start(bf16[288,2048]{1,0:T(8,128)(2,1)} %copy-done.7) | copy-start | bytes 3538948
  333.8 538.5 %reduce-scatter.8.cloned.1.call-start = ((), (), s32[]{:S(2)}) async-start(), calls=%async_computation.8 | async-start | bytes 7864320 | tf_op jit(solution)/shard_map/reduce_scatter | solution.py:186
  333.9 64.0 %collective-permute-start.18 = (bf16[288,2048]{1,0:T(8,128)(2,1)}, bf16[288,2048]{1,0:T(8,128)(2,1)S(1)}, u32[]{:S(2)}, u32[]{:S(2)}) collective-permute-start(bf16[288,2048]{1,0:T(8,128)(2,1)} %collective-permute-done.17), channel_id=1, source_target_pairs={{1,0},{0,1},{3,2},{2,3},{5,4},{4,5},{7,6},{6,7},{9,8},{8,9},{11,10... | collective-permute-start | bytes 3538952 | tf_op jit(solution)/shard_map/ppermute | solution.py:154
  375.7 56.8 %copy-start.30 = (bf16[288,2048]{1,0:T(8,128)(2,1)}, bf16[288,2048]{1,0:T(8,128)(2,1)S(1)}, u32[]{:S(2)}) copy-start(bf16[288,2048]{1,0:T(8,128)(2,1)S(1)} %multiply_convert_fusion.2) | copy-start | bytes 3538948
  375.8 39.0 %collective-permute-start.8 = (bf16[288,2048]{1,0:T(8,128)(2,1)S(1)}, bf16[288,2048]{1,0:T(8,128)(2,1)S(1)}, u32[]{:S(2)}, u32[]{:S(2)}) collective-permute-start(bf16[288,2048]{1,0:T(8,128)(2,1)S(1)} %multiply_convert_fusion.2), channel_id=1, source_target_pairs={{1,0},{0,1},{3,2},{2,3},{5,4},{4,5},{7,6},{6,7},{9,8},{8,9},{11,10... | collective-permute-start | bytes 3538952 | tf_op jit(solution)/shard_map/ppermute | solution.py:154
  399.4 17.3 %collective-permute-start.19 = (bf16[576,2048]{1,0:T(8,128)(2,1)S(1)}, bf16[576,2048]{1,0:T(8,128)(2,1)S(1)}, u32[]{:S(2)}, u32[]{:S(2)}) collective-permute-start(bf16[576,2048]{1,0:T(8,128)(2,1)S(1)} %pad_maximum_fusion.8), channel_id=1, source_target_pairs={{4,0},{0,4},{5,1},{1,5},{6,2},{2,6},{7,3},{3,7},{12,8},{8,12},{13,... | collective-permute-start | bytes 7077896 | tf_op jit(solution)/shard_map/ppermute | solution.py:156
  415.1 4.7 collective-permute-start.9
  419.8 12.7 %copy-start.52 = (bf16[288,2048]{1,0:T(8,128)(2,1)S(1)}, bf16[288,2048]{1,0:T(8,128)(2,1)}, u32[]{:S(2)}) copy-start(bf16[288,2048]{1,0:T(8,128)(2,1)} %copy-done.51) | copy-start | bytes 3538948
  419.8 12.7 %copy-start.94 = (bf16[2048,3072]{0,1:T(8,128)(2,1)S(1)}, bf16[2048,3072]{0,1:T(8,128)(2,1)}, u32[]{:S(2)}) copy-start(bf16[2048,3072]{0,1:T(8,128)(2,1)} %all-gather.7.cloned.1.call-done) | copy-start | bytes 37748740
  485.0 14.9 %collective-permute-start.20 = (bf16[576,2048]{1,0:T(8,128)(2,1)S(1)}, bf16[576,2048]{1,0:T(8,128)(2,1)S(1)}, u32[]{:S(2)}, u32[]{:S(2)}) collective-permute-start(bf16[576,2048]{1,0:T(8,128)(2,1)S(1)} %slice.345), channel_id=1, source_target_pairs={{4,0},{0,4},{5,1},{1,5},{6,2},{2,6},{7,3},{3,7},{12,8},{8,12},{13,... | collective-permute-start | bytes 7077896 | tf_op jit(solution)/shard_map/ppermute | solution.py:163
  499.6 4.6 collective-permute-start.14
  503.1 28.9 %collective-permute-start.21 = (bf16[288,2048]{1,0:T(8,128)(2,1)S(1)}, bf16[288,2048]{1,0:T(8,128)(2,1)S(1)}, u32[]{:S(2)}, u32[]{:S(2)}) collective-permute-start(bf16[288,2048]{1,0:T(8,128)(2,1)S(1)} %slice.349), channel_id=1, source_target_pairs={{1,0},{0,1},{3,2},{2,3},{5,4},{4,5},{7,6},{6,7},{9,8},{8,9},{11,10... | collective-permute-start | bytes 3538952 | tf_op jit(solution)/shard_map/ppermute | solution.py:168
  505.5 51.2 %collective-permute-start.15 = (bf16[288,2048]{1,0:T(8,128)(2,1)S(1)}, bf16[288,2048]{1,0:T(8,128)(2,1)S(1)}, u32[]{:S(2)}, u32[]{:S(2)}) collective-permute-start(bf16[288,2048]{1,0:T(8,128)(2,1)S(1)} %slice.350), channel_id=1, source_target_pairs={{1,0},{0,1},{3,2},{2,3},{5,4},{4,5},{7,6},{6,7},{9,8},{8,9},{11,10... | collective-permute-start | bytes 3538952 | tf_op jit(solution)/shard_map/ppermute | solution.py:168
  561.1 43.2 %copy-start.37 = (bf16[288,2048]{1,0:T(8,128)(2,1)}, bf16[288,2048]{1,0:T(8,128)(2,1)S(1)}, u32[]{:S(2)}) copy-start(bf16[288,2048]{1,0:T(8,128)(2,1)S(1)} %get-tuple-element.446) | copy-start | bytes 3538948
  561.1 27.4 %collective-permute-start.22 = (bf16[288,2048]{1,0:T(8,128)(2,1)S(1)}, bf16[288,2048]{1,0:T(8,128)(2,1)S(1)}, u32[]{:S(2)}, u32[]{:S(2)}) collective-permute-start(bf16[288,2048]{1,0:T(8,128)(2,1)S(1)} %get-tuple-element.446), channel_id=1, source_target_pairs={{1,0},{0,1},{3,2},{2,3},{5,4},{4,5},{7,6},{6,7},{9,8},{8,9},{11,10... | collective-permute-start | bytes 3538952 | tf_op jit(solution)/shard_map/ppermute | solution.py:154
  591.2 13.2 %collective-permute-start.23 = (bf16[576,2048]{1,0:T(8,128)(2,1)}, bf16[576,2048]{1,0:T(8,128)(2,1)}, u32[]{:S(2)}, u32[]{:S(2)}) collective-permute-start(bf16[576,2048]{1,0:T(8,128)(2,1)} %pad_maximum_fusion.9), channel_id=1, source_target_pairs={{4,0},{0,4},{5,1},{1,5},{6,2},{2,6},{7,3},{3,7},{12,8},{8,12},{13,... | collective-permute-start | bytes 7077896 | tf_op jit(solution)/shard_map/ppermute | solution.py:156
  604.3 270.4 %reduce-scatter.4.cloned.1.call-start = ((), (), s32[]{:S(2)}) async-start(), calls=%async_computation.6 | async-start | bytes 7864320 | tf_op jit(solution)/shard_map/reduce_scatter | solution.py:186
  710.9 194.1 %reduce-scatter.6.cloned.1.call-start = ((), (), s32[]{:S(2)}) async-start(), calls=%async_computation.7 | async-start | bytes 15728640 | tf_op jit(solution)/shard_map/reduce_scatter | solution.py:186
  712.5 11.2 %copy-start.97 = (bf16[1152,1536]{1,0:T(8,128)(2,1)S(1)}, bf16[1152,1536]{1,0:T(8,128)(2,1)}, u32[]{:S(2)}) copy-start(bf16[1152,1536]{1,0:T(8,128)(2,1)} %get-tuple-element.460) | copy-start | bytes 10616836
  760.5 4.6 collective-permute-start.24
  760.8 9.6 collective-permute-start.16
  768.4 42.0 %copy-start.9 = (bf16[288,2048]{1,0:T(8,128)(2,1)S(1)}, bf16[288,2048]{1,0:T(8,128)(2,1)}, u32[]{:S(2)}) copy-start(bf16[288,2048]{1,0:T(8,128)(2,1)} %copy-done.7) | copy-start | bytes 3538948
  768.4 42.0 %copy-start.72 = (f32[1,2,8,128]{3,1,2,0:T(2,128)S(1)}, f32[1,2,8,128]{3,1,2,0:T(2,128)}, u32[]{:S(2)}) copy-start(f32[1,2,8,128]{3,1,2,0:T(2,128)} %copy-done.71) | copy-start | bytes 24580
  768.4 42.0 %copy-start.81 = (f32[288]{0:T(512)S(1)}, f32[288]{0:T(512)}, u32[]{:S(2)}) copy-start(f32[288]{0:T(512)} %copy-done.80) | copy-start | bytes 3460
  769.6 40.8 %collective-permute-start.25 = (bf16[288,2048]{1,0:T(8,128)(2,1)}, bf16[288,2048]{1,0:T(8,128)(2,1)S(1)}, u32[]{:S(2)}, u32[]{:S(2)}) collective-permute-start(bf16[288,2048]{1,0:T(8,128)(2,1)} %slice.348), channel_id=1, source_target_pairs={{1,0},{0,1},{3,2},{2,3},{5,4},{4,5},{7,6},{6,7},{9,8},{8,9},{11,10... | collective-permute-start | bytes 3538952 | tf_op jit(solution)/shard_map/ppermute | solution.py:168
  770.4 43.6 %copy-start.78 = (f32[2048]{0:T(1024)S(1)}, f32[2048]{0:T(1024)}, u32[]{:S(2)}) copy-start(f32[2048]{0:T(1024)} %get-tuple-element.388) | copy-start | bytes 24580
  770.4 43.6 %copy-start.88 = (f32[128]{0:T(128)S(1)}, f32[128]{0:T(128)}, u32[]{:S(2)}) copy-start(f32[128]{0:T(128)} %get-tuple-element.394) | copy-start | bytes 1540
  770.4 43.6 %copy-start.89 = (f32[128]{0:T(128)S(1)}, f32[128]{0:T(128)}, u32[]{:S(2)}) copy-start(f32[128]{0:T(128)} %get-tuple-element.392) | copy-start | bytes 1540
  770.4 84.2 %copy-start.83 = (f32[288]{0:T(512)S(1)}, f32[288]{0:T(512)}, u32[]{:S(2)}) copy-start(f32[288]{0:T(512)} %copy-done.82) | copy-start | bytes 3460
  770.4 43.5 %copy-start.43 = (bf16[288,2048]{1,0:T(8,128)(2,1)}, bf16[288,2048]{1,0:T(8,128)(2,1)S(1)}, u32[]{:S(2)}) copy-start(bf16[288,2048]{1,0:T(8,128)(2,1)S(1)} %collective-permute-done.16) | copy-start | bytes 3538948
  859.8 47.3 %collective-permute-start.26 = (bf16[288,2048]{1,0:T(8,128)(2,1)}, bf16[288,2048]{1,0:T(8,128)(2,1)}, u32[]{:S(2)}, u32[]{:S(2)}) collective-permute-start(bf16[288,2048]{1,0:T(8,128)(2,1)} %get-tuple-element.442), channel_id=1, source_target_pairs={{0,0},{2,4},{4,2},{6,6},{1,1},{3,5},{5,3},{7,7},{8,8},{10,12},{12,... | collective-permute-start | bytes 3538952 | tf_op jit(solution)/shard_map/ppermute | solution.py:149
  874.7 35.5 %collective-permute-start.31 = (bf16[256,1536]{0,1:T(8,128)(2,1)}, bf16[256,1536]{0,1:T(8,128)(2,1)S(1)}, u32[]{:S(2)}, u32[]{:S(2)}) collective-permute-start(bf16[256,1536]{0,1:T(8,128)(2,1)} %broadcast_select_fusion.13), channel_id=1, source_target_pairs={{4,0},{0,4},{5,1},{1,5},{6,2},{2,6},{7,3},{3,7},{12,8},{8,12},{13,... | collective-permute-start | bytes 2359304 | tf_op jit(solution)/shard_map/ppermute | solution.py:190
  877.3 36.5 %collective-permute-start.27 = (bf16[256,1536]{0,1:T(8,128)(2,1)}, bf16[256,1536]{0,1:T(8,128)(2,1)}, u32[]{:S(2)}, u32[]{:S(2)}) collective-permute-start(bf16[256,1536]{0,1:T(8,128)(2,1)} %broadcast_select_fusion.15), channel_id=1, source_target_pairs={{4,0},{0,4},{5,1},{1,5},{6,2},{2,6},{7,3},{3,7},{12,8},{8,12},{13,... | collective-permute-start | bytes 2359304 | tf_op jit(solution)/shard_map/ppermute | solution.py:190
  907.0 8.9 collective-permute-start.29
  911.2 88.8 %collective-permute-start.32 = (bf16[256,1536]{0,1:T(8,128)(2,1)S(1)}, bf16[256,1536]{0,1:T(8,128)(2,1)S(1)}, u32[]{:S(2)}, u32[]{:S(2)}) collective-permute-start(bf16[256,1536]{0,1:T(8,128)(2,1)S(1)} %broadcast_select_fusion.7), channel_id=1, source_target_pairs={{2,0},{0,2},{3,1},{1,3},{6,4},{4,6},{7,5},{5,7},{10,8},{8,10},{11,... | collective-permute-start | bytes 2359304 | tf_op jit(solution)/shard_map/ppermute | solution.py:192
  916.0 84.1 %copy-start.40 = (bf16[256,1536]{0,1:T(8,128)(2,1)S(1)}, bf16[256,1536]{0,1:T(8,128)(2,1)}, u32[]{:S(2)}) copy-start(bf16[256,1536]{0,1:T(8,128)(2,1)} %copy-done.39) | copy-start | bytes 2359300
  916.0 101.0 %collective-permute-start.28 = (bf16[256,1536]{0,1:T(8,128)(2,1)}, bf16[256,1536]{0,1:T(8,128)(2,1)}, u32[]{:S(2)}, u32[]{:S(2)}) collective-permute-start(bf16[256,1536]{0,1:T(8,128)(2,1)} %broadcast_select_fusion.8), channel_id=1, source_target_pairs={{2,0},{0,2},{3,1},{1,3},{6,4},{4,6},{7,5},{5,7},{10,8},{8,10},{11,... | collective-permute-start | bytes 2359304 | tf_op jit(solution)/shard_map/ppermute | solution.py:192
  917.7 132.5 %collective-permute-start.30 = (bf16[256,3072]{0,1:T(8,128)(2,1)}, bf16[256,3072]{0,1:T(8,128)(2,1)}, u32[]{:S(2)}, u32[]{:S(2)}) collective-permute-start(bf16[256,3072]{0,1:T(8,128)(2,1)} %broadcast_select_fusion), channel_id=1, source_target_pairs={{2,0},{0,2},{3,1},{1,3},{6,4},{4,6},{7,5},{5,7},{10,8},{8,10},{11,... | collective-permute-start | bytes 4718600 | tf_op jit(solution)/shard_map/ppermute | solution.py:192
  (79 other events, 227.9 us)
Sparse Core Ops, SparseCore 0:
  54.3 71.2 all-gather.4
  179.3 123.1 all-gather.6
  333.9 68.6 all-gather.8
  604.4 68.4 reduce-scatter.7
  711.0 68.9 reduce-scatter.3
  783.0 121.9 reduce-scatter.5

commit v2 on v1

--- a/solution.py
+++ b/solution.py
@@ -1,6 +1,10 @@
+import functools
+
 import jax
 import jax.numpy as jnp
 from jax import lax
+from jax.experimental import pallas as pl
+from jax.experimental.pallas import tpu as pltpu
 from jax.sharding import Mesh
 from jax.sharding import PartitionSpec as P
 
@@ -141,6 +145,520 @@
     return (query_grad.reshape(grouped_rows, kv_heads * repeat, head_size), key_grad, value_grad)
 
 
+MESH = pl.DeviceIdType.MESH
+CHUNKS = 3
+
+
+def remote(source, target, send_sem, recv_sem, **place):
+    return pltpu.make_async_remote_copy(
+        src_ref=source,
+        dst_ref=target,
+        send_sem=send_sem,
+        recv_sem=recv_sem,
+        device_id=place,
+        device_id_type=MESH,
+    )
+
+
+def rows_at(index, size):
+    return pl.ds(pl.multiple_of(index * size, size), size)
+
+
+def entry_kernel(nd, tl, *refs):
+    (q_ref, k_ref, v_ref, o_ref, tok_ref, gain_ref) = refs[:6]
+    (qkv_full, o_full, tok_full, gain_full) = refs[6:10]
+    (stage, tok_stage) = refs[10:12]
+    (zs, zr, cs, li, lo, xs, xr, ts, tr, tli, tlo, ls, lr, fs, fr, gs, gr, gl) = refs[12:]
+    d, c, h, l = (lax.axis_index(name) for name in ("d", "c", "h", "l"))
+    same = c == h
+    apart = c != h
+    rows = q_ref.shape[0]
+    own = tok_ref.shape[0]
+    chunk = own // CHUNKS
+    q_cols, kv_cols = q_ref.shape[1], k_ref.shape[1]
+    weights = (
+        (q_ref, qkv_full, 0, 0),
+        (k_ref, qkv_full, q_cols, q_cols),
+        (v_ref, qkv_full, q_cols + kv_cols, q_cols + kv_cols),
+        (o_ref, o_full, 0, q_cols + 2 * kv_cols),
+    )
+
+    def block(j, row):
+        source, full, start, _ = weights[j]
+        return full.at[rows_at(row, rows), pl.ds(start, source.shape[1])]
+
+    def held(j):
+        source, _, _, start = weights[j]
+        return stage.at[:, pl.ds(start, source.shape[1])]
+
+    def from_far(j, part):
+        return remote(block(j, d * 2 + part), block(j, d * 2 + part), zs.at[j], zr.at[j, part], h=1 - h)
+
+    def to_far(j):
+        return remote(weights[j][0], block(j, d * 2 + c), zs.at[j], zr.at[j, c], c=h, h=1 - h)
+
+    def to_core(j):
+        return remote(weights[j][0], block(j, d * 2 + c), cs.at[j], zr.at[j, c], c=h)
+
+    def local_in(j):
+        return pltpu.make_async_copy(weights[j][0], held(j), li.at[j])
+
+    def local_out(j):
+        return pltpu.make_async_copy(held(j), block(j, d * 2 + c), lo.at[j])
+
+    def tokens_at(index, k):
+        return tok_full.at[pl.ds(index * own + k * chunk, chunk)]
+
+    def trade_tokens(k):
+        return remote(tok_ref.at[pl.ds(k * chunk, chunk)], tokens_at(0, k), ts.at[k], tr.at[k], c=h, h=c)
+
+    def along(step, k):
+        return remote(
+            tokens_at(0, k),
+            tokens_at(tl - step, k),
+            ls.at[(step - 1) * CHUNKS + k],
+            lr.at[(tl - step - 1) * CHUNKS + k],
+            l=lax.rem(l + step, tl),
+        )
+
+    def from_along(index, k):
+        return remote(
+            tokens_at(index, k),
+            tokens_at(index, k),
+            ls.at[(index - 1) * CHUNKS + k],
+            lr.at[(index - 1) * CHUNKS + k],
+            l=l,
+        )
+
+    def across(index, k):
+        at = index * CHUNKS + k
+        return remote(tokens_at(index, k), tokens_at(tl + index, k), fs.at[at], fr.at[at], c=1 - c)
+
+    def gain_peer(step):
+        place = lax.rem(d * 2 + c + step, 2 * nd)
+        return place // 2, lax.rem(place, 2)
+
+    def gains_to(step):
+        to_d, to_c = gain_peer(step)
+        return remote(
+            gain_ref, gain_full.at[d * 2 + c], gs.at[step - 1], gr.at[2 * nd - step - 1], d=to_d, c=to_c
+        )
+
+    def gains_from(step):
+        from_d, from_c = gain_peer(step)
+        return remote(
+            gain_ref, gain_full.at[from_d * 2 + from_c], gs.at[step - 1], gr.at[step - 1], d=from_d, c=from_c
+        )
+
+    def local_gains():
+        return pltpu.make_async_copy(gain_ref, gain_full.at[d * 2 + c], gl)
+
+    local_gains().start()
+    for j in range(3):
+        to_far(j).start()
+
+        @pl.when(apart)
+        def _():
+            to_core(j).start()
+
+    @pl.when(apart)
+    def _():
+        for k in range(CHUNKS):
+            trade_tokens(k).start()
+
+    to_far(3).start()
+
+    @pl.when(apart)
+    def _():
+        to_core(3).start()
+
+    @pl.when(same)
+    def _():
+        pltpu.make_async_copy(tok_ref, tok_stage, tli).start()
+        for j in range(4):
+            local_in(j).start()
+        pltpu.make_async_copy(tok_ref, tok_stage, tli).wait()
+        for k in range(CHUNKS):
+            part = pl.ds(k * chunk, chunk)
+            pltpu.make_async_copy(tok_stage.at[part], tokens_at(0, k), tlo.at[k]).start()
+        for j in range(4):
+            local_in(j).wait()
+            local_out(j).start()
+
+    for step in range(1, 2 * nd):
+        gains_to(step).start()
+
+    if nd == 4:
+        side_x = d + 1 - 2 * lax.rem(d, 2)
+        side_y = d + 2 - 4 * (d // 2)
+        hops = (
+            (0, d, side_x),
+            (1, d, side_x),
+            (0, d, side_y),
+            (1, d, side_y),
+            (0, side_x, side_y),
+            (1, side_y, side_x),
+        )
+        sources = (
+            (0, side_x),
+            (1, side_x),
+            (0, side_y),
+            (1, side_y),
+            (0, side_x + side_y - d),
+            (1, side_x + side_y - d),
+        )
+        first, relayed = 4, ((0, 4), (3, 5))
+    else:
+        hops = tuple((part, d, lax.rem(d + step, nd)) for step in range(1, nd) for part in range(2))
+        sources = tuple(
+            (part, lax.rem(d + nd - step, nd)) for step in range(1, nd) for part in range(2)
+        )
+        first, relayed = len(hops), ()
+
+    def hop(j, kind):
+        part, of, to = hops[kind]
+        at = block(j, of * 2 + part)
+        return remote(at, at, xs.at[j, kind], xr.at[j, kind], d=to)
+
+    def arrived(j, kind):
+        part, of = sources[kind]
+        at = block(j, of * 2 + part)
+        return remote(at, at, xs.at[j, kind], xr.at[j, kind], d=hops[kind][2])
+
+    def spread(j):
+        for part in range(2):
+            here = jnp.logical_and(same, c == part)
+
+            @pl.when(here)
+            def _():
+                local_out(j).wait()
+
+            @pl.when(jnp.logical_not(here))
+            def _():
+                from_far(j, part).wait_recv()
+
+            for kind in range(first):
+                if hops[kind][0] == part:
+                    hop(j, kind).start()
+
+    def relay(j):
+        for after, kind in relayed:
+            arrived(j, after).wait_recv()
+            hop(j, kind).start()
+
+    spread(0)
+    spread(1)
+    relay(0)
+    spread(2)
+    relay(1)
+    for k in range(CHUNKS):
+
+        @pl.when(same)
+        def _():
+            part = pl.ds(k * chunk, chunk)
+            pltpu.make_async_copy(tok_stage.at[part], tokens_at(0, k), tlo.at[k]).wait()
+
+        @pl.when(apart)
+        def _():
+            remote(tokens_at(0, k), tokens_at(0, k), ts.at[k], tr.at[k], c=1 - c, h=1 - h).wait_recv()
+
+        for step in range(1, tl):
+            along(step, k).start()
+        across(0, k).start()
+    relay(2)
+    spread(3)
+    for k in range(CHUNKS):
+        for index in range(1, tl):
+            from_along(index, k).wait_recv()
+            across(index, k).start()
+    relay(3)
+
+    handled = {after for after, _ in relayed}
+    for j in range(4):
+        for kind in range(len(hops)):
+            if kind not in handled:
+                arrived(j, kind).wait_recv()
+            hop(j, kind).wait_send()
+        to_far(j).wait_send()
+    for k in range(CHUNKS):
+        for index in range(tl):
+            across(index, k).wait()
+        for step in range(1, tl):
+            along(step, k).wait_send()
+    for step in range(1, 2 * nd):
+        gains_from(step).wait_recv()
+        gains_to(step).wait_send()
+    local_gains().wait()
+
+    @pl.when(apart)
+    def _():
+        for j in range(4):
+            to_core(j).wait_send()
+        for k in range(CHUNKS):
+            trade_tokens(k).wait_send()
+
+
+def enter(q_weight, key_matrix, value_matrix, o_weight, tokens, gains):
+    nd, tl = lax.axis_size("d"), lax.axis_size("l")
+    rows, q_cols = q_weight.shape
+    kv_cols = key_matrix.shape[1]
+    own, width = tokens.shape
+    hops = 6 if nd == 4 else 2 * (nd - 1)
+    dma = pltpu.SemaphoreType.DMA
+    return pl.pallas_call(
+        functools.partial(entry_kernel, nd, tl),
+        name="entry",
+        out_shape=(
+            jax.ShapeDtypeStruct((width, q_cols + 2 * kv_cols), jnp.bfloat16),
+            jax.ShapeDtypeStruct((width, o_weight.shape[1]), jnp.bfloat16),
+            jax.ShapeDtypeStruct((2 * tl * own, width), jnp.bfloat16),
+            jax.ShapeDtypeStruct((2 * nd,) + gains.shape, jnp.float32),
+        ),
+        in_specs=[pl.BlockSpec(memory_space=pl.ANY)] * 6,
+        out_specs=[pl.BlockSpec(memory_space=pl.ANY)] * 4,
+        scratch_shapes=[
+            pltpu.VMEM((rows, q_cols + 2 * kv_cols + o_weight.shape[1]), jnp.bfloat16),
+            pltpu.VMEM((own, width), jnp.bfloat16),
+            dma((4,)),
+            dma((4, 2)),
+            dma((4,)),
+            dma((4,)),
+            dma((4,)),
+            dma((4, hops)),
+            dma((4, hops)),
+            dma((CHUNKS,)),
+            dma((CHUNKS,)),
+            dma,
+            dma((CHUNKS,)),
+            dma(((tl - 1) * CHUNKS,)),
+            dma(((tl - 1) * CHUNKS,)),
+            dma((tl * CHUNKS,)),
+            dma((tl * CHUNKS,)),
+            dma((2 * nd - 1,)),
+            dma((2 * nd - 1,)),
+            dma,
+        ],
+        compiler_params=pltpu.CompilerParams(has_side_effects=True),
+        cost_estimate=pl.CostEstimate(flops=0, bytes_accessed=250_000_000, transcendentals=0),
+    )(q_weight, key_matrix, value_matrix, o_weight, tokens, gains)
+
+
+def exchange_kernel(tl, epilogue, aux_count, out_count, gather, *refs):
+    partial = refs[0]
+    aux = refs[1 : 1 + aux_count]
+    outs = refs[1 + aux_count : 1 + aux_count + out_count]
+    rest = refs[1 + aux_count + out_count :]
+    if gather:
+        full, rest = rest[0], rest[1:]
+        finished, ls, lr, fs, fr, keep, rest = rest[0], *rest[1:6], rest[6:]
+    mine, other, sums, arrivals, cs, cr, loc, ss, sr = rest
+    c, l = lax.axis_index("c"), lax.axis_index("l")
+    own = arrivals.shape[0] // (tl - 1)
+    chunk = own // CHUNKS
+
+    barrier = pltpu.get_barrier_semaphore()
+    pl.semaphore_signal(barrier, inc=1, device_id={"c": 1 - c}, device_id_type=MESH)
+    for step in range(1, tl):
+        pl.semaphore_signal(
+            barrier, inc=1, device_id={"l": lax.rem(l + step, tl)}, device_id_type=MESH
+        )
+    pl.semaphore_wait(barrier, tl)
+
+    def part(base, k):
+        return rows_at(base * CHUNKS + k, chunk)
+
+    def to_core(index, k):
+        at = index * CHUNKS + k
+        return remote(
+            partial.at[part(tl + index, k)], other.at[part(index, k)], cs.at[at], cr.at[at], c=1 - c
+        )
+
+    def local(index, k):
+        return pltpu.make_async_copy(
+            partial.at[part(index, k)], mine.at[part(index, k)], loc.at[index * CHUNKS + k]
+        )
+
+    def along(step, k):
+        at = (step - 1) * CHUNKS + k
+        return remote(
+            sums.at[part(step - 1, k)],
+            arrivals.at[part(step - 1, k)],
+            ss.at[at],
+            sr.at[at],
+            l=lax.rem(l + step, tl),
+        )
+
+    order = list(range(1, tl)) + [0]
+    for index in order:
+        for k in range(CHUNKS):
+            to_core(index, k).start()
+            local(index, k).start()
+
+    def both(index, k):
+        local(index, k).wait()
+        to_core(index, k).wait_recv()
+        at = part(index, k)
+        return mine[at, :].astype(jnp.float32) + other[at, :].astype(jnp.float32)
+
+    for step in range(1, tl):
+
+        def pass_on(k, carry):
+            sums[part(step - 1, k), :] = both(step, k).astype(jnp.bfloat16)
+            along(step, k).start()
+            return carry
+
+        lax.fori_loop(0, CHUNKS, pass_on, 0)
+
+    def gathered(index, k):
+        return full.at[part(index, k)]
+
+    def keep_own(k):
+        return pltpu.make_async_copy(finished.at[part(0, k)], gathered(0, k), keep.at[k])
+
+    def own_along(step, k):
+        return remote(
+            finished.at[part(0, k)],
+            gathered(tl - step, k),
+            ls.at[(step - 1) * CHUNKS + k],
+            lr.at[(tl - step - 1) * CHUNKS + k],
+            l=lax.rem(l + step, tl),
+        )
+
+    def from_along(index, k):
+        at = (index - 1) * CHUNKS + k
+        return remote(gathered(index, k), gathered(index, k), ls.at[at], lr.at[at], l=l)
+
+    def across(index, k):
+        source = finished.at[part(0, k)] if index == 0 else gathered(index, k)
+        at = index * CHUNKS + k
+        return remote(source, gathered(tl + index, k), fs.at[at], fr.at[at], c=1 - c)
+
+    def finish(k, carry):
+        total = both(0, k)
+        for step in range(1, tl):
+            along(step, k).wait_recv()
+            total = total + arrivals[part(step - 1, k), :].astype(jnp.float32)
+        row = epilogue(total, part(0, k), k, aux, outs)
+        if gather:
+            finished[part(0, k), :] = row
+            keep_own(k).start()
+            for step in range(1, tl):
+                own_along(step, k).start()
+            across(0, k).start()
+        return carry
+
+    lax.fori_loop(0, CHUNKS, finish, 0)
+    if gather:
+        for k in range(CHUNKS):
+            for index in range(1, tl):
+                from_along(index, k).wait_recv()
+                across(index, k).start()
+        for k in range(CHUNKS):
+            keep_own(k).wait()
+            for index in range(tl):
+                across(index, k).wait()
+            for step in range(1, tl):
+                own_along(step, k).wait_send()
+    for k in range(CHUNKS):
+        for index in range(tl):
+            to_core(index, k).wait_send()
+        for step in range(1, tl):
+            along(step, k).wait_send()
+
+
+def exchange(name, collective_id, partial, aux, outs, epilogue, gather):
+    tl = lax.axis_size("l")
+    total, width = partial.shape
+    own = total // (2 * tl)
+    dma = pltpu.SemaphoreType.DMA
+    vmem = pl.BlockSpec(memory_space=pltpu.VMEM)
+    anywhere = pl.BlockSpec(memory_space=pl.ANY)
+    out_shape = list(outs)
+    out_specs = [vmem] * len(outs)
+    scratch = []
+    if gather:
+        out_shape.append(jax.ShapeDtypeStruct((total, width), jnp.bfloat16))
+        out_specs.append(anywhere)
+        scratch += [
+            pltpu.VMEM((own, width), jnp.bfloat16),
+            dma(((tl - 1) * CHUNKS,)),
+            dma(((tl - 1) * CHUNKS,)),
+            dma((tl * CHUNKS,)),
+            dma((tl * CHUNKS,)),
+            dma((CHUNKS,)),
+        ]
+    scratch += [
+        pltpu.VMEM((tl * own, width), jnp.bfloat16),
+        pltpu.VMEM((tl * own, width), jnp.bfloat16),
+        pltpu.VMEM(((tl - 1) * own, width), jnp.bfloat16),
+        pltpu.VMEM(((tl - 1) * own, width), jnp.bfloat16),
+        dma((tl * CHUNKS,)),
+        dma((tl * CHUNKS,)),
+        dma((tl * CHUNKS,)),
+        dma(((tl - 1) * CHUNKS,)),
+        dma(((tl - 1) * CHUNKS,)),
+    ]
+    return pl.pallas_call(
+        functools.partial(exchange_kernel, tl, epilogue, len(aux), len(outs), gather),
+        name=name,
+        out_shape=tuple(out_shape),
+        in_specs=[anywhere] + [vmem] * len(aux),
+        out_specs=out_specs,
+        scratch_shapes=scratch,
+        compiler_params=pltpu.CompilerParams(
+            has_side_effects=True, collective_id=collective_id, vmem_limit_bytes=40 << 20
+        ),
+        cost_estimate=pl.CostEstimate(
+            flops=0, bytes_accessed=200_000_000 if gather else 110_000_000, transcendentals=0
+        ),
+    )(partial, *aux)
+
+
+def middle_rows(total, rows, k, aux, outs):
+    stream, gain = aux
+    value = stream[rows, :].astype(jnp.float32) + total
+    outs[0][rows, :] = value
+    return rms_scale(value, gain[...]).astype(jnp.bfloat16)
+
+
+def norm_pull(value, gain, grad):
+    scale = lax.rsqrt(jnp.mean(value * value, axis=-1, keepdims=True) + EPS)
+    scaled = grad * gain
+    inner = jnp.mean(value * scaled, axis=-1, keepdims=True)
+    return scale * scaled - value * (scale * scale * scale * inner), jnp.sum(
+        grad * value * scale, axis=0, keepdims=True
+    )
+
+
+def add_rows(out, value, k):
+    @pl.when(k == 0)
+    def _():
+        out[...] = value
+
+    @pl.when(k > 0)
+    def _():
+        out[...] += value
+
+
+def middle_pull_rows(total, rows, k, aux, outs):
+    middle, cotangent, gain = aux
+    pulled, gain_part = norm_pull(middle[rows, :], gain[...], total)
+    value = cotangent[rows, :].astype(jnp.float32) + pulled
+    outs[0][rows, :] = value
+    add_rows(outs[1], gain_part, k)
+    return value.astype(jnp.bfloat16)
+
+
+def stream_pull_rows(total, rows, k, aux, outs):
+    stream, gradient, gain = aux
+    pulled, gain_part = norm_pull(stream[rows, :].astype(jnp.float32), gain[...], total)
+    value = gradient[rows, :] + pulled
+    outs[0][rows, :] = value
+    outs[1][rows, :] = value.astype(jnp.bfloat16)
+    add_rows(outs[2], gain_part, k)
+    return None
+
+
 def shift_perm(size, step):
     return [((place + step) % size, place) for place in range(size)]
 
@@ -149,9 +667,11 @@
     return lax.ppermute(values, ("c", "h"), [(0, 0), (1, 2), (2, 1), (3, 3)])
 
 
-def gather_tokens(own):
+def gather_tokens(own, *first):
     places = lax.axis_size("l")
-    parts = [own] + [lax.ppermute(own, "l", shift_perm(places, step)) for step in range(1, places)]
+    parts = [own] + [
+        after(lax.ppermute(own, "l", shift_perm(places, step)), *first) for step in range(1, places)
+    ]
     half = jnp.concatenate(parts, axis=0)
     return jnp.concatenate([half, lax.ppermute(half, "c", shift_perm(2, 1))], axis=0)
 
@@ -169,16 +689,49 @@
     return own
 
 
-def gather_weights(shard):
-    core, upper = lax.axis_index("c"), lax.axis_index("h")
-    far = lax.ppermute(shard, "h", shift_perm(2, 1))
-    same = core == upper
-    mine = jnp.where(same, shard, far)
-    other = lax.ppermute(jnp.where(same, far, shard), "c", shift_perm(2, 1))
-    rows = jnp.concatenate(
-        [jnp.where(core == 0, mine, other), jnp.where(core == 0, other, mine)], axis=0
-    )
-    return lax.all_gather(rows, "d", axis=0, tiled=True)
+def after(value, *others):
+    return lax.optimization_barrier((value,) + others)[0]
+
+
+def core_halves(shard):
+    core = lax.axis_index("c")
+    half = shard.shape[-1] // 2
+    first, second = shard[..., :half], shard[..., half:]
+    mine = jnp.where(core == 0, first, second)
+    other = lax.ppermute(jnp.where(core == 0, second, first), "c", shift_perm(2, 1))
+    both = jnp.where(core == 0, jnp.stack([mine, other]), jnp.stack([other, mine]))
+    return jnp.moveaxis(both, 0, -3).reshape(shard.shape[:-2] + (2 * shard.shape[-2], half))
+
+
+def return_halves(near, far):
+    core = lax.axis_index("c")
+    sums = near.astype(jnp.float32) + lax.ppermute(far, "h", shift_perm(2, 1)).astype(jnp.float32)
+    rows = sums.shape[0] // 2
+    first, second = sums[:rows], sums[rows:]
+    mine = jnp.where(core == 0, first, second)
+    sent = jnp.where(core == 0, second, first).astype(jnp.bfloat16)
+    other = lax.ppermute(sent, "c", shift_perm(2, 1)).astype(jnp.float32)
+    return mine, other
+
+
+def columns_of(mine, other):
+    core = lax.axis_index("c")
+    return jnp.concatenate(
+        [jnp.where(core == 0, mine, other), jnp.where(core == 0, other, mine)], axis=1
+    )
+
+
+def sum_over_d(partial):
+    return lax.psum_scatter(partial.astype(jnp.bfloat16), "d", scatter_dimension=0, tiled=True)
+
+
+def as_row(values):
+    return values.reshape(1, -1)
+
+
+def split(values):
+    half = values.shape[1] // 2
+    return values[:, :half], values[:, half:]
 
 
 def scatter_weights(partial):
@@ -214,25 +767,29 @@
     places = lax.axis_size("l")
     core, place = lax.axis_index("c"), lax.axis_index("l")
     q_cols, kv_cols, ff_cols = q_weight.shape[2], key_matrix.shape[2], gate_weight.shape[2]
-
-    tokens = trade(tokens)
-    labels = trade(segment_ids)[0]
-    attn_weights = gather_weights(
-        jnp.concatenate([q_weight[0], key_matrix[0], value_matrix[0], o_weight[0]], axis=1)
-    )
-    mid_weights = gather_weights(jnp.concatenate([gate_weight[0], up_weight[0]], axis=1))
-    down_full = gather_weights(down_weight[0])
-    cotangent = trade(cotangent)
-
-    gains = lax.all_gather(
-        jnp.concatenate([attn_gain[0], mlp_gain[0], q_gain[0], k_gain[0]]), ("d", "c"), axis=0
-    ).astype(jnp.float32)
+    half_cols = ff_cols // 2
+
+    gate_half = core_halves(gate_weight[0])
+    up_half = core_halves(up_weight[0])
+    mid_rows = jnp.concatenate([gate_half, up_half], axis=1)
+    down_rows = core_halves(down_weight[0])
+    mid_near = lax.all_gather(mid_rows, "d", axis=0, tiled=True)
+    down_near = lax.all_gather(down_rows, "d", axis=0, tiled=True)
+
     cut = attn_gain.shape[1]
     head_cut = q_gain.shape[1]
+    gains = jnp.concatenate([attn_gain[0], mlp_gain[0], q_gain[0], k_gain[0]]).astype(jnp.float32)
+    gains = jnp.pad(gains, (0, 1024 - gains.shape[0])).reshape(8, 128)
+    labels = trade(segment_ids)[0]
+    qkv_full, o_full, group, gains = enter(
+        q_weight[0], key_matrix[0], value_matrix[0], o_weight[0], after(tokens, mid_rows), gains
+    )
+    mid_far = lax.ppermute(after(mid_rows, group), "h", shift_perm(2, 1))
+    gains = gains.reshape(gains.shape[0], -1)
     attn_scale = gains[:, :cut].reshape(-1)
     mlp_scale = gains[:, cut : 2 * cut].reshape(-1)
     q_scale = gains[:, 2 * cut : 2 * cut + head_cut].reshape(-1)
-    k_scale = gains[:, 2 * cut + head_cut :].reshape(-1)
+    k_scale = gains[:, 2 * cut + head_cut : 2 * cut + 2 * head_cut].reshape(-1)
 
     order = jnp.stack(
         [
@@ -245,24 +802,15 @@
     labels = labels.reshape(2 * places, own_rows)[order].reshape(-1)
     cosine, sine_table = rotary_tables(labels, row_index)
 
-    stream = tokens.astype(jnp.float32)
-    normed = gather_tokens(rms_scale(stream, attn_scale).astype(jnp.bfloat16))
+    stream = group[:own_rows]
+    normed = rms_scale(group.astype(jnp.float32), attn_scale).astype(jnp.bfloat16)
     rows = normed.shape[0]
     head_count, kv_heads = q_cols // HEAD_WIDTH, kv_cols // HEAD_WIDTH
-    q_full = attn_weights[:, :q_cols]
-    k_full = attn_weights[:, q_cols : q_cols + kv_cols]
-    v_full = attn_weights[:, q_cols + kv_cols : q_cols + 2 * kv_cols]
-    o_full = attn_weights[:, q_cols + 2 * kv_cols :]
-    queries = jnp.dot(normed, q_full, preferred_element_type=jnp.float32).reshape(
-        rows, head_count, HEAD_WIDTH
-    )
-    keys = jnp.dot(normed, k_full, preferred_element_type=jnp.float32).reshape(
-        rows, kv_heads, HEAD_WIDTH
-    )
+    qkv = jnp.dot(normed, qkv_full, preferred_element_type=jnp.float32)
+    queries = qkv[:, :q_cols].reshape(rows, head_count, HEAD_WIDTH)
+    keys = qkv[:, q_cols : q_cols + kv_cols].reshape(rows, kv_heads, HEAD_WIDTH)
     value_reduced = (
-        jnp.dot(normed, v_full, preferred_element_type=jnp.float32)
-        .reshape(rows, kv_heads, HEAD_WIDTH)
-        .astype(jnp.bfloat16)
+        qkv[:, q_cols + kv_cols :].reshape(rows, kv_heads, HEAD_WIDTH).astype(jnp.bfloat16)
     )
     query_reduced = rotate(rms_scale(queries, q_scale), cosine, sine_table).astype(jnp.bfloat16)
     key_reduced = rotate(rms_scale(keys, k_scale), cosine, sine_table).astype(jnp.bfloat16)
@@ -270,41 +818,69 @@
     attended, totals = attend_forward(
         query_reduced, key_reduced, value_reduced, labels, row_index
     )
-    middle = stream + scatter_tokens(contract_cols(attended, o_full))
-
-    normed_mid = gather_tokens(rms_scale(middle, mlp_scale).astype(jnp.bfloat16))
-    gate_full, up_full = mid_weights[:, :ff_cols], mid_weights[:, ff_cols:]
-    gate_raw = jnp.dot(normed_mid, gate_full, preferred_element_type=jnp.float32)
-    up_raw = jnp.dot(normed_mid, up_full, preferred_element_type=jnp.float32)
-    hidden = swiglu(gate_raw, up_raw).astype(jnp.bfloat16)
-    branch = scatter_tokens(contract_cols(hidden, down_full))
-    activations = trade((middle + branch).astype(jnp.bfloat16))
-
-    grad_rows = gather_tokens(cotangent)
-    gradient = cotangent.astype(jnp.float32)
-    down_grad = scatter_weights(contract_rows(grad_rows, hidden))
-    hidden_grad = jnp.dot(grad_rows, down_full, preferred_element_type=jnp.float32)
-    _, pull_back = jax.vjp(swiglu, gate_raw, up_raw)
-    gate_grad, up_grad = pull_back(hidden_grad)
-    gate_low = gate_grad.astype(jnp.bfloat16)
-    up_low = up_grad.astype(jnp.bfloat16)
-    mid_grad = scatter_weights(
+    mid_far = lax.all_gather(after(mid_far, attended, down_near), "d", axis=0, tiled=True)
+    down_far = lax.ppermute(after(down_rows, attended), "h", shift_perm(2, 1))
+    cotangent = trade(after(cotangent, attended))
+
+    def whole(values):
+        return jax.ShapeDtypeStruct((own_rows, width), values)
+
+    gain_sum = jax.ShapeDtypeStruct((1, width), jnp.float32)
+    middle, normed_mid = exchange(
+        "attention_sum",
+        1,
+        contract_cols(attended, o_full).astype(jnp.bfloat16),
+        (stream, as_row(mlp_scale)),
+        (whole(jnp.float32),),
+        middle_rows,
+        True,
+    )
+    down_far = lax.all_gather(after(down_far, normed_mid), "d", axis=0, tiled=True)
+    cotangent = after(cotangent, normed_mid)
+
+    gate_near, up_near = split(jnp.dot(normed_mid, mid_near, preferred_element_type=jnp.float32))
+    hidden_near = swiglu(gate_near, up_near).astype(jnp.bfloat16)
+    gate_far, up_far = split(jnp.dot(normed_mid, mid_far, preferred_element_type=jnp.float32))
+    hidden_far = swiglu(gate_far, up_far).astype(jnp.bfloat16)
+    grad_rows = gather_tokens(cotangent, hidden_near)
+    down_grads = sum_over_d(
         jnp.concatenate(
             [
-                contract_rows(normed_mid, gate_low).astype(jnp.bfloat16),
-                contract_rows(normed_mid, up_low).astype(jnp.bfloat16),
+                contract_rows(grad_rows, hidden_near).astype(jnp.bfloat16),
+                contract_rows(grad_rows, hidden_far).astype(jnp.bfloat16),
             ],
             axis=1,
         )
     )
-    normed_grad = scatter_tokens(
-        contract_cols(gate_low, gate_full) + contract_cols(up_low, up_full)
-    )
-    _, pull_norm = jax.vjp(rms_scale, middle, mlp_scale)
-    middle_grad, mlp_gain_grad = pull_norm(normed_grad)
-    gradient = gradient + middle_grad
-
-    grad_rows = gather_tokens(gradient.astype(jnp.bfloat16))
+
+    def hidden_pull(gate, up, down):
+        hidden_grad = jnp.dot(grad_rows, down, preferred_element_type=jnp.float32)
+        _, pull_back = jax.vjp(swiglu, gate, up)
+        gate_grad, up_grad = pull_back(hidden_grad)
+        return jnp.concatenate(
+            [gate_grad.astype(jnp.bfloat16), up_grad.astype(jnp.bfloat16)], axis=1
+        )
+
+    mid_back_near = hidden_pull(gate_near, up_near, down_near)
+    mid_back_far = hidden_pull(gate_far, up_far, down_far)
+    mid_grad_far = contract_rows(normed_mid, mid_back_far).astype(jnp.bfloat16)
+    mid_sum_far = sum_over_d(mid_grad_far)
+    normed_grad = (contract_cols(mid_back_near, mid_near) + contract_cols(mid_back_far, mid_far)).astype(
+        jnp.bfloat16
+    )
+    gradient, mlp_gain_grad, grad_rows = exchange(
+        "middle_pull",
+        2,
+        after(normed_grad, mid_grad_far),
+        (middle, cotangent, as_row(mlp_scale)),
+        (whole(jnp.float32), gain_sum),
+        middle_pull_rows,
+        True,
+    )
+    mid_grad_near = contract_rows(normed_mid, after(mid_back_near, grad_rows)).astype(jnp.bfloat16)
+    mid_sum_near = sum_over_d(mid_grad_near)
+
+    grad_rows = after(grad_rows, mid_grad_near)
     out_grad = jnp.dot(grad_rows, o_full, preferred_element_type=jnp.float32).astype(jnp.bfloat16)
     o_wgrad = contract_rows(grad_rows, attended)
     query_grad, key_grad, value_grad = attend_backward(
@@ -324,33 +900,44 @@
     query_raw_grad, q_gain_grad = pull_query(query_grad)
     _, pull_key = jax.vjp(query_path, keys, k_scale)
     key_raw_grad, k_gain_grad = pull_key(key_grad)
-    query_back = query_raw_grad.reshape(rows, -1).astype(jnp.bfloat16)
-    key_back = key_raw_grad.reshape(rows, -1).astype(jnp.bfloat16)
-    value_back = value_grad.reshape(rows, -1).astype(jnp.bfloat16)
+    qkv_back = jnp.concatenate(
+        [
+            query_raw_grad.reshape(rows, -1).astype(jnp.bfloat16),
+            key_raw_grad.reshape(rows, -1).astype(jnp.bfloat16),
+            value_grad.reshape(rows, -1).astype(jnp.bfloat16),
+        ],
+        axis=1,
+    )
+    qkv_grad = contract_rows(normed, qkv_back).astype(jnp.bfloat16)
     attn_grad = scatter_weights(
-        jnp.concatenate(
-            [
-                contract_rows(normed, query_back).astype(jnp.bfloat16),
-                contract_rows(normed, key_back).astype(jnp.bfloat16),
-                contract_rows(normed, value_back).astype(jnp.bfloat16),
-                o_wgrad.astype(jnp.bfloat16),
-            ],
-            axis=1,
-        )
-    )
-    normed_grad = scatter_tokens(
-        contract_cols(query_back, q_full)
-        + contract_cols(key_back, k_full)
-        + contract_cols(value_back, v_full)
-    )
-    _, pull_norm = jax.vjp(rms_scale, stream, attn_scale)
-    stream_grad, attn_gain_grad = pull_norm(normed_grad)
-    gradient = gradient + stream_grad
-    moved = trade(gradient.astype(jnp.bfloat16))
+        after(jnp.concatenate([qkv_grad, o_wgrad.astype(jnp.bfloat16)], axis=1), mid_sum_far)
+    )
+    gradient, moved, attn_gain_grad = exchange(
+        "stream_pull",
+        3,
+        contract_cols(after(qkv_back, qkv_grad), qkv_full).astype(jnp.bfloat16),
+        (stream, gradient, as_row(attn_scale)),
+        (whole(jnp.float32), whole(jnp.bfloat16), gain_sum),
+        stream_pull_rows,
+        False,
+    )
+    moved = trade(moved)
     gradient = jnp.where(core == lax.axis_index("h"), gradient, moved.astype(jnp.float32))
 
+    hidden_near = after(hidden_near, attn_gain_grad)
+    branch = scatter_tokens(
+        contract_cols(hidden_near, down_near) + contract_cols(hidden_far, down_far)
+    )
+    activations = trade((middle + branch).astype(jnp.bfloat16))
+
+    split_at = down_rows.shape[1]
+    down_grad = columns_of(*return_halves(down_grads[:, :split_at], down_grads[:, split_at:]))
+    mine, other = return_halves(mid_sum_near, mid_sum_far)
+    gate_grad = columns_of(mine[:, :half_cols], other[:, :half_cols])
+    up_grad = columns_of(mine[:, half_cols:], other[:, half_cols:])
+
     sums = lax.psum(
-        jnp.concatenate([attn_gain_grad, mlp_gain_grad, q_gain_grad, k_gain_grad]),
+        jnp.concatenate([attn_gain_grad[0], mlp_gain_grad[0], q_gain_grad, k_gain_grad]),
         ("d", "c", "h", "l"),
     )
     row = lax.axis_index("d") * 2 + core
@@ -369,8 +956,8 @@
         owned(2 * width, HEAD_WIDTH, head_cut),
         owned(2 * width + HEAD_WIDTH, HEAD_WIDTH, head_cut),
         owned(width, width, cut),
-        mid_grad[None, :, :ff_cols],
-        mid_grad[None, :, ff_cols:],
+        gate_grad[None],
+        up_grad[None],
         down_grad[None],
     )
 

time: 1070 us -> 983 us (0.919)
  waiting for transfers between devices: 470 us -> 201 us
  Pallas kernels: 0 us -> 254 us
  other arithmetic: 119 us -> 91.7 us
  local copies, waits for them, and re-layouts: 134 us -> 111 us
  starting transfers between devices: 55.5 us -> 34.3 us
    pallas_call x0 -> x4, Pallas kernels: none -> 254 us  [the longest x3 174 us: exchange(): pl.pallas_call(functools.partial(exchange_kernel, tl, epilogue, len(aux),...]
    ppermute x4 -> x1, waiting for transfers between devices: 126 us -> 0.01 us  [scatter_tokens(): lax.ppermute(sent, 'l', shift_perm(places, -step)).astype(jnp.float32)]
    ppermute x3 -> x1, waiting for transfers between devices: 113 us -> 33.8 us  [scatter_weights(): far = lax.ppermute(jnp.where(same, other, mine), 'h', shift_perm(2, 1))]
    ppermute x4 -> x1, waiting for transfers between devices: 74.4 us -> 13.8 us  [gather_tokens(): lax.ppermute(own, 'l', shift_perm(places, step))]
    reduce_scatter x3 -> x1, waiting for transfers between devices: 27.4 us -> 0.01 us  [scatter_weights(): lax.psum_scatter(partial.astype(jnp.bfloat16), 'd', scatter_dimension=0,...]
    unnamed x1 -> x0, blocking collectives: 25.7 us -> none
    ppermute x6 -> x9, waiting for transfers between devices: 125 us -> 147 us  [the longest x2 102 us: return_halves(): lax.ppermute(far, 'h', shift_perm(2, 1)).astype(jnp.float32)]
    unnamed x210 -> x183, local copies, waits for them, and re-layouts: 51.2 us -> 29.2 us
  transfers between devices with their start and end apart: 39 -> 27, of which waited for: 19 -> 7; matrix products, arithmetic and copies ran while one was open for 34% -> 35% of each run, Pallas kernels for 0% -> 26%
where the time goes in v2:
time: 983 us; the launch traced here: 975 us
  Pallas kernels  254 us (26%)
  matrix products  209 us (21%)
  waiting for transfers between devices  201 us (20%)
  local copies, waits for them, and re-layouts  111 us (11%)
  other arithmetic  91.7 us (9%)
  blocking collectives  58.8 us (6%)
  starting transfers between devices  34.3 us (3%)
  between operations  15.9 us (2%)
    pallas_call x3, Pallas kernels, exchange(): pl.pallas_call(functools.partial(exchange_kernel, tl, epilogue, len(aux),...  174 us
    ppermute x2, waiting for transfers between devices, return_halves(): lax.ppermute(far, 'h', shift_perm(2, 1)).astype(jnp.float32)  102 us
    pallas_call x1, Pallas kernels, enter(): pl.pallas_call(functools.partial(entry_kernel, nd, tl), name='entry', out...  79.7 us
    psum x1, blocking collectives, per_device(): lax.psum(jnp.concatenate([attn_gain_grad[0], mlp_gain_grad[0], q_gain_gra...  58.8 us
    dot_general x6, matrix products, contract_rows(): lax.dot_general(left, right, (((0,), (0,)), ((), ())), preferred_element_...  50.4 us
    dot_general x6, matrix products, contract_cols(): lax.dot_general(left, right, (((1,), (1,)), ((), ())), preferred_element_...  48.7 us
    ppermute x1, waiting for transfers between devices, per_device(): mid_far = lax.ppermute(after(mid_rows, group), 'h', shift_perm(2, 1))  45.9 us
    ppermute x1, waiting for transfers between devices, scatter_weights(): far = lax.ppermute(jnp.where(same, other, mine), 'h', shift_perm(2, 1))  33.8 us
  transfers between devices with their start and end apart: 27, of which 7 were waited for; matrix products, arithmetic and copies ran while one was open for 35% of the time, Pallas kernels for 26%

profile of v2, /device:TPU:0, one launch (start us, length us, event | category | flops | bytes accessed | tf_op | source)
XLA Modules:
  0.0 975.1 jit_solution(9401512706054452257)
XLA Ops:
  13.2 5.4 collective-permute-start.6
  33.2 79.7 %entry.1 = (bf16[2048,1024]{1,0:T(8,128)(2,1)}, bf16[2048,512]{1,0:T(8,128)(2,1)}, bf16[1152,2048]{1,0:T(8,128)(2,1)}, f32[8,8,128]{2,1,0:T(8,128)}) custom-call(bf16[256,512]{1,0:T(8,128)(2,1)} %bitcast.303, bf16[256,256]{1,0:T(8,128)(2,1)} %bitcast.305, bf16[256,256]{1,0:T(8,128)(2,1)} %bitcast.306, bf16[256,512]{1,0:T(8,128)(2,1)} %bitcast.304, ...), custom_call_target="tpu_custom_call" | custom-call | bytes 250000000 | tf_op jit(solution)/shard_map/entry/pallas_call | solution.py:408
  112.9 3.3 fusion.47
  119.3 9.4 fusion.64
  141.7 2.9 reshape.571
  144.6 7.3 copy.164
  158.5 3.7 copy.165
  162.2 3.8 copy.166
  166.0 2.6 copy.130
  168.6 7.3 fusion.62
  177.5 20.2 %while.28 = (s32[]{:T(128)}, bf16[2,576,2,2,128]{4,3,2,1,0:T(2,128)(2,1)}, f32[2,2,2,576,1]{3,2,1,4,0:T(2,128)}, s32[2,576]{1,0:T(2,128)}, s32[4,288]{1,0:T(4,12...) while((s32[]{:T(128)}, ...), condition=%wide.region_7.8_spmd.clone, body=%wide.region_5.7_spmd.clone.sunk | while | flops 1379818368 | bytes 36285120 | solution.py:96
  179.6 3.1 bitcast_reduce_fusion.2
  182.7 3.1 fusion.141
  189.7 3.1 bitcast_reduce_fusion.2
  192.8 3.1 fusion.141
  197.7 4.3 reshape.553
  202.0 45.9 %collective-permute-done.8 = bf16[512,1536]{1,0:T(8,128)(2,1)} collective-permute-done((bf16[512,1536]{1,0:T(8,128)(2,1)}, bf16[512,1536]{1,0:T(8,128)(2,1)}, u32[]{:S(2)}, u32[]{:S(2)}) %collective-permute-start.8) | collective-permute-done | bytes 1572896 | tf_op jit(solution)/shard_map/ppermute | solution.py:787
  250.0 2.7 collective-permute-start.7
  254.4 5.2 convolution_convert_fusion.3.refs_0_
  259.6 85.9 %attention_sum.1 = (f32[288,2048]{1,0:T(8,128)S(1)}, bf16[1152,2048]{1,0:T(8,128)(2,1)S(1)}) custom-call(bf16[1152,2048]{1,0:T(8,128)(2,1)S(1)} %convolution_convert_fusion.3.refs_0_, bf16[288,2048]{1,0:T(8,128)(2,1)S(1)} %slice.155.refs_1_, f32[1,2048]{1,0:T(1,128)S(1)} %bitcast.273), custom_call_target="tpu_custom_call" | custom-call | bytes 200000000 | tf_op jit(solution)/shard_map/attention_sum/pallas_call | solution.py:601
  348.3 11.1 %fusion.89 = f32[1152,1536]{1,0:T(8,128)S(1)} fusion(bf16[1152,2048]{1,0:T(8,128)(2,1)} %copy-done.7, bf16[2048,1536]{1,0:T(8,128)(2,1)} %all-gather.5.cloned.1.call-done), kind=kOutput, calls=%fused_computation.222 | convolution fusion | flops 7247757312 | bytes 18087936 | tf_op jit(solution)/shard_map/dot_general | solution.py:841
  359.4 2.8 multiply_convert_fusion.3
  362.8 13.8 %collective-permute-done.4 = bf16[288,2048]{1,0:T(8,128)(2,1)} collective-permute-done((bf16[288,2048]{1,0:T(8,128)(2,1)S(1)}, bf16[288,2048]{1,0:T(8,128)(2,1)}, u32[]{:S(2)}, u32[]{:S(2)}) %collective-permute-start.4) | collective-permute-done | bytes 1179680 | tf_op jit(solution)/shard_map/ppermute | solution.py:673
  384.2 13.0 %fusion.90 = f32[1152,1536]{1,0:T(8,128)} fusion(bf16[1152,2048]{1,0:T(8,128)(2,1)} %copy-done.7, bf16[2048,1536]{1,0:T(8,128)(2,1)} %all-gather.11.cloned.1.call-done), kind=kOutput, calls=%fused_computation.223 | convolution fusion | flops 7247757312 | bytes 18087936 | tf_op jit(solution)/shard_map/dot_general | solution.py:843
  397.3 11.7 %fusion.55 = (bf16[1152,768]{1,0:T(8,128)(2,1)S(1)}, bf16[1152,768]{1,0:T(8,128)(2,1)S(1)}, bf16[1152,768]{1,0:T(8,128)(2,1)}) fusion(f32[1152,1536]{1,0:T(8,128)} %fusion.90, bf16[1152,2048]{1,0:T(8,128)(2,1)} %constant_dynamic-update-slice_fusion, bf16[2048,768]{1,0:T(8,128)(2,1)} %all-gather.9.cloned.1.call-done), kind=kOutput, calls=%fused_computation.81 | convolution fusion | flops 3638034432 | bytes 20250624 | tf_op jit(solution)/shard_map/dot_general | solution.py:857
  410.7 12.7 %convolution_convert_fusion.2 = bf16[2048,1536]{1,0:T(8,128)(2,1)} fusion(bf16[1152,2048]{1,0:T(8,128)(2,1)} %copy-done.7, bf16[1152,768]{1,0:T(8,128)(2,1)S(1)} %get-tuple-element.438, bf16[1152,768]{1,0:T(8,128)(2,1)S(1)} %get-tuple-element.437), kind=kOutput, calls=%fused_computation.67 | convolution fusion | flops 7257980928 | bytes 14548992 | tf_op jit(solution)/shard_map/dot_general | solution.py:50
  423.5 7.4 convolution_convert_fusion.6
  430.9 7.6 convolution_convert_fusion.5
  438.5 3.1 pad_maximum_fusion.1
  441.7 10.6 %fusion.52 = (bf16[1152,768]{1,0:T(8,128)(2,1)S(1)}, bf16[1152,768]{1,0:T(8,128)(2,1)S(1)}) fusion(f32[1152,1536]{1,0:T(8,128)} %copy-done.31, bf16[1152,2048]{1,0:T(8,128)(2,1)} %constant_dynamic-update-slice_fusion, bf16[2048,768]{1,0:T(8,128)(2,1)} %all-gather.7.cloned.1.call-done), kind=kOutput, calls=%fused_computation.78 | convolution fusion | flops 3636264960 | bytes 18481152 | tf_op jit(solution)/shard_map/dot_general | solution.py:857
  454.4 12.1 %fusion.83 = f32[1152,2048]{1,0:T(8,128)} fusion(bf16[2048,1536]{1,0:T(8,128)(2,1)} %all-gather.5.cloned.1.call-done, bf16[1152,768]{1,0:T(8,128)(2,1)S(1)} %get-tuple-element.440, bf16[1152,768]{1,0:T(8,128)(2,1)S(1)} %get-tuple-element.439), kind=kOutput, calls=%fused_computation.216 | convolution fusion | flops 7254835200 | bytes 19267584 | tf_op jit(solution)/shard_map/dot_general | solution.py:56
  466.5 13.0 %add_convert_fusion.refs_0_ = bf16[1152,2048]{1,0:T(8,128)(2,1)} fusion(f32[1152,2048]{1,0:T(8,128)} %fusion.83, bf16[2048,1536]{1,0:T(8,128)(2,1)} %all-gather.11.cloned.1.call-done, bf16[1152,768]{1,0:T(8,128)(2,1)S(1)} %copy-done.87, bf16[1152,768]{1,0:T(8,128)(2,1)S(1)} %copy-done.85), kind=kOutput, calls=%fused_computation.63 | convolution fusion | flops 7259553792 | bytes 23986176 | tf_op jit(solution)/shard_map/dot_general | solution.py:56
  479.5 57.3 %middle_pull.1 = (f32[288,2048]{1,0:T(8,128)S(1)}, f32[1,2048]{1,0:T(1,128)S(1)}, bf16[1152,2048]{1,0:T(8,128)(2,1)S(1)}) custom-call(bf16[1152,2048]{1,0:T(8,128)(2,1)} %add_convert_fusion.refs_0_, f32[288,2048]{1,0:T(8,128)S(1)} %get-tuple-element.167.refs_1_, bf16[288,2048]{1,0:T(8,128)(2,1)S(1)} %collective-permute-done.3.refs_2_, f32[1,2048]{1,0:T(1,128)S(1)} %bitcast.274), custom_call_target="tpu_custom_call" | custom-call | bytes 200000000 | tf_op jit(solution)/shard_map/middle_pull/pallas_call | solution.py:601
  540.4 10.4 %convolution_convert_fusion.1 = bf16[2048,1536]{1,0:T(8,128)(2,1)} fusion(bf16[1152,2048]{1,0:T(8,128)(2,1)S(1)} %bitcast.281, bf16[1152,1536]{1,0:T(8,128)(2,1)S(1)} %copy-done.32), kind=kOutput, calls=%fused_computation.66 | convolution fusion | flops 7250903040 | bytes 14548992 | tf_op jit(solution)/shard_map/dot_general | solution.py:50
  550.9 6.8 convolution_convert_fusion.8
  557.7 3.9 reshape_reshape.8
  561.6 66.7 %while.29 = (s32[]{:T(128)}, f32[1152,2,128]{0,2,1:T(8,128)S(1)}, f32[1152,2,128]{0,2,1:T(8,128)}, f32[2,576,2,2,128]{4,1,0,3,2:T(8,128)}, bf16[2,576,2,2,128]{4...) while((s32[]{:T(128)}, f32[1152,2,128]{0,2,1:T(8,128)S(1)}, ...), condition=%wide.region_10.11_spmd.clone, body=%wide.region_8.10_spmd.clone.sunk | while | flops 3425033216 | bytes 207860080 | solution.py:142
  569.1 2.8 fusion.148
  572.7 4.0 fusion.149
  577.9 2.8 copy-done.9
  583.0 2.6 fusion.153
  585.5 4.6 fusion.151
  591.7 3.3 fusion.152
  602.5 2.8 fusion.148
  606.0 4.0 fusion.149
  611.3 2.8 copy-done.9
  618.9 4.2 fusion.151
  624.7 3.7 fusion.152
  628.3 3.2 copy.146
  642.1 4.1 convolution_convert_fusion.7
  646.9 8.2 convolution_convert_fusion.4
  655.1 4.9 pad_maximum_fusion
  663.2 5.4 convolution_convert_fusion.refs_0_
  668.6 30.9 %stream_pull.1 = (f32[288,2048]{1,0:T(8,128)S(1)}, bf16[288,2048]{1,0:T(8,128)(2,1)S(1)}, f32[1,2048]{1,0:T(1,128)S(1)}) custom-call(bf16[1152,2048]{1,0:T(8,128)(2,1)S(1)} %convolution_convert_fusion.refs_0_, bf16[288,2048]{1,0:T(8,128)(2,1)S(1)} %copy-done.1, f32[288,2048]{1,0:T(8,128)S(1)} %copy-done.3, f32[1,2048]{1,0:T(1,128)S(1)} %bitcast.275), custom_call_target="tpu_custom_call" | custom-call | bytes 110000000 | tf_op jit(solution)/shard_map/stream_pull/pallas_call | solution.py:601
  699.6 6.3 fusion.91
  705.9 6.7 convolution_add_fusion
  713.0 4.5 collective-permute-done.9
  725.8 58.8 %psum.7 = f32[4352]{0:T(1024)} all-reduce(f32[4352]{0:T(1024)} %pad_maximum_fusion.13), channel_id=1, replica_groups=mesh['d'=4,'c'=2,'h'=2,'l'=2] {'d','c','h','l'}, use_global_device_ids=true, to_apply=%region_15.16 | all-reduce | flops 4352 | bytes 34816 | tf_op jit(solution)/shard_map/psum | solution.py:939
  792.0 2.6 fusion.60
  797.4 73.5 %collective-permute-done.17 = bf16[512,768]{1,0:T(8,128)(2,1)S(1)} collective-permute-done((bf16[512,768]{1,0:T(8,128)(2,1)S(1)}, bf16[512,768]{1,0:T(8,128)(2,1)S(1)}, u32[]{:S(2)}, u32[]{:S(2)}) %collective-permute-start.17) | collective-permute-done | bytes 786464 | tf_op jit(solution)/shard_map/ppermute | solution.py:708
  871.2 3.0 convert_select_fusion
  876.5 28.1 %collective-permute-done.15 = bf16[512,1536]{1,0:T(8,128)(2,1)} collective-permute-done((bf16[512,1536]{1,0:T(8,128)(2,1)}, bf16[512,1536]{1,0:T(8,128)(2,1)}, u32[]{:S(2)}, u32[]{:S(2)}) %collective-permute-start.15) | collective-permute-done | bytes 1572896 | tf_op jit(solution)/shard_map/ppermute | solution.py:708
  907.9 14.6 %collective-permute-start.16 = (bf16[256,1536]{1,0:T(8,128)(2,1)}, bf16[256,1536]{1,0:T(8,128)(2,1)}, u32[]{:S(2)}, u32[]{:S(2)}) collective-permute-start(bf16[256,1536]{1,0:T(8,128)(2,1)} %select_convert_fusion), channel_id=1, source_target_pairs={{4,0},{0,4},{5,1},{1,5},{6,2},{2,6},{7,3},{3,7},{12,8},{8,12},{13,... | collective-permute-start | bytes 2359304 | tf_op jit(solution)/shard_map/ppermute | solution.py:713
  930.8 33.8 %collective-permute-done.14 = bf16[256,1536]{1,0:T(8,128)(2,1)S(1)} collective-permute-done((bf16[256,1536]{1,0:T(8,128)(2,1)S(1)}, bf16[256,1536]{1,0:T(8,128)(2,1)S(1)}, u32[]{:S(2)}, u32[]{:S(2)}) %collective-permute-start.14) | collective-permute-done | bytes 786464 | tf_op jit(solution)/shard_map/ppermute | solution.py:745
  (408 shorter events, 153.6 us)
Async XLA Ops:
  7.2 240.7 %all-gather.7.cloned.1.call-start = ((), (), s32[]{:S(2)}) async-start(), calls=%async_computation.5 | async-start | bytes 3932160 | tf_op jit(solution)/shard_map/all_gather | solution.py:777
  7.3 11.3 %copy-start.73 = (bf16[1,256]{1,0:T(2,128)(2,1)S(1)}, bf16[1,256]{1,0:T(2,128)(2,1)}, u32[]{:S(2)}) copy-start(bf16[1,256]{1,0:T(2,128)(2,1)} %param.20) | copy-start | bytes 1540
  7.3 11.4 %copy-start.74 = (bf16[1,256]{1,0:T(2,128)(2,1)S(1)}, bf16[1,256]{1,0:T(2,128)(2,1)}, u32[]{:S(2)}) copy-start(bf16[1,256]{1,0:T(2,128)(2,1)} %param.27) | copy-start | bytes 1540
  7.3 13.1 %copy-start.75 = (bf16[1,16]{1,0:T(2,128)(2,1)S(1)}, bf16[1,16]{1,0:T(2,128)(2,1)}, u32[]{:S(2)}) copy-start(bf16[1,16]{1,0:T(2,128)(2,1)} %param.26) | copy-start | bytes 100
  7.3 13.1 %copy-start.76 = (bf16[1,16]{1,0:T(2,128)(2,1)S(1)}, bf16[1,16]{1,0:T(2,128)(2,1)}, u32[]{:S(2)}) copy-start(bf16[1,16]{1,0:T(2,128)(2,1)} %param.25) | copy-start | bytes 100
  9.3 19.3 %collective-permute-start.1 = (bf16[256,768]{1,0:T(8,128)(2,1)}, bf16[256,768]{1,0:T(8,128)(2,1)S(1)}, u32[]{:S(2)}, u32[]{:S(2)}) collective-permute-start(bf16[256,768]{1,0:T(8,128)(2,1)} %get-tuple-element.463), channel_id=1, source_target_pairs={{4,0},{0,4},{5,1},{1,5},{6,2},{2,6},{7,3},{3,7},{12,8},{8,12},{13,... | collective-permute-start | bytes 1179656 | tf_op jit(solution)/shard_map/ppermute | solution.py:701
  11.7 19.0 %collective-permute-start.2 = (bf16[256,768]{1,0:T(8,128)(2,1)}, bf16[256,768]{1,0:T(8,128)(2,1)}, u32[]{:S(2)}, u32[]{:S(2)}) collective-permute-start(bf16[256,768]{1,0:T(8,128)(2,1)} %get-tuple-element.465), channel_id=1, source_target_pairs={{4,0},{0,4},{5,1},{1,5},{6,2},{2,6},{7,3},{3,7},{12,8},{8,12},{13,... | collective-permute-start | bytes 1179656 | tf_op jit(solution)/shard_map/ppermute | solution.py:701
  11.7 10.4 %collective-permute-start = (s32[1,1152]{1,0:T(1,128)S(1)}, s32[1,1152]{1,0:T(1,128)S(1)}, u32[]{:S(2)}, u32[]{:S(2)}) collective-permute-start(s32[1,1152]{1,0:T(1,128)S(1)} %copy-done.81), channel_id=1, source_target_pairs={{0,0},{2,4},{4,2},{6,6},{1,1},{3,5},{5,3},{7,7},{8,8},{10,12},{12,... | collective-permute-start | bytes 13832 | tf_op jit(solution)/shard_map/ppermute | solution.py:667
  13.2 103.7 %collective-permute-start.6 = (bf16[256,768]{1,0:T(8,128)(2,1)}, bf16[256,768]{1,0:T(8,128)(2,1)}, u32[]{:S(2)}, u32[]{:S(2)}) collective-permute-start(bf16[256,768]{1,0:T(8,128)(2,1)} %get-tuple-element.461), channel_id=1, source_target_pairs={{4,0},{0,4},{5,1},{1,5},{6,2},{2,6},{7,3},{3,7},{12,8},{8,12},{13,... | collective-permute-start | bytes 1179656 | tf_op jit(solution)/shard_map/ppermute | solution.py:701
  28.6 109.6 %copy-start.26 = (f32[1152,128]{0,1:T(8,128)}, f32[1152,128]{0,1:T(8,128)S(1)}, u32[]{:S(2)}) copy-start(f32[1152,128]{0,1:T(8,128)S(1)} %get-tuple-element.481) | copy-start | bytes 1769476
  28.6 109.6 %copy-start.28 = (f32[1152,128]{0,1:T(8,128)}, f32[1152,128]{0,1:T(8,128)S(1)}, u32[]{:S(2)}) copy-start(f32[1152,128]{0,1:T(8,128)S(1)} %get-tuple-element.482) | copy-start | bytes 1769476
  119.0 229.3 %all-gather.5.cloned.1.call-start = ((), (), s32[]{:S(2)}) async-start(), calls=%async_computation.4 | async-start | bytes 7864320 | tf_op jit(solution)/shard_map/all_gather | solution.py:776
  130.8 10.8 %copy-start.19 = (f32[1152,512]{0,1:T(8,128)}, f32[1152,512]{0,1:T(8,128)S(1)}, u32[]{:S(2)}) copy-start(f32[1152,512]{0,1:T(8,128)S(1)} %slice.194) | copy-start | bytes 7077892
  144.6 7.3 copy-start.64
  156.6 227.6 %all-gather.11.cloned.1.call-start = ((), (), s32[]{:S(2)}) async-start(), calls=%async_computation.7 | async-start | bytes 7864320 | tf_op jit(solution)/shard_map/all_gather | solution.py:821
  162.2 6.4 copy-start.30
  162.2 6.4 copy-start.38
  177.4 70.5 %collective-permute-start.8 = (bf16[512,1536]{1,0:T(8,128)(2,1)}, bf16[512,1536]{1,0:T(8,128)(2,1)}, u32[]{:S(2)}, u32[]{:S(2)}) collective-permute-start(bf16[512,1536]{1,0:T(8,128)(2,1)} %pad_maximum_fusion.8), channel_id=1, source_target_pairs={{2,0},{0,2},{3,1},{1,3},{6,4},{4,6},{7,5},{5,7},{10,8},{8,10},{11,... | collective-permute-start | bytes 4718600 | tf_op jit(solution)/shard_map/ppermute | solution.py:787
  197.6 50.3 %copy-start.47 = (s32[4,288]{1,0:T(4,128)}, s32[4,288]{1,0:T(4,128)S(1)}, u32[]{:S(2)}) copy-start(s32[4,288]{1,0:T(4,128)S(1)} %get-tuple-element.781) | copy-start | bytes 13828
  197.6 56.6 %copy-start.16 = (bf16[1152,2,128]{2,0,1:T(8,128)(2,1)}, bf16[1152,2,128]{2,0,1:T(8,128)(2,1)S(1)}, u32[]{:S(2)}) copy-start(bf16[1152,2,128]{2,0,1:T(8,128)(2,1)S(1)} %get-tuple-element.758) | copy-start | bytes 1769476
  197.6 56.7 %copy-start.18 = (bf16[1152,2,128]{2,0,1:T(8,128)(2,1)}, bf16[1152,2,128]{2,0,1:T(8,128)(2,1)S(1)}, u32[]{:S(2)}) copy-start(bf16[1152,2,128]{2,0,1:T(8,128)(2,1)S(1)} %get-tuple-element.759) | copy-start | bytes 1769476
  197.6 56.7 %copy-start.22 = (bf16[2,576,2,2,128]{4,1,3,2,0:T(8,128)(2,1)}, bf16[2,576,2,2,128]{4,1,3,2,0:T(8,128)(2,1)S(1)}, u32[]{:S(2)}) copy-start(bf16[2,576,2,2,128]{4,1,3,2,0:T(8,128)(2,1)S(1)} %get-tuple-element.760) | copy-start | bytes 3538948
  197.6 56.7 %copy-start.55 = (s32[2,576]{1,0:T(2,128)}, s32[2,576]{1,0:T(2,128)S(1)}, u32[]{:S(2)}) copy-start(s32[2,576]{1,0:T(2,128)S(1)} %get-tuple-element.790) | copy-start | bytes 13828
  202.0 52.4 %copy-start.62 = (f32[1,1,8,256]{3,2,1,0:T(8,128)S(1)}, f32[1,1,8,256]{3,2,1,0:T(8,128)}, u32[]{:S(2)}) copy-start(f32[1,1,8,256]{3,2,1,0:T(8,128)} %get-tuple-element.467) | copy-start | bytes 24580
  247.9 149.3 %all-gather.9.cloned.1.call-start = ((), (), s32[]{:S(2)}) async-start(), calls=%async_computation.6 | async-start | bytes 3932160 | tf_op jit(solution)/shard_map/all_gather | solution.py:838
  248.0 6.4 copy-start.41
  248.0 100.2 %collective-permute-start.3 = (bf16[288,2048]{1,0:T(8,128)(2,1)}, bf16[288,2048]{1,0:T(8,128)(2,1)S(1)}, u32[]{:S(2)}, u32[]{:S(2)}) collective-permute-start(bf16[288,2048]{1,0:T(8,128)(2,1)} %param.31), channel_id=1, source_target_pairs={{0,0},{2,4},{4,2},{6,6},{1,1},{3,5},{5,3},{7,7},{8,8},{10,12},{12,... | collective-permute-start | bytes 3538952 | tf_op jit(solution)/shard_map/ppermute | solution.py:667
  250.0 97.6 %collective-permute-start.7 = (bf16[512,768]{1,0:T(8,128)(2,1)}, bf16[512,768]{1,0:T(8,128)(2,1)}, u32[]{:S(2)}, u32[]{:S(2)}) collective-permute-start(bf16[512,768]{1,0:T(8,128)(2,1)} %bitcast.291), channel_id=1, source_target_pairs={{2,0},{0,2},{3,1},{1,3},{6,4},{4,6},{7,5},{5,7},{10,8},{8,10},{11,... | collective-permute-start | bytes 2359304 | tf_op jit(solution)/shard_map/ppermute | solution.py:822
  254.3 5.3 copy-start
  347.7 312.2 %reduce-scatter.5.cloned.1.call-start = ((), (), s32[]{:S(2)}) async-start(), calls=%async_computation.8 | async-start | bytes 7864320 | tf_op jit(solution)/shard_map/reduce_scatter | solution.py:725
  348.2 28.4 %collective-permute-start.4 = (bf16[288,2048]{1,0:T(8,128)(2,1)S(1)}, bf16[288,2048]{1,0:T(8,128)(2,1)}, u32[]{:S(2)}, u32[]{:S(2)}) collective-permute-start(bf16[288,2048]{1,0:T(8,128)(2,1)S(1)} %collective-permute-done.3.refs_2_), channel_id=1, source_target_pairs={{1,0},{0,1},{3,2},{2,3},{5,4},{4,5},{7,6},{6,7},{9,8},{8,9},{11,10... | collective-permute-start | bytes 3538952 | tf_op jit(solution)/shard_map/ppermute | solution.py:673
  378.1 4.6 collective-permute-start.5
  423.5 363.2 %reduce-scatter.11.cloned.1.call-start = ((), (), s32[]{:S(2)}) async-start(), calls=%async_computation.11 | async-start | bytes 7864320 | tf_op jit(solution)/shard_map/reduce_scatter | solution.py:725
  423.5 7.4 copy-start.82
  441.6 434.8 %reduce-scatter.9.cloned.1.call-start = ((), (), s32[]{:S(2)}) async-start(), calls=%async_computation.10 | async-start | bytes 7864320 | tf_op jit(solution)/shard_map/reduce_scatter | solution.py:725
  454.4 12.1 %copy-start.85 = (bf16[1152,768]{1,0:T(8,128)(2,1)S(1)}, bf16[1152,768]{1,0:T(8,128)(2,1)}, u32[]{:S(2)}) copy-start(bf16[1152,768]{1,0:T(8,128)(2,1)} %copy-done.84) | copy-start | bytes 5308420
  454.4 12.1 %copy-start.87 = (bf16[1152,768]{1,0:T(8,128)(2,1)S(1)}, bf16[1152,768]{1,0:T(8,128)(2,1)}, u32[]{:S(2)}) copy-start(bf16[1152,768]{1,0:T(8,128)(2,1)} %copy-done.86) | copy-start | bytes 5308420
  454.4 85.9 %slice-start.2 = ((s8[4718592]{0:T(1024)(128)(4,1)}), s8[4194304]{0:T(1024)(128)(4,1)S(1)}, s32[]{:S(2)}) async-start(s8[4718592]{0:T(1024)(128)(4,1)} %bitcast.280), calls=%async_computation.14 | async-start | bytes 8388608
  466.5 73.8 %slice-start.3 = ((s8[4718592]{0:T(1024)(128)(4,1)}), s8[524288]{0:T(1024)(128)(4,1)S(1)}, s32[]{:S(2)}) async-start(s8[4718592]{0:T(1024)(128)(4,1)} %bitcast.280), calls=%async_computation.15 | async-start | bytes 1048576
  479.5 60.9 %copy-start.32 = (bf16[1152,1536]{1,0:T(8,128)(2,1)S(1)}, bf16[1152,1536]{1,0:T(8,128)(2,1)}, u32[]{:S(2)}) copy-start(bf16[1152,1536]{1,0:T(8,128)(2,1)} %pad_maximum_fusion.2) | copy-start | bytes 10616836
  550.8 371.7 %reduce-scatter.7.cloned.1.call-start = ((), (), s32[]{:S(2)}) async-start(), calls=%async_computation.9 | async-start | bytes 7864320 | tf_op jit(solution)/shard_map/reduce_scatter | solution.py:739
  585.5 6.1 copy-start.10
  618.9 5.8 copy-start.10
  633.1 13.6 %copy-start.35 = (bf16[1152,2,128]{0,2,1:T(8,128)(2,1)}, bf16[1152,2,128]{0,2,1:T(8,128)(2,1)S(1)}, u32[]{:S(2)}) copy-start(bf16[1152,2,128]{0,2,1:T(8,128)(2,1)S(1)} %convert_element_type.180) | copy-start | bytes 1769476
  640.8 5.9 slice-start.5
  663.2 5.4 copy-start.1
  663.2 5.4 copy-start.3
  668.6 30.9 %copy-start.39 = (bf16[1152,768]{1,0:T(8,128)(2,1)S(1)}, bf16[1152,768]{1,0:T(8,128)(2,1)}, u32[]{:S(2)}) copy-start(bf16[1152,768]{1,0:T(8,128)(2,1)} %multiply_convert_fusion.3) | copy-start | bytes 5308420
  668.6 30.9 %copy-start.79 = (bf16[2048,768]{1,0:T(8,128)(2,1)S(1)}, bf16[2048,768]{1,0:T(8,128)(2,1)}, u32[]{:S(2)}) copy-start(bf16[2048,768]{1,0:T(8,128)(2,1)} %all-gather.7.cloned.1.call-done) | copy-start | bytes 9437188
  699.5 6.4 copy-start.4
  699.6 6.4 copy-start.80
  699.6 6.4 copy-start.83
  713.0 4.6 collective-permute-start.9
  721.9 70.1 %collective-permute-start.10 = (bf16[288,2048]{1,0:T(8,128)(2,1)}, bf16[288,2048]{1,0:T(8,128)(2,1)}, u32[]{:S(2)}, u32[]{:S(2)}) collective-permute-start(bf16[288,2048]{1,0:T(8,128)(2,1)} %slice.326), channel_id=1, source_target_pairs={{1,0},{0,1},{3,2},{2,3},{5,4},{4,5},{7,6},{6,7},{9,8},{8,9},{11,10... | collective-permute-start | bytes 3538952 | tf_op jit(solution)/shard_map/ppermute | solution.py:688
  722.9 148.3 %collective-permute-start.12 = (bf16[288,2048]{1,0:T(8,128)(2,1)S(1)}, bf16[288,2048]{1,0:T(8,128)(2,1)}, u32[]{:S(2)}, u32[]{:S(2)}) collective-permute-start(bf16[288,2048]{1,0:T(8,128)(2,1)S(1)} %get-tuple-element.189), channel_id=1, source_target_pairs={{0,0},{2,4},{4,2},{6,6},{1,1},{3,5},{5,3},{7,7},{8,8},{10,12},{12,... | collective-permute-start | bytes 3538952 | tf_op jit(solution)/shard_map/ppermute | solution.py:667
  787.8 83.0 %collective-permute-start.17 = (bf16[512,768]{1,0:T(8,128)(2,1)S(1)}, bf16[512,768]{1,0:T(8,128)(2,1)S(1)}, u32[]{:S(2)}, u32[]{:S(2)}) collective-permute-start(bf16[512,768]{1,0:T(8,128)(2,1)S(1)} %slice.231), channel_id=1, source_target_pairs={{2,0},{0,2},{3,1},{1,3},{6,4},{4,6},{7,5},{5,7},{10,8},{8,10},{11,... | collective-permute-start | bytes 2359304 | tf_op jit(solution)/shard_map/ppermute | solution.py:708
  790.4 80.4 %copy-start.40 = (bf16[512,1536]{1,0:T(8,128)(2,1)S(1)}, bf16[512,1536]{1,0:T(8,128)(2,1)}, u32[]{:S(2)}) copy-start(bf16[512,1536]{1,0:T(8,128)(2,1)} %reduce-scatter.11.cloned.1.call-done) | copy-start | bytes 4718596
  790.4 114.1 %collective-permute-start.15 = (bf16[512,1536]{1,0:T(8,128)(2,1)}, bf16[512,1536]{1,0:T(8,128)(2,1)}, u32[]{:S(2)}, u32[]{:S(2)}) collective-permute-start(bf16[512,1536]{1,0:T(8,128)(2,1)} %reduce-scatter.5.cloned.1.call-done), channel_id=1, source_target_pairs={{2,0},{0,2},{3,1},{1,3},{6,4},{4,6},{7,5},{5,7},{10,8},{8,10},{11,... | collective-permute-start | bytes 4718600 | tf_op jit(solution)/shard_map/ppermute | solution.py:708
  794.6 76.6 %copy-start.5 = (f32[288,2048]{1,0:T(8,128)S(1)}, f32[288,2048]{1,0:T(8,128)}, u32[]{:S(2)}) copy-start(f32[288,2048]{1,0:T(8,128)} %copy-done.4) | copy-start | bytes 7077892
  794.6 79.6 %collective-permute-start.11 = (bf16[288,2048]{1,0:T(8,128)(2,1)S(1)}, bf16[288,2048]{1,0:T(8,128)(2,1)S(1)}, u32[]{:S(2)}, u32[]{:S(2)}) collective-permute-start(bf16[288,2048]{1,0:T(8,128)(2,1)S(1)} %fusion.60), channel_id=1, source_target_pairs={{0,0},{2,4},{4,2},{6,6},{1,1},{3,5},{5,3},{7,7},{8,8},{10,12},{12,... | collective-permute-start | bytes 3538952 | tf_op jit(solution)/shard_map/ppermute | solution.py:667
  871.1 4.1 collective-permute-start.18
  907.9 18.0 %collective-permute-start.16 = (bf16[256,1536]{1,0:T(8,128)(2,1)}, bf16[256,1536]{1,0:T(8,128)(2,1)}, u32[]{:S(2)}, u32[]{:S(2)}) collective-permute-start(bf16[256,1536]{1,0:T(8,128)(2,1)} %select_convert_fusion), channel_id=1, source_target_pairs={{4,0},{0,4},{5,1},{1,5},{6,2},{2,6},{7,3},{3,7},{12,8},{8,12},{13,... | collective-permute-start | bytes 2359304 | tf_op jit(solution)/shard_map/ppermute | solution.py:713
  924.1 3.2 collective-permute-start.13
  927.7 36.9 %collective-permute-start.14 = (bf16[256,1536]{1,0:T(8,128)(2,1)S(1)}, bf16[256,1536]{1,0:T(8,128)(2,1)S(1)}, u32[]{:S(2)}, u32[]{:S(2)}) collective-permute-start(bf16[256,1536]{1,0:T(8,128)(2,1)S(1)} %broadcast_select_fusion.2), channel_id=1, source_target_pairs={{2,0},{0,2},{3,1},{1,3},{6,4},{4,6},{7,5},{5,7},{10,8},{8,10},{11,... | collective-permute-start | bytes 2359304 | tf_op jit(solution)/shard_map/ppermute | solution.py:745
  (66 other events, 163.7 us)
Sparse Core Ops, SparseCore 0:
  119.1 46.3 all-gather.6
  168.0 70.0 all-gather.4
  248.0 69.2 all-gather.10
  347.8 42.7 all-gather.8
  423.6 68.8 reduce-scatter.4
  495.3 70.0 reduce-scatter.10
  568.4 70.0 reduce-scatter.8
  660.1 70.4 reduce-scatter.6

commit v3 on v2

--- a/solution.py
+++ b/solution.py
@@ -8,10 +8,9 @@
 from jax.sharding import Mesh
 from jax.sharding import PartitionSpec as P
 
+
 HEAD_WIDTH = 128
-DECODER_LAYERS = 1
 NSEQ = 3
-QBLOCK = 576
 
 
 EPS = 1e-06
@@ -20,12 +19,6 @@
 
 def rms_scale(values, gain):
     return values * lax.rsqrt(jnp.mean(values * values, axis=-1, keepdims=True) + EPS) * gain
-
-
-def rotate(values, cosine, sine_table):
-    half_size = values.shape[-1] // 2
-    turned = jnp.concatenate([-values[..., half_size:], values[..., :half_size]], axis=-1)
-    return values * cosine + turned * sine_table
 
 
 def swiglu(gate_raw, up_raw):
@@ -41,9 +34,13 @@
     position = (row_index - first_row).astype(jnp.float32)
     frequency = THETA ** (-(jnp.arange(HEAD_WIDTH // 2, dtype=jnp.float32) * (2.0 / HEAD_WIDTH)))
     angles = position[:, None] * frequency[None, :]
-    cosine = jnp.concatenate([jnp.cos(angles), jnp.cos(angles)], axis=1)[:, None, :]
-    sine_table = jnp.concatenate([jnp.sin(angles), jnp.sin(angles)], axis=1)[:, None, :]
-    return (cosine, sine_table)
+    sine = jnp.sin(angles)
+    cosine = jnp.cos(angles)
+    return (
+        jnp.concatenate([cosine, cosine], axis=1),
+        jnp.concatenate([-sine, sine], axis=1),
+        first_row[:, None],
+    )
 
 
 def contract_rows(left, right):
@@ -56,93 +53,6 @@
     return lax.dot_general(
         left, right, (((1,), (1,)), ((), ())), preferred_element_type=jnp.float32
     )
-
-
-def block_items(queries, sequence_labels, columns):
-    grouped_rows, kv_heads, repeat, head_size = queries.shape
-    blocks = grouped_rows // QBLOCK
-    return (
-        (
-            queries.reshape(blocks, QBLOCK, kv_heads, repeat, head_size),
-            sequence_labels.reshape(blocks, QBLOCK),
-            columns.reshape(blocks, QBLOCK),
-        ),
-        columns,
-    )
-
-
-def attend_forward(queries, key_reduced, value_reduced, sequence_labels, row_index):
-    grouped_rows, kv_heads, repeat, head_size = queries.shape
-    score_scale = HEAD_WIDTH ** (-0.5)
-    items, columns = block_items(queries, sequence_labels, row_index)
-
-    def one_block(block_item):
-        q_block, id_block, row_block = block_item
-        allowed = (id_block[:, None] == sequence_labels[None, :]) & (
-            columns[None, :] <= row_block[:, None]
-        )
-        scores = (
-            jnp.einsum("qgrd,kgd->grqk", q_block, key_reduced, preferred_element_type=jnp.float32)
-            * score_scale
-        )
-        weights = jnp.where(allowed[None, None], jnp.exp(scores), 0.0)
-        totals = jnp.sum(weights, axis=-1, keepdims=True)
-        shares = (weights / totals).astype(jnp.bfloat16)
-        attention_result = jnp.einsum(
-            "grqk,kgd->qgrd", shares, value_reduced, preferred_element_type=jnp.float32
-        )
-        return (attention_result.astype(jnp.bfloat16), totals)
-
-    attention_result, totals = lax.map(one_block, items)
-    return (attention_result.reshape(grouped_rows, kv_heads * repeat * head_size), totals)
-
-
-def attend_backward(
-    queries, key_reduced, value_reduced, sequence_labels, row_index, totals, out_grad
-):
-    grouped_rows, kv_heads, repeat, head_size = queries.shape
-    score_scale = HEAD_WIDTH ** (-0.5)
-    items, columns = block_items(queries, sequence_labels, row_index)
-    grad_blocks = out_grad.reshape(grouped_rows // QBLOCK, QBLOCK, kv_heads, repeat, head_size)
-
-    def one_block(running, block_item):
-        key_grad, value_grad = running
-        q_block, id_block, row_block, total_block, grad_block = block_item
-        allowed = (id_block[:, None] == sequence_labels[None, :]) & (
-            columns[None, :] <= row_block[:, None]
-        )
-        scores = (
-            jnp.einsum("qgrd,kgd->grqk", q_block, key_reduced, preferred_element_type=jnp.float32)
-            * score_scale
-        )
-        shares = jnp.where(allowed[None, None], jnp.exp(scores), 0.0) / total_block
-        low_shares = shares.astype(jnp.bfloat16)
-        share_grad = jnp.einsum(
-            "qgrd,kgd->grqk", grad_block, value_reduced, preferred_element_type=jnp.float32
-        )
-        row_inner = jnp.sum(shares * share_grad, axis=-1, keepdims=True)
-        score_grad = (shares * (share_grad - row_inner)).astype(jnp.bfloat16)
-        query_grad = (
-            jnp.einsum(
-                "grqk,kgd->qgrd", score_grad, key_reduced, preferred_element_type=jnp.float32
-            )
-            * score_scale
-        )
-        key_grad = (
-            key_grad
-            + jnp.einsum("grqk,qgrd->kgd", score_grad, q_block, preferred_element_type=jnp.float32)
-            * score_scale
-        )
-        value_grad = value_grad + jnp.einsum(
-            "grqk,qgrd->kgd", low_shares, grad_block, preferred_element_type=jnp.float32
-        )
-        return ((key_grad, value_grad), query_grad)
-
-    zero_keys = jnp.zeros(key_reduced.shape, jnp.float32)
-    (key_grad, value_grad), query_grad = lax.scan(
-        one_block, (zero_keys, zero_keys), items + (totals, grad_blocks)
-    )
-    return (query_grad.reshape(grouped_rows, kv_heads * repeat, head_size), key_grad, value_grad)
 
 
 MESH = pl.DeviceIdType.MESH
@@ -566,7 +476,7 @@
             along(step, k).wait_send()
 
 
-def exchange(name, collective_id, partial, aux, outs, epilogue, gather):
+def exchange(collective_id, partial, aux, outs, epilogue, gather):
     tl = lax.axis_size("l")
     total, width = partial.shape
     own = total // (2 * tl)
@@ -600,7 +510,6 @@
     ]
     return pl.pallas_call(
         functools.partial(exchange_kernel, tl, epilogue, len(aux), len(outs), gather),
-        name=name,
         out_shape=tuple(out_shape),
         in_specs=[anywhere] + [vmem] * len(aux),
         out_specs=out_specs,
@@ -659,6 +568,252 @@
     return None
 
 
+def key_tile(rows):
+    return next(size for size in (384, 256, 128) if rows % size == 0)
+
+
+def turn(values):
+    return pltpu.roll(values, HEAD_WIDTH // 2, 1)
+
+
+def head_norm(values):
+    return lax.rsqrt(jnp.mean(values * values, axis=-1, keepdims=True) + EPS)
+
+
+def tile_mask(first, start, tile, row0, rows):
+    keys = start + lax.broadcasted_iota(jnp.int32, (rows, tile), 1)
+    last = row0 + lax.broadcasted_iota(jnp.int32, (rows, tile), 0)
+    return jnp.logical_and(keys >= first, keys <= last)
+
+
+def dot_last(left, right):
+    return lax.dot_general(
+        left, right, (((1,), (1,)), ((), ())), preferred_element_type=jnp.float32
+    )
+
+
+def attention_kernel(blocks, repeat, order_ref, *refs):
+    q, k, v, cosine, sine, q_gain, k_gain, first = refs[:8]
+    qr, kr, vb, out, total = refs[8:13]
+    acc, den = refs[13:]
+    rows = q.shape[0] // blocks
+    tile = key_tile(q.shape[0])
+    scale = HEAD_WIDTH**-0.5
+
+    def rotated(values, gain, at):
+        scaled = values * head_norm(values) * gain
+        return (scaled * cosine[at, :] + turn(scaled) * sine[at, :]).astype(jnp.bfloat16)
+
+    def prepare(i, carry):
+        at, to = rows_at(i, rows), rows_at(order_ref[i], rows)
+        for r in range(repeat):
+            head = slice(r * HEAD_WIDTH, (r + 1) * HEAD_WIDTH)
+            qr[at, head] = rotated(q[at, head], q_gain[...], at)
+        kr[to, :] = rotated(k[at, :], k_gain[...], at)
+        vb[to, :] = v[at, :].astype(jnp.bfloat16)
+        return carry
+
+    lax.fori_loop(0, blocks, prepare, 0)
+
+    def attend(i, carry):
+        at = rows_at(i, rows)
+        row0 = order_ref[i] * rows
+        acc[...] = jnp.zeros_like(acc)
+        den[...] = jnp.zeros_like(den)
+
+        def over_keys(t, inner):
+            keys = rows_at(t, tile)
+            mask = tile_mask(first[at, :], t * tile, tile, row0, rows)
+            for r in range(repeat):
+                head = slice(r * HEAD_WIDTH, (r + 1) * HEAD_WIDTH)
+                scores = dot_last(qr[at, head], kr[keys, :]) * scale
+                weights = jnp.where(mask, jnp.exp(scores), 0.0)
+                den[r] += jnp.sum(weights, axis=-1, keepdims=True)
+                acc[r] += jnp.dot(
+                    weights.astype(jnp.bfloat16), vb[keys, :], preferred_element_type=jnp.float32
+                )
+            return inner
+
+        lax.fori_loop(0, (row0 + rows + tile - 1) // tile, over_keys, 0)
+        for r in range(repeat):
+            head = slice(r * HEAD_WIDTH, (r + 1) * HEAD_WIDTH)
+            out[at, head] = (acc[r] / den[r]).astype(jnp.bfloat16)
+            total[at, r : r + 1] = den[r]
+        return carry
+
+    lax.fori_loop(0, blocks, attend, 0)
+
+
+def attention_specs(rows, q_heads, kv_heads):
+    repeat = q_heads // kv_heads
+
+    def columns(width, start=0):
+        return pl.BlockSpec((rows, width * HEAD_WIDTH), lambda g, order: (0, start // width + g))
+
+    def fixed(*shape):
+        return pl.BlockSpec(shape, lambda g, order: (0, 0))
+
+    raw = [columns(repeat), columns(1, q_heads), columns(1, q_heads + kv_heads)]
+    tables = [
+        fixed(rows, HEAD_WIDTH),
+        fixed(rows, HEAD_WIDTH),
+        fixed(1, HEAD_WIDTH),
+        fixed(1, HEAD_WIDTH),
+        fixed(rows, 1),
+    ]
+    return repeat, columns, fixed, raw, tables
+
+
+def attention(qkv, tables, order, q_heads, kv_heads):
+    rows = qkv.shape[0]
+    blocks = order.shape[0]
+    repeat, columns, _, raw, table_specs = attention_specs(rows, q_heads, kv_heads)
+    wide, narrow = q_heads * HEAD_WIDTH, kv_heads * HEAD_WIDTH
+    return pl.pallas_call(
+        functools.partial(attention_kernel, blocks, repeat),
+        name="attention",
+        out_shape=(
+            jax.ShapeDtypeStruct((rows, wide), jnp.bfloat16),
+            jax.ShapeDtypeStruct((rows, narrow), jnp.bfloat16),
+            jax.ShapeDtypeStruct((rows, narrow), jnp.bfloat16),
+            jax.ShapeDtypeStruct((rows, wide), jnp.bfloat16),
+            jax.ShapeDtypeStruct((rows, narrow), jnp.float32),
+        ),
+        grid_spec=pltpu.PrefetchScalarGridSpec(
+            num_scalar_prefetch=1,
+            grid=(kv_heads,),
+            in_specs=raw + table_specs,
+            out_specs=[columns(repeat), columns(1), columns(1), columns(repeat), columns(1)],
+            scratch_shapes=[
+                pltpu.VMEM((repeat, rows // blocks, HEAD_WIDTH), jnp.float32),
+                pltpu.VMEM((repeat, rows // blocks, 1), jnp.float32),
+            ],
+        ),
+        compiler_params=pltpu.CompilerParams(vmem_limit_bytes=50 << 20),
+        cost_estimate=pl.CostEstimate(
+            flops=4 * rows * rows * wide, bytes_accessed=60_000_000, transcendentals=0
+        ),
+    )(order, qkv, qkv, qkv, *tables)
+
+
+def attention_pull_kernel(blocks, repeat, order_ref, *refs):
+    q, k, cosine, sine, q_gain, k_gain, first, qr, kr, vb, total, grad = refs[:12]
+    dq, dk, dv, dq_gain, dk_gain = refs[12:17]
+    shares, share_grads, dq_acc, dk_acc, dv_acc, inner_sum = refs[17:]
+    rows = q.shape[0] // blocks
+    tile = key_tile(q.shape[0])
+    scale = HEAD_WIDTH**-0.5
+    dk_acc[...] = jnp.zeros_like(dk_acc)
+    dv_acc[...] = jnp.zeros_like(dv_acc)
+
+    @pl.when(pl.program_id(0) == 0)
+    def _():
+        dq_gain[...] = jnp.zeros_like(dq_gain)
+        dk_gain[...] = jnp.zeros_like(dk_gain)
+
+    def pull(raw, gain, turned_grad, at, gain_out):
+        scaled_grad = turned_grad * cosine[at, :] + turn(turned_grad * sine[at, :])
+        r = head_norm(raw)
+        gain_out[0:1, :] += jnp.sum(scaled_grad * raw * r, axis=0, keepdims=True)
+        scaled = scaled_grad * gain
+        inner = jnp.mean(raw * scaled, axis=-1, keepdims=True)
+        return (r * scaled - raw * (r * r * r * inner)).astype(jnp.bfloat16)
+
+    def over_rows(i, carry):
+        at = rows_at(i, rows)
+        row0 = order_ref[i] * rows
+        tiles = (row0 + rows + tile - 1) // tile
+        dq_acc[...] = jnp.zeros_like(dq_acc)
+        inner_sum[...] = jnp.zeros_like(inner_sum)
+
+        def first_pass(t, inner):
+            keys = rows_at(t, tile)
+            mask = tile_mask(first[at, :], t * tile, tile, row0, rows)
+            for r in range(repeat):
+                head = slice(r * HEAD_WIDTH, (r + 1) * HEAD_WIDTH)
+                scores = dot_last(qr[at, head], kr[keys, :]) * scale
+                share = jnp.where(mask, jnp.exp(scores), 0.0) * (1.0 / total[at, r : r + 1])
+                share_grad = dot_last(grad[at, head], vb[keys, :])
+                inner_sum[r] += jnp.sum(share * share_grad, axis=-1, keepdims=True)
+                shares[t, r] = share
+                share_grads[t, r] = share_grad
+            return inner
+
+        lax.fori_loop(0, tiles, first_pass, 0)
+
+        def second_pass(t, inner):
+            keys = rows_at(t, tile)
+            for r in range(repeat):
+                head = slice(r * HEAD_WIDTH, (r + 1) * HEAD_WIDTH)
+                share = shares[t, r]
+                score_grad = (share * (share_grads[t, r] - inner_sum[r])).astype(jnp.bfloat16)
+                dq_acc[r] += jnp.dot(score_grad, kr[keys, :], preferred_element_type=jnp.float32)
+                dk_acc[keys, :] += contract_rows(score_grad, qr[at, head])
+                dv_acc[keys, :] += contract_rows(share.astype(jnp.bfloat16), grad[at, head])
+            return inner
+
+        lax.fori_loop(0, tiles, second_pass, 0)
+        for r in range(repeat):
+            head = slice(r * HEAD_WIDTH, (r + 1) * HEAD_WIDTH)
+            dq[at, head] = pull(q[at, head], q_gain[...], dq_acc[r] * scale, at, dq_gain)
+        return carry
+
+    lax.fori_loop(0, blocks, over_rows, 0)
+
+    def finish(i, carry):
+        at, to = rows_at(i, rows), rows_at(order_ref[i], rows)
+        dk[at, :] = pull(k[at, :], k_gain[...], dk_acc[to, :] * scale, at, dk_gain)
+        dv[at, :] = dv_acc[to, :].astype(jnp.bfloat16)
+        return carry
+
+    lax.fori_loop(0, blocks, finish, 0)
+
+
+def attention_pull(qkv, tables, order, kept, grad, q_heads, kv_heads):
+    rows = qkv.shape[0]
+    blocks = order.shape[0]
+    repeat, columns, fixed, raw, table_specs = attention_specs(rows, q_heads, kv_heads)
+    wide, narrow = q_heads * HEAD_WIDTH, kv_heads * HEAD_WIDTH
+    own, tile = rows // blocks, key_tile(rows)
+    return pl.pallas_call(
+        functools.partial(attention_pull_kernel, blocks, repeat),
+        name="attention_pull",
+        out_shape=(
+            jax.ShapeDtypeStruct((rows, wide), jnp.bfloat16),
+            jax.ShapeDtypeStruct((rows, narrow), jnp.bfloat16),
+            jax.ShapeDtypeStruct((rows, narrow), jnp.bfloat16),
+            jax.ShapeDtypeStruct((8, HEAD_WIDTH), jnp.float32),
+            jax.ShapeDtypeStruct((8, HEAD_WIDTH), jnp.float32),
+        ),
+        grid_spec=pltpu.PrefetchScalarGridSpec(
+            num_scalar_prefetch=1,
+            grid=(kv_heads,),
+            in_specs=raw[:2]
+            + table_specs
+            + [columns(repeat), columns(1), columns(1), columns(1), columns(repeat)],
+            out_specs=[
+                columns(repeat),
+                columns(1),
+                columns(1),
+                fixed(8, HEAD_WIDTH),
+                fixed(8, HEAD_WIDTH),
+            ],
+            scratch_shapes=[
+                pltpu.VMEM((rows // tile, repeat, own, tile), jnp.float32),
+                pltpu.VMEM((rows // tile, repeat, own, tile), jnp.float32),
+                pltpu.VMEM((repeat, own, HEAD_WIDTH), jnp.float32),
+                pltpu.VMEM((rows, HEAD_WIDTH), jnp.float32),
+                pltpu.VMEM((rows, HEAD_WIDTH), jnp.float32),
+                pltpu.VMEM((repeat, own, 1), jnp.float32),
+            ],
+        ),
+        compiler_params=pltpu.CompilerParams(vmem_limit_bytes=56 << 20),
+        cost_estimate=pl.CostEstimate(
+            flops=10 * rows * rows * wide, bytes_accessed=120_000_000, transcendentals=0
+        ),
+    )(order, qkv, qkv, *tables, *kept, grad)
+
+
 def shift_perm(size, step):
     return [((place + step) % size, place) for place in range(size)]
 
@@ -705,7 +860,8 @@
 
 def return_halves(near, far):
     core = lax.axis_index("c")
-    sums = near.astype(jnp.float32) + lax.ppermute(far, "h", shift_perm(2, 1)).astype(jnp.float32)
+    far = lax.ppermute(far, "h", shift_perm(2, 1))
+    sums = near.astype(jnp.float32) + far.astype(jnp.float32)
     rows = sums.shape[0] // 2
     first, second = sums[:rows], sums[rows:]
     mine = jnp.where(core == 0, first, second)
@@ -781,16 +937,6 @@
     gains = jnp.concatenate([attn_gain[0], mlp_gain[0], q_gain[0], k_gain[0]]).astype(jnp.float32)
     gains = jnp.pad(gains, (0, 1024 - gains.shape[0])).reshape(8, 128)
     labels = trade(segment_ids)[0]
-    qkv_full, o_full, group, gains = enter(
-        q_weight[0], key_matrix[0], value_matrix[0], o_weight[0], after(tokens, mid_rows), gains
-    )
-    mid_far = lax.ppermute(after(mid_rows, group), "h", shift_perm(2, 1))
-    gains = gains.reshape(gains.shape[0], -1)
-    attn_scale = gains[:, :cut].reshape(-1)
-    mlp_scale = gains[:, cut : 2 * cut].reshape(-1)
-    q_scale = gains[:, 2 * cut : 2 * cut + head_cut].reshape(-1)
-    k_scale = gains[:, 2 * cut + head_cut : 2 * cut + 2 * head_cut].reshape(-1)
-
     order = jnp.stack(
         [
             ((core + core_step) % 2) * places + (place + step) % places
@@ -800,34 +946,34 @@
     )
     row_index = (order[:, None] * own_rows + jnp.arange(own_rows, dtype=jnp.int32)[None, :]).reshape(-1)
     labels = labels.reshape(2 * places, own_rows)[order].reshape(-1)
-    cosine, sine_table = rotary_tables(labels, row_index)
+    cosine, sine, first_row = rotary_tables(labels, row_index)
+    qkv_full, o_full, group, gains = enter(
+        q_weight[0], key_matrix[0], value_matrix[0], o_weight[0], after(tokens, mid_rows), gains
+    )
+    mid_far = lax.ppermute(after(mid_rows, group), "h", shift_perm(2, 1))
+    down_far = lax.ppermute(after(down_rows, group), "h", shift_perm(2, 1))
+    cotangent = trade(after(cotangent, group))
+    gains = gains.reshape(gains.shape[0], -1)
+    attn_scale = gains[:, :cut].reshape(-1)
+    mlp_scale = gains[:, cut : 2 * cut].reshape(-1)
+    q_scale = gains[:, 2 * cut : 2 * cut + head_cut].reshape(-1)
+    k_scale = gains[:, 2 * cut + head_cut : 2 * cut + 2 * head_cut].reshape(-1)
 
     stream = group[:own_rows]
     normed = rms_scale(group.astype(jnp.float32), attn_scale).astype(jnp.bfloat16)
-    rows = normed.shape[0]
     head_count, kv_heads = q_cols // HEAD_WIDTH, kv_cols // HEAD_WIDTH
     qkv = jnp.dot(normed, qkv_full, preferred_element_type=jnp.float32)
-    queries = qkv[:, :q_cols].reshape(rows, head_count, HEAD_WIDTH)
-    keys = qkv[:, q_cols : q_cols + kv_cols].reshape(rows, kv_heads, HEAD_WIDTH)
-    value_reduced = (
-        qkv[:, q_cols + kv_cols :].reshape(rows, kv_heads, HEAD_WIDTH).astype(jnp.bfloat16)
-    )
-    query_reduced = rotate(rms_scale(queries, q_scale), cosine, sine_table).astype(jnp.bfloat16)
-    key_reduced = rotate(rms_scale(keys, k_scale), cosine, sine_table).astype(jnp.bfloat16)
-    query_reduced = query_reduced.reshape(rows, kv_heads, head_count // kv_heads, HEAD_WIDTH)
-    attended, totals = attend_forward(
-        query_reduced, key_reduced, value_reduced, labels, row_index
+    tables = (cosine, sine, as_row(q_scale), as_row(k_scale), first_row)
+    query_reduced, key_reduced, value_reduced, attended, totals = attention(
+        qkv, tables, order, head_count, kv_heads
     )
     mid_far = lax.all_gather(after(mid_far, attended, down_near), "d", axis=0, tiled=True)
-    down_far = lax.ppermute(after(down_rows, attended), "h", shift_perm(2, 1))
-    cotangent = trade(after(cotangent, attended))
 
     def whole(values):
         return jax.ShapeDtypeStruct((own_rows, width), values)
 
     gain_sum = jax.ShapeDtypeStruct((1, width), jnp.float32)
     middle, normed_mid = exchange(
-        "attention_sum",
         1,
         contract_cols(attended, o_full).astype(jnp.bfloat16),
         (stream, as_row(mlp_scale)),
@@ -842,7 +988,7 @@
     hidden_near = swiglu(gate_near, up_near).astype(jnp.bfloat16)
     gate_far, up_far = split(jnp.dot(normed_mid, mid_far, preferred_element_type=jnp.float32))
     hidden_far = swiglu(gate_far, up_far).astype(jnp.bfloat16)
-    grad_rows = gather_tokens(cotangent, hidden_near)
+    grad_rows = gather_tokens(cotangent, hidden_far)
     down_grads = sum_over_d(
         jnp.concatenate(
             [
@@ -869,7 +1015,6 @@
         jnp.bfloat16
     )
     gradient, mlp_gain_grad, grad_rows = exchange(
-        "middle_pull",
         2,
         after(normed_grad, mid_grad_far),
         (middle, cotangent, as_row(mlp_scale)),
@@ -883,37 +1028,21 @@
     grad_rows = after(grad_rows, mid_grad_near)
     out_grad = jnp.dot(grad_rows, o_full, preferred_element_type=jnp.float32).astype(jnp.bfloat16)
     o_wgrad = contract_rows(grad_rows, attended)
-    query_grad, key_grad, value_grad = attend_backward(
-        query_reduced,
-        key_reduced,
-        value_reduced,
-        labels,
-        row_index,
-        totals,
-        out_grad.reshape(query_reduced.shape),
-    )
-
-    def query_path(raw_values, scales):
-        return rotate(rms_scale(raw_values, scales), cosine, sine_table)
-
-    _, pull_query = jax.vjp(query_path, queries, q_scale)
-    query_raw_grad, q_gain_grad = pull_query(query_grad)
-    _, pull_key = jax.vjp(query_path, keys, k_scale)
-    key_raw_grad, k_gain_grad = pull_key(key_grad)
-    qkv_back = jnp.concatenate(
-        [
-            query_raw_grad.reshape(rows, -1).astype(jnp.bfloat16),
-            key_raw_grad.reshape(rows, -1).astype(jnp.bfloat16),
-            value_grad.reshape(rows, -1).astype(jnp.bfloat16),
-        ],
-        axis=1,
-    )
+    query_back, key_back, value_back, q_gain_grad, k_gain_grad = attention_pull(
+        qkv,
+        tables,
+        order,
+        (query_reduced, key_reduced, value_reduced, totals),
+        out_grad,
+        head_count,
+        kv_heads,
+    )
+    qkv_back = jnp.concatenate([query_back, key_back, value_back], axis=1)
     qkv_grad = contract_rows(normed, qkv_back).astype(jnp.bfloat16)
     attn_grad = scatter_weights(
         after(jnp.concatenate([qkv_grad, o_wgrad.astype(jnp.bfloat16)], axis=1), mid_sum_far)
     )
     gradient, moved, attn_gain_grad = exchange(
-        "stream_pull",
         3,
         contract_cols(after(qkv_back, qkv_grad), qkv_full).astype(jnp.bfloat16),
         (stream, gradient, as_row(attn_scale)),
@@ -937,7 +1066,7 @@
     up_grad = columns_of(mine[:, half_cols:], other[:, half_cols:])
 
     sums = lax.psum(
-        jnp.concatenate([attn_gain_grad[0], mlp_gain_grad[0], q_gain_grad, k_gain_grad]),
+        jnp.concatenate([attn_gain_grad[0], mlp_gain_grad[0], q_gain_grad[0], k_gain_grad[0]]),
         ("d", "c", "h", "l"),
     )
     row = lax.axis_index("d") * 2 + core

time: 983 us -> 906 us (0.922)
  local copies, waits for them, and re-layouts: 111 us -> 39.7 us
  Pallas kernels: 254 us -> 308 us
  matrix products: 209 us -> 162 us
  other arithmetic: 91.7 us -> 45.9 us
  waiting for transfers between devices: 201 us -> 223 us
  starting transfers between devices: 34.3 us -> 46.1 us
    pallas_call x0 -> x2, Pallas kernels: none -> 54.6 us  [the longest x1 34.5 us: attention_pull(): pl.pallas_call(functools.partial(attention_pull_kernel, blocks, repeat),...]
    dot_general x14 -> x0, matrix products: 47.1 us -> none  [the longest x4 14.2 us: one_block(): jnp.einsum('qgrd,kgd->grqk', q_block, key_reduced, preferred_element_type...]
    all_gather x1, waiting for transfers between devices: 0.02 us -> 34.9 us  [per_device(): mid_near = lax.all_gather(mid_rows, 'd', axis=0, tiled=True)]
    reshape x4 -> x0, local copies, waits for them, and re-layouts: 17.8 us -> none  [the longest x2 10.2 us: per_device(): queries = qkv[:, :q_cols].reshape(rows, head_count, HEAD_WIDTH)]
    ppermute x1, starting transfers between devices: 0.07 us -> 16.5 us  [gather_tokens(): lax.ppermute(half, 'c', shift_perm(2, 1))]
    while x32 -> x0, local copies, waits for them, and re-layouts: 13.9 us -> none
    convert_element_type x8 -> x1, other arithmetic: 15.9 us -> 2.84 us  [per_device(): hidden_far = swiglu(gate_far, up_far).astype(jnp.bfloat16)]
    ppermute x1, waiting for transfers between devices: 45.9 us -> 34.6 us  [per_device(): mid_far = lax.ppermute(after(mid_rows, group), 'h', shift_perm(2, 1))]
  transfers between devices with their start and end apart: 27 -> 27, of which waited for: 7 -> 8; matrix products, arithmetic and copies ran while one was open for 35% -> 25% of each run, Pallas kernels for 26% -> 34%
where the time goes in v3:
time: 906 us; the launch traced here: 897 us
  Pallas kernels  308 us (34%)
  waiting for transfers between devices  223 us (25%)
  matrix products  162 us (18%)
  blocking collectives  57.6 us (6%)
  starting transfers between devices  46.1 us (5%)
  other arithmetic  45.9 us (5%)
  local copies, waits for them, and re-layouts  39.7 us (4%)
  between operations  15.7 us (2%)
    pallas_call x3, Pallas kernels, exchange(): pl.pallas_call(functools.partial(exchange_kernel, tl, epilogue, len(aux),...  163 us
    ppermute x2, waiting for transfers between devices, return_halves(): far = lax.ppermute(far, 'h', shift_perm(2, 1))  102 us
    pallas_call x1, Pallas kernels, enter(): pl.pallas_call(functools.partial(entry_kernel, nd, tl), name='entry', out...  89.8 us
    psum x1, blocking collectives, per_device(): lax.psum(jnp.concatenate([attn_gain_grad[0], mlp_gain_grad[0], q_gain_gra...  57.6 us
    dot_general x6, matrix products, contract_cols(): lax.dot_general(left, right, (((1,), (1,)), ((), ())), preferred_element_...  52.5 us
    dot_general x6, matrix products, contract_rows(): lax.dot_general(left, right, (((0,), (0,)), ((), ())), preferred_element_...  51.1 us
    all_gather x1, waiting for transfers between devices, per_device(): mid_near = lax.all_gather(mid_rows, 'd', axis=0, tiled=True)  34.9 us
    ppermute x1, waiting for transfers between devices, per_device(): mid_far = lax.ppermute(after(mid_rows, group), 'h', shift_perm(2, 1))  34.6 us
  transfers between devices with their start and end apart: 27, of which 8 were waited for; matrix products, arithmetic and copies ran while one was open for 25% of the time, Pallas kernels for 34%

profile of v3, /device:TPU:0, one launch (start us, length us, event | category | flops | bytes accessed | tf_op | source)
XLA Modules:
  0.0 897.5 jit_solution(15265324181914761884)
XLA Ops:
  9.1 1.9 select_bitcast_fusion
  16.2 2.1 fusion.16
  19.1 1.5 maximum_select_fusion
  20.7 89.8 %entry.1 = (bf16[2048,1024]{1,0:T(8,128)(2,1)}, bf16[2048,512]{1,0:T(8,128)(2,1)}, bf16[1152,2048]{1,0:T(8,128)(2,1)}, f32[8,8,128]{2,1,0:T(8,128)}) custom-call(bf16[256,512]{1,0:T(8,128)(2,1)} %bitcast.126, bf16[256,256]{1,0:T(8,128)(2,1)} %bitcast.128, bf16[256,256]{1,0:T(8,128)(2,1)} %bitcast.129, bf16[256,512]{1,0:T(8,128)(2,1)} %bitcast.127, ...), custom_call_target="tpu_custom_call" | custom-call | bytes 250000000 | tf_op jit(solution)/shard_map/entry/pallas_call | solution.py:318
  112.1 2.3 collective-permute-start.5
  114.5 3.3 fusion
  117.8 9.1 %fusion.14.refs_0_.refs_1_.refs_2_ = f32[1152,1024]{1,0:T(8,128)} fusion(bf16[2048,1024]{1,0:T(8,128)(2,1)} %get-tuple-element.52, bf16[1152,2048]{1,0:T(8,128)(2,1)S(1)} %copy-done.18, f32[2048]{0:T(1024)S(1)} %bitcast.133, f32[1152]{0:T(1024)S(1)} %add_rsqrt_fusion), kind=kOutput, calls=%fused_computation.54 | convolution fusion | flops 4841275392 | bytes 13644288 | tf_op jit(solution)/shard_map/dot_general | solution.py:965
  127.0 20.2 %attention.1 = (bf16[1152,512]{1,0:T(8,128)(2,1)}, bf16[1152,256]{1,0:T(8,128)(2,1)S(1)}, bf16[1152,256]{1,0:T(8,128)(2,1)S(1)}, bf16[1152,512]{1,0:T(8,128)(2,1)}, f32[1152,256]{1,0:T(8,128)}) custom-call(s32[4]{0:T(128)S(1)} %get-tuple-element.86.order_ref, f32[1152,1024]{1,0:T(8,128)} %fusion.14.refs_0_.refs_1_.refs_2_, ...), custom_call_target="tpu_custom_call" | custom-call | flops 2717908992 | bytes 60000000 | tf_op jit(solution)/shard_map/attention/pallas_call | solution.py:672
  148.8 34.6 %collective-permute-done.5 = bf16[512,1536]{1,0:T(8,128)(2,1)} collective-permute-done((bf16[512,1536]{1,0:T(8,128)(2,1)S(1)}, bf16[512,1536]{1,0:T(8,128)(2,1)}, u32[]{:S(2)}, u32[]{:S(2)}) %collective-permute-start.5) | collective-permute-done | bytes 1572896 | tf_op jit(solution)/shard_map/ppermute | solution.py:953
  183.8 1.6 slice.132.refs_1_
  185.4 4.5 convolution_convert_fusion.3.refs_0_
  190.0 75.3 %shard_map.237 = (f32[288,2048]{1,0:T(8,128)S(1)}, bf16[1152,2048]{1,0:T(8,128)(2,1)S(1)}) custom-call(bf16[1152,2048]{1,0:T(8,128)(2,1)S(1)} %convolution_convert_fusion.3.refs_0_, bf16[288,2048]{1,0:T(8,128)(2,1)S(1)} %slice.132.refs_1_, f32[1,2048]{1,0:T(1,128)S(1)} %bitcast.108), custom_call_target="tpu_custom_call" | custom-call | bytes 200000000 | tf_op jit(solution)/shard_map/pallas_call | solution.py:511
  265.3 2.1 copy-done.12
  268.4 1.9 collective-permute-start.3
  270.5 11.3 %fusion.34 = f32[1152,1536]{1,0:T(8,128)S(1)} fusion(bf16[1152,2048]{1,0:T(8,128)(2,1)} %copy-done.12, bf16[2048,1536]{1,0:T(8,128)(2,1)} %all-gather.9.cloned.1.call-done), kind=kOutput, calls=%fused_computation.129 | convolution fusion | flops 7247757312 | bytes 18087936 | tf_op jit(solution)/shard_map/dot_general | solution.py:989
  281.8 2.8 multiply_convert_fusion.2
  285.2 13.3 %collective-permute-done.4 = bf16[288,2048]{1,0:T(8,128)(2,1)} collective-permute-done((bf16[288,2048]{1,0:T(8,128)(2,1)S(1)}, bf16[288,2048]{1,0:T(8,128)(2,1)}, u32[]{:S(2)}, u32[]{:S(2)}) %collective-permute-start.4) | collective-permute-done | bytes 1179680 | tf_op jit(solution)/shard_map/ppermute | solution.py:828
  298.5 1.4 pad_maximum_fusion.4
  299.9 16.5 %collective-permute-start.7 = (bf16[576,2048]{1,0:T(8,128)(2,1)S(1)}, bf16[576,2048]{1,0:T(8,128)(2,1)S(1)}, u32[]{:S(2)}, u32[]{:S(2)}) collective-permute-start(bf16[576,2048]{1,0:T(8,128)(2,1)S(1)} %pad_maximum_fusion.4), channel_id=1, source_target_pairs={{4,0},{0,4},{5,1},{1,5},{6,2},{2,6},{7,3},{3,7},{12,8},{8,12},{13,... | collective-permute-start | bytes 7077896 | tf_op jit(solution)/shard_map/ppermute | solution.py:831
  317.7 2.4 constant_dynamic-update-slice_fusion.1
  320.6 1.6 constant_dynamic-update-slice_fusion
  322.3 10.5 %fusion.8 = (bf16[1152,768]{1,0:T(8,128)(2,1)S(1)}, bf16[1152,768]{1,0:T(8,128)(2,1)S(1)}) fusion(f32[1152,1536]{1,0:T(8,128)} %copy-done.19, bf16[1152,2048]{1,0:T(8,128)(2,1)} %constant_dynamic-update-slice_fusion, bf16[2048,768]{1,0:T(8,128)(2,1)} %all-gather.11.cloned.1.call-done), kind=kOutput, calls=%fused_computation.24 | convolution fusion | flops 3636264960 | bytes 18481152 | tf_op jit(solution)/shard_map/dot_general | solution.py:1003
  334.6 12.8 %convolution_convert_fusion.2 = bf16[2048,1536]{1,0:T(8,128)(2,1)} fusion(bf16[1152,2048]{1,0:T(8,128)(2,1)} %copy-done.12, bf16[1152,768]{1,0:T(8,128)(2,1)S(1)} %get-tuple-element.88, bf16[1152,768]{1,0:T(8,128)(2,1)S(1)} %get-tuple-element.87), kind=kOutput, calls=%fused_computation.10 | convolution fusion | flops 7257980928 | bytes 14548992 | tf_op jit(solution)/shard_map/dot_general | solution.py:47
  347.9 34.9 %all-gather.5.cloned.1.call-done = bf16[2048,1536]{1,0:T(8,128)(2,1)} async-done(((bf16[512,1536]{1,0:T(8,128)(2,1)}), bf16[2048,1536]{1,0:T(8,128)(2,1)}) %all-gather.5.cloned.1.call-update) | async-done | bytes 6291472 | tf_op jit(solution)/shard_map/all_gather | solution.py:932
  382.9 11.2 %fusion.33 = f32[1152,1536]{1,0:T(8,128)S(1)} fusion(bf16[1152,2048]{1,0:T(8,128)(2,1)} %copy-done.12, bf16[2048,1536]{1,0:T(8,128)(2,1)} %all-gather.5.cloned.1.call-done), kind=kOutput, calls=%fused_computation.128 | convolution fusion | flops 7247757312 | bytes 18087936 | tf_op jit(solution)/shard_map/dot_general | solution.py:987
  394.1 7.3 convolution_convert_fusion.5
  401.4 9.0 %fusion.5 = (bf16[1152,768]{1,0:T(8,128)(2,1)}, bf16[1152,768]{1,0:T(8,128)(2,1)}, bf16[1152,768]{1,0:T(8,128)(2,1)S(1)}) fusion(f32[1152,1536]{1,0:T(8,128)S(1)} %fusion.33, bf16[1152,2048]{1,0:T(8,128)(2,1)} %constant_dynamic-update-slice_fusion, bf16[2048,768]{1,0:T(8,128)(2,1)S(1)} %copy-done.43), kind=kOutput, calls=%fused_computation.21 | convolution fusion | flops 3638034432 | bytes 20250624 | tf_op jit(solution)/shard_map/dot_general | solution.py:1003
  411.6 7.5 convolution_convert_fusion.6
  419.1 3.1 pad_maximum_fusion.1
  422.5 13.3 %fusion.29 = f32[1152,2048]{1,0:T(8,128)} fusion(bf16[2048,1536]{1,0:T(8,128)(2,1)} %all-gather.5.cloned.1.call-done, bf16[1152,768]{1,0:T(8,128)(2,1)} %get-tuple-element.90, bf16[1152,768]{1,0:T(8,128)(2,1)} %get-tuple-element.89), kind=kOutput, calls=%fused_computation.124 | convolution fusion | flops 7254835200 | bytes 19267584 | tf_op jit(solution)/shard_map/dot_general | solution.py:53
  435.8 13.1 %add_convert_fusion.refs_0_ = bf16[1152,2048]{1,0:T(8,128)(2,1)} fusion(f32[1152,2048]{1,0:T(8,128)} %fusion.29, bf16[2048,1536]{1,0:T(8,128)(2,1)} %all-gather.9.cloned.1.call-done, bf16[1152,768]{1,0:T(8,128)(2,1)S(1)} %copy-done.54, bf16[1152,768]{1,0:T(8,128)(2,1)S(1)} %copy-done.52), kind=kOutput, calls=%fused_computation.6 | convolution fusion | flops 7259553792 | bytes 23986176 | tf_op jit(solution)/shard_map/dot_general | solution.py:53
  448.9 57.2 %shard_map.238 = (f32[288,2048]{1,0:T(8,128)S(1)}, f32[1,2048]{1,0:T(1,128)S(1)}, bf16[1152,2048]{1,0:T(8,128)(2,1)S(1)}) custom-call(bf16[1152,2048]{1,0:T(8,128)(2,1)} %add_convert_fusion.refs_0_, f32[288,2048]{1,0:T(8,128)S(1)} %get-tuple-element.55.refs_1_, bf16[288,2048]{1,0:T(8,128)(2,1)S(1)} %collective-permute-done.3.refs_2_, f32[1,2048]{1,0:T(1,128)S(1)} %bitcast.109), custom_call_target="tpu_custom_call" | custom-call | bytes 200000000 | tf_op jit(solution)/shard_map/pallas_call | solution.py:511
  507.5 2.0 copy-done.13
  509.5 10.4 %convolution_convert_fusion.1 = bf16[2048,1536]{1,0:T(8,128)(2,1)} fusion(bf16[1152,2048]{1,0:T(8,128)(2,1)S(1)} %bitcast.114, bf16[1152,1536]{1,0:T(8,128)(2,1)S(1)} %pad_maximum_fusion.2), kind=kOutput, calls=%fused_computation.9 | convolution fusion | flops 7250903040 | bytes 14548992 | tf_op jit(solution)/shard_map/dot_general | solution.py:47
  520.1 6.8 convolution_convert_fusion.8.refs_11_
  526.9 34.5 %attention_pull.1 = (bf16[1152,512]{1,0:T(8,128)(2,1)}, bf16[1152,256]{1,0:T(8,128)(2,1)}, bf16[1152,256]{1,0:T(8,128)(2,1)}, f32[8,128]{1,0:T(8,128)}, f32[8,128]{1,0:T(8,128)}) custom-call(s32[4]{0:T(128)} %copy-done.11, f32[1152,1024]{1,0:T(8,128)} %fusion.14.refs_0_.refs_1_.refs_2_, f32[1152,1024]{1,0:T(8,128)} %fusion.14.refs_0_.refs_1_.refs_2_, ...), custom_call_target="tpu_custom_call" | custom-call | flops 6794772480 | bytes 120000000 | tf_op jit(solution)/shard_map/attention_pull/pallas_call | solution.py:778
  561.3 1.5 constant_dynamic-update-slice_fusion.5
  564.2 4.1 convolution_convert_fusion.7
  568.4 8.9 convolution_convert_fusion.4
  577.3 3.2 pad_maximum_fusion
  581.2 7.9 convolution_convert_fusion.refs_0_
  589.1 30.9 %shard_map.239 = (f32[288,2048]{1,0:T(8,128)S(1)}, bf16[288,2048]{1,0:T(8,128)(2,1)S(1)}, f32[1,2048]{1,0:T(1,128)S(1)}) custom-call(bf16[1152,2048]{1,0:T(8,128)(2,1)S(1)} %convolution_convert_fusion.refs_0_, bf16[288,2048]{1,0:T(8,128)(2,1)S(1)} %copy-done.1, f32[288,2048]{1,0:T(8,128)S(1)} %copy-done.6, f32[1,2048]{1,0:T(1,128)S(1)} %bitcast.110), custom_call_target="tpu_custom_call" | custom-call | bytes 110000000 | tf_op jit(solution)/shard_map/pallas_call | solution.py:511
  620.1 6.4 fusion.35
  626.5 7.3 convolution_add_fusion
  634.2 4.5 collective-permute-done.9
  639.8 2.2 copy-done.16
  643.3 1.7 collective-permute-start.10
  644.9 1.7 collective-permute-start.12
  648.6 57.6 %psum.7 = f32[4352]{0:T(1024)} all-reduce(f32[4352]{0:T(1024)} %pad_maximum_fusion.10), channel_id=1, replica_groups=mesh['d'=4,'c'=2,'h'=2,'l'=2] {'d','c','h','l'}, use_global_device_ids=true, to_apply=%region_3.4 | all-reduce | flops 4352 | bytes 34816 | tf_op jit(solution)/shard_map/psum | solution.py:1068
  709.3 1.5 collective-permute-start.17
  712.0 1.5 collective-permute-start.15
  713.6 2.6 fusion.12
  718.9 73.6 %collective-permute-done.17 = bf16[512,768]{1,0:T(8,128)(2,1)S(1)} collective-permute-done((bf16[512,768]{1,0:T(8,128)(2,1)S(1)}, bf16[512,768]{1,0:T(8,128)(2,1)S(1)}, u32[]{:S(2)}, u32[]{:S(2)}) %collective-permute-start.17) | collective-permute-done | bytes 786464 | tf_op jit(solution)/shard_map/ppermute | solution.py:863
  792.8 3.0 convert_select_fusion
  796.8 1.3 convert_select_fusion.2
  798.1 28.0 %collective-permute-done.15 = bf16[512,1536]{1,0:T(8,128)(2,1)} collective-permute-done((bf16[512,1536]{1,0:T(8,128)(2,1)}, bf16[512,1536]{1,0:T(8,128)(2,1)}, u32[]{:S(2)}, u32[]{:S(2)}) %collective-permute-start.15) | collective-permute-done | bytes 1572896 | tf_op jit(solution)/shard_map/ppermute | solution.py:863
  826.1 2.3 convert_add_fusion
  829.5 14.7 %collective-permute-start.16 = (bf16[256,1536]{1,0:T(8,128)(2,1)}, bf16[256,1536]{1,0:T(8,128)(2,1)}, u32[]{:S(2)}, u32[]{:S(2)}) collective-permute-start(bf16[256,1536]{1,0:T(8,128)(2,1)} %select_convert_fusion), channel_id=1, source_target_pairs={{4,0},{0,4},{5,1},{1,5},{6,2},{2,6},{7,3},{3,7},{12,8},{8,12},{13,... | collective-permute-start | bytes 2359304 | tf_op jit(solution)/shard_map/ppermute | solution.py:869
  844.1 1.5 broadcast_select_fusion
  845.7 2.7 maximum_bitcast_fusion.2
  848.6 1.4 convert_element_type.138
  850.7 1.4 maximum_bitcast_fusion
  852.1 1.4 maximum_bitcast_fusion.1
  853.4 33.5 %collective-permute-done.14 = bf16[256,1536]{1,0:T(8,128)(2,1)S(1)} collective-permute-done((bf16[256,1536]{1,0:T(8,128)(2,1)S(1)}, bf16[256,1536]{1,0:T(8,128)(2,1)S(1)}, u32[]{:S(2)}, u32[]{:S(2)}) %collective-permute-start.14) | collective-permute-done | bytes 786464 | tf_op jit(solution)/shard_map/ppermute | solution.py:901
  (223 shorter events, 40.3 us)
Async XLA Ops:
  7.2 5.1 copy-start.48
  7.2 5.8 copy-start.38
  7.2 5.8 copy-start.39
  7.2 5.9 copy-start.40
  7.2 5.9 copy-start.41
  7.2 176.2 %all-gather.7.cloned.1.call-start = ((), (), s32[]{:S(2)}) async-start(), calls=%async_computation.5 | async-start | bytes 3932160 | tf_op jit(solution)/shard_map/all_gather | solution.py:933
  8.5 10.4 %collective-permute-start.1 = (bf16[256,768]{1,0:T(8,128)(2,1)S(1)}, bf16[256,768]{1,0:T(8,128)(2,1)S(1)}, u32[]{:S(2)}, u32[]{:S(2)}) collective-permute-start(bf16[256,768]{1,0:T(8,128)(2,1)S(1)} %get-tuple-element.107), channel_id=1, source_target_pairs={{4,0},{0,4},{5,1},{1,5},{6,2},{2,6},{7,3},{3,7},{12,8},{8,12},{13,... | collective-permute-start | bytes 1179656 | tf_op jit(solution)/shard_map/ppermute | solution.py:856
  11.0 2.9 collective-permute-start.6
  11.8 7.3 collective-permute-start
  12.3 2.9 collective-permute-start.2
  14.9 255.6 %all-gather.9.cloned.1.call-start = ((), (), s32[]{:S(2)}) async-start(), calls=%async_computation.6 | async-start | bytes 7864320 | tf_op jit(solution)/shard_map/all_gather | solution.py:970
  15.0 112.0 %copy-start.11 = (s32[4]{0:T(128)}, s32[4]{0:T(128)S(1)}, u32[]{:S(2)}) copy-start(s32[4]{0:T(128)S(1)} %get-tuple-element.86.order_ref) | copy-start | bytes 52
  18.5 108.5 %copy-start.2 = (s32[1152,1]{1,0:T(8,128)}, s32[1152,1]{1,0:T(8,128)S(1)}, u32[]{:S(2)}) copy-start(s32[1152,1]{1,0:T(8,128)S(1)} %reduce_sum.33.refs_7_.refs_6_) | copy-start | bytes 13828
  18.9 108.1 %copy-start.7 = (f32[1152,128]{1,0:T(8,128)}, f32[1152,128]{1,0:T(8,128)S(1)}, u32[]{:S(2)}) copy-start(f32[1152,128]{1,0:T(8,128)S(1)} %get-tuple-element.120.refs_3_.refs_2_) | copy-start | bytes 1769476
  18.9 108.1 %copy-start.8 = (f32[1152,128]{1,0:T(8,128)}, f32[1152,128]{1,0:T(8,128)S(1)}, u32[]{:S(2)}) copy-start(f32[1152,128]{1,0:T(8,128)S(1)} %get-tuple-element.121.refs_4_.refs_3_) | copy-start | bytes 1769476
  20.7 106.2 %copy-start.20 = (bf16[512,1536]{1,0:T(8,128)(2,1)}, bf16[512,1536]{1,0:T(8,128)(2,1)S(1)}, u32[]{:S(2)}) copy-start(bf16[512,1536]{1,0:T(8,128)(2,1)S(1)} %pad_maximum_fusion.7) | copy-start | bytes 4718596
  111.9 15.1 %copy-start.34 = (f32[1,2,8,128]{3,1,2,0:T(2,128)}, f32[1,2,8,128]{3,1,2,0:T(2,128)S(1)}, u32[]{:S(2)}) copy-start(f32[1,2,8,128]{3,1,2,0:T(2,128)S(1)} %copy.62) | copy-start | bytes 24580
  112.0 15.0 %copy-start.9 = (f32[1,128]{1,0:T(1,128)}, f32[1,128]{1,0:T(1,128)S(1)}, u32[]{:S(2)}) copy-start(f32[1,128]{1,0:T(1,128)S(1)} %reshape_reshape.11.refs_5_.refs_4_) | copy-start | bytes 1540
  112.1 14.9 %copy-start.10 = (f32[1,128]{1,0:T(1,128)}, f32[1,128]{1,0:T(1,128)S(1)}, u32[]{:S(2)}) copy-start(f32[1,128]{1,0:T(1,128)S(1)} %reshape_reshape.12.refs_6_.refs_5_) | copy-start | bytes 1540
  112.1 5.7 copy-start.18
  112.1 71.3 %collective-permute-start.5 = (bf16[512,1536]{1,0:T(8,128)(2,1)S(1)}, bf16[512,1536]{1,0:T(8,128)(2,1)}, u32[]{:S(2)}, u32[]{:S(2)}) collective-permute-start(bf16[512,1536]{1,0:T(8,128)(2,1)S(1)} %pad_maximum_fusion.7), channel_id=1, source_target_pairs={{2,0},{0,2},{3,1},{1,3},{6,4},{4,6},{7,5},{5,7},{10,8},{8,10},{11,... | collective-permute-start | bytes 4718600 | tf_op jit(solution)/shard_map/ppermute | solution.py:953
  117.8 9.2 %copy-start.36 = (f32[1152]{0:T(1024)}, f32[1152]{0:T(1024)S(1)}, u32[]{:S(2)}) copy-start(f32[1152]{0:T(1024)S(1)} %add_rsqrt_fusion) | copy-start | bytes 13828
  183.5 138.8 %all-gather.11.cloned.1.call-start = ((), (), s32[]{:S(2)}) async-start(), calls=%async_computation.7 | async-start | bytes 3932160 | tf_op jit(solution)/shard_map/all_gather | solution.py:984
  183.8 83.7 %collective-permute-start.8 = (bf16[512,768]{1,0:T(8,128)(2,1)}, bf16[512,768]{1,0:T(8,128)(2,1)S(1)}, u32[]{:S(2)}, u32[]{:S(2)}) collective-permute-start(bf16[512,768]{1,0:T(8,128)(2,1)} %bitcast.118), channel_id=1, source_target_pairs={{2,0},{0,2},{3,1},{1,3},{6,4},{4,6},{7,5},{5,7},{10,8},{8,10},{11,... | collective-permute-start | bytes 2359304 | tf_op jit(solution)/shard_map/ppermute | solution.py:954
  268.3 114.5 %all-gather.5.cloned.1.call-start = ((), (), s32[]{:S(2)}) async-start(), calls=%async_computation.4 | async-start | bytes 7864320 | tf_op jit(solution)/shard_map/all_gather | solution.py:932
  268.4 2.0 collective-permute-start.3
  270.3 310.1 %reduce-scatter.5.cloned.1.call-start = ((), (), s32[]{:S(2)}) async-start(), calls=%async_computation.8 | async-start | bytes 7864320 | tf_op jit(solution)/shard_map/reduce_scatter | solution.py:881
  270.4 28.1 %collective-permute-start.4 = (bf16[288,2048]{1,0:T(8,128)(2,1)S(1)}, bf16[288,2048]{1,0:T(8,128)(2,1)}, u32[]{:S(2)}, u32[]{:S(2)}) collective-permute-start(bf16[288,2048]{1,0:T(8,128)(2,1)S(1)} %collective-permute-done.3.refs_2_), channel_id=1, source_target_pairs={{1,0},{0,1},{3,2},{2,3},{5,4},{4,5},{7,6},{6,7},{9,8},{8,9},{11,10... | collective-permute-start | bytes 3538952 | tf_op jit(solution)/shard_map/ppermute | solution.py:828
  299.9 20.7 %collective-permute-start.7 = (bf16[576,2048]{1,0:T(8,128)(2,1)S(1)}, bf16[576,2048]{1,0:T(8,128)(2,1)S(1)}, u32[]{:S(2)}, u32[]{:S(2)}) collective-permute-start(bf16[576,2048]{1,0:T(8,128)(2,1)S(1)} %pad_maximum_fusion.4), channel_id=1, source_target_pairs={{4,0},{0,4},{5,1},{1,5},{6,2},{2,6},{7,3},{3,7},{12,8},{8,12},{13,... | collective-permute-start | bytes 7077896 | tf_op jit(solution)/shard_map/ppermute | solution.py:831
  347.5 360.7 %reduce-scatter.11.cloned.1.call-start = ((), (), s32[]{:S(2)}) async-start(), calls=%async_computation.11 | async-start | bytes 7864320 | tf_op jit(solution)/shard_map/reduce_scatter | solution.py:881
  382.9 11.2 %copy-start.24 = (bf16[1152,768]{1,0:T(8,128)(2,1)S(1)}, bf16[1152,768]{1,0:T(8,128)(2,1)}, u32[]{:S(2)}) copy-start(bf16[1152,768]{1,0:T(8,128)(2,1)} %multiply_convert_fusion.2) | copy-start | bytes 5308420
  394.1 7.3 copy-start.43
  422.2 375.9 %reduce-scatter.9.cloned.1.call-start = ((), (), s32[]{:S(2)}) async-start(), calls=%async_computation.10 | async-start | bytes 7864320 | tf_op jit(solution)/shard_map/reduce_scatter | solution.py:881
  422.4 13.3 %copy-start.52 = (bf16[1152,768]{1,0:T(8,128)(2,1)S(1)}, bf16[1152,768]{1,0:T(8,128)(2,1)}, u32[]{:S(2)}) copy-start(bf16[1152,768]{1,0:T(8,128)(2,1)} %copy-done.51) | copy-start | bytes 5308420
  422.5 13.3 %copy-start.54 = (bf16[1152,768]{1,0:T(8,128)(2,1)S(1)}, bf16[1152,768]{1,0:T(8,128)(2,1)}, u32[]{:S(2)}) copy-start(bf16[1152,768]{1,0:T(8,128)(2,1)} %copy-done.53) | copy-start | bytes 5308420
  422.5 87.1 %slice-start = ((s8[4718592]{0:T(1024)(128)(4,1)}), s8[4194304]{0:T(1024)(128)(4,1)S(1)}, s32[]{:S(2)}) async-start(s8[4718592]{0:T(1024)(128)(4,1)} %bitcast.113), calls=%async_computation.12 | async-start | bytes 8388608
  435.7 73.8 %slice-start.1 = ((s8[4718592]{0:T(1024)(128)(4,1)}), s8[524288]{0:T(1024)(128)(4,1)S(1)}, s32[]{:S(2)}) async-start(s8[4718592]{0:T(1024)(128)(4,1)} %bitcast.113), calls=%async_computation.13 | async-start | bytes 1048576
  448.9 57.2 %copy-start.22 = (bf16[1152,768]{1,0:T(8,128)(2,1)S(1)}, bf16[1152,768]{1,0:T(8,128)(2,1)}, u32[]{:S(2)}) copy-start(bf16[1152,768]{1,0:T(8,128)(2,1)} %get-tuple-element.89) | copy-start | bytes 5308420
  448.9 57.2 %copy-start.23 = (bf16[1152,768]{1,0:T(8,128)(2,1)S(1)}, bf16[1152,768]{1,0:T(8,128)(2,1)}, u32[]{:S(2)}) copy-start(bf16[1152,768]{1,0:T(8,128)(2,1)} %get-tuple-element.90) | copy-start | bytes 5308420
  520.0 324.2 %reduce-scatter.7.cloned.1.call-start = ((), (), s32[]{:S(2)}) async-start(), calls=%async_computation.9 | async-start | bytes 7864320 | tf_op jit(solution)/shard_map/reduce_scatter | solution.py:895
  520.0 44.1 %slice-start.2 = ((s8[4718592]{0:T(1024)(128)(4,1)}), s8[4194304]{0:T(1024)(128)(4,1)S(1)}, s32[]{:S(2)}) async-start(s8[4718592]{0:T(1024)(128)(4,1)} %bitcast.115), calls=%async_computation.14 | async-start | bytes 8388608
  526.9 37.3 %slice-start.3 = ((s8[4718592]{0:T(1024)(128)(4,1)}), s8[524288]{0:T(1024)(128)(4,1)S(1)}, s32[]{:S(2)}) async-start(s8[4718592]{0:T(1024)(128)(4,1)} %bitcast.115), calls=%async_computation.15 | async-start | bytes 1048576
  568.4 8.9 copy-start.21
  581.2 7.9 copy-start.1
  581.2 7.9 copy-start.6
  589.1 30.9 %copy-start.44 = (bf16[2048,768]{1,0:T(8,128)(2,1)S(1)}, bf16[2048,768]{1,0:T(8,128)(2,1)}, u32[]{:S(2)}) copy-start(bf16[2048,768]{1,0:T(8,128)(2,1)} %all-gather.7.cloned.1.call-done) | copy-start | bytes 9437188
  589.1 30.9 %copy-start.50 = (bf16[1152,768]{1,0:T(8,128)(2,1)S(1)}, bf16[1152,768]{1,0:T(8,128)(2,1)}, u32[]{:S(2)}) copy-start(bf16[1152,768]{1,0:T(8,128)(2,1)} %copy-done.49) | copy-start | bytes 5308420
  620.0 6.4 copy-start.3
  620.1 6.4 copy-start.25
  620.1 6.4 copy-start.45
  634.2 4.6 collective-permute-start.9
  643.3 70.3 %collective-permute-start.10 = (bf16[288,2048]{1,0:T(8,128)(2,1)}, bf16[288,2048]{1,0:T(8,128)(2,1)}, u32[]{:S(2)}, u32[]{:S(2)}) collective-permute-start(bf16[288,2048]{1,0:T(8,128)(2,1)} %slice.289), channel_id=1, source_target_pairs={{1,0},{0,1},{3,2},{2,3},{5,4},{4,5},{7,6},{6,7},{9,8},{8,9},{11,10... | collective-permute-start | bytes 3538952 | tf_op jit(solution)/shard_map/ppermute | solution.py:843
  644.9 147.8 %collective-permute-start.12 = (bf16[288,2048]{1,0:T(8,128)(2,1)S(1)}, bf16[288,2048]{1,0:T(8,128)(2,1)}, u32[]{:S(2)}, u32[]{:S(2)}) collective-permute-start(bf16[288,2048]{1,0:T(8,128)(2,1)S(1)} %get-tuple-element.80), channel_id=1, source_target_pairs={{0,0},{2,4},{4,2},{6,6},{1,1},{3,5},{5,3},{7,7},{8,8},{10,12},{12,... | collective-permute-start | bytes 3538952 | tf_op jit(solution)/shard_map/ppermute | solution.py:822
  709.3 83.1 %collective-permute-start.17 = (bf16[512,768]{1,0:T(8,128)(2,1)S(1)}, bf16[512,768]{1,0:T(8,128)(2,1)S(1)}, u32[]{:S(2)}, u32[]{:S(2)}) collective-permute-start(bf16[512,768]{1,0:T(8,128)(2,1)S(1)} %slice.203), channel_id=1, source_target_pairs={{2,0},{0,2},{3,1},{1,3},{6,4},{4,6},{7,5},{5,7},{10,8},{8,10},{11,... | collective-permute-start | bytes 2359304 | tf_op jit(solution)/shard_map/ppermute | solution.py:863
  712.0 5.0 copy-start.42
  712.0 80.4 %copy-start.26 = (bf16[512,1536]{1,0:T(8,128)(2,1)S(1)}, bf16[512,1536]{1,0:T(8,128)(2,1)}, u32[]{:S(2)}) copy-start(bf16[512,1536]{1,0:T(8,128)(2,1)} %reduce-scatter.11.cloned.1.call-done) | copy-start | bytes 4718596
  712.0 114.1 %collective-permute-start.15 = (bf16[512,1536]{1,0:T(8,128)(2,1)}, bf16[512,1536]{1,0:T(8,128)(2,1)}, u32[]{:S(2)}, u32[]{:S(2)}) collective-permute-start(bf16[512,1536]{1,0:T(8,128)(2,1)} %reduce-scatter.5.cloned.1.call-done), channel_id=1, source_target_pairs={{2,0},{0,2},{3,1},{1,3},{6,4},{4,6},{7,5},{5,7},{10,8},{8,10},{11,... | collective-permute-start | bytes 4718600 | tf_op jit(solution)/shard_map/ppermute | solution.py:863
  716.1 76.6 %copy-start.4 = (f32[288,2048]{1,0:T(8,128)S(1)}, f32[288,2048]{1,0:T(8,128)}, u32[]{:S(2)}) copy-start(f32[288,2048]{1,0:T(8,128)} %copy-done.3) | copy-start | bytes 7077892
  716.2 79.7 %collective-permute-start.11 = (bf16[288,2048]{1,0:T(8,128)(2,1)S(1)}, bf16[288,2048]{1,0:T(8,128)(2,1)S(1)}, u32[]{:S(2)}, u32[]{:S(2)}) collective-permute-start(bf16[288,2048]{1,0:T(8,128)(2,1)S(1)} %fusion.12), channel_id=1, source_target_pairs={{0,0},{2,4},{4,2},{6,6},{1,1},{3,5},{5,3},{7,7},{8,8},{10,12},{12,... | collective-permute-start | bytes 3538952 | tf_op jit(solution)/shard_map/ppermute | solution.py:822
  792.7 4.1 collective-permute-start.18
  829.5 19.1 %collective-permute-start.16 = (bf16[256,1536]{1,0:T(8,128)(2,1)}, bf16[256,1536]{1,0:T(8,128)(2,1)}, u32[]{:S(2)}, u32[]{:S(2)}) collective-permute-start(bf16[256,1536]{1,0:T(8,128)(2,1)} %select_convert_fusion), channel_id=1, source_target_pairs={{4,0},{0,4},{5,1},{1,5},{6,2},{2,6},{7,3},{3,7},{12,8},{8,12},{13,... | collective-permute-start | bytes 2359304 | tf_op jit(solution)/shard_map/ppermute | solution.py:869
  845.6 4.4 collective-permute-start.13
  850.1 36.8 %collective-permute-start.14 = (bf16[256,1536]{1,0:T(8,128)(2,1)S(1)}, bf16[256,1536]{1,0:T(8,128)(2,1)S(1)}, u32[]{:S(2)}, u32[]{:S(2)}) collective-permute-start(bf16[256,1536]{1,0:T(8,128)(2,1)S(1)} %broadcast_select_fusion.2), channel_id=1, source_target_pairs={{2,0},{0,2},{3,1},{1,3},{6,4},{4,6},{7,5},{5,7},{10,8},{8,10},{11,... | collective-permute-start | bytes 2359304 | tf_op jit(solution)/shard_map/ppermute | solution.py:901
  853.4 35.8 %copy-start.28 = (bf16[288,2048]{1,0:T(8,128)(2,1)S(1)}, bf16[288,2048]{1,0:T(8,128)(2,1)}, u32[]{:S(2)}) copy-start(bf16[288,2048]{1,0:T(8,128)(2,1)} %copy-done.27) | copy-start | bytes 3538948
  (22 other events, 51.1 us)
Sparse Core Ops, SparseCore 0:
  15.0 61.2 all-gather.6
  183.6 69.6 all-gather.8
  268.5 42.0 all-gather.10
  312.8 70.0 all-gather.4
  385.7 70.0 reduce-scatter.4
  458.6 70.0 reduce-scatter.10
  531.6 70.0 reduce-scatter.8
  604.6 70.7 reduce-scatter.6

commit v4 on v3

--- a/solution.py
+++ b/solution.py
@@ -72,6 +72,66 @@
 
 def rows_at(index, size):
     return pl.ds(pl.multiple_of(index * size, size), size)
+
+
+def hop_plan(nd, d):
+    if nd == 4:
+        side_x = d + 1 - 2 * lax.rem(d, 2)
+        side_y = d + 2 - 4 * (d // 2)
+        corner = side_x + side_y - d
+        hops = (
+            (0, d, side_x),
+            (1, d, side_x),
+            (0, d, side_y),
+            (1, d, side_y),
+            (0, side_x, side_y),
+            (1, side_y, side_x),
+        )
+        sources = ((0, side_x), (1, side_x), (0, side_y), (1, side_y), (0, corner), (1, corner))
+        return hops, sources, 4, ((0, 4), (3, 5))
+    steps = [(part, step) for step in range(1, nd) for part in range(2)]
+    hops = tuple((part, d, lax.rem(d + step, nd)) for part, step in steps)
+    sources = tuple((part, lax.rem(d + nd - step, nd)) for part, step in steps)
+    return hops, sources, len(hops), ()
+
+
+def hop_count(nd):
+    return 6 if nd == 4 else 2 * (nd - 1)
+
+
+class Spread:
+    def __init__(self, nd, d, block, send_sem, recv_sem):
+        self.hops, self.sources, self.first, self.relayed = hop_plan(nd, d)
+        self.block, self.send_sem, self.recv_sem = block, send_sem, recv_sem
+
+    def copy(self, j, kind, part, of):
+        at = self.block(j, of * 2 + part)
+        return remote(
+            at, at, self.send_sem.at[j, kind], self.recv_sem.at[j, kind], d=self.hops[kind][2]
+        )
+
+    def hop(self, j, kind):
+        return self.copy(j, kind, *self.hops[kind][:2])
+
+    def arrived(self, j, kind):
+        return self.copy(j, kind, *self.sources[kind])
+
+    def send(self, j, part):
+        for kind in range(self.first):
+            if self.hops[kind][0] == part:
+                self.hop(j, kind).start()
+
+    def relay(self, j):
+        for after_kind, kind in self.relayed:
+            self.arrived(j, after_kind).wait_recv()
+            self.hop(j, kind).start()
+
+    def finish(self, j):
+        handled = {after_kind for after_kind, _ in self.relayed}
+        for kind in range(len(self.hops)):
+            if kind not in handled:
+                self.arrived(j, kind).wait_recv()
+            self.hop(j, kind).wait_send()
 
 
 def entry_kernel(nd, tl, *refs):
@@ -198,42 +258,7 @@
     for step in range(1, 2 * nd):
         gains_to(step).start()
 
-    if nd == 4:
-        side_x = d + 1 - 2 * lax.rem(d, 2)
-        side_y = d + 2 - 4 * (d // 2)
-        hops = (
-            (0, d, side_x),
-            (1, d, side_x),
-            (0, d, side_y),
-            (1, d, side_y),
-            (0, side_x, side_y),
-            (1, side_y, side_x),
-        )
-        sources = (
-            (0, side_x),
-            (1, side_x),
-            (0, side_y),
-            (1, side_y),
-            (0, side_x + side_y - d),
-            (1, side_x + side_y - d),
-        )
-        first, relayed = 4, ((0, 4), (3, 5))
-    else:
-        hops = tuple((part, d, lax.rem(d + step, nd)) for step in range(1, nd) for part in range(2))
-        sources = tuple(
-            (part, lax.rem(d + nd - step, nd)) for step in range(1, nd) for part in range(2)
-        )
-        first, relayed = len(hops), ()
-
-    def hop(j, kind):
-        part, of, to = hops[kind]
-        at = block(j, of * 2 + part)
-        return remote(at, at, xs.at[j, kind], xr.at[j, kind], d=to)
-
-    def arrived(j, kind):
-        part, of = sources[kind]
-        at = block(j, of * 2 + part)
-        return remote(at, at, xs.at[j, kind], xr.at[j, kind], d=hops[kind][2])
+    over_d = Spread(nd, d, block, xs, xr)
 
     def spread(j):
         for part in range(2):
@@ -247,15 +272,9 @@
             def _():
                 from_far(j, part).wait_recv()
 
-            for kind in range(first):
-                if hops[kind][0] == part:
-                    hop(j, kind).start()
-
-    def relay(j):
-        for after, kind in relayed:
-            arrived(j, after).wait_recv()
-            hop(j, kind).start()
-
+            over_d.send(j, part)
+
+    relay = over_d.relay
     spread(0)
     spread(1)
     relay(0)
@@ -283,12 +302,8 @@
             across(index, k).start()
     relay(3)
 
-    handled = {after for after, _ in relayed}
     for j in range(4):
-        for kind in range(len(hops)):
-            if kind not in handled:
-                arrived(j, kind).wait_recv()
-            hop(j, kind).wait_send()
+        over_d.finish(j)
         to_far(j).wait_send()
     for k in range(CHUNKS):
         for index in range(tl):
@@ -313,7 +328,7 @@
     rows, q_cols = q_weight.shape
     kv_cols = key_matrix.shape[1]
     own, width = tokens.shape
-    hops = 6 if nd == 4 else 2 * (nd - 1)
+    hops = hop_count(nd)
     dma = pltpu.SemaphoreType.DMA
     return pl.pallas_call(
         functools.partial(entry_kernel, nd, tl),
@@ -353,16 +368,26 @@
     )(q_weight, key_matrix, value_matrix, o_weight, tokens, gains)
 
 
-def exchange_kernel(tl, epilogue, aux_count, out_count, gather, *refs):
+PIECES = 3
+
+
+def exchange_kernel(nd, tl, epilogue, aux_count, out_count, gather, carry_weights, *refs):
     partial = refs[0]
     aux = refs[1 : 1 + aux_count]
-    outs = refs[1 + aux_count : 1 + aux_count + out_count]
-    rest = refs[1 + aux_count + out_count :]
+    refs = refs[1 + aux_count :]
+    if carry_weights:
+        weight_rows, refs = refs[0], refs[1:]
+    outs = refs[:out_count]
+    rest = refs[out_count:]
     if gather:
         full, rest = rest[0], rest[1:]
+    if carry_weights:
+        weights, ws, wr, xs, xr, rest = rest[0], *rest[1:5], rest[5:]
+    if gather:
         finished, ls, lr, fs, fr, keep, rest = rest[0], *rest[1:6], rest[6:]
     mine, other, sums, arrivals, cs, cr, loc, ss, sr = rest
     c, l = lax.axis_index("c"), lax.axis_index("l")
+    d, h = lax.axis_index("d"), lax.axis_index("h")
     own = arrivals.shape[0] // (tl - 1)
     chunk = own // CHUNKS
 
@@ -372,7 +397,16 @@
         pl.semaphore_signal(
             barrier, inc=1, device_id={"l": lax.rem(l + step, tl)}, device_id_type=MESH
         )
-    pl.semaphore_wait(barrier, tl)
+    partners = tl
+    if carry_weights:
+        pl.semaphore_signal(barrier, inc=1, device_id={"h": 1 - h}, device_id_type=MESH)
+        partners += 1
+        for step in range(1, nd):
+            pl.semaphore_signal(
+                barrier, inc=1, device_id={"d": lax.rem(d + step, nd)}, device_id_type=MESH
+            )
+        partners += nd - 1
+    pl.semaphore_wait(barrier, partners)
 
     def part(base, k):
         return rows_at(base * CHUNKS + k, chunk)
@@ -397,6 +431,33 @@
             sr.at[at],
             l=lax.rem(l + step, tl),
         )
+
+    if carry_weights:
+        half = weight_rows.shape[0] // 2
+        piece = weight_rows.shape[1] // PIECES
+
+        def block(j, row):
+            return weights.at[rows_at(row, half), pl.ds(j * piece, piece)]
+
+        def from_far(j, row_part):
+            return remote(
+                weight_rows.at[pl.ds(row_part * half, half), pl.ds(j * piece, piece)],
+                block(j, d * 2 + row_part),
+                ws.at[j, row_part],
+                wr.at[j, row_part],
+                h=1 - h,
+            )
+
+        over_d = Spread(nd, d, block, xs, xr)
+
+        def spread(j):
+            for row_part in range(2):
+                from_far(j, row_part).wait_recv()
+                over_d.send(j, row_part)
+
+        for j in range(PIECES):
+            for row_part in range(2):
+                from_far(j, row_part).start()
 
     order = list(range(1, tl)) + [0]
     for index in order:
@@ -457,18 +518,32 @@
             across(0, k).start()
         return carry
 
-    lax.fori_loop(0, CHUNKS, finish, 0)
+    if carry_weights:
+        for k in range(CHUNKS):
+            finish(k, 0)
+            spread(k)
+            if k:
+                over_d.relay(k - 1)
+    else:
+        lax.fori_loop(0, CHUNKS, finish, 0)
     if gather:
         for k in range(CHUNKS):
             for index in range(1, tl):
                 from_along(index, k).wait_recv()
                 across(index, k).start()
+        if carry_weights:
+            over_d.relay(PIECES - 1)
         for k in range(CHUNKS):
             keep_own(k).wait()
             for index in range(tl):
                 across(index, k).wait()
             for step in range(1, tl):
                 own_along(step, k).wait_send()
+    if carry_weights:
+        for j in range(PIECES):
+            over_d.finish(j)
+            for row_part in range(2):
+                from_far(j, row_part).wait_send()
     for k in range(CHUNKS):
         for index in range(tl):
             to_core(index, k).wait_send()
@@ -476,8 +551,8 @@
             along(step, k).wait_send()
 
 
-def exchange(collective_id, partial, aux, outs, epilogue, gather):
-    tl = lax.axis_size("l")
+def exchange(collective_id, partial, aux, outs, epilogue, gather, weight_rows=None):
+    nd, tl = lax.axis_size("d"), lax.axis_size("l")
     total, width = partial.shape
     own = total // (2 * tl)
     dma = pltpu.SemaphoreType.DMA
@@ -486,9 +561,22 @@
     out_shape = list(outs)
     out_specs = [vmem] * len(outs)
     scratch = []
+    given = ()
     if gather:
         out_shape.append(jax.ShapeDtypeStruct((total, width), jnp.bfloat16))
         out_specs.append(anywhere)
+    if weight_rows is not None:
+        given = (weight_rows,)
+        rows, cols = weight_rows.shape
+        out_shape.append(jax.ShapeDtypeStruct((nd * rows, cols), jnp.bfloat16))
+        out_specs.append(anywhere)
+        scratch += [
+            dma((PIECES, 2)),
+            dma((PIECES, 2)),
+            dma((PIECES, hop_count(nd))),
+            dma((PIECES, hop_count(nd))),
+        ]
+    if gather:
         scratch += [
             pltpu.VMEM((own, width), jnp.bfloat16),
             dma(((tl - 1) * CHUNKS,)),
@@ -509,9 +597,11 @@
         dma(((tl - 1) * CHUNKS,)),
     ]
     return pl.pallas_call(
-        functools.partial(exchange_kernel, tl, epilogue, len(aux), len(outs), gather),
+        functools.partial(
+            exchange_kernel, nd, tl, epilogue, len(aux), len(outs), gather, bool(given)
+        ),
         out_shape=tuple(out_shape),
-        in_specs=[anywhere] + [vmem] * len(aux),
+        in_specs=[anywhere] + [vmem] * len(aux) + [anywhere] * len(given),
         out_specs=out_specs,
         scratch_shapes=scratch,
         compiler_params=pltpu.CompilerParams(
@@ -520,7 +610,7 @@
         cost_estimate=pl.CostEstimate(
             flops=0, bytes_accessed=200_000_000 if gather else 110_000_000, transcendentals=0
         ),
-    )(partial, *aux)
+    )(partial, *aux, *given)
 
 
 def middle_rows(total, rows, k, aux, outs):
@@ -831,7 +921,7 @@
     return jnp.concatenate([half, lax.ppermute(half, "c", shift_perm(2, 1))], axis=0)
 
 
-def scatter_tokens(partial):
+def scatter_tokens(partial, *first):
     places = lax.axis_size("l")
     half = partial.shape[0] // 2
     rows = half // places
@@ -840,7 +930,9 @@
     own = total[:rows]
     for step in range(1, places):
         sent = total[step * rows : (step + 1) * rows].astype(jnp.bfloat16)
-        own = own + lax.ppermute(sent, "l", shift_perm(places, -step)).astype(jnp.float32)
+        moved = lax.ppermute(sent, "l", shift_perm(places, -step))
+        moved = after(moved, *first)
+        own = own + moved.astype(jnp.float32)
     return own
 
 
@@ -929,7 +1021,6 @@
     up_half = core_halves(up_weight[0])
     mid_rows = jnp.concatenate([gate_half, up_half], axis=1)
     down_rows = core_halves(down_weight[0])
-    mid_near = lax.all_gather(mid_rows, "d", axis=0, tiled=True)
     down_near = lax.all_gather(down_rows, "d", axis=0, tiled=True)
 
     cut = attn_gain.shape[1]
@@ -950,7 +1041,7 @@
     qkv_full, o_full, group, gains = enter(
         q_weight[0], key_matrix[0], value_matrix[0], o_weight[0], after(tokens, mid_rows), gains
     )
-    mid_far = lax.ppermute(after(mid_rows, group), "h", shift_perm(2, 1))
+    mid_near = lax.all_gather(after(mid_rows, group), "d", axis=0, tiled=True)
     down_far = lax.ppermute(after(down_rows, group), "h", shift_perm(2, 1))
     cotangent = trade(after(cotangent, group))
     gains = gains.reshape(gains.shape[0], -1)
@@ -967,28 +1058,29 @@
     query_reduced, key_reduced, value_reduced, attended, totals = attention(
         qkv, tables, order, head_count, kv_heads
     )
-    mid_far = lax.all_gather(after(mid_far, attended, down_near), "d", axis=0, tiled=True)
+    down_far = lax.all_gather(after(down_far, attended), "d", axis=0, tiled=True)
 
     def whole(values):
         return jax.ShapeDtypeStruct((own_rows, width), values)
 
     gain_sum = jax.ShapeDtypeStruct((1, width), jnp.float32)
-    middle, normed_mid = exchange(
+    middle, normed_mid, mid_far = exchange(
         1,
         contract_cols(attended, o_full).astype(jnp.bfloat16),
         (stream, as_row(mlp_scale)),
         (whole(jnp.float32),),
         middle_rows,
         True,
-    )
-    down_far = lax.all_gather(after(down_far, normed_mid), "d", axis=0, tiled=True)
+        mid_rows,
+    )
     cotangent = after(cotangent, normed_mid)
 
     gate_near, up_near = split(jnp.dot(normed_mid, mid_near, preferred_element_type=jnp.float32))
     hidden_near = swiglu(gate_near, up_near).astype(jnp.bfloat16)
     gate_far, up_far = split(jnp.dot(normed_mid, mid_far, preferred_element_type=jnp.float32))
     hidden_far = swiglu(gate_far, up_far).astype(jnp.bfloat16)
-    grad_rows = gather_tokens(cotangent, hidden_far)
+    branch = contract_cols(hidden_near, down_near) + contract_cols(hidden_far, down_far)
+    grad_rows = gather_tokens(cotangent, branch)
     down_grads = sum_over_d(
         jnp.concatenate(
             [
@@ -1038,6 +1130,9 @@
         kv_heads,
     )
     qkv_back = jnp.concatenate([query_back, key_back, value_back], axis=1)
+    mid_sum_far = after(mid_sum_far, query_back)
+    branch = scatter_tokens(branch, query_back)
+    activations = trade((middle + branch).astype(jnp.bfloat16))
     qkv_grad = contract_rows(normed, qkv_back).astype(jnp.bfloat16)
     attn_grad = scatter_weights(
         after(jnp.concatenate([qkv_grad, o_wgrad.astype(jnp.bfloat16)], axis=1), mid_sum_far)
@@ -1052,12 +1147,6 @@
     )
     moved = trade(moved)
     gradient = jnp.where(core == lax.axis_index("h"), gradient, moved.astype(jnp.float32))
-
-    hidden_near = after(hidden_near, attn_gain_grad)
-    branch = scatter_tokens(
-        contract_cols(hidden_near, down_near) + contract_cols(hidden_far, down_far)
-    )
-    activations = trade((middle + branch).astype(jnp.bfloat16))
 
     split_at = down_rows.shape[1]
     down_grad = columns_of(*return_halves(down_grads[:, :split_at], down_grads[:, split_at:]))

time: 906 us -> 883 us (0.975)
  waiting for transfers between devices: 223 us -> 152 us
  Pallas kernels: 308 us -> 357 us
  blocking collectives: 57.6 us -> 48.1 us
    pallas_call x3, Pallas kernels: 163 us -> 220 us  [exchange(): pl.pallas_call(functools.partial(exchange_kernel, nd, tl, epilogue, len(a...]
    ppermute x2 -> x1, waiting for transfers between devices: 34.6 us -> 0.01 us  [scatter_tokens(): moved = lax.ppermute(sent, 'l', shift_perm(places, -step))]
    all_gather x3 -> x2, waiting for transfers between devices: 34.9 us -> 9.54 us  [the longest x1 9.53 us: per_device(): lax.all_gather(after(down_far, attended), 'd', axis=0, tiled=True)]
    ppermute x1, starting transfers between devices: 16.5 us -> 0.07 us  [gather_tokens(): lax.ppermute(half, 'c', shift_perm(2, 1))]
    ppermute x1, waiting for transfers between devices: 13.3 us -> 0.01 us  [gather_tokens(): lax.ppermute(own, 'l', shift_perm(places, step))]
    psum x1, blocking collectives: 57.6 us -> 48.1 us  [per_device(): lax.psum(jnp.concatenate([attn_gain_grad[0], mlp_gain_grad[0], q_gain_gra...]
    ppermute x4, starting transfers between devices: 5.11 us -> 14.3 us  [trade(): return lax.ppermute(values, ('c', 'h'), [(0, 0), (1, 2), (2, 1), (3, 3)])]
    unnamed x128 -> x124, local copies, waits for them, and re-layouts: 24.2 us -> 20.1 us
  transfers between devices with their start and end apart: 27 -> 25, of which waited for: 8 -> 6; matrix products, arithmetic and copies ran while one was open for 25% -> 25% of each run, Pallas kernels for 34% -> 31%
where the time goes in v4:
time: 883 us; the launch traced here: 877 us
  Pallas kernels  357 us (40%)
  matrix products  168 us (19%)
  waiting for transfers between devices  152 us (17%)
  other arithmetic  53 us (6%)
  blocking collectives  48.1 us (5%)
  starting transfers between devices  44.8 us (5%)
  local copies, waits for them, and re-layouts  38.3 us (4%)
  between operations  15.6 us (2%)
    pallas_call x3, Pallas kernels, exchange(): pl.pallas_call(functools.partial(exchange_kernel, nd, tl, epilogue, len(a...  220 us
    ppermute x2, waiting for transfers between devices, return_halves(): far = lax.ppermute(far, 'h', shift_perm(2, 1))  102 us
    pallas_call x1, Pallas kernels, enter(): pl.pallas_call(functools.partial(entry_kernel, nd, tl), name='entry', out...  83.2 us
    dot_general x6, matrix products, contract_cols(): lax.dot_general(left, right, (((1,), (1,)), ((), ())), preferred_element_...  58.1 us
    dot_general x6, matrix products, contract_rows(): lax.dot_general(left, right, (((0,), (0,)), ((), ())), preferred_element_...  48.8 us
    psum x1, blocking collectives, per_device(): lax.psum(jnp.concatenate([attn_gain_grad[0], mlp_gain_grad[0], q_gain_gra...  48.1 us
    pallas_call x1, Pallas kernels, attention_pull(): pl.pallas_call(functools.partial(attention_pull_kernel, blocks, repeat),...  34.4 us
    ppermute x1, waiting for transfers between devices, scatter_weights(): far = lax.ppermute(jnp.where(same, other, mine), 'h', shift_perm(2, 1))  34 us
  transfers between devices with their start and end apart: 25, of which 6 were waited for; matrix products, arithmetic and copies ran while one was open for 25% of the time, Pallas kernels for 31%

profile of v4, /device:TPU:0, one launch (start us, length us, event | category | flops | bytes accessed | tf_op | source)
XLA Modules:
  0.0 876.8 jit_solution(18261636636031407694)
XLA Ops:
  11.6 1.3 fusion.25.refs_5_
  14.5 83.2 %entry.1 = (bf16[2048,1024]{1,0:T(8,128)(2,1)}, bf16[2048,512]{1,0:T(8,128)(2,1)}, bf16[1152,2048]{1,0:T(8,128)(2,1)}, f32[8,8,128]{2,1,0:T(8,128)}) custom-call(bf16[256,512]{1,0:T(8,128)(2,1)} %bitcast.129, bf16[256,256]{1,0:T(8,128)(2,1)} %bitcast.131, bf16[256,256]{1,0:T(8,128)(2,1)} %bitcast.132, bf16[256,512]{1,0:T(8,128)(2,1)} %bitcast.130, ...), custom_call_target="tpu_custom_call" | custom-call | bytes 250000000 | tf_op jit(solution)/shard_map/entry/pallas_call | solution.py:333
  98.5 5.5 collective-permute-start.3
  105.4 2.1 fusion.16
  110.1 1.6 slice.132.refs_1_
  111.9 3.2 collective-permute-start.4
  115.2 10.8 %collective-permute-start.7 = (bf16[288,2048]{1,0:T(8,128)(2,1)}, bf16[288,2048]{1,0:T(8,128)(2,1)}, u32[]{:S(2)}, u32[]{:S(2)}) collective-permute-start(bf16[288,2048]{1,0:T(8,128)(2,1)} %param.27), channel_id=1, source_target_pairs={{0,0},{2,4},{4,2},{6,6},{1,1},{3,5},{5,3},{7,7},{8,8},{10,12},{12,... | collective-permute-start | bytes 3538952 | tf_op jit(solution)/shard_map/ppermute | solution.py:912
  126.0 3.3 fusion
  129.3 9.2 %fusion.14.refs_0_.refs_1_.refs_2_ = f32[1152,1024]{1,0:T(8,128)} fusion(bf16[2048,1024]{1,0:T(8,128)(2,1)S(1)} %copy-done.41, bf16[1152,2048]{1,0:T(8,128)(2,1)} %get-tuple-element.51, f32[2048]{0:T(1024)S(1)} %bitcast.136, f32[1152]{0:T(1024)S(1)} %add_rsqrt_fusion), kind=kOutput, calls=%fused_computation.54 | convolution fusion | flops 4841275392 | bytes 13644288 | tf_op jit(solution)/shard_map/dot_general | solution.py:1056
  138.6 20.2 %attention.1 = (bf16[1152,512]{1,0:T(8,128)(2,1)}, bf16[1152,256]{1,0:T(8,128)(2,1)S(1)}, bf16[1152,256]{1,0:T(8,128)(2,1)S(1)}, bf16[1152,512]{1,0:T(8,128)(2,1)}, f32[1152,256]{1,0:T(8,128)}) custom-call(s32[4]{0:T(128)S(1)} %get-tuple-element.88.order_ref, f32[1152,1024]{1,0:T(8,128)} %fusion.14.refs_0_.refs_1_.refs_2_, ...), custom_call_target="tpu_custom_call" | custom-call | flops 2717908992 | bytes 60000000 | tf_op jit(solution)/shard_map/attention/pallas_call | solution.py:762
  160.5 4.3 convolution_convert_fusion.3.refs_0_
  164.8 112.4 %shard_map.237 = (f32[288,2048]{1,0:T(8,128)S(1)}, bf16[1152,2048]{1,0:T(8,128)(2,1)S(1)}, bf16[2048,1536]{1,0:T(8,128)(2,1)}) custom-call(bf16[1152,2048]{1,0:T(8,128)(2,1)S(1)} %convolution_convert_fusion.3.refs_0_, bf16[288,2048]{1,0:T(8,128)(2,1)S(1)} %slice.132.refs_1_, f32[1,2048]{1,0:T(1,128)S(1)} %bitcast.108, bf16[512,1536]{1,0:T(8,128)(2,1)S(1)} %copy-done), custom_call_target="tpu_custom_call" | custom-call | bytes 200000000 | tf_op jit(solution)/shard_map/pallas_call | solution.py:599
  277.2 13.1 %fusion.35 = f32[1152,1536]{1,0:T(8,128)} fusion(bf16[1152,2048]{1,0:T(8,128)(2,1)S(1)} %get-tuple-element.57, bf16[2048,1536]{1,0:T(8,128)(2,1)} %get-tuple-element.59), kind=kOutput, calls=%fused_computation.130 | convolution fusion | flops 7247757312 | bytes 18087936 | tf_op jit(solution)/shard_map/dot_general | solution.py:1080
  290.6 5.3 multiply_convert_fusion.2
  296.0 11.4 %fusion.33 = f32[1152,1536]{1,0:T(8,128)S(1)} fusion(bf16[1152,2048]{1,0:T(8,128)(2,1)} %copy-done.13, bf16[2048,1536]{1,0:T(8,128)(2,1)} %all-gather.4.cloned.1.call-done), kind=kOutput, calls=%fused_computation.128 | convolution fusion | flops 7247757312 | bytes 18087936 | tf_op jit(solution)/shard_map/dot_general | solution.py:1078
  307.3 2.8 copy-done.19
  310.2 2.3 multiply_convert_fusion.3
  312.4 10.4 %fusion.34 = f32[1152,2048]{1,0:T(8,128)} fusion(bf16[1152,768]{1,0:T(8,128)(2,1)} %multiply_convert_fusion.3, bf16[2048,768]{1,0:T(8,128)(2,1)} %all-gather.6.cloned.1.call-done), kind=kOutput, calls=%fused_computation.129 | convolution fusion | flops 3623878656 | bytes 14352384 | tf_op jit(solution)/shard_map/dot_general | solution.py:53
  322.9 9.5 %all-gather.8.cloned.1.call-done = bf16[2048,768]{1,0:T(8,128)(2,1)} async-done(((bf16[512,768]{1,0:T(8,128)(2,1)}), bf16[2048,768]{1,0:T(8,128)(2,1)}) %all-gather.8.cloned.1.call-update) | async-done | bytes 3145744 | tf_op jit(solution)/shard_map/all_gather | solution.py:1061
  332.4 12.6 %convolution_add_fusion = f32[1152,2048]{1,0:T(8,128)} fusion(f32[1152,2048]{1,0:T(8,128)} %fusion.34, bf16[1152,768]{1,0:T(8,128)(2,1)} %multiply_convert_fusion.2, bf16[2048,768]{1,0:T(8,128)(2,1)} %all-gather.8.cloned.1.call-done), kind=kOutput, calls=%fused_computation.7 | convolution fusion | flops 3626237952 | bytes 23789568 | tf_op jit(solution)/shard_map/dot_general | solution.py:53
  345.0 1.8 pad_maximum_fusion.4
  346.9 1.4 constant_dynamic-update-slice_fusion.2
  348.3 1.5 constant_dynamic-update-slice_fusion.1
  349.8 1.6 collective-permute-done.9
  351.6 9.3 %fusion.8 = (bf16[1152,768]{1,0:T(8,128)(2,1)S(1)}, bf16[1152,768]{1,0:T(8,128)(2,1)S(1)}) fusion(f32[1152,1536]{1,0:T(8,128)} %fusion.35, bf16[1152,2048]{1,0:T(8,128)(2,1)S(1)} %constant_dynamic-update-slice_fusion, bf16[2048,768]{1,0:T(8,128)(2,1)S(1)} %copy-done.43), kind=kOutput, calls=%fused_computation.24 | convolution fusion | flops 3636264960 | bytes 18481152 | tf_op jit(solution)/shard_map/dot_general | solution.py:1095
  362.8 10.7 %convolution_convert_fusion.2 = bf16[2048,1536]{1,0:T(8,128)(2,1)} fusion(bf16[1152,2048]{1,0:T(8,128)(2,1)S(1)} %bitcast.114, bf16[1152,768]{1,0:T(8,128)(2,1)S(1)} %get-tuple-element.90, bf16[1152,768]{1,0:T(8,128)(2,1)S(1)} %get-tuple-element.89), kind=kOutput, calls=%fused_computation.10 | convolution fusion | flops 7257980928 | bytes 14548992 | tf_op jit(solution)/shard_map/dot_general | solution.py:47
  373.5 7.4 convolution_convert_fusion.5
  380.9 7.2 convolution_convert_fusion.6
  388.1 3.2 pad_maximum_fusion.1
  391.5 10.8 %fusion.5 = (bf16[1152,768]{1,0:T(8,128)(2,1)S(1)}, bf16[1152,768]{1,0:T(8,128)(2,1)S(1)}) fusion(f32[1152,1536]{1,0:T(8,128)} %copy-done.19, bf16[1152,2048]{1,0:T(8,128)(2,1)} %copy-done.33, bf16[2048,768]{1,0:T(8,128)(2,1)} %all-gather.6.cloned.1.call-done), kind=kOutput, calls=%fused_computation.21 | convolution fusion | flops 3636264960 | bytes 18481152 | tf_op jit(solution)/shard_map/dot_general | solution.py:1095
  403.6 12.1 %fusion.29 = f32[1152,2048]{1,0:T(8,128)} fusion(bf16[2048,1536]{1,0:T(8,128)(2,1)} %all-gather.4.cloned.1.call-done, bf16[1152,768]{1,0:T(8,128)(2,1)S(1)} %get-tuple-element.92, bf16[1152,768]{1,0:T(8,128)(2,1)S(1)} %get-tuple-element.91), kind=kOutput, calls=%fused_computation.124 | convolution fusion | flops 7254835200 | bytes 19267584 | tf_op jit(solution)/shard_map/dot_general | solution.py:53
  415.7 13.3 %add_convert_fusion.refs_0_ = bf16[1152,2048]{1,0:T(8,128)(2,1)} fusion(f32[1152,2048]{1,0:T(8,128)} %fusion.29, bf16[2048,1536]{1,0:T(8,128)(2,1)} %get-tuple-element.59, bf16[1152,768]{1,0:T(8,128)(2,1)S(1)} %copy-done.50, bf16[1152,768]{1,0:T(8,128)(2,1)S(1)} %copy-done.48), kind=kOutput, calls=%fused_computation.6 | convolution fusion | flops 7259553792 | bytes 23986176 | tf_op jit(solution)/shard_map/dot_general | solution.py:53
  429.1 58.7 %shard_map.238 = (f32[288,2048]{1,0:T(8,128)S(1)}, f32[1,2048]{1,0:T(1,128)S(1)}, bf16[1152,2048]{1,0:T(8,128)(2,1)S(1)}) custom-call(bf16[1152,2048]{1,0:T(8,128)(2,1)} %add_convert_fusion.refs_0_, f32[288,2048]{1,0:T(8,128)S(1)} %get-tuple-element.56.refs_1_, bf16[288,2048]{1,0:T(8,128)(2,1)} %collective-permute-done.7.refs_2_, f32[1,2048]{1,0:T(1,128)S(1)} %bitcast.109), custom_call_target="tpu_custom_call" | custom-call | bytes 200000000 | tf_op jit(solution)/shard_map/pallas_call | solution.py:599
  489.2 1.5 copy-done.14
  490.7 10.5 %convolution_convert_fusion.1 = bf16[2048,1536]{1,0:T(8,128)(2,1)} fusion(bf16[1152,2048]{1,0:T(8,128)(2,1)S(1)} %bitcast.116, bf16[1152,1536]{1,0:T(8,128)(2,1)S(1)} %pad_maximum_fusion.2), kind=kOutput, calls=%fused_computation.9 | convolution fusion | flops 7250903040 | bytes 14548992 | tf_op jit(solution)/shard_map/dot_general | solution.py:47
  501.3 6.8 convolution_convert_fusion.8.refs_11_
  508.1 34.4 %attention_pull.1 = (bf16[1152,512]{1,0:T(8,128)(2,1)}, bf16[1152,256]{1,0:T(8,128)(2,1)}, bf16[1152,256]{1,0:T(8,128)(2,1)}, f32[8,128]{1,0:T(8,128)}, f32[8,128]{1,0:T(8,128)}) custom-call(s32[4]{0:T(128)} %copy-done.12, f32[1152,1024]{1,0:T(8,128)} %fusion.14.refs_0_.refs_1_.refs_2_, f32[1152,1024]{1,0:T(8,128)} %fusion.14.refs_0_.refs_1_.refs_2_, ...), custom_call_target="tpu_custom_call" | custom-call | flops 6794772480 | bytes 120000000 | tf_op jit(solution)/shard_map/attention_pull/pallas_call | solution.py:868
  542.6 1.6 constant_dynamic-update-slice_fusion.5
  545.5 4.1 convolution_convert_fusion.7
  549.6 9.0 %convolution_convert_fusion.4 = bf16[2048,1024]{1,0:T(8,128)(2,1)S(1)} fusion(bf16[1152,1024]{1,0:T(8,128)(2,1)S(1)} %constant_dynamic-update-slice_fusion.3, bf16[1152,2048]{1,0:T(8,128)(2,1)} %get-tuple-element.51, f32[2048]{0:T(1024)S(1)} %bitcast.137, f32[1152]{0:T(1024)S(1)} %copy-done.39), kind=kOutput, calls=%fused_computation.18 | convolution fusion | flops 4843372544 | bytes 11284992 | tf_op jit(solution)/shard_map/dot_general | solution.py:47
  558.7 3.2 pad_maximum_fusion
  561.9 4.2 slice.288
  566.5 4.5 collective-permute-done.5
  571.0 3.8 slice_add_fusion
  574.8 1.4 slice.289
  576.2 1.8 collective-permute-start.6
  578.0 5.3 convolution_convert_fusion.refs_0_
  583.4 48.5 %shard_map.239 = (f32[288,2048]{1,0:T(8,128)S(1)}, bf16[288,2048]{1,0:T(8,128)(2,1)}, f32[1,2048]{1,0:T(1,128)S(1)}) custom-call(bf16[1152,2048]{1,0:T(8,128)(2,1)S(1)} %convolution_convert_fusion.refs_0_, bf16[288,2048]{1,0:T(8,128)(2,1)S(1)} %slice.132.refs_1_, f32[288,2048]{1,0:T(8,128)S(1)} %copy-done.3, f32[1,2048]{1,0:T(1,128)S(1)} %bitcast.110), custom_call_target="tpu_custom_call" | custom-call | bytes 110000000 | tf_op jit(solution)/shard_map/pallas_call | solution.py:599
  631.9 1.4 copy-done.4
  633.3 1.9 collective-permute-start.11
  637.2 48.1 %psum.7 = f32[4352]{0:T(1024)} all-reduce(f32[4352]{0:T(1024)} %pad_maximum_fusion.10), channel_id=1, replica_groups=mesh['d'=4,'c'=2,'h'=2,'l'=2] {'d','c','h','l'}, use_global_device_ids=true, to_apply=%region_3.4 | all-reduce | flops 4352 | bytes 34816 | tf_op jit(solution)/shard_map/psum | solution.py:1157
  690.5 2.3 collective-permute-start.14
  692.8 2.6 fusion.12
  698.1 73.1 %collective-permute-done.16 = bf16[512,768]{1,0:T(8,128)(2,1)S(1)} collective-permute-done((bf16[512,768]{1,0:T(8,128)(2,1)S(1)}, bf16[512,768]{1,0:T(8,128)(2,1)S(1)}, u32[]{:S(2)}, u32[]{:S(2)}) %collective-permute-start.16) | collective-permute-done | bytes 786464 | tf_op jit(solution)/shard_map/ppermute | solution.py:955
  771.6 1.7 convert_select_fusion
  775.6 29.3 %collective-permute-done.14 = bf16[512,1536]{1,0:T(8,128)(2,1)} collective-permute-done((bf16[512,1536]{1,0:T(8,128)(2,1)}, bf16[512,1536]{1,0:T(8,128)(2,1)}, u32[]{:S(2)}, u32[]{:S(2)}) %collective-permute-start.14) | collective-permute-done | bytes 1572896 | tf_op jit(solution)/shard_map/ppermute | solution.py:955
  804.9 2.3 convert_add_fusion
  808.3 14.7 %collective-permute-start.15 = (bf16[256,1536]{1,0:T(8,128)(2,1)}, bf16[256,1536]{1,0:T(8,128)(2,1)}, u32[]{:S(2)}, u32[]{:S(2)}) collective-permute-start(bf16[256,1536]{1,0:T(8,128)(2,1)} %select_convert_fusion), channel_id=1, source_target_pairs={{4,0},{0,4},{5,1},{1,5},{6,2},{2,6},{7,3},{3,7},{12,8},{8,12},{13,... | collective-permute-start | bytes 2359304 | tf_op jit(solution)/shard_map/ppermute | solution.py:961
  823.0 1.5 broadcast_select_fusion
  824.5 2.7 maximum_bitcast_fusion.2
  827.4 1.4 convert_element_type.138
  829.5 1.4 maximum_bitcast_fusion
  830.9 1.4 maximum_bitcast_fusion.1
  832.2 34.0 %collective-permute-done.13 = bf16[256,1536]{1,0:T(8,128)(2,1)S(1)} collective-permute-done((bf16[256,1536]{1,0:T(8,128)(2,1)S(1)}, bf16[256,1536]{1,0:T(8,128)(2,1)S(1)}, u32[]{:S(2)}, u32[]{:S(2)}) %collective-permute-start.13) | collective-permute-done | bytes 786464 | tf_op jit(solution)/shard_map/ppermute | solution.py:993
  (216 shorter events, 37.1 us)
Async XLA Ops:
  7.2 288.8 %all-gather.4.cloned.1.call-start = ((), (), s32[]{:S(2)}) async-start(), calls=%async_computation.4 | async-start | bytes 7864320 | tf_op jit(solution)/shard_map/all_gather | solution.py:1044
  8.4 4.6 collective-permute-start.1
  10.1 3.0 collective-permute-start
  13.2 84.5 %copy-start.46 = (s32[1,1152]{1,0:T(1,128)S(1)}, s32[1,1152]{1,0:T(1,128)}, u32[]{:S(2)}) copy-start(s32[1,1152]{1,0:T(1,128)} %param.15) | copy-start | bytes 13828
  13.3 85.2 %copy-start.29 = (bf16[1,256,1536]{2,1,0:T(8,128)(2,1)S(1)}, bf16[1,256,1536]{2,1,0:T(8,128)(2,1)}, u32[]{:S(2)}) copy-start(bf16[1,256,1536]{2,1,0:T(8,128)(2,1)} %param.26) | copy-start | bytes 2359300
  97.7 214.7 %all-gather.6.cloned.1.call-start = ((), (), s32[]{:S(2)}) async-start(), calls=%async_computation.5 | async-start | bytes 3932160 | tf_op jit(solution)/shard_map/all_gather | solution.py:1024
  97.8 6.6 collective-permute-start.2
  98.5 9.7 %copy-start.35 = (f32[8,8,128]{2,1,0:T(8,128)S(1)}, f32[8,8,128]{2,1,0:T(8,128)}, u32[]{:S(2)}) copy-start(f32[8,8,128]{2,1,0:T(8,128)} %get-tuple-element.52) | copy-start | bytes 98308
  98.5 9.6 %collective-permute-start.3 = (bf16[256,768]{1,0:T(8,128)(2,1)S(1)}, bf16[256,768]{1,0:T(8,128)(2,1)S(1)}, u32[]{:S(2)}, u32[]{:S(2)}) collective-permute-start(bf16[256,768]{1,0:T(8,128)(2,1)S(1)} %get-tuple-element.104), channel_id=1, source_target_pairs={{4,0},{0,4},{5,1},{1,5},{6,2},{2,6},{7,3},{3,7},{12,8},{8,12},{13,... | collective-permute-start | bytes 1179656 | tf_op jit(solution)/shard_map/ppermute | solution.py:948
  104.2 34.3 %copy-start.12 = (s32[4]{0:T(128)}, s32[4]{0:T(128)S(1)}, u32[]{:S(2)}) copy-start(s32[4]{0:T(128)S(1)} %get-tuple-element.88.order_ref) | copy-start | bytes 52
  107.7 30.8 %copy-start.1 = (s32[1152,1]{1,0:T(8,128)}, s32[1152,1]{1,0:T(8,128)S(1)}, u32[]{:S(2)}) copy-start(s32[1152,1]{1,0:T(8,128)S(1)} %reduce_sum.33.refs_7_.refs_6_) | copy-start | bytes 13828
  108.1 30.4 %copy-start.6 = (f32[1152,128]{1,0:T(8,128)}, f32[1152,128]{1,0:T(8,128)S(1)}, u32[]{:S(2)}) copy-start(f32[1152,128]{1,0:T(8,128)S(1)} %get-tuple-element.121.refs_3_.refs_2_) | copy-start | bytes 1769476
  108.1 30.4 %copy-start.7 = (f32[1152,128]{1,0:T(8,128)}, f32[1152,128]{1,0:T(8,128)S(1)}, u32[]{:S(2)}) copy-start(f32[1152,128]{1,0:T(8,128)S(1)} %get-tuple-element.122.refs_4_.refs_3_) | copy-start | bytes 1769476
  110.0 222.4 %all-gather.8.cloned.1.call-start = ((), (), s32[]{:S(2)}) async-start(), calls=%async_computation.6 | async-start | bytes 3932160 | tf_op jit(solution)/shard_map/all_gather | solution.py:1061
  111.7 26.8 %copy-start.36 = (f32[1,2,8,128]{3,1,2,0:T(2,128)}, f32[1,2,8,128]{3,1,2,0:T(2,128)S(1)}, u32[]{:S(2)}) copy-start(f32[1,2,8,128]{3,1,2,0:T(2,128)S(1)} %copy.62) | copy-start | bytes 24580
  111.8 26.8 %copy-start.10 = (f32[1,128]{1,0:T(1,128)}, f32[1,128]{1,0:T(1,128)S(1)}, u32[]{:S(2)}) copy-start(f32[1,128]{1,0:T(1,128)S(1)} %reshape_reshape.11.refs_5_.refs_4_) | copy-start | bytes 1540
  111.9 26.7 %copy-start.11 = (f32[1,128]{1,0:T(1,128)}, f32[1,128]{1,0:T(1,128)S(1)}, u32[]{:S(2)}) copy-start(f32[1,128]{1,0:T(1,128)S(1)} %reshape_reshape.12.refs_6_.refs_5_) | copy-start | bytes 1540
  111.9 17.5 %copy-start.41 = (bf16[2048,1024]{1,0:T(8,128)(2,1)S(1)}, bf16[2048,1024]{1,0:T(8,128)(2,1)}, u32[]{:S(2)}) copy-start(bf16[2048,1024]{1,0:T(8,128)(2,1)} %get-tuple-element.53) | copy-start | bytes 12582916
  111.9 52.9 %copy-start.8 = (f32[1,1,8,256]{3,1,2,0:T(1,128)}, f32[1,1,8,256]{3,1,2,0:T(1,128)S(1)}, u32[]{:S(2)}) copy-start(f32[1,1,8,256]{3,1,2,0:T(1,128)S(1)} %copy.63) | copy-start | bytes 24580
  111.9 178.4 %collective-permute-start.4 = (bf16[512,768]{1,0:T(8,128)(2,1)}, bf16[512,768]{1,0:T(8,128)(2,1)}, u32[]{:S(2)}, u32[]{:S(2)}) collective-permute-start(bf16[512,768]{1,0:T(8,128)(2,1)} %bitcast.120), channel_id=1, source_target_pairs={{2,0},{0,2},{3,1},{1,3},{6,4},{4,6},{7,5},{5,7},{10,8},{8,10},{11,... | collective-permute-start | bytes 2359304 | tf_op jit(solution)/shard_map/ppermute | solution.py:1045
  115.2 180.8 %collective-permute-start.7 = (bf16[288,2048]{1,0:T(8,128)(2,1)}, bf16[288,2048]{1,0:T(8,128)(2,1)}, u32[]{:S(2)}, u32[]{:S(2)}) collective-permute-start(bf16[288,2048]{1,0:T(8,128)(2,1)} %param.27), channel_id=1, source_target_pairs={{0,0},{2,4},{4,2},{6,6},{1,1},{3,5},{5,3},{7,7},{8,8},{10,12},{12,... | collective-permute-start | bytes 3538952 | tf_op jit(solution)/shard_map/ppermute | solution.py:912
  129.3 9.2 %copy-start.38 = (f32[1152]{0:T(1024)}, f32[1152]{0:T(1024)S(1)}, u32[]{:S(2)}) copy-start(f32[1152]{0:T(1024)S(1)} %add_rsqrt_fusion) | copy-start | bytes 13828
  138.6 21.9 %copy-start.44 = (bf16[2048,512]{1,0:T(8,128)(2,1)S(1)}, bf16[2048,512]{1,0:T(8,128)(2,1)}, u32[]{:S(2)}) copy-start(bf16[2048,512]{1,0:T(8,128)(2,1)} %get-tuple-element.55) | copy-start | bytes 6291460
  277.2 13.2 %copy-start.13 = (bf16[1152,2048]{1,0:T(8,128)(2,1)}, bf16[1152,2048]{1,0:T(8,128)(2,1)S(1)}, u32[]{:S(2)}) copy-start(bf16[1152,2048]{1,0:T(8,128)(2,1)S(1)} %get-tuple-element.57) | copy-start | bytes 14155780
  290.4 271.5 %reduce-scatter.5.cloned.1.call-start = ((), (), s32[]{:S(2)}) async-start(), calls=%async_computation.7 | async-start | bytes 7864320 | tf_op jit(solution)/shard_map/reduce_scatter | solution.py:973
  295.9 49.1 %collective-permute-start.8 = (bf16[288,2048]{1,0:T(8,128)(2,1)}, bf16[288,2048]{1,0:T(8,128)(2,1)}, u32[]{:S(2)}, u32[]{:S(2)}) collective-permute-start(bf16[288,2048]{1,0:T(8,128)(2,1)} %collective-permute-done.7.refs_2_), channel_id=1, source_target_pairs={{1,0},{0,1},{3,2},{2,3},{5,4},{4,5},{7,6},{6,7},{9,8},{8,9},{11,10... | collective-permute-start | bytes 3538952 | tf_op jit(solution)/shard_map/ppermute | solution.py:918
  346.8 4.6 collective-permute-start.9
  351.4 11.4 %slice-start = ((s8[4718592]{0:T(1024)(128)(4,1)}), s8[4194304]{0:T(1024)(128)(4,1)S(1)}, s32[]{:S(2)}) async-start(s8[4718592]{0:T(1024)(128)(4,1)} %bitcast.113), calls=%async_computation.11 | async-start | bytes 8388608
  351.6 9.3 %copy-start.33 = (bf16[1152,2048]{1,0:T(8,128)(2,1)}, bf16[1152,2048]{1,0:T(8,128)(2,1)S(1)}, u32[]{:S(2)}) copy-start(bf16[1152,2048]{1,0:T(8,128)(2,1)S(1)} %constant_dynamic-update-slice_fusion) | copy-start | bytes 14155780
  351.6 11.2 %slice-start.1 = ((s8[4718592]{0:T(1024)(128)(4,1)}), s8[524288]{0:T(1024)(128)(4,1)S(1)}, s32[]{:S(2)}) async-start(s8[4718592]{0:T(1024)(128)(4,1)} %bitcast.113), calls=%async_computation.12 | async-start | bytes 1048576
  373.4 313.9 %reduce-scatter.11.cloned.1.call-start = ((), (), s32[]{:S(2)}) async-start(), calls=%async_computation.10 | async-start | bytes 7864320 | tf_op jit(solution)/shard_map/reduce_scatter | solution.py:973
  373.5 7.4 copy-start.25
  391.3 384.3 %reduce-scatter.9.cloned.1.call-start = ((), (), s32[]{:S(2)}) async-start(), calls=%async_computation.9 | async-start | bytes 7864320 | tf_op jit(solution)/shard_map/reduce_scatter | solution.py:973
  402.3 13.4 %copy-start.23 = (bf16[1152,768]{1,0:T(8,128)(2,1)}, bf16[1152,768]{1,0:T(8,128)(2,1)S(1)}, u32[]{:S(2)}) copy-start(bf16[1152,768]{1,0:T(8,128)(2,1)S(1)} %get-tuple-element.92) | copy-start | bytes 5308420
  403.6 12.1 %copy-start.48 = (bf16[1152,768]{1,0:T(8,128)(2,1)S(1)}, bf16[1152,768]{1,0:T(8,128)(2,1)}, u32[]{:S(2)}) copy-start(bf16[1152,768]{1,0:T(8,128)(2,1)} %copy-done.47) | copy-start | bytes 5308420
  403.6 12.1 %copy-start.50 = (bf16[1152,768]{1,0:T(8,128)(2,1)S(1)}, bf16[1152,768]{1,0:T(8,128)(2,1)}, u32[]{:S(2)}) copy-start(bf16[1152,768]{1,0:T(8,128)(2,1)} %copy-done.49) | copy-start | bytes 5308420
  403.6 87.1 %slice-start.2 = ((s8[4718592]{0:T(1024)(128)(4,1)}), s8[4194304]{0:T(1024)(128)(4,1)S(1)}, s32[]{:S(2)}) async-start(s8[4718592]{0:T(1024)(128)(4,1)} %bitcast.115), calls=%async_computation.13 | async-start | bytes 8388608
  415.7 13.4 %copy-start.9 = (f32[1,1,8,256]{3,1,2,0:T(1,128)S(1)}, f32[1,1,8,256]{3,1,2,0:T(1,128)}, u32[]{:S(2)}) copy-start(f32[1,1,8,256]{3,1,2,0:T(1,128)} %copy-done.8) | copy-start | bytes 24580
  415.7 75.0 %slice-start.3 = ((s8[4718592]{0:T(1024)(128)(4,1)}), s8[524288]{0:T(1024)(128)(4,1)S(1)}, s32[]{:S(2)}) async-start(s8[4718592]{0:T(1024)(128)(4,1)} %bitcast.115), calls=%async_computation.14 | async-start | bytes 1048576
  429.1 58.7 %copy-start.22 = (bf16[1152,768]{1,0:T(8,128)(2,1)S(1)}, bf16[1152,768]{1,0:T(8,128)(2,1)}, u32[]{:S(2)}) copy-start(bf16[1152,768]{1,0:T(8,128)(2,1)} %copy-done.21) | copy-start | bytes 5308420
  429.1 58.7 %copy-start.24 = (bf16[1152,768]{1,0:T(8,128)(2,1)S(1)}, bf16[1152,768]{1,0:T(8,128)(2,1)}, u32[]{:S(2)}) copy-start(bf16[1152,768]{1,0:T(8,128)(2,1)} %copy-done.23) | copy-start | bytes 5308420
  501.2 321.8 %reduce-scatter.7.cloned.1.call-start = ((), (), s32[]{:S(2)}) async-start(), calls=%async_computation.8 | async-start | bytes 7864320 | tf_op jit(solution)/shard_map/reduce_scatter | solution.py:987
  501.3 44.1 %slice-start.4 = ((s8[4718592]{0:T(1024)(128)(4,1)}), s8[4194304]{0:T(1024)(128)(4,1)S(1)}, s32[]{:S(2)}) async-start(s8[4718592]{0:T(1024)(128)(4,1)} %bitcast.117), calls=%async_computation.15 | async-start | bytes 8388608
  508.1 37.3 %slice-start.5 = ((s8[4718592]{0:T(1024)(128)(4,1)}), s8[524288]{0:T(1024)(128)(4,1)S(1)}, s32[]{:S(2)}) async-start(s8[4718592]{0:T(1024)(128)(4,1)} %bitcast.117), calls=%async_computation.16 | async-start | bytes 1048576
  549.6 9.0 %copy-start.20 = (bf16[2048,512]{1,0:T(8,128)(2,1)S(1)}, bf16[2048,512]{1,0:T(8,128)(2,1)}, u32[]{:S(2)}) copy-start(bf16[2048,512]{1,0:T(8,128)(2,1)} %convolution_convert_fusion.7) | copy-start | bytes 6291460
  561.9 4.6 copy-start.34
  566.1 4.9 collective-permute-start.5
  566.5 11.5 %copy-start.31 = (bf16[1152,1024]{1,0:T(8,128)(2,1)S(1)}, bf16[1152,1024]{1,0:T(8,128)(2,1)}, u32[]{:S(2)}) copy-start(bf16[1152,1024]{1,0:T(8,128)(2,1)} %copy-done.30) | copy-start | bytes 7077892
  566.5 11.5 %copy-start.42 = (bf16[2048,1024]{1,0:T(8,128)(2,1)S(1)}, bf16[2048,1024]{1,0:T(8,128)(2,1)}, u32[]{:S(2)}) copy-start(bf16[2048,1024]{1,0:T(8,128)(2,1)} %get-tuple-element.53) | copy-start | bytes 12582916
  574.8 8.6 copy-start.17
  576.2 7.2 copy-start.3
  576.2 114.3 %collective-permute-start.6 = (bf16[288,2048]{1,0:T(8,128)(2,1)}, bf16[288,2048]{1,0:T(8,128)(2,1)}, u32[]{:S(2)}, u32[]{:S(2)}) collective-permute-start(bf16[288,2048]{1,0:T(8,128)(2,1)} %slice.289), channel_id=1, source_target_pairs={{1,0},{0,1},{3,2},{2,3},{5,4},{4,5},{7,6},{6,7},{9,8},{8,9},{11,10... | collective-permute-start | bytes 3538952 | tf_op jit(solution)/shard_map/ppermute | solution.py:933
  633.3 138.3 %collective-permute-start.11 = (bf16[288,2048]{1,0:T(8,128)(2,1)}, bf16[288,2048]{1,0:T(8,128)(2,1)S(1)}, u32[]{:S(2)}, u32[]{:S(2)}) collective-permute-start(bf16[288,2048]{1,0:T(8,128)(2,1)} %get-tuple-element.80), channel_id=1, source_target_pairs={{0,0},{2,4},{4,2},{6,6},{1,1},{3,5},{5,3},{7,7},{8,8},{10,12},{12,... | collective-permute-start | bytes 3538952 | tf_op jit(solution)/shard_map/ppermute | solution.py:912
  688.5 82.7 %collective-permute-start.16 = (bf16[512,768]{1,0:T(8,128)(2,1)S(1)}, bf16[512,768]{1,0:T(8,128)(2,1)S(1)}, u32[]{:S(2)}, u32[]{:S(2)}) collective-permute-start(bf16[512,768]{1,0:T(8,128)(2,1)S(1)} %slice.203), channel_id=1, source_target_pairs={{2,0},{0,2},{3,1},{1,3},{6,4},{4,6},{7,5},{5,7},{10,8},{8,10},{11,... | collective-permute-start | bytes 2359304 | tf_op jit(solution)/shard_map/ppermute | solution.py:955
  690.5 5.7 copy-start.40
  690.5 80.7 %copy-start.26 = (bf16[512,1536]{1,0:T(8,128)(2,1)S(1)}, bf16[512,1536]{1,0:T(8,128)(2,1)}, u32[]{:S(2)}) copy-start(bf16[512,1536]{1,0:T(8,128)(2,1)} %reduce-scatter.11.cloned.1.call-done) | copy-start | bytes 4718596
  690.5 114.4 %collective-permute-start.14 = (bf16[512,1536]{1,0:T(8,128)(2,1)}, bf16[512,1536]{1,0:T(8,128)(2,1)}, u32[]{:S(2)}, u32[]{:S(2)}) collective-permute-start(bf16[512,1536]{1,0:T(8,128)(2,1)} %reduce-scatter.5.cloned.1.call-done), channel_id=1, source_target_pairs={{2,0},{0,2},{3,1},{1,3},{6,4},{4,6},{7,5},{5,7},{10,8},{8,10},{11,... | collective-permute-start | bytes 4718600 | tf_op jit(solution)/shard_map/ppermute | solution.py:955
  695.4 76.2 %copy-start.5 = (f32[288,2048]{1,0:T(8,128)S(1)}, f32[288,2048]{1,0:T(8,128)}, u32[]{:S(2)}) copy-start(f32[288,2048]{1,0:T(8,128)} %copy-done.4) | copy-start | bytes 7077892
  695.4 77.9 %collective-permute-start.10 = (bf16[288,2048]{1,0:T(8,128)(2,1)S(1)}, bf16[288,2048]{1,0:T(8,128)(2,1)S(1)}, u32[]{:S(2)}, u32[]{:S(2)}) collective-permute-start(bf16[288,2048]{1,0:T(8,128)(2,1)S(1)} %fusion.12), channel_id=1, source_target_pairs={{0,0},{2,4},{4,2},{6,6},{1,1},{3,5},{5,3},{7,7},{8,8},{10,12},{12,... | collective-permute-start | bytes 3538952 | tf_op jit(solution)/shard_map/ppermute | solution.py:912
  771.5 2.8 collective-permute-start.17
  808.3 19.1 %collective-permute-start.15 = (bf16[256,1536]{1,0:T(8,128)(2,1)}, bf16[256,1536]{1,0:T(8,128)(2,1)}, u32[]{:S(2)}, u32[]{:S(2)}) collective-permute-start(bf16[256,1536]{1,0:T(8,128)(2,1)} %select_convert_fusion), channel_id=1, source_target_pairs={{4,0},{0,4},{5,1},{1,5},{6,2},{2,6},{7,3},{3,7},{12,8},{8,12},{13,... | collective-permute-start | bytes 2359304 | tf_op jit(solution)/shard_map/ppermute | solution.py:961
  824.4 4.4 collective-permute-start.12
  829.0 37.3 %collective-permute-start.13 = (bf16[256,1536]{1,0:T(8,128)(2,1)S(1)}, bf16[256,1536]{1,0:T(8,128)(2,1)S(1)}, u32[]{:S(2)}, u32[]{:S(2)}) collective-permute-start(bf16[256,1536]{1,0:T(8,128)(2,1)S(1)} %broadcast_select_fusion.2), channel_id=1, source_target_pairs={{2,0},{0,2},{3,1},{1,3},{6,4},{4,6},{7,5},{5,7},{10,8},{8,10},{11,... | collective-permute-start | bytes 2359304 | tf_op jit(solution)/shard_map/ppermute | solution.py:993
  832.2 36.2 %copy-start.28 = (bf16[288,2048]{1,0:T(8,128)(2,1)S(1)}, bf16[288,2048]{1,0:T(8,128)(2,1)}, u32[]{:S(2)}) copy-start(bf16[288,2048]{1,0:T(8,128)(2,1)} %copy-done.27) | copy-start | bytes 3538948
  (18 other events, 42.8 us)
Sparse Core Ops, SparseCore 0:
  97.9 72.6 all-gather.3
  172.3 46.7 all-gather.5
  290.5 41.8 all-gather.7
  373.6 70.0 reduce-scatter.4
  446.5 70.0 reduce-scatter.10
  519.4 70.0 reduce-scatter.8
  592.5 70.7 reduce-scatter.6

commit v5 on v4

--- a/solution.py
+++ b/solution.py
@@ -224,23 +224,18 @@
         return pltpu.make_async_copy(gain_ref, gain_full.at[d * 2 + c], gl)
 
     local_gains().start()
-    for j in range(3):
-        to_far(j).start()
-
-        @pl.when(apart)
-        def _():
-            to_core(j).start()
 
     @pl.when(apart)
     def _():
         for k in range(CHUNKS):
             trade_tokens(k).start()
 
-    to_far(3).start()
-
-    @pl.when(apart)
-    def _():
-        to_core(3).start()
+    for j in range(4):
+        to_far(j).start()
+
+        @pl.when(apart)
+        def _():
+            to_core(j).start()
 
     @pl.when(same)
     def _():
@@ -275,31 +270,31 @@
             over_d.send(j, part)
 
     relay = over_d.relay
+    for k in range(CHUNKS):
+
+        @pl.when(same)
+        def _():
+            part = pl.ds(k * chunk, chunk)
+            pltpu.make_async_copy(tok_stage.at[part], tokens_at(0, k), tlo.at[k]).wait()
+
+        @pl.when(apart)
+        def _():
+            remote(tokens_at(0, k), tokens_at(0, k), ts.at[k], tr.at[k], c=1 - c, h=1 - h).wait_recv()
+
+        for step in range(1, tl):
+            along(step, k).start()
+        across(0, k).start()
     spread(0)
     spread(1)
     relay(0)
     spread(2)
     relay(1)
     for k in range(CHUNKS):
-
-        @pl.when(same)
-        def _():
-            part = pl.ds(k * chunk, chunk)
-            pltpu.make_async_copy(tok_stage.at[part], tokens_at(0, k), tlo.at[k]).wait()
-
-        @pl.when(apart)
-        def _():
-            remote(tokens_at(0, k), tokens_at(0, k), ts.at[k], tr.at[k], c=1 - c, h=1 - h).wait_recv()
-
-        for step in range(1, tl):
-            along(step, k).start()
-        across(0, k).start()
-    relay(2)
-    spread(3)
-    for k in range(CHUNKS):
         for index in range(1, tl):
             from_along(index, k).wait_recv()
             across(index, k).start()
+    relay(2)
+    spread(3)
     relay(3)
 
     for j in range(4):
@@ -368,7 +363,7 @@
     )(q_weight, key_matrix, value_matrix, o_weight, tokens, gains)
 
 
-PIECES = 3
+PIECES = 6
 
 
 def exchange_kernel(nd, tl, epilogue, aux_count, out_count, gather, carry_weights, *refs):
@@ -455,10 +450,6 @@
                 from_far(j, row_part).wait_recv()
                 over_d.send(j, row_part)
 
-        for j in range(PIECES):
-            for row_part in range(2):
-                from_far(j, row_part).start()
-
     order = list(range(1, tl)) + [0]
     for index in order:
         for k in range(CHUNKS):
@@ -479,6 +470,11 @@
             return carry
 
         lax.fori_loop(0, CHUNKS, pass_on, 0)
+
+    if carry_weights:
+        for j in range(PIECES):
+            for row_part in range(2):
+                from_far(j, row_part).start()
 
     def gathered(index, k):
         return full.at[part(index, k)]
@@ -521,9 +517,10 @@
     if carry_weights:
         for k in range(CHUNKS):
             finish(k, 0)
-            spread(k)
-            if k:
-                over_d.relay(k - 1)
+        for j in range(PIECES // 2):
+            spread(j)
+            if j:
+                over_d.relay(j - 1)
     else:
         lax.fori_loop(0, CHUNKS, finish, 0)
     if gather:
@@ -532,6 +529,9 @@
                 from_along(index, k).wait_recv()
                 across(index, k).start()
         if carry_weights:
+            for j in range(PIECES // 2, PIECES):
+                spread(j)
+                over_d.relay(j - 1)
             over_d.relay(PIECES - 1)
         for k in range(CHUNKS):
             keep_own(k).wait()
@@ -914,9 +914,8 @@
 
 def gather_tokens(own, *first):
     places = lax.axis_size("l")
-    parts = [own] + [
-        after(lax.ppermute(own, "l", shift_perm(places, step)), *first) for step in range(1, places)
-    ]
+    moved = [lax.ppermute(own, "l", shift_perm(places, step)) for step in range(1, places)]
+    parts = [own] + [after(part, *first) for part in moved]
     half = jnp.concatenate(parts, axis=0)
     return jnp.concatenate([half, lax.ppermute(half, "c", shift_perm(2, 1))], axis=0)
 
@@ -984,7 +983,7 @@
 
 def scatter_weights(partial):
     core, upper = lax.axis_index("c"), lax.axis_index("h")
-    rows = lax.psum_scatter(partial.astype(jnp.bfloat16), "d", scatter_dimension=0, tiled=True)
+    rows = sum_over_d(partial)
     half = rows.shape[0] // 2
     first, second = rows[:half], rows[half:]
     mine = jnp.where(core == 0, first, second)
@@ -1075,21 +1074,22 @@
     )
     cotangent = after(cotangent, normed_mid)
 
-    gate_near, up_near = split(jnp.dot(normed_mid, mid_near, preferred_element_type=jnp.float32))
+    mid = jnp.dot(normed_mid, mid_near, preferred_element_type=jnp.float32)
+    gate_near, up_near = split(mid)
     hidden_near = swiglu(gate_near, up_near).astype(jnp.bfloat16)
-    gate_far, up_far = split(jnp.dot(normed_mid, mid_far, preferred_element_type=jnp.float32))
+    mid = jnp.dot(normed_mid, mid_far, preferred_element_type=jnp.float32)
+    gate_far, up_far = split(mid)
     hidden_far = swiglu(gate_far, up_far).astype(jnp.bfloat16)
-    branch = contract_cols(hidden_near, down_near) + contract_cols(hidden_far, down_far)
-    grad_rows = gather_tokens(cotangent, branch)
-    down_grads = sum_over_d(
-        jnp.concatenate(
-            [
-                contract_rows(grad_rows, hidden_near).astype(jnp.bfloat16),
-                contract_rows(grad_rows, hidden_far).astype(jnp.bfloat16),
-            ],
-            axis=1,
-        )
-    )
+    grad_rows = gather_tokens(cotangent, hidden_near, hidden_far)
+    down_partial = jnp.concatenate(
+        [
+            contract_rows(grad_rows, hidden_near).astype(jnp.bfloat16),
+            contract_rows(grad_rows, hidden_far).astype(jnp.bfloat16),
+        ],
+        axis=1,
+    )
+    down_grads = sum_over_d(down_partial)
+    grad_rows = after(grad_rows, down_partial)
 
     def hidden_pull(gate, up, down):
         hidden_grad = jnp.dot(grad_rows, down, preferred_element_type=jnp.float32)
@@ -1130,9 +1130,6 @@
         kv_heads,
     )
     qkv_back = jnp.concatenate([query_back, key_back, value_back], axis=1)
-    mid_sum_far = after(mid_sum_far, query_back)
-    branch = scatter_tokens(branch, query_back)
-    activations = trade((middle + branch).astype(jnp.bfloat16))
     qkv_grad = contract_rows(normed, qkv_back).astype(jnp.bfloat16)
     attn_grad = scatter_weights(
         after(jnp.concatenate([qkv_grad, o_wgrad.astype(jnp.bfloat16)], axis=1), mid_sum_far)
@@ -1147,6 +1144,12 @@
     )
     moved = trade(moved)
     gradient = jnp.where(core == lax.axis_index("h"), gradient, moved.astype(jnp.float32))
+
+    hidden_near = after(hidden_near, attn_gain_grad)
+    branch = scatter_tokens(
+        contract_cols(hidden_near, down_near) + contract_cols(hidden_far, down_far)
+    )
+    activations = trade((middle + branch).astype(jnp.bfloat16))
 
     split_at = down_rows.shape[1]
     down_grad = columns_of(*return_halves(down_grads[:, :split_at], down_grads[:, split_at:]))

time: 883 us -> 909 us (1.029)
  waiting for transfers between devices: 152 us -> 165 us
  local copies, waits for them, and re-layouts: 38.3 us -> 50.5 us
  matrix products: 168 us -> 156 us
  blocking collectives: 48.1 us -> 57.4 us
    unnamed x124 -> x150, local copies, waits for them, and re-layouts: 20.1 us -> 33.3 us
    ppermute x1, waiting for transfers between devices: 0.01 us -> 12.6 us  [gather_tokens(): lax.ppermute(own, 'l', shift_perm(places, step))]
    ppermute x3, starting transfers between devices: 6.16 us -> 18.6 us  [core_halves(): lax.ppermute(jnp.where(core == 0, second, first), 'c', shift_perm(2, 1))]
    all_gather x1, waiting for transfers between devices: 0.01 us -> 11.7 us  [per_device(): down_near = lax.all_gather(down_rows, 'd', axis=0, tiled=True)]
    all_gather x1, waiting for transfers between devices: 9.53 us -> 0.01 us  [per_device(): lax.all_gather(after(down_far, attended), 'd', axis=0, tiled=True)]
    psum x1, blocking collectives: 48.1 us -> 57.4 us  [per_device(): lax.psum(jnp.concatenate([attn_gain_grad[0], mlp_gain_grad[0], q_gain_gra...]
  transfers between devices with their start and end apart: 25 -> 25, of which waited for: 6 -> 9; matrix products, arithmetic and copies ran while one was open for 25% -> 26% of each run, Pallas kernels for 31% -> 30%
where the time goes in v5:
time: 909 us; the launch traced here: 901 us
  Pallas kernels  351 us (39%)
  waiting for transfers between devices  165 us (18%)
  matrix products  156 us (17%)
  blocking collectives  57.4 us (6%)
  other arithmetic  53.6 us (6%)
  starting transfers between devices  51.8 us (6%)
  local copies, waits for them, and re-layouts  50.5 us (6%)
  between operations  15.4 us (2%)
    pallas_call x3, Pallas kernels, exchange(): pl.pallas_call(functools.partial(exchange_kernel, nd, tl, epilogue, len(a...  217 us
    ppermute x2, waiting for transfers between devices, return_halves(): far = lax.ppermute(far, 'h', shift_perm(2, 1))  101 us
    pallas_call x1, Pallas kernels, enter(): pl.pallas_call(functools.partial(entry_kernel, nd, tl), name='entry', out...  78.7 us
    psum x1, blocking collectives, per_device(): lax.psum(jnp.concatenate([attn_gain_grad[0], mlp_gain_grad[0], q_gain_gra...  57.4 us
    dot_general x6, matrix products, contract_cols(): lax.dot_general(left, right, (((1,), (1,)), ((), ())), preferred_element_...  50.7 us
    dot_general x6, matrix products, contract_rows(): lax.dot_general(left, right, (((0,), (0,)), ((), ())), preferred_element_...  44.8 us
    pallas_call x1, Pallas kernels, attention_pull(): pl.pallas_call(functools.partial(attention_pull_kernel, blocks, repeat),...  34.8 us
    unnamed x150, local copies, waits for them, and re-layouts  33.3 us
  transfers between devices with their start and end apart: 25, of which 9 were waited for; matrix products, arithmetic and copies ran while one was open for 26% of the time, Pallas kernels for 30%

profile of v5, /device:TPU:0, one launch (start us, length us, event | category | flops | bytes accessed | tf_op | source)
XLA Modules:
  0.0 900.6 jit_solution(14781827625990762713)
XLA Ops:
  13.2 78.7 %entry.1 = (bf16[2048,1024]{1,0:T(8,128)(2,1)}, bf16[2048,512]{1,0:T(8,128)(2,1)}, bf16[1152,2048]{1,0:T(8,128)(2,1)}, f32[8,8,128]{2,1,0:T(8,128)}) custom-call(bf16[256,512]{1,0:T(8,128)(2,1)} %bitcast.126, bf16[256,256]{1,0:T(8,128)(2,1)} %bitcast.128, bf16[256,256]{1,0:T(8,128)(2,1)} %bitcast.129, bf16[256,512]{1,0:T(8,128)(2,1)} %bitcast.127, ...), custom_call_target="tpu_custom_call" | custom-call | bytes 250000000 | tf_op jit(solution)/shard_map/entry/pallas_call | solution.py:328
  93.7 17.9 %collective-permute-start.6 = (bf16[256,768]{0,1:T(8,128)(2,1)}, bf16[256,768]{0,1:T(8,128)(2,1)}, u32[]{:S(2)}, u32[]{:S(2)}) collective-permute-start(bf16[256,768]{0,1:T(8,128)(2,1)} %get-tuple-element.143), channel_id=1, source_target_pairs={{4,0},{0,4},{5,1},{1,5},{6,2},{2,6},{7,3},{3,7},{12,8},{8,12},{13,... | collective-permute-start | bytes 1179656 | tf_op jit(solution)/shard_map/ppermute | solution.py:947
  113.2 2.1 fusion.16
  115.8 1.8 slice.132.refs_1_
  118.5 10.4 %collective-permute-start.3 = (bf16[288,2048]{1,0:T(8,128)(2,1)}, bf16[288,2048]{1,0:T(8,128)(2,1)}, u32[]{:S(2)}, u32[]{:S(2)}) collective-permute-start(bf16[288,2048]{1,0:T(8,128)(2,1)} %param.27), channel_id=1, source_target_pairs={{0,0},{2,4},{4,2},{6,6},{1,1},{3,5},{5,3},{7,7},{8,8},{10,12},{12,... | collective-permute-start | bytes 3538952 | tf_op jit(solution)/shard_map/ppermute | solution.py:912
  128.8 2.1 maximum_select_fusion.2
  131.0 2.3 copy.72
  133.3 3.5 fusion
  136.9 9.4 %fusion.14.refs_0_.refs_1_.refs_2_ = f32[1152,1024]{1,0:T(8,128)} fusion(bf16[2048,1024]{1,0:T(8,128)(2,1)S(1)} %copy-done.51, bf16[1152,2048]{1,0:T(8,128)(2,1)} %get-tuple-element.51, f32[2048]{0:T(1024)S(1)} %bitcast.133, f32[1152]{0:T(1024)S(1)} %add_rsqrt_fusion), kind=kOutput, calls=%fused_computation.54 | convolution fusion | flops 4841275392 | bytes 13644288 | tf_op jit(solution)/shard_map/dot_general | solution.py:1055
  146.3 20.2 %attention.1 = (bf16[1152,512]{1,0:T(8,128)(2,1)}, bf16[1152,256]{1,0:T(8,128)(2,1)S(1)}, bf16[1152,256]{1,0:T(8,128)(2,1)S(1)}, bf16[1152,512]{1,0:T(8,128)(2,1)}, f32[1152,256]{1,0:T(8,128)}) custom-call(s32[4]{0:T(128)S(1)} %get-tuple-element.127.order_ref, f32[1152,1024]{1,0:T(8,128)} %fusion.14.refs_0_.refs_1_.refs_2_, ...), custom_call_target="tpu_custom_call" | custom-call | flops 2717908992 | bytes 60000000 | tf_op jit(solution)/shard_map/attention/pallas_call | solution.py:762
  168.2 4.3 convolution_convert_fusion.3.refs_0_
  172.5 127.8 %shard_map.237 = (f32[288,2048]{1,0:T(8,128)S(1)}, bf16[1152,2048]{1,0:T(8,128)(2,1)S(1)}, bf16[2048,1536]{1,0:T(8,128)(2,1)}) custom-call(bf16[1152,2048]{1,0:T(8,128)(2,1)S(1)} %convolution_convert_fusion.3.refs_0_, bf16[288,2048]{1,0:T(8,128)(2,1)S(1)} %slice.132.refs_1_, f32[1,2048]{1,0:T(1,128)S(1)} %bitcast.108, bf16[512,1536]{1,0:T(8,128)(2,1)S(1)} %copy-done), custom_call_target="tpu_custom_call" | custom-call | bytes 200000000 | tf_op jit(solution)/shard_map/pallas_call | solution.py:599
  300.4 12.0 %fusion.34 = f32[1152,1536]{1,0:T(8,128)S(1)} fusion(bf16[1152,2048]{1,0:T(8,128)(2,1)S(1)} %get-tuple-element.57, bf16[2048,1536]{1,0:T(8,128)(2,1)} %get-tuple-element.65), kind=kOutput, calls=%fused_computation.129 | convolution fusion | flops 7247757312 | bytes 18087936 | tf_op jit(solution)/shard_map/dot_general | solution.py:1080
  312.4 2.8 multiply_convert_fusion.2
  316.0 11.5 %fusion.33 = f32[1152,1536]{1,0:T(8,128)S(1)} fusion(bf16[1152,2048]{1,0:T(8,128)(2,1)} %copy-done.14, bf16[2048,1536]{1,0:T(8,128)(2,1)} %all-gather.4.cloned.1.call-done), kind=kOutput, calls=%fused_computation.128 | convolution fusion | flops 7247757312 | bytes 18087936 | tf_op jit(solution)/shard_map/dot_general | solution.py:1077
  327.5 2.9 multiply_convert_fusion.3
  331.0 12.6 %collective-permute-done.4 = bf16[288,2048]{1,0:T(8,128)(2,1)S(1)} collective-permute-done((bf16[288,2048]{1,0:T(8,128)(2,1)}, bf16[288,2048]{1,0:T(8,128)(2,1)S(1)}, u32[]{:S(2)}, u32[]{:S(2)}) %collective-permute-start.4) | collective-permute-done | bytes 1179680 | tf_op jit(solution)/shard_map/ppermute | solution.py:917
  343.5 2.9 pad_maximum_fusion.4
  348.0 3.3 collective-permute-done.5
  351.3 1.9 constant_dynamic-update-slice_fusion
  353.3 4.7 convolution_convert_fusion.6
  357.9 4.7 convolution_convert_fusion.5
  362.6 3.8 pad_maximum_fusion
  366.4 10.8 %fusion.8 = (bf16[1152,768]{1,0:T(8,128)(2,1)S(1)}, bf16[1152,768]{1,0:T(8,128)(2,1)S(1)}) fusion(f32[1152,1536]{1,0:T(8,128)} %copy-done.24, bf16[1152,2048]{1,0:T(8,128)(2,1)} %copy-done.39, bf16[2048,768]{1,0:T(8,128)(2,1)} %all-gather.8.cloned.1.call-done), kind=kOutput, calls=%fused_computation.24 | convolution fusion | flops 3636264960 | bytes 18481152 | tf_op jit(solution)/shard_map/dot_general | solution.py:1095
  379.0 12.7 %convolution_convert_fusion.2 = bf16[2048,1536]{0,1:T(8,128)(2,1)} fusion(bf16[1152,2048]{1,0:T(8,128)(2,1)} %copy-done.14, bf16[1152,768]{1,0:T(8,128)(2,1)S(1)} %get-tuple-element.129, bf16[1152,768]{1,0:T(8,128)(2,1)S(1)} %get-tuple-element.128), kind=kOutput, calls=%fused_computation.10 | convolution fusion | flops 7257980928 | bytes 14548992 | tf_op jit(solution)/shard_map/dot_general | solution.py:47
  392.5 11.7 %all-gather.6.cloned.1.call-done = bf16[2048,768]{1,0:T(8,128)(2,1)} async-done(((bf16[512,768]{1,0:T(8,128)(2,1)}), bf16[2048,768]{1,0:T(8,128)(2,1)}) %all-gather.6.cloned.1.call-update) | async-done | bytes 3145744 | tf_op jit(solution)/shard_map/all_gather | solution.py:1023
  404.2 10.2 %fusion.5 = (bf16[1152,768]{1,0:T(8,128)(2,1)S(1)}, bf16[1152,768]{1,0:T(8,128)(2,1)S(1)}) fusion(f32[1152,1536]{1,0:T(8,128)} %copy-done.23, bf16[1152,2048]{1,0:T(8,128)(2,1)} %copy-done.39, bf16[2048,768]{1,0:T(8,128)(2,1)} %all-gather.6.cloned.1.call-done), kind=kOutput, calls=%fused_computation.21 | convolution fusion | flops 3636264960 | bytes 18481152 | tf_op jit(solution)/shard_map/dot_general | solution.py:1095
  415.6 12.0 %fusion.29 = f32[1152,2048]{1,0:T(8,128)} fusion(bf16[2048,1536]{1,0:T(8,128)(2,1)} %all-gather.4.cloned.1.call-done, bf16[1152,768]{1,0:T(8,128)(2,1)S(1)} %get-tuple-element.131, bf16[1152,768]{1,0:T(8,128)(2,1)S(1)} %get-tuple-element.130), kind=kOutput, calls=%fused_computation.124 | convolution fusion | flops 7254835200 | bytes 19267584 | tf_op jit(solution)/shard_map/dot_general | solution.py:53
  427.5 13.6 %add_convert_fusion.refs_0_ = bf16[1152,2048]{1,0:T(8,128)(2,1)} fusion(f32[1152,2048]{1,0:T(8,128)} %fusion.29, bf16[2048,1536]{1,0:T(8,128)(2,1)} %get-tuple-element.65, bf16[1152,768]{1,0:T(8,128)(2,1)} %copy-done.60, bf16[1152,768]{1,0:T(8,128)(2,1)S(1)} %copy-done.59), kind=kOutput, calls=%fused_computation.6 | convolution fusion | flops 7259553792 | bytes 23986176 | tf_op jit(solution)/shard_map/dot_general | solution.py:53
  441.2 58.6 %shard_map.238 = (f32[288,2048]{1,0:T(8,128)S(1)}, f32[1,2048]{1,0:T(1,128)S(1)}, bf16[1152,2048]{1,0:T(8,128)(2,1)S(1)}) custom-call(bf16[1152,2048]{1,0:T(8,128)(2,1)} %add_convert_fusion.refs_0_, f32[288,2048]{1,0:T(8,128)S(1)} %copy-done.2, bf16[288,2048]{1,0:T(8,128)(2,1)} %collective-permute-done.3.refs_2_, f32[1,2048]{1,0:T(1,128)S(1)} %bitcast.109), custom_call_target="tpu_custom_call" | custom-call | bytes 200000000 | tf_op jit(solution)/shard_map/pallas_call | solution.py:599
  501.3 1.5 copy-done.15
  502.7 10.6 %convolution_convert_fusion.1 = bf16[2048,1536]{0,1:T(8,128)(2,1)} fusion(bf16[1152,2048]{1,0:T(8,128)(2,1)S(1)} %bitcast.114, bf16[1152,1536]{1,0:T(8,128)(2,1)S(1)} %pad_maximum_fusion.2), kind=kOutput, calls=%fused_computation.9 | convolution fusion | flops 7250903040 | bytes 14548992 | tf_op jit(solution)/shard_map/dot_general | solution.py:47
  513.4 1.5 copy-done.55
  515.0 6.2 convolution_convert_fusion.8.refs_11_
  521.2 34.8 %attention_pull.1 = (bf16[1152,512]{1,0:T(8,128)(2,1)}, bf16[1152,256]{1,0:T(8,128)(2,1)}, bf16[1152,256]{1,0:T(8,128)(2,1)}, f32[8,128]{1,0:T(8,128)}, f32[8,128]{1,0:T(8,128)}) custom-call(s32[4]{0:T(128)} %copy-done.13, f32[1152,1024]{1,0:T(8,128)} %fusion.14.refs_0_.refs_1_.refs_2_, f32[1152,1024]{1,0:T(8,128)} %fusion.14.refs_0_.refs_1_.refs_2_, ...), custom_call_target="tpu_custom_call" | custom-call | flops 6794772480 | bytes 120000000 | tf_op jit(solution)/shard_map/attention_pull/pallas_call | solution.py:868
  555.9 1.6 constant_dynamic-update-slice_fusion.5
  558.8 3.2 convolution_convert_fusion.7
  562.0 9.1 %convolution_convert_fusion.4 = bf16[2048,1024]{0,1:T(8,128)(2,1)S(1)} fusion(bf16[1152,1024]{1,0:T(8,128)(2,1)S(1)} %constant_dynamic-update-slice_fusion.3, bf16[1152,2048]{1,0:T(8,128)(2,1)} %get-tuple-element.51, f32[2048]{0:T(1024)S(1)} %bitcast.134, f32[1152]{0:T(1024)S(1)} %copy-done.45), kind=kOutput, calls=%fused_computation.18 | convolution fusion | flops 4843372544 | bytes 11284992 | tf_op jit(solution)/shard_map/dot_general | solution.py:47
  571.1 3.7 pad_maximum_fusion.1
  576.8 7.6 convolution_convert_fusion.refs_0_
  584.5 30.9 %shard_map.239 = (f32[288,2048]{1,0:T(8,128)S(1)}, bf16[288,2048]{1,0:T(8,128)(2,1)S(1)}, f32[1,2048]{1,0:T(1,128)S(1)}) custom-call(bf16[1152,2048]{1,0:T(8,128)(2,1)S(1)} %convolution_convert_fusion.refs_0_, bf16[288,2048]{1,0:T(8,128)(2,1)S(1)} %slice.132.refs_1_, f32[288,2048]{1,0:T(8,128)S(1)} %copy-done.8, f32[1,2048]{1,0:T(1,128)S(1)} %bitcast.110), custom_call_target="tpu_custom_call" | custom-call | bytes 110000000 | tf_op jit(solution)/shard_map/pallas_call | solution.py:599
  615.5 6.5 fusion.35
  622.0 6.8 convolution_add_fusion
  629.3 4.5 collective-permute-done.8
  634.8 2.2 copy-done.20
  639.6 1.7 collective-permute-start.11
  643.2 57.4 %psum.7 = f32[4352]{0:T(1024)} all-reduce(f32[4352]{0:T(1024)} %pad_maximum_fusion.10), channel_id=1, replica_groups=mesh['d'=4,'c'=2,'h'=2,'l'=2] {'d','c','h','l'}, use_global_device_ids=true, to_apply=%region_3.4 | all-reduce | flops 4352 | bytes 34816 | tf_op jit(solution)/shard_map/psum | solution.py:1160
  703.8 1.7 collective-permute-start.16
  708.1 2.6 fusion.12
  713.4 73.7 %collective-permute-done.16 = bf16[512,768]{0,1:T(8,128)(2,1)S(1)} collective-permute-done((bf16[512,768]{0,1:T(8,128)(2,1)S(1)}, bf16[512,768]{0,1:T(8,128)(2,1)S(1)}, u32[]{:S(2)}, u32[]{:S(2)}) %collective-permute-start.16) | collective-permute-done | bytes 786464 | tf_op jit(solution)/shard_map/ppermute | solution.py:954
  787.5 3.0 convert_select_fusion
  792.8 27.8 %collective-permute-done.14 = bf16[512,1536]{0,1:T(8,128)(2,1)} collective-permute-done((bf16[512,1536]{0,1:T(8,128)(2,1)}, bf16[512,1536]{0,1:T(8,128)(2,1)}, u32[]{:S(2)}, u32[]{:S(2)}) %collective-permute-start.14) | collective-permute-done | bytes 1572896 | tf_op jit(solution)/shard_map/ppermute | solution.py:954
  820.6 2.3 convert_add_fusion
  823.9 14.7 %collective-permute-start.15 = (bf16[256,1536]{0,1:T(8,128)(2,1)}, bf16[256,1536]{0,1:T(8,128)(2,1)}, u32[]{:S(2)}, u32[]{:S(2)}) collective-permute-start(bf16[256,1536]{0,1:T(8,128)(2,1)} %select_convert_fusion), channel_id=1, source_target_pairs={{4,0},{0,4},{5,1},{1,5},{6,2},{2,6},{7,3},{3,7},{12,8},{8,12},{13,... | collective-permute-start | bytes 2359304 | tf_op jit(solution)/shard_map/ppermute | solution.py:960
  838.6 2.3 broadcast_select_fusion
  840.9 2.6 maximum_bitcast_fusion.2
  843.5 3.0 copy.86
  848.2 2.2 broadcast_select_fusion.2
  850.4 1.5 slice_select_fusion.3
  852.0 1.6 copy.85
  853.6 1.6 maximum_bitcast_fusion
  855.2 1.6 copy.84
  856.8 30.5 %collective-permute-done.13 = bf16[256,1536]{0,1:T(8,128)(2,1)} collective-permute-done((bf16[256,1536]{0,1:T(8,128)(2,1)}, bf16[256,1536]{0,1:T(8,128)(2,1)}, u32[]{:S(2)}, u32[]{:S(2)}) %collective-permute-start.13) | collective-permute-done | bytes 786464 | tf_op jit(solution)/shard_map/ppermute | solution.py:992
  887.3 1.5 convert_add_fusion.2
  (244 shorter events, 48.5 us)
Async XLA Ops:
  7.2 308.7 %all-gather.4.cloned.1.call-start = ((), (), s32[]{:S(2)}) async-start(), calls=%async_computation.4 | async-start | bytes 7864320 | tf_op jit(solution)/shard_map/all_gather | solution.py:1043
  8.8 1.9 collective-permute-start
  9.7 1.8 collective-permute-start.1
  11.9 80.1 %copy-start.57 = (s32[1,1152]{1,0:T(1,128)S(1)}, s32[1,1152]{1,0:T(1,128)}, u32[]{:S(2)}) copy-start(s32[1,1152]{1,0:T(1,128)} %param.15) | copy-start | bytes 13828
  11.9 80.7 %copy-start.35 = (bf16[1,256,1536]{2,1,0:T(8,128)(2,1)S(1)}, bf16[1,256,1536]{2,1,0:T(8,128)(2,1)}, u32[]{:S(2)}) copy-start(bf16[1,256,1536]{2,1,0:T(8,128)(2,1)} %param.26) | copy-start | bytes 2359300
  91.9 274.5 %all-gather.8.cloned.1.call-start = ((), (), s32[]{:S(2)}) async-start(), calls=%async_computation.6 | async-start | bytes 3932160 | tf_op jit(solution)/shard_map/all_gather | solution.py:1060
  92.0 20.0 %collective-permute-start.2 = (s32[1,1152]{1,0:T(1,128)S(1)}, s32[1,1152]{1,0:T(1,128)S(1)}, u32[]{:S(2)}, u32[]{:S(2)}) collective-permute-start(s32[1,1152]{1,0:T(1,128)S(1)} %copy-done.57), channel_id=1, source_target_pairs={{0,0},{2,4},{4,2},{6,6},{1,1},{3,5},{5,3},{7,7},{8,8},{10,12},{12,... | collective-permute-start | bytes 13832 | tf_op jit(solution)/shard_map/ppermute | solution.py:912
  93.7 35.1 %collective-permute-start.6 = (bf16[256,768]{0,1:T(8,128)(2,1)}, bf16[256,768]{0,1:T(8,128)(2,1)}, u32[]{:S(2)}, u32[]{:S(2)}) collective-permute-start(bf16[256,768]{0,1:T(8,128)(2,1)} %get-tuple-element.143), channel_id=1, source_target_pairs={{4,0},{0,4},{5,1},{1,5},{6,2},{2,6},{7,3},{3,7},{12,8},{8,12},{13,... | collective-permute-start | bytes 1179656 | tf_op jit(solution)/shard_map/ppermute | solution.py:947
  111.8 34.4 %copy-start.13 = (s32[4]{0:T(128)}, s32[4]{0:T(128)S(1)}, u32[]{:S(2)}) copy-start(s32[4]{0:T(128)S(1)} %get-tuple-element.127.order_ref) | copy-start | bytes 52
  113.2 33.1 %copy-start.4 = (s32[1152,1]{1,0:T(8,128)}, s32[1152,1]{1,0:T(8,128)S(1)}, u32[]{:S(2)}) copy-start(s32[1152,1]{1,0:T(8,128)S(1)} %reduce_sum.33.refs_7_.refs_6_) | copy-start | bytes 13828
  113.2 4.4 copy-start.41
  115.7 30.5 %copy-start.9 = (f32[1152,128]{1,0:T(8,128)}, f32[1152,128]{1,0:T(8,128)S(1)}, u32[]{:S(2)}) copy-start(f32[1152,128]{1,0:T(8,128)S(1)} %get-tuple-element.160.refs_3_.refs_2_) | copy-start | bytes 1769476
  115.7 30.5 %copy-start.10 = (f32[1152,128]{1,0:T(8,128)}, f32[1152,128]{1,0:T(8,128)S(1)}, u32[]{:S(2)}) copy-start(f32[1152,128]{1,0:T(8,128)S(1)} %get-tuple-element.161.refs_4_.refs_3_) | copy-start | bytes 1769476
  118.2 18.6 %copy-start.42 = (f32[1,2,8,128]{3,1,2,0:T(2,128)}, f32[1,2,8,128]{3,1,2,0:T(2,128)S(1)}, u32[]{:S(2)}) copy-start(f32[1,2,8,128]{3,1,2,0:T(2,128)S(1)} %copy.92) | copy-start | bytes 24580
  118.4 27.9 %copy-start.11 = (f32[1,128]{1,0:T(1,128)}, f32[1,128]{1,0:T(1,128)S(1)}, u32[]{:S(2)}) copy-start(f32[1,128]{1,0:T(1,128)S(1)} %reshape_reshape.11.refs_5_.refs_4_) | copy-start | bytes 1540
  118.5 27.8 %copy-start.12 = (f32[1,128]{1,0:T(1,128)}, f32[1,128]{1,0:T(1,128)S(1)}, u32[]{:S(2)}) copy-start(f32[1,128]{1,0:T(1,128)S(1)} %reshape_reshape.12.refs_6_.refs_5_) | copy-start | bytes 1540
  118.5 197.4 %collective-permute-start.3 = (bf16[288,2048]{1,0:T(8,128)(2,1)}, bf16[288,2048]{1,0:T(8,128)(2,1)}, u32[]{:S(2)}, u32[]{:S(2)}) collective-permute-start(bf16[288,2048]{1,0:T(8,128)(2,1)} %param.27), channel_id=1, source_target_pairs={{0,0},{2,4},{4,2},{6,6},{1,1},{3,5},{5,3},{7,7},{8,8},{10,12},{12,... | collective-permute-start | bytes 3538952 | tf_op jit(solution)/shard_map/ppermute | solution.py:912
  133.3 182.5 %collective-permute-start.7 = (bf16[512,768]{1,0:T(8,128)(2,1)}, bf16[512,768]{1,0:T(8,128)(2,1)}, u32[]{:S(2)}, u32[]{:S(2)}) collective-permute-start(bf16[512,768]{1,0:T(8,128)(2,1)} %bitcast.117), channel_id=1, source_target_pairs={{2,0},{0,2},{3,1},{1,3},{6,4},{4,6},{7,5},{5,7},{10,8},{8,10},{11,... | collective-permute-start | bytes 2359304 | tf_op jit(solution)/shard_map/ppermute | solution.py:1044
  136.8 9.5 %copy-start.44 = (f32[1152]{0:T(1024)}, f32[1152]{0:T(1024)S(1)}, u32[]{:S(2)}) copy-start(f32[1152]{0:T(1024)S(1)} %add_rsqrt_fusion) | copy-start | bytes 13828
  146.3 21.9 %copy-start.54 = (bf16[2048,512]{1,0:T(8,128)(2,1)S(1)}, bf16[2048,512]{1,0:T(8,128)(2,1)}, u32[]{:S(2)}) copy-start(bf16[2048,512]{1,0:T(8,128)(2,1)} %get-tuple-element.55) | copy-start | bytes 6291460
  168.2 4.3 copy-start
  300.3 12.1 %copy-start.1 = (f32[288,2048]{1,0:T(8,128)}, f32[288,2048]{1,0:T(8,128)S(1)}, u32[]{:S(2)}) copy-start(f32[288,2048]{1,0:T(8,128)S(1)} %get-tuple-element.56.refs_1_) | copy-start | bytes 7077892
  300.3 12.1 %copy-start.14 = (bf16[1152,2048]{1,0:T(8,128)(2,1)}, bf16[1152,2048]{1,0:T(8,128)(2,1)S(1)}, u32[]{:S(2)}) copy-start(bf16[1152,2048]{1,0:T(8,128)(2,1)S(1)} %get-tuple-element.57) | copy-start | bytes 14155780
  315.8 88.4 %all-gather.6.cloned.1.call-start = ((), (), s32[]{:S(2)}) async-start(), calls=%async_computation.5 | async-start | bytes 3932160 | tf_op jit(solution)/shard_map/all_gather | solution.py:1023
  315.9 27.6 %collective-permute-start.4 = (bf16[288,2048]{1,0:T(8,128)(2,1)}, bf16[288,2048]{1,0:T(8,128)(2,1)S(1)}, u32[]{:S(2)}, u32[]{:S(2)}) collective-permute-start(bf16[288,2048]{1,0:T(8,128)(2,1)} %collective-permute-done.3.refs_2_), channel_id=1, source_target_pairs={{1,0},{0,1},{3,2},{2,3},{5,4},{4,5},{7,6},{6,7},{9,8},{8,9},{11,10... | collective-permute-start | bytes 3538952 | tf_op jit(solution)/shard_map/ppermute | solution.py:917
  346.4 4.9 collective-permute-start.5
  346.4 228.4 %reduce-scatter.5.cloned.1.call-start = ((), (), s32[]{:S(2)}) async-start(), calls=%async_computation.7 | async-start | bytes 7864320 | tf_op jit(solution)/shard_map/reduce_scatter | solution.py:972
  347.9 5.3 copy-start.29
  353.2 4.7 copy-start.39
  353.2 4.7 copy-start.27
  391.7 310.9 %reduce-scatter.11.cloned.1.call-start = ((), (), s32[]{:S(2)}) async-start(), calls=%async_computation.10 | async-start | bytes 7864320 | tf_op jit(solution)/shard_map/reduce_scatter | solution.py:972
  392.3 400.5 %reduce-scatter.9.cloned.1.call-start = ((), (), s32[]{:S(2)}) async-start(), calls=%async_computation.9 | async-start | bytes 7864320 | tf_op jit(solution)/shard_map/reduce_scatter | solution.py:972
  415.6 12.0 %copy-start.59 = (bf16[1152,768]{1,0:T(8,128)(2,1)S(1)}, bf16[1152,768]{1,0:T(8,128)(2,1)}, u32[]{:S(2)}) copy-start(bf16[1152,768]{1,0:T(8,128)(2,1)} %copy-done.58) | copy-start | bytes 5308420
  415.6 87.2 %slice-start = ((s8[4718592]{0:T(1024)(128)(4,1)}), s8[4194304]{0:T(1024)(128)(4,1)S(1)}, s32[]{:S(2)}) async-start(s8[4718592]{0:T(1024)(128)(4,1)} %bitcast.113), calls=%async_computation.11 | async-start | bytes 8388608
  427.5 13.6 %copy-start.2 = (f32[288,2048]{1,0:T(8,128)S(1)}, f32[288,2048]{1,0:T(8,128)}, u32[]{:S(2)}) copy-start(f32[288,2048]{1,0:T(8,128)} %copy-done.1) | copy-start | bytes 7077892
  427.5 75.2 %slice-start.1 = ((s8[4718592]{0:T(1024)(128)(4,1)}), s8[524288]{0:T(1024)(128)(4,1)S(1)}, s32[]{:S(2)}) async-start(s8[4718592]{0:T(1024)(128)(4,1)} %bitcast.113), calls=%async_computation.12 | async-start | bytes 1048576
  441.2 58.7 %copy-start.26 = (bf16[1152,768]{1,0:T(8,128)(2,1)S(1)}, bf16[1152,768]{1,0:T(8,128)(2,1)}, u32[]{:S(2)}) copy-start(bf16[1152,768]{1,0:T(8,128)(2,1)} %copy-done.25) | copy-start | bytes 5308420
  513.4 325.2 %reduce-scatter.7.cloned.1.call-start = ((), (), s32[]{:S(2)}) async-start(), calls=%async_computation.8 | async-start | bytes 7864320 | tf_op jit(solution)/shard_map/reduce_scatter | solution.py:972
  515.0 43.8 %slice-start.2 = ((s8[4718592]{0:T(1024)(128)(4,1)}), s8[4194304]{0:T(1024)(128)(4,1)S(1)}, s32[]{:S(2)}) async-start(s8[4718592]{0:T(1024)(128)(4,1)} %bitcast.115), calls=%async_computation.13 | async-start | bytes 8388608
  521.2 37.6 %slice-start.3 = ((s8[4718592]{0:T(1024)(128)(4,1)}), s8[524288]{0:T(1024)(128)(4,1)S(1)}, s32[]{:S(2)}) async-start(s8[4718592]{0:T(1024)(128)(4,1)} %bitcast.115), calls=%async_computation.14 | async-start | bytes 1048576
  576.8 7.6 copy-start.8
  584.5 31.0 %copy-start.30 = (bf16[1152,768]{1,0:T(8,128)(2,1)S(1)}, bf16[1152,768]{1,0:T(8,128)(2,1)}, u32[]{:S(2)}) copy-start(bf16[1152,768]{1,0:T(8,128)(2,1)} %multiply_convert_fusion.3) | copy-start | bytes 5308420
  584.5 31.0 %copy-start.53 = (bf16[2048,768]{1,0:T(8,128)(2,1)S(1)}, bf16[2048,768]{1,0:T(8,128)(2,1)}, u32[]{:S(2)}) copy-start(bf16[2048,768]{1,0:T(8,128)(2,1)} %all-gather.6.cloned.1.call-done) | copy-start | bytes 9437188
  615.4 6.6 copy-start.5
  615.4 6.6 copy-start.16
  615.5 6.6 copy-start.28
  615.5 6.5 copy-start.52
  629.2 10.4 %copy-start.17 = (bf16[288,2048]{1,0:T(8,128)(2,1)S(1)}, bf16[288,2048]{1,0:T(8,128)(2,1)}, u32[]{:S(2)}) copy-start(bf16[288,2048]{1,0:T(8,128)(2,1)} %copy-done.16) | copy-start | bytes 3538948
  629.2 4.6 collective-permute-start.8
  637.1 71.0 %copy-start.3 = (f32[288,2048]{1,0:T(8,128)S(1)}, f32[288,2048]{1,0:T(8,128)}, u32[]{:S(2)}) copy-start(f32[288,2048]{1,0:T(8,128)} %copy-done.1) | copy-start | bytes 7077892
  638.3 68.4 %collective-permute-start.9 = (bf16[288,2048]{1,0:T(8,128)(2,1)}, bf16[288,2048]{1,0:T(8,128)(2,1)}, u32[]{:S(2)}, u32[]{:S(2)}) collective-permute-start(bf16[288,2048]{1,0:T(8,128)(2,1)} %slice.289), channel_id=1, source_target_pairs={{1,0},{0,1},{3,2},{2,3},{5,4},{4,5},{7,6},{6,7},{9,8},{8,9},{11,10... | collective-permute-start | bytes 3538952 | tf_op jit(solution)/shard_map/ppermute | solution.py:932
  639.6 147.9 %collective-permute-start.11 = (bf16[288,2048]{1,0:T(8,128)(2,1)S(1)}, bf16[288,2048]{1,0:T(8,128)(2,1)}, u32[]{:S(2)}, u32[]{:S(2)}) collective-permute-start(bf16[288,2048]{1,0:T(8,128)(2,1)S(1)} %copy-done.17), channel_id=1, source_target_pairs={{0,0},{2,4},{4,2},{6,6},{1,1},{3,5},{5,3},{7,7},{8,8},{10,12},{12,... | collective-permute-start | bytes 3538952 | tf_op jit(solution)/shard_map/ppermute | solution.py:912
  703.8 83.3 %collective-permute-start.16 = (bf16[512,768]{0,1:T(8,128)(2,1)S(1)}, bf16[512,768]{0,1:T(8,128)(2,1)S(1)}, u32[]{:S(2)}, u32[]{:S(2)}) collective-permute-start(bf16[512,768]{0,1:T(8,128)(2,1)S(1)} %slice.203), channel_id=1, source_target_pairs={{2,0},{0,2},{3,1},{1,3},{6,4},{4,6},{7,5},{5,7},{10,8},{8,10},{11,... | collective-permute-start | bytes 2359304 | tf_op jit(solution)/shard_map/ppermute | solution.py:954
  706.6 4.9 copy-start.50
  706.6 80.4 %copy-start.31 = (bf16[512,1536]{0,1:T(8,128)(2,1)S(1)}, bf16[512,1536]{0,1:T(8,128)(2,1)}, u32[]{:S(2)}) copy-start(bf16[512,1536]{0,1:T(8,128)(2,1)} %reduce-scatter.11.cloned.1.call-done) | copy-start | bytes 4718596
  706.7 113.9 %collective-permute-start.14 = (bf16[512,1536]{0,1:T(8,128)(2,1)}, bf16[512,1536]{0,1:T(8,128)(2,1)}, u32[]{:S(2)}, u32[]{:S(2)}) collective-permute-start(bf16[512,1536]{0,1:T(8,128)(2,1)} %reduce-scatter.5.cloned.1.call-done), channel_id=1, source_target_pairs={{2,0},{0,2},{3,1},{1,3},{6,4},{4,6},{7,5},{5,7},{10,8},{8,10},{11,... | collective-permute-start | bytes 4718600 | tf_op jit(solution)/shard_map/ppermute | solution.py:954
  710.6 76.8 %copy-start.6 = (f32[288,2048]{1,0:T(8,128)S(1)}, f32[288,2048]{1,0:T(8,128)}, u32[]{:S(2)}) copy-start(f32[288,2048]{1,0:T(8,128)} %copy-done.5) | copy-start | bytes 7077892
  710.6 79.8 %collective-permute-start.10 = (bf16[288,2048]{1,0:T(8,128)(2,1)S(1)}, bf16[288,2048]{1,0:T(8,128)(2,1)S(1)}, u32[]{:S(2)}, u32[]{:S(2)}) collective-permute-start(bf16[288,2048]{1,0:T(8,128)(2,1)S(1)} %fusion.12), channel_id=1, source_target_pairs={{0,0},{2,4},{4,2},{6,6},{1,1},{3,5},{5,3},{7,7},{8,8},{10,12},{12,... | collective-permute-start | bytes 3538952 | tf_op jit(solution)/shard_map/ppermute | solution.py:912
  787.4 4.1 collective-permute-start.17
  823.9 22.8 %collective-permute-start.15 = (bf16[256,1536]{0,1:T(8,128)(2,1)}, bf16[256,1536]{0,1:T(8,128)(2,1)}, u32[]{:S(2)}, u32[]{:S(2)}) collective-permute-start(bf16[256,1536]{0,1:T(8,128)(2,1)} %select_convert_fusion), channel_id=1, source_target_pairs={{4,0},{0,4},{5,1},{1,5},{6,2},{2,6},{7,3},{3,7},{12,8},{8,12},{13,... | collective-permute-start | bytes 2359304 | tf_op jit(solution)/shard_map/ppermute | solution.py:960
  840.9 7.2 collective-permute-start.12
  850.4 36.9 %collective-permute-start.13 = (bf16[256,1536]{0,1:T(8,128)(2,1)}, bf16[256,1536]{0,1:T(8,128)(2,1)}, u32[]{:S(2)}, u32[]{:S(2)}) collective-permute-start(bf16[256,1536]{0,1:T(8,128)(2,1)} %broadcast_select_fusion.2), channel_id=1, source_target_pairs={{2,0},{0,2},{3,1},{1,3},{6,4},{4,6},{7,5},{5,7},{10,8},{8,10},{11,... | collective-permute-start | bytes 2359304 | tf_op jit(solution)/shard_map/ppermute | solution.py:992
  853.6 33.7 %copy-start.22 = (bf16[512,1536]{0,1:T(8,128)(2,1)S(1)}, bf16[512,1536]{0,1:T(8,128)(2,1)}, u32[]{:S(2)}) copy-start(bf16[512,1536]{0,1:T(8,128)(2,1)} %reduce-scatter.7.cloned.1.call-done) | copy-start | bytes 4718596
  888.8 3.8 copy-start.33
  (26 other events, 57.9 us)
Sparse Core Ops, SparseCore 0:
  92.0 84.0 all-gather.3
  315.9 42.4 all-gather.7
  360.3 43.8 all-gather.5
  407.0 70.0 reduce-scatter.4
  479.9 70.0 reduce-scatter.10
  552.8 70.0 reduce-scatter.8
  625.8 70.7 reduce-scatter.6

commit v6 on v5

--- a/solution.py
+++ b/solution.py
@@ -72,6 +72,16 @@
 
 def rows_at(index, size):
     return pl.ds(pl.multiple_of(index * size, size), size)
+
+
+WEIGHTS = 5
+ENTRY_START = (
+    "w0", "t0", "w1", "w2", "t1", "w3", "w4", "t2",
+)
+ENTRY_ORDER = (
+    "s0", "t0", "s1", "r0", "s2", "r1", "t1", "s3", "r2", "s4", "r3", "t2", "r4", "a0", "a1",
+    "a2",
+)
 
 
 def hop_plan(nd, d):
@@ -146,20 +156,23 @@
     own = tok_ref.shape[0]
     chunk = own // CHUNKS
     q_cols, kv_cols = q_ref.shape[1], k_ref.shape[1]
+    o_half = o_ref.shape[1] // 2
+    qkv_cols = q_cols + 2 * kv_cols
     weights = (
-        (q_ref, qkv_full, 0, 0),
-        (k_ref, qkv_full, q_cols, q_cols),
-        (v_ref, qkv_full, q_cols + kv_cols, q_cols + kv_cols),
-        (o_ref, o_full, 0, q_cols + 2 * kv_cols),
+        (q_ref, qkv_full, 0, q_cols, 0),
+        (k_ref, qkv_full, q_cols, kv_cols, q_cols),
+        (v_ref, qkv_full, q_cols + kv_cols, kv_cols, q_cols + kv_cols),
+        (o_ref.at[:, pl.ds(0, o_half)], o_full, 0, o_half, qkv_cols),
+        (o_ref.at[:, pl.ds(o_half, o_half)], o_full, o_half, o_half, qkv_cols + o_half),
     )
 
     def block(j, row):
-        source, full, start, _ = weights[j]
-        return full.at[rows_at(row, rows), pl.ds(start, source.shape[1])]
+        _, full, start, cols, _ = weights[j]
+        return full.at[rows_at(row, rows), pl.ds(start, cols)]
 
     def held(j):
-        source, _, _, start = weights[j]
-        return stage.at[:, pl.ds(start, source.shape[1])]
+        _, _, _, cols, start = weights[j]
+        return stage.at[:, pl.ds(start, cols)]
 
     def from_far(j, part):
         return remote(block(j, d * 2 + part), block(j, d * 2 + part), zs.at[j], zr.at[j, part], h=1 - h)
@@ -225,28 +238,31 @@
 
     local_gains().start()
 
-    @pl.when(apart)
-    def _():
-        for k in range(CHUNKS):
-            trade_tokens(k).start()
-
-    for j in range(4):
+    def start_weights(j):
         to_far(j).start()
 
         @pl.when(apart)
         def _():
             to_core(j).start()
 
+    def start_tokens(k):
+        @pl.when(apart)
+        def _():
+            trade_tokens(k).start()
+
+    for step in ENTRY_START:
+        {"w": start_weights, "t": start_tokens}[step[0]](int(step[1:]))
+
     @pl.when(same)
     def _():
         pltpu.make_async_copy(tok_ref, tok_stage, tli).start()
-        for j in range(4):
+        for j in range(WEIGHTS):
             local_in(j).start()
         pltpu.make_async_copy(tok_ref, tok_stage, tli).wait()
         for k in range(CHUNKS):
             part = pl.ds(k * chunk, chunk)
             pltpu.make_async_copy(tok_stage.at[part], tokens_at(0, k), tlo.at[k]).start()
-        for j in range(4):
+        for j in range(WEIGHTS):
             local_in(j).wait()
             local_out(j).start()
 
@@ -270,8 +286,8 @@
             over_d.send(j, part)
 
     relay = over_d.relay
-    for k in range(CHUNKS):
-
+
+    def own_tokens(k):
         @pl.when(same)
         def _():
             part = pl.ds(k * chunk, chunk)
@@ -284,20 +300,17 @@
         for step in range(1, tl):
             along(step, k).start()
         across(0, k).start()
-    spread(0)
-    spread(1)
-    relay(0)
-    spread(2)
-    relay(1)
-    for k in range(CHUNKS):
+
+    def pass_across(k):
         for index in range(1, tl):
             from_along(index, k).wait_recv()
             across(index, k).start()
-    relay(2)
-    spread(3)
-    relay(3)
-
-    for j in range(4):
+
+    steps = {"t": own_tokens, "s": spread, "r": relay, "a": pass_across}
+    for step in ENTRY_ORDER:
+        steps[step[0]](int(step[1:]))
+
+    for j in range(WEIGHTS):
         over_d.finish(j)
         to_far(j).wait_send()
     for k in range(CHUNKS):
@@ -312,7 +325,7 @@
 
     @pl.when(apart)
     def _():
-        for j in range(4):
+        for j in range(WEIGHTS):
             to_core(j).wait_send()
         for k in range(CHUNKS):
             trade_tokens(k).wait_send()
@@ -339,13 +352,13 @@
         scratch_shapes=[
             pltpu.VMEM((rows, q_cols + 2 * kv_cols + o_weight.shape[1]), jnp.bfloat16),
             pltpu.VMEM((own, width), jnp.bfloat16),
-            dma((4,)),
-            dma((4, 2)),
-            dma((4,)),
-            dma((4,)),
-            dma((4,)),
-            dma((4, hops)),
-            dma((4, hops)),
+            dma((WEIGHTS,)),
+            dma((WEIGHTS, 2)),
+            dma((WEIGHTS,)),
+            dma((WEIGHTS,)),
+            dma((WEIGHTS,)),
+            dma((WEIGHTS, hops)),
+            dma((WEIGHTS, hops)),
             dma((CHUNKS,)),
             dma((CHUNKS,)),
             dma,
@@ -364,6 +377,10 @@
 
 
 PIECES = 6
+SUM_ORDER = (
+    "s0", "f0", "s1", "r0", "f1", "s2", "r1", "f2", "s3", "r2", "s4", "r3", "s5", "r4", "r5",
+    "a0", "a1", "a2",
+)
 
 
 def exchange_kernel(nd, tl, epilogue, aux_count, out_count, gather, carry_weights, *refs):
@@ -450,6 +467,10 @@
                 from_far(j, row_part).wait_recv()
                 over_d.send(j, row_part)
 
+        for j in range(PIECES):
+            for row_part in range(2):
+                from_far(j, row_part).start()
+
     order = list(range(1, tl)) + [0]
     for index in order:
         for k in range(CHUNKS):
@@ -470,11 +491,6 @@
             return carry
 
         lax.fori_loop(0, CHUNKS, pass_on, 0)
-
-    if carry_weights:
-        for j in range(PIECES):
-            for row_part in range(2):
-                from_far(j, row_part).start()
 
     def gathered(index, k):
         return full.at[part(index, k)]
@@ -514,25 +530,26 @@
             across(0, k).start()
         return carry
 
+    def pass_across(k):
+        for index in range(1, tl):
+            from_along(index, k).wait_recv()
+            across(index, k).start()
+
     if carry_weights:
-        for k in range(CHUNKS):
-            finish(k, 0)
-        for j in range(PIECES // 2):
-            spread(j)
-            if j:
-                over_d.relay(j - 1)
+        steps = {
+            "s": spread,
+            "r": over_d.relay,
+            "f": lambda k: finish(k, 0),
+            "a": pass_across,
+        }
+        for step in SUM_ORDER:
+            steps[step[0]](int(step[1:]))
     else:
         lax.fori_loop(0, CHUNKS, finish, 0)
+        if gather:
+            for k in range(CHUNKS):
+                pass_across(k)
     if gather:
-        for k in range(CHUNKS):
-            for index in range(1, tl):
-                from_along(index, k).wait_recv()
-                across(index, k).start()
-        if carry_weights:
-            for j in range(PIECES // 2, PIECES):
-                spread(j)
-                over_d.relay(j - 1)
-            over_d.relay(PIECES - 1)
         for k in range(CHUNKS):
             keep_own(k).wait()
             for index in range(tl):
@@ -613,6 +630,64 @@
     )(partial, *aux, *given)
 
 
+def gain_kernel(nd, tl, tiles, out, got, send_sem, recv_sem):
+    d, c, h, l = (lax.axis_index(name) for name in ("d", "c", "h", "l"))
+    count = 4 * nd * tl
+    me = ((d * 2 + c) * 2 + h) * tl + l
+
+    def to(step):
+        place = lax.rem(me + step, count)
+        to_l = lax.rem(place, tl)
+        to_h = lax.rem(place // tl, 2)
+        row = place // (2 * tl)
+        return remote(
+            tiles.at[row],
+            got.at[step - 1],
+            send_sem.at[step - 1],
+            recv_sem.at[step - 1],
+            d=row // 2,
+            c=lax.rem(row, 2),
+            h=to_h,
+            l=to_l,
+        )
+
+    def start(step, carry):
+        to(step).start()
+        return carry
+
+    def add(step, total):
+        to(step).wait_recv()
+        return total + got[step - 1]
+
+    def drain(step, carry):
+        to(step).wait_send()
+        return carry
+
+    lax.fori_loop(1, count, start, 0)
+    out[...] = lax.fori_loop(1, count, add, tiles[d * 2 + c])
+    lax.fori_loop(1, count, drain, 0)
+
+
+def gain_total(tiles):
+    nd, tl = lax.axis_size("d"), lax.axis_size("l")
+    others = 4 * nd * tl - 1
+    vmem = pl.BlockSpec(memory_space=pltpu.VMEM)
+    return pl.pallas_call(
+        functools.partial(gain_kernel, nd, tl),
+        name="gain_total",
+        out_shape=jax.ShapeDtypeStruct(tiles.shape[1:], jnp.float32),
+        in_specs=[vmem],
+        out_specs=vmem,
+        scratch_shapes=[
+            pltpu.VMEM((others,) + tiles.shape[1:], jnp.float32),
+            pltpu.SemaphoreType.DMA((others,)),
+            pltpu.SemaphoreType.DMA((others,)),
+        ],
+        compiler_params=pltpu.CompilerParams(has_side_effects=True),
+        cost_estimate=pl.CostEstimate(flops=0, bytes_accessed=40_000_000, transcendentals=0),
+    )(tiles)
+
+
 def middle_rows(total, rows, k, aux, outs):
     stream, gain = aux
     value = stream[rows, :].astype(jnp.float32) + total
@@ -1157,26 +1232,28 @@
     gate_grad = columns_of(mine[:, :half_cols], other[:, :half_cols])
     up_grad = columns_of(mine[:, half_cols:], other[:, half_cols:])
 
-    sums = lax.psum(
-        jnp.concatenate([attn_gain_grad[0], mlp_gain_grad[0], q_gain_grad[0], k_gain_grad[0]]),
-        ("d", "c", "h", "l"),
-    )
-    row = lax.axis_index("d") * 2 + core
-
-    def owned(start, whole, part):
-        return lax.dynamic_slice(sums[start : start + whole], (row * part,), (part,))[None]
+    devices = gains.shape[0]
+    sums = jnp.concatenate(
+        [
+            part.reshape(devices, -1)
+            for part in (attn_gain_grad[0], mlp_gain_grad[0], q_gain_grad[0], k_gain_grad[0])
+        ],
+        axis=1,
+    )
+    sums = jnp.pad(sums, ((0, 0), (0, 1024 - sums.shape[1]))).reshape(devices, 8, 128)
+    sums = gain_total(sums).reshape(1, -1)
 
     return (
         activations,
         gradient,
-        owned(0, width, cut),
+        sums[:, :cut],
         attn_grad[None, :, :q_cols],
         attn_grad[None, :, q_cols : q_cols + kv_cols],
         attn_grad[None, :, q_cols + kv_cols : q_cols + 2 * kv_cols],
         attn_grad[None, :, q_cols + 2 * kv_cols :],
-        owned(2 * width, HEAD_WIDTH, head_cut),
-        owned(2 * width + HEAD_WIDTH, HEAD_WIDTH, head_cut),
-        owned(width, width, cut),
+        sums[:, 2 * cut : 2 * cut + head_cut],
+        sums[:, 2 * cut + head_cut : 2 * cut + 2 * head_cut],
+        sums[:, cut : 2 * cut],
         gate_grad[None],
         up_grad[None],
         down_grad[None],

time: 909 us -> 870 us (0.957)
  blocking collectives: 57.4 us -> 0 us
  waiting for transfers between devices: 165 us -> 200 us
  starting transfers between devices: 51.8 us -> 25.8 us
    psum x1 -> x0, blocking collectives: 57.4 us -> none  [per_device(): lax.psum(jnp.concatenate([attn_gain_grad[0], mlp_gain_grad[0], q_gain_gra...]
    ppermute x2, waiting for transfers between devices: 101 us -> 138 us  [return_halves(): far = lax.ppermute(far, 'h', shift_perm(2, 1))]
    pallas_call x0 -> x1, Pallas kernels: none -> 21.9 us  [gain_total(): pl.pallas_call(functools.partial(gain_kernel, nd, tl), name='gain_total',...]
    pallas_call x3, Pallas kernels: 217 us -> 197 us  [exchange(): pl.pallas_call(functools.partial(exchange_kernel, nd, tl, epilogue, len(a...]
    ppermute x2, starting transfers between devices: 14.7 us -> 0.07 us  [return_halves(): other = lax.ppermute(sent, 'c', shift_perm(2, 1)).astype(jnp.float32)]
    ppermute x3, starting transfers between devices: 18.6 us -> 4.48 us  [core_halves(): lax.ppermute(jnp.where(core == 0, second, first), 'c', shift_perm(2, 1))]
    unnamed x150 -> x149, local copies, waits for them, and re-layouts: 33.3 us -> 33.9 us
  transfers between devices with their start and end apart: 25 -> 25, of which waited for: 9 -> 9; matrix products, arithmetic and copies ran while one was open for 26% -> 28% of each run, Pallas kernels for 30% -> 32%
where the time goes in v6:
time: 870 us; the launch traced here: 862 us
  Pallas kernels  355 us (41%)
  waiting for transfers between devices  200 us (23%)
  matrix products  155 us (18%)
  other arithmetic  56.3 us (6%)
  local copies, waits for them, and re-layouts  54 us (6%)
  starting transfers between devices  25.8 us (3%)
  between operations  15.4 us (2%)
    pallas_call x3, Pallas kernels, exchange(): pl.pallas_call(functools.partial(exchange_kernel, nd, tl, epilogue, len(a...  197 us
    ppermute x2, waiting for transfers between devices, return_halves(): far = lax.ppermute(far, 'h', shift_perm(2, 1))  138 us
    pallas_call x1, Pallas kernels, enter(): pl.pallas_call(functools.partial(entry_kernel, nd, tl), name='entry', out...  80.3 us
    dot_general x6, matrix products, contract_cols(): lax.dot_general(left, right, (((1,), (1,)), ((), ())), preferred_element_...  50.7 us
    dot_general x6, matrix products, contract_rows(): lax.dot_general(left, right, (((0,), (0,)), ((), ())), preferred_element_...  44.8 us
    pallas_call x1, Pallas kernels, attention_pull(): pl.pallas_call(functools.partial(attention_pull_kernel, blocks, repeat),...  34.8 us
    unnamed x149, local copies, waits for them, and re-layouts  33.9 us
    ppermute x1, waiting for transfers between devices, scatter_weights(): far = lax.ppermute(jnp.where(same, other, mine), 'h', shift_perm(2, 1))  29.6 us
  transfers between devices with their start and end apart: 25, of which 9 were waited for; matrix products, arithmetic and copies ran while one was open for 28% of the time, Pallas kernels for 32%

profile of v6, /device:TPU:0, one launch (start us, length us, event | category | flops | bytes accessed | tf_op | source)
XLA Modules:
  0.0 861.5 jit_solution(5562810132410975344)
XLA Ops:
  13.2 80.3 %entry.1 = (bf16[2048,1024]{1,0:T(8,128)(2,1)}, bf16[2048,512]{1,0:T(8,128)(2,1)}, bf16[1152,2048]{1,0:T(8,128)(2,1)}, f32[8,8,128]{2,1,0:T(8,128)}) custom-call(bf16[256,512]{1,0:T(8,128)(2,1)} %bitcast.118, bf16[256,256]{1,0:T(8,128)(2,1)} %bitcast.121, bf16[256,256]{1,0:T(8,128)(2,1)} %bitcast.122, bf16[256,512]{1,0:T(8,128)(2,1)} %bitcast.119, ...), custom_call_target="tpu_custom_call" | custom-call | bytes 250000000 | tf_op jit(solution)/shard_map/entry/pallas_call | solution.py:341
  95.4 3.8 collective-permute-start.6
  100.8 2.1 fusion.16
  103.3 1.8 slice.132.refs_1_
  106.0 10.3 %collective-permute-start.3 = (bf16[288,2048]{1,0:T(8,128)(2,1)}, bf16[288,2048]{1,0:T(8,128)(2,1)}, u32[]{:S(2)}, u32[]{:S(2)}) collective-permute-start(bf16[288,2048]{1,0:T(8,128)(2,1)} %param.27), channel_id=1, source_target_pairs={{0,0},{2,4},{4,2},{6,6},{1,1},{3,5},{5,3},{7,7},{8,8},{10,12},{12,... | collective-permute-start | bytes 3538952 | tf_op jit(solution)/shard_map/ppermute | solution.py:987
  116.3 2.1 maximum_select_fusion.2
  118.5 2.3 copy.72
  120.7 3.5 fusion
  124.3 9.4 %fusion.14.refs_0_.refs_1_.refs_2_ = f32[1152,1024]{1,0:T(8,128)} fusion(bf16[2048,1024]{1,0:T(8,128)(2,1)S(1)} %copy-done.50, bf16[1152,2048]{1,0:T(8,128)(2,1)} %get-tuple-element.51, f32[2048]{0:T(1024)S(1)} %bitcast.128, f32[1152]{0:T(1024)S(1)} %add_rsqrt_fusion), kind=kOutput, calls=%fused_computation.54 | convolution fusion | flops 4841275392 | bytes 13644288 | tf_op jit(solution)/shard_map/dot_general | solution.py:1130
  133.8 20.2 %attention.1 = (bf16[1152,512]{1,0:T(8,128)(2,1)}, bf16[1152,256]{1,0:T(8,128)(2,1)S(1)}, bf16[1152,256]{1,0:T(8,128)(2,1)S(1)}, bf16[1152,512]{1,0:T(8,128)(2,1)}, f32[1152,256]{1,0:T(8,128)}) custom-call(s32[4]{0:T(128)S(1)} %get-tuple-element.127.order_ref, f32[1152,1024]{1,0:T(8,128)} %fusion.14.refs_0_.refs_1_.refs_2_, ...), custom_call_target="tpu_custom_call" | custom-call | flops 2717908992 | bytes 60000000 | tf_op jit(solution)/shard_map/attention/pallas_call | solution.py:837
  155.7 4.3 convolution_convert_fusion.3.refs_0_
  159.9 107.8 %shard_map.237 = (f32[288,2048]{1,0:T(8,128)S(1)}, bf16[1152,2048]{1,0:T(8,128)(2,1)S(1)}, bf16[2048,1536]{1,0:T(8,128)(2,1)}) custom-call(bf16[1152,2048]{1,0:T(8,128)(2,1)S(1)} %convolution_convert_fusion.3.refs_0_, bf16[288,2048]{1,0:T(8,128)(2,1)S(1)} %slice.132.refs_1_, f32[1,2048]{1,0:T(1,128)S(1)} %bitcast.102, bf16[512,1536]{1,0:T(8,128)(2,1)S(1)} %copy-done), custom_call_target="tpu_custom_call" | custom-call | bytes 200000000 | tf_op jit(solution)/shard_map/pallas_call | solution.py:616
  267.7 12.0 %fusion.35 = f32[1152,1536]{1,0:T(8,128)S(1)} fusion(bf16[1152,2048]{1,0:T(8,128)(2,1)S(1)} %get-tuple-element.57, bf16[2048,1536]{1,0:T(8,128)(2,1)} %get-tuple-element.65), kind=kOutput, calls=%fused_computation.132 | convolution fusion | flops 7247757312 | bytes 18087936 | tf_op jit(solution)/shard_map/dot_general | solution.py:1155
  279.8 2.7 multiply_convert_fusion.2
  283.4 11.5 %fusion.34 = f32[1152,1536]{1,0:T(8,128)S(1)} fusion(bf16[1152,2048]{1,0:T(8,128)(2,1)} %copy-done.14, bf16[2048,1536]{1,0:T(8,128)(2,1)} %all-gather.4.cloned.1.call-done), kind=kOutput, calls=%fused_computation.131 | convolution fusion | flops 7247757312 | bytes 18087936 | tf_op jit(solution)/shard_map/dot_general | solution.py:1152
  294.9 2.8 multiply_convert_fusion.3
  298.2 13.6 %collective-permute-done.4 = bf16[288,2048]{1,0:T(8,128)(2,1)S(1)} collective-permute-done((bf16[288,2048]{1,0:T(8,128)(2,1)}, bf16[288,2048]{1,0:T(8,128)(2,1)S(1)}, u32[]{:S(2)}, u32[]{:S(2)}) %collective-permute-start.4) | collective-permute-done | bytes 1179680 | tf_op jit(solution)/shard_map/ppermute | solution.py:992
  311.8 2.9 pad_maximum_fusion.4
  316.3 3.3 collective-permute-done.5
  319.6 1.9 constant_dynamic-update-slice_fusion
  321.5 4.7 convolution_convert_fusion.6
  326.2 4.7 convolution_convert_fusion.5
  330.9 3.8 pad_maximum_fusion
  334.7 10.4 %fusion.8 = (bf16[1152,768]{1,0:T(8,128)(2,1)S(1)}, bf16[1152,768]{1,0:T(8,128)(2,1)S(1)}) fusion(f32[1152,1536]{1,0:T(8,128)} %copy-done.24, bf16[1152,2048]{1,0:T(8,128)(2,1)} %copy-done.39, bf16[2048,768]{1,0:T(8,128)(2,1)} %all-gather.8.cloned.1.call-done), kind=kOutput, calls=%fused_computation.24 | convolution fusion | flops 3636264960 | bytes 18481152 | tf_op jit(solution)/shard_map/dot_general | solution.py:1170
  346.9 12.7 %convolution_convert_fusion.2 = bf16[2048,1536]{0,1:T(8,128)(2,1)} fusion(bf16[1152,2048]{1,0:T(8,128)(2,1)} %copy-done.14, bf16[1152,768]{1,0:T(8,128)(2,1)S(1)} %get-tuple-element.129, bf16[1152,768]{1,0:T(8,128)(2,1)S(1)} %get-tuple-element.128), kind=kOutput, calls=%fused_computation.10 | convolution fusion | flops 7257980928 | bytes 14548992 | tf_op jit(solution)/shard_map/dot_general | solution.py:47
  360.4 10.2 %all-gather.6.cloned.1.call-done = bf16[2048,768]{1,0:T(8,128)(2,1)} async-done(((bf16[512,768]{1,0:T(8,128)(2,1)}), bf16[2048,768]{1,0:T(8,128)(2,1)}) %all-gather.6.cloned.1.call-update) | async-done | bytes 3145744 | tf_op jit(solution)/shard_map/all_gather | solution.py:1098
  370.6 10.2 %fusion.5 = (bf16[1152,768]{1,0:T(8,128)(2,1)S(1)}, bf16[1152,768]{1,0:T(8,128)(2,1)S(1)}) fusion(f32[1152,1536]{1,0:T(8,128)} %copy-done.23, bf16[1152,2048]{1,0:T(8,128)(2,1)} %copy-done.39, bf16[2048,768]{1,0:T(8,128)(2,1)} %all-gather.6.cloned.1.call-done), kind=kOutput, calls=%fused_computation.21 | convolution fusion | flops 3636264960 | bytes 18481152 | tf_op jit(solution)/shard_map/dot_general | solution.py:1170
  381.9 12.0 %fusion.30 = f32[1152,2048]{1,0:T(8,128)} fusion(bf16[2048,1536]{1,0:T(8,128)(2,1)} %all-gather.4.cloned.1.call-done, bf16[1152,768]{1,0:T(8,128)(2,1)S(1)} %get-tuple-element.131, bf16[1152,768]{1,0:T(8,128)(2,1)S(1)} %get-tuple-element.130), kind=kOutput, calls=%fused_computation.127 | convolution fusion | flops 7254835200 | bytes 19267584 | tf_op jit(solution)/shard_map/dot_general | solution.py:53
  393.9 13.6 %add_convert_fusion.refs_0_ = bf16[1152,2048]{1,0:T(8,128)(2,1)} fusion(f32[1152,2048]{1,0:T(8,128)} %fusion.30, bf16[2048,1536]{1,0:T(8,128)(2,1)} %get-tuple-element.65, bf16[1152,768]{1,0:T(8,128)(2,1)} %copy-done.59, bf16[1152,768]{1,0:T(8,128)(2,1)S(1)} %copy-done.58), kind=kOutput, calls=%fused_computation.6 | convolution fusion | flops 7259553792 | bytes 23986176 | tf_op jit(solution)/shard_map/dot_general | solution.py:53
  407.5 58.6 %shard_map.238 = (f32[288,2048]{1,0:T(8,128)S(1)}, f32[1,2048]{1,0:T(1,128)S(1)}, bf16[1152,2048]{1,0:T(8,128)(2,1)S(1)}) custom-call(bf16[1152,2048]{1,0:T(8,128)(2,1)} %add_convert_fusion.refs_0_, f32[288,2048]{1,0:T(8,128)S(1)} %copy-done.2, bf16[288,2048]{1,0:T(8,128)(2,1)} %collective-permute-done.3.refs_2_, f32[1,2048]{1,0:T(1,128)S(1)} %bitcast.103), custom_call_target="tpu_custom_call" | custom-call | bytes 200000000 | tf_op jit(solution)/shard_map/pallas_call | solution.py:616
  467.6 1.5 copy-done.15
  469.2 10.6 %convolution_convert_fusion.1 = bf16[2048,1536]{0,1:T(8,128)(2,1)} fusion(bf16[1152,2048]{1,0:T(8,128)(2,1)S(1)} %bitcast.106, bf16[1152,1536]{1,0:T(8,128)(2,1)S(1)} %pad_maximum_fusion.2), kind=kOutput, calls=%fused_computation.9 | convolution fusion | flops 7250903040 | bytes 14548992 | tf_op jit(solution)/shard_map/dot_general | solution.py:47
  479.8 1.5 copy-done.54
  481.4 6.2 convolution_convert_fusion.8.refs_11_
  487.6 34.8 %attention_pull.1 = (bf16[1152,512]{1,0:T(8,128)(2,1)}, bf16[1152,256]{1,0:T(8,128)(2,1)}, bf16[1152,256]{1,0:T(8,128)(2,1)}, f32[8,128]{1,0:T(8,128)}, f32[8,128]{1,0:T(8,128)}) custom-call(s32[4]{0:T(128)} %copy-done.13, f32[1152,1024]{1,0:T(8,128)} %fusion.14.refs_0_.refs_1_.refs_2_, f32[1152,1024]{1,0:T(8,128)} %fusion.14.refs_0_.refs_1_.refs_2_, ...), custom_call_target="tpu_custom_call" | custom-call | flops 6794772480 | bytes 120000000 | tf_op jit(solution)/shard_map/attention_pull/pallas_call | solution.py:943
  522.4 1.6 constant_dynamic-update-slice_fusion.5
  525.3 3.2 convolution_convert_fusion.7
  528.5 9.1 %convolution_convert_fusion.4 = bf16[2048,1024]{0,1:T(8,128)(2,1)S(1)} fusion(bf16[1152,1024]{1,0:T(8,128)(2,1)S(1)} %constant_dynamic-update-slice_fusion.3, bf16[1152,2048]{1,0:T(8,128)(2,1)} %get-tuple-element.51, f32[2048]{0:T(1024)S(1)} %bitcast.129, f32[1152]{0:T(1024)S(1)} %copy-done.45), kind=kOutput, calls=%fused_computation.18 | convolution fusion | flops 4843372544 | bytes 11284992 | tf_op jit(solution)/shard_map/dot_general | solution.py:47
  537.6 3.7 pad_maximum_fusion.1
  543.3 7.6 convolution_convert_fusion.refs_0_
  550.9 30.9 %shard_map.239 = (f32[288,2048]{1,0:T(8,128)S(1)}, bf16[288,2048]{1,0:T(8,128)(2,1)S(1)}, f32[1,2048]{1,0:T(1,128)S(1)}) custom-call(bf16[1152,2048]{1,0:T(8,128)(2,1)S(1)} %convolution_convert_fusion.refs_0_, bf16[288,2048]{1,0:T(8,128)(2,1)S(1)} %slice.132.refs_1_, f32[288,2048]{1,0:T(8,128)S(1)} %copy-done.8, f32[1,2048]{1,0:T(1,128)S(1)} %bitcast.104), custom_call_target="tpu_custom_call" | custom-call | bytes 110000000 | tf_op jit(solution)/shard_map/pallas_call | solution.py:616
  581.9 6.5 fusion.36
  588.4 6.7 convolution_add_fusion
  595.7 4.5 collective-permute-done.8
  601.2 2.1 copy-done.20
  616.8 21.9 %gain_total.1 = f32[8,128]{1,0:T(8,128)} custom-call(f32[8,8,128]{2,1,0:T(8,128)} %bitcast.120), custom_call_target="tpu_custom_call" | custom-call | bytes 40000000 | tf_op jit(solution)/shard_map/gain_total/pallas_call | solution.py:675
  638.7 1.7 collective-permute-start.11
  642.8 2.9 collective-permute-start.16
  645.7 2.6 fusion.12
  649.2 2.3 collective-permute-start.14
  652.8 109.8 %collective-permute-done.16 = bf16[512,768]{0,1:T(8,128)(2,1)S(1)} collective-permute-done((bf16[512,768]{0,1:T(8,128)(2,1)S(1)}, bf16[512,768]{0,1:T(8,128)(2,1)S(1)}, u32[]{:S(2)}, u32[]{:S(2)}) %collective-permute-start.16) | collective-permute-done | bytes 786464 | tf_op jit(solution)/shard_map/ppermute | solution.py:1029
  763.0 3.0 convert_select_fusion
  768.3 28.2 %collective-permute-done.14 = bf16[512,1536]{0,1:T(8,128)(2,1)} collective-permute-done((bf16[512,1536]{0,1:T(8,128)(2,1)}, bf16[512,1536]{0,1:T(8,128)(2,1)}, u32[]{:S(2)}, u32[]{:S(2)}) %collective-permute-start.14) | collective-permute-done | bytes 1572896 | tf_op jit(solution)/shard_map/ppermute | solution.py:1029
  796.5 2.3 convert_add_fusion
  799.9 2.3 broadcast_select_fusion
  802.7 2.6 maximum_bitcast_fusion.2
  805.3 3.0 copy.86
  810.0 2.2 broadcast_select_fusion.2
  812.2 1.5 slice_select_fusion.3
  813.8 1.6 copy.85
  815.4 1.6 maximum_bitcast_fusion
  817.0 1.6 copy.84
  818.6 29.6 %collective-permute-done.13 = bf16[256,1536]{0,1:T(8,128)(2,1)} collective-permute-done((bf16[256,1536]{0,1:T(8,128)(2,1)}, bf16[256,1536]{0,1:T(8,128)(2,1)}, u32[]{:S(2)}, u32[]{:S(2)}) %collective-permute-start.13) | collective-permute-done | bytes 786464 | tf_op jit(solution)/shard_map/ppermute | solution.py:1067
  848.2 1.5 convert_add_fusion.2
  (246 shorter events, 54.0 us)
Async XLA Ops:
  7.2 276.1 %all-gather.4.cloned.1.call-start = ((), (), s32[]{:S(2)}) async-start(), calls=%async_computation.4 | async-start | bytes 7864320 | tf_op jit(solution)/shard_map/all_gather | solution.py:1118
  8.8 1.9 collective-permute-start
  9.7 1.8 collective-permute-start.1
  11.9 81.7 %copy-start.56 = (s32[1,1152]{1,0:T(1,128)S(1)}, s32[1,1152]{1,0:T(1,128)}, u32[]{:S(2)}) copy-start(s32[1,1152]{1,0:T(1,128)} %param.15) | copy-start | bytes 13828
  11.9 82.4 %copy-start.35 = (bf16[1,256,1536]{2,1,0:T(8,128)(2,1)S(1)}, bf16[1,256,1536]{2,1,0:T(8,128)(2,1)}, u32[]{:S(2)}) copy-start(bf16[1,256,1536]{2,1,0:T(8,128)(2,1)} %param.26) | copy-start | bytes 2359300
  93.6 241.1 %all-gather.8.cloned.1.call-start = ((), (), s32[]{:S(2)}) async-start(), calls=%async_computation.6 | async-start | bytes 3932160 | tf_op jit(solution)/shard_map/all_gather | solution.py:1135
  93.6 5.9 collective-permute-start.2
  95.4 20.9 %collective-permute-start.6 = (bf16[256,768]{0,1:T(8,128)(2,1)}, bf16[256,768]{0,1:T(8,128)(2,1)}, u32[]{:S(2)}, u32[]{:S(2)}) collective-permute-start(bf16[256,768]{0,1:T(8,128)(2,1)} %get-tuple-element.143), channel_id=1, source_target_pairs={{4,0},{0,4},{5,1},{1,5},{6,2},{2,6},{7,3},{3,7},{12,8},{8,12},{13,... | collective-permute-start | bytes 1179656 | tf_op jit(solution)/shard_map/ppermute | solution.py:1022
  99.4 34.3 %copy-start.13 = (s32[4]{0:T(128)}, s32[4]{0:T(128)S(1)}, u32[]{:S(2)}) copy-start(s32[4]{0:T(128)S(1)} %get-tuple-element.127.order_ref) | copy-start | bytes 52
  100.8 33.0 %copy-start.4 = (s32[1152,1]{1,0:T(8,128)}, s32[1152,1]{1,0:T(8,128)S(1)}, u32[]{:S(2)}) copy-start(s32[1152,1]{1,0:T(8,128)S(1)} %reduce_sum.33.refs_7_.refs_6_) | copy-start | bytes 13828
  100.8 4.3 copy-start.41
  103.3 30.4 %copy-start.9 = (f32[1152,128]{1,0:T(8,128)}, f32[1152,128]{1,0:T(8,128)S(1)}, u32[]{:S(2)}) copy-start(f32[1152,128]{1,0:T(8,128)S(1)} %get-tuple-element.160.refs_3_.refs_2_) | copy-start | bytes 1769476
  103.3 30.4 %copy-start.10 = (f32[1152,128]{1,0:T(8,128)}, f32[1152,128]{1,0:T(8,128)S(1)}, u32[]{:S(2)}) copy-start(f32[1152,128]{1,0:T(8,128)S(1)} %get-tuple-element.161.refs_4_.refs_3_) | copy-start | bytes 1769476
  105.7 18.5 %copy-start.42 = (f32[1,2,8,128]{3,1,2,0:T(2,128)}, f32[1,2,8,128]{3,1,2,0:T(2,128)S(1)}, u32[]{:S(2)}) copy-start(f32[1,2,8,128]{3,1,2,0:T(2,128)S(1)} %copy.92) | copy-start | bytes 24580
  105.9 27.9 %copy-start.11 = (f32[1,128]{1,0:T(1,128)}, f32[1,128]{1,0:T(1,128)S(1)}, u32[]{:S(2)}) copy-start(f32[1,128]{1,0:T(1,128)S(1)} %reshape_reshape.11.refs_5_.refs_4_) | copy-start | bytes 1540
  106.0 27.8 %copy-start.12 = (f32[1,128]{1,0:T(1,128)}, f32[1,128]{1,0:T(1,128)S(1)}, u32[]{:S(2)}) copy-start(f32[1,128]{1,0:T(1,128)S(1)} %reshape_reshape.12.refs_6_.refs_5_) | copy-start | bytes 1540
  106.0 177.3 %collective-permute-start.3 = (bf16[288,2048]{1,0:T(8,128)(2,1)}, bf16[288,2048]{1,0:T(8,128)(2,1)}, u32[]{:S(2)}, u32[]{:S(2)}) collective-permute-start(bf16[288,2048]{1,0:T(8,128)(2,1)} %param.27), channel_id=1, source_target_pairs={{0,0},{2,4},{4,2},{6,6},{1,1},{3,5},{5,3},{7,7},{8,8},{10,12},{12,... | collective-permute-start | bytes 3538952 | tf_op jit(solution)/shard_map/ppermute | solution.py:987
  120.7 3.6 copy-start.50
  120.7 162.4 %collective-permute-start.7 = (bf16[512,768]{1,0:T(8,128)(2,1)}, bf16[512,768]{1,0:T(8,128)(2,1)}, u32[]{:S(2)}, u32[]{:S(2)}) collective-permute-start(bf16[512,768]{1,0:T(8,128)(2,1)} %bitcast.109), channel_id=1, source_target_pairs={{2,0},{0,2},{3,1},{1,3},{6,4},{4,6},{7,5},{5,7},{10,8},{8,10},{11,... | collective-permute-start | bytes 2359304 | tf_op jit(solution)/shard_map/ppermute | solution.py:1119
  124.2 9.5 %copy-start.44 = (f32[1152]{0:T(1024)}, f32[1152]{0:T(1024)S(1)}, u32[]{:S(2)}) copy-start(f32[1152]{0:T(1024)S(1)} %add_rsqrt_fusion) | copy-start | bytes 13828
  133.8 21.9 %copy-start.53 = (bf16[2048,512]{1,0:T(8,128)(2,1)S(1)}, bf16[2048,512]{1,0:T(8,128)(2,1)}, u32[]{:S(2)}) copy-start(bf16[2048,512]{1,0:T(8,128)(2,1)} %get-tuple-element.55) | copy-start | bytes 6291460
  155.6 4.3 copy-start
  267.7 12.1 %copy-start.1 = (f32[288,2048]{1,0:T(8,128)}, f32[288,2048]{1,0:T(8,128)S(1)}, u32[]{:S(2)}) copy-start(f32[288,2048]{1,0:T(8,128)S(1)} %get-tuple-element.56.refs_1_) | copy-start | bytes 7077892
  267.7 12.0 %copy-start.14 = (bf16[1152,2048]{1,0:T(8,128)(2,1)}, bf16[1152,2048]{1,0:T(8,128)(2,1)S(1)}, u32[]{:S(2)}) copy-start(bf16[1152,2048]{1,0:T(8,128)(2,1)S(1)} %get-tuple-element.57) | copy-start | bytes 14155780
  283.2 87.4 %all-gather.6.cloned.1.call-start = ((), (), s32[]{:S(2)}) async-start(), calls=%async_computation.5 | async-start | bytes 3932160 | tf_op jit(solution)/shard_map/all_gather | solution.py:1098
  283.2 28.5 %collective-permute-start.4 = (bf16[288,2048]{1,0:T(8,128)(2,1)}, bf16[288,2048]{1,0:T(8,128)(2,1)S(1)}, u32[]{:S(2)}, u32[]{:S(2)}) collective-permute-start(bf16[288,2048]{1,0:T(8,128)(2,1)} %collective-permute-done.3.refs_2_), channel_id=1, source_target_pairs={{1,0},{0,1},{3,2},{2,3},{5,4},{4,5},{7,6},{6,7},{9,8},{8,9},{11,10... | collective-permute-start | bytes 3538952 | tf_op jit(solution)/shard_map/ppermute | solution.py:992
  314.7 4.9 collective-permute-start.5
  314.7 226.6 %reduce-scatter.5.cloned.1.call-start = ((), (), s32[]{:S(2)}) async-start(), calls=%async_computation.7 | async-start | bytes 7864320 | tf_op jit(solution)/shard_map/reduce_scatter | solution.py:1047
  316.1 5.3 copy-start.29
  321.5 4.7 copy-start.39
  321.5 4.7 copy-start.27
  359.6 282.0 %reduce-scatter.11.cloned.1.call-start = ((), (), s32[]{:S(2)}) async-start(), calls=%async_computation.10 | async-start | bytes 7864320 | tf_op jit(solution)/shard_map/reduce_scatter | solution.py:1047
  360.2 408.1 %reduce-scatter.9.cloned.1.call-start = ((), (), s32[]{:S(2)}) async-start(), calls=%async_computation.9 | async-start | bytes 7864320 | tf_op jit(solution)/shard_map/reduce_scatter | solution.py:1047
  381.9 12.0 %copy-start.58 = (bf16[1152,768]{1,0:T(8,128)(2,1)S(1)}, bf16[1152,768]{1,0:T(8,128)(2,1)}, u32[]{:S(2)}) copy-start(bf16[1152,768]{1,0:T(8,128)(2,1)} %copy-done.57) | copy-start | bytes 5308420
  381.9 87.2 %slice-start = ((s8[4718592]{0:T(1024)(128)(4,1)}), s8[4194304]{0:T(1024)(128)(4,1)S(1)}, s32[]{:S(2)}) async-start(s8[4718592]{0:T(1024)(128)(4,1)} %bitcast.105), calls=%async_computation.11 | async-start | bytes 8388608
  393.9 13.6 %copy-start.2 = (f32[288,2048]{1,0:T(8,128)S(1)}, f32[288,2048]{1,0:T(8,128)}, u32[]{:S(2)}) copy-start(f32[288,2048]{1,0:T(8,128)} %copy-done.1) | copy-start | bytes 7077892
  393.9 75.2 %slice-start.1 = ((s8[4718592]{0:T(1024)(128)(4,1)}), s8[524288]{0:T(1024)(128)(4,1)S(1)}, s32[]{:S(2)}) async-start(s8[4718592]{0:T(1024)(128)(4,1)} %bitcast.105), calls=%async_computation.12 | async-start | bytes 1048576
  407.5 58.7 %copy-start.26 = (bf16[1152,768]{1,0:T(8,128)(2,1)S(1)}, bf16[1152,768]{1,0:T(8,128)(2,1)}, u32[]{:S(2)}) copy-start(bf16[1152,768]{1,0:T(8,128)(2,1)} %copy-done.25) | copy-start | bytes 5308420
  479.8 320.1 %reduce-scatter.7.cloned.1.call-start = ((), (), s32[]{:S(2)}) async-start(), calls=%async_computation.8 | async-start | bytes 7864320 | tf_op jit(solution)/shard_map/reduce_scatter | solution.py:1047
  481.4 43.8 %slice-start.2 = ((s8[4718592]{0:T(1024)(128)(4,1)}), s8[4194304]{0:T(1024)(128)(4,1)S(1)}, s32[]{:S(2)}) async-start(s8[4718592]{0:T(1024)(128)(4,1)} %bitcast.107), calls=%async_computation.13 | async-start | bytes 8388608
  487.6 37.6 %slice-start.3 = ((s8[4718592]{0:T(1024)(128)(4,1)}), s8[524288]{0:T(1024)(128)(4,1)S(1)}, s32[]{:S(2)}) async-start(s8[4718592]{0:T(1024)(128)(4,1)} %bitcast.107), calls=%async_computation.14 | async-start | bytes 1048576
  543.3 7.7 copy-start.8
  550.9 31.0 %copy-start.30 = (bf16[1152,768]{1,0:T(8,128)(2,1)S(1)}, bf16[1152,768]{1,0:T(8,128)(2,1)}, u32[]{:S(2)}) copy-start(bf16[1152,768]{1,0:T(8,128)(2,1)} %multiply_convert_fusion.3) | copy-start | bytes 5308420
  550.9 31.0 %copy-start.52 = (bf16[2048,768]{1,0:T(8,128)(2,1)S(1)}, bf16[2048,768]{1,0:T(8,128)(2,1)}, u32[]{:S(2)}) copy-start(bf16[2048,768]{1,0:T(8,128)(2,1)} %all-gather.6.cloned.1.call-done) | copy-start | bytes 9437188
  581.9 6.6 copy-start.5
  581.9 6.5 copy-start.16
  581.9 6.5 copy-start.28
  581.9 6.5 copy-start.51
  595.5 43.1 %copy-start.17 = (bf16[288,2048]{1,0:T(8,128)(2,1)S(1)}, bf16[288,2048]{1,0:T(8,128)(2,1)}, u32[]{:S(2)}) copy-start(bf16[288,2048]{1,0:T(8,128)(2,1)} %copy-done.16) | copy-start | bytes 3538948
  595.5 4.6 collective-permute-start.8
  603.3 42.4 %copy-start.3 = (f32[288,2048]{1,0:T(8,128)S(1)}, f32[288,2048]{1,0:T(8,128)}, u32[]{:S(2)}) copy-start(f32[288,2048]{1,0:T(8,128)} %copy-done.1) | copy-start | bytes 7077892
  604.5 37.1 %collective-permute-start.9 = (bf16[288,2048]{1,0:T(8,128)(2,1)}, bf16[288,2048]{1,0:T(8,128)(2,1)}, u32[]{:S(2)}, u32[]{:S(2)}) collective-permute-start(bf16[288,2048]{1,0:T(8,128)(2,1)} %slice.289), channel_id=1, source_target_pairs={{1,0},{0,1},{3,2},{2,3},{5,4},{4,5},{7,6},{6,7},{9,8},{8,9},{11,10... | collective-permute-start | bytes 3538952 | tf_op jit(solution)/shard_map/ppermute | solution.py:1007
  638.7 124.3 %collective-permute-start.11 = (bf16[288,2048]{1,0:T(8,128)(2,1)S(1)}, bf16[288,2048]{1,0:T(8,128)(2,1)}, u32[]{:S(2)}, u32[]{:S(2)}) collective-permute-start(bf16[288,2048]{1,0:T(8,128)(2,1)S(1)} %copy-done.17), channel_id=1, source_target_pairs={{0,0},{2,4},{4,2},{6,6},{1,1},{3,5},{5,3},{7,7},{8,8},{10,12},{12,... | collective-permute-start | bytes 3538952 | tf_op jit(solution)/shard_map/ppermute | solution.py:987
  642.8 119.8 %copy-start.31 = (bf16[512,1536]{0,1:T(8,128)(2,1)S(1)}, bf16[512,1536]{0,1:T(8,128)(2,1)}, u32[]{:S(2)}) copy-start(bf16[512,1536]{0,1:T(8,128)(2,1)} %reduce-scatter.11.cloned.1.call-done) | copy-start | bytes 4718596
  642.8 119.8 %collective-permute-start.16 = (bf16[512,768]{0,1:T(8,128)(2,1)S(1)}, bf16[512,768]{0,1:T(8,128)(2,1)S(1)}, u32[]{:S(2)}, u32[]{:S(2)}) collective-permute-start(bf16[512,768]{0,1:T(8,128)(2,1)S(1)} %slice.203), channel_id=1, source_target_pairs={{2,0},{0,2},{3,1},{1,3},{6,4},{4,6},{7,5},{5,7},{10,8},{8,10},{11,... | collective-permute-start | bytes 2359304 | tf_op jit(solution)/shard_map/ppermute | solution.py:1029
  648.3 114.7 %copy-start.6 = (f32[288,2048]{1,0:T(8,128)S(1)}, f32[288,2048]{1,0:T(8,128)}, u32[]{:S(2)}) copy-start(f32[288,2048]{1,0:T(8,128)} %copy-done.5) | copy-start | bytes 7077892
  648.3 117.7 %collective-permute-start.10 = (bf16[288,2048]{1,0:T(8,128)(2,1)S(1)}, bf16[288,2048]{1,0:T(8,128)(2,1)S(1)}, u32[]{:S(2)}, u32[]{:S(2)}) collective-permute-start(bf16[288,2048]{1,0:T(8,128)(2,1)S(1)} %fusion.12), channel_id=1, source_target_pairs={{0,0},{2,4},{4,2},{6,6},{1,1},{3,5},{5,3},{7,7},{8,8},{10,12},{12,... | collective-permute-start | bytes 3538952 | tf_op jit(solution)/shard_map/ppermute | solution.py:987
  649.2 147.3 %collective-permute-start.14 = (bf16[512,1536]{0,1:T(8,128)(2,1)}, bf16[512,1536]{0,1:T(8,128)(2,1)}, u32[]{:S(2)}, u32[]{:S(2)}) collective-permute-start(bf16[512,1536]{0,1:T(8,128)(2,1)} %reduce-scatter.5.cloned.1.call-done), channel_id=1, source_target_pairs={{2,0},{0,2},{3,1},{1,3},{6,4},{4,6},{7,5},{5,7},{10,8},{8,10},{11,... | collective-permute-start | bytes 4718600 | tf_op jit(solution)/shard_map/ppermute | solution.py:1029
  762.9 4.1 collective-permute-start.17
  799.9 8.7 %collective-permute-start.15 = (bf16[256,1536]{0,1:T(8,128)(2,1)}, bf16[256,1536]{0,1:T(8,128)(2,1)}, u32[]{:S(2)}, u32[]{:S(2)}) collective-permute-start(bf16[256,1536]{0,1:T(8,128)(2,1)} %select_convert_fusion), channel_id=1, source_target_pairs={{4,0},{0,4},{5,1},{1,5},{6,2},{2,6},{7,3},{3,7},{12,8},{8,12},{13,... | collective-permute-start | bytes 2359304 | tf_op jit(solution)/shard_map/ppermute | solution.py:1035
  802.2 7.7 collective-permute-start.12
  812.2 36.0 %collective-permute-start.13 = (bf16[256,1536]{0,1:T(8,128)(2,1)}, bf16[256,1536]{0,1:T(8,128)(2,1)}, u32[]{:S(2)}, u32[]{:S(2)}) collective-permute-start(bf16[256,1536]{0,1:T(8,128)(2,1)} %broadcast_select_fusion.2), channel_id=1, source_target_pairs={{2,0},{0,2},{3,1},{1,3},{6,4},{4,6},{7,5},{5,7},{10,8},{8,10},{11,... | collective-permute-start | bytes 2359304 | tf_op jit(solution)/shard_map/ppermute | solution.py:1067
  815.4 32.8 %copy-start.22 = (bf16[512,1536]{0,1:T(8,128)(2,1)S(1)}, bf16[512,1536]{0,1:T(8,128)(2,1)}, u32[]{:S(2)}) copy-start(bf16[512,1536]{0,1:T(8,128)(2,1)} %reduce-scatter.7.cloned.1.call-done) | copy-start | bytes 4718596
  849.7 3.8 copy-start.33
  (25 other events, 54.1 us)
Sparse Core Ops, SparseCore 0:
  93.7 69.2 all-gather.3
  283.3 41.4 all-gather.7
  326.7 43.8 all-gather.5
  373.4 70.0 reduce-scatter.4
  446.3 70.0 reduce-scatter.10
  519.2 70.0 reduce-scatter.8
  592.2 71.4 reduce-scatter.6

commit v7 on v6

--- a/solution.py
+++ b/solution.py
@@ -110,21 +110,28 @@
 
 
 class Spread:
-    def __init__(self, nd, d, block, send_sem, recv_sem):
+    def __init__(self, nd, d, block, send_sem, recv_sem, own=None):
         self.hops, self.sources, self.first, self.relayed = hop_plan(nd, d)
         self.block, self.send_sem, self.recv_sem = block, send_sem, recv_sem
-
-    def copy(self, j, kind, part, of):
-        at = self.block(j, of * 2 + part)
+        self.own = own or (lambda j, part: block(j, d * 2 + part))
+
+    def copy(self, j, kind, source, part, of):
         return remote(
-            at, at, self.send_sem.at[j, kind], self.recv_sem.at[j, kind], d=self.hops[kind][2]
+            source,
+            self.block(j, of * 2 + part),
+            self.send_sem.at[j, kind],
+            self.recv_sem.at[j, kind],
+            d=self.hops[kind][2],
         )
 
     def hop(self, j, kind):
-        return self.copy(j, kind, *self.hops[kind][:2])
+        part, of, _ = self.hops[kind]
+        source = self.own(j, part) if kind < self.first else self.block(j, of * 2 + part)
+        return self.copy(j, kind, source, part, of)
 
     def arrived(self, j, kind):
-        return self.copy(j, kind, *self.sources[kind])
+        part, of = self.sources[kind]
+        return self.copy(j, kind, self.block(j, of * 2 + part), part, of)
 
     def send(self, j, part):
         for kind in range(self.first):
@@ -145,10 +152,11 @@
 
 
 def entry_kernel(nd, tl, *refs):
-    (q_ref, k_ref, v_ref, o_ref, tok_ref, gain_ref) = refs[:6]
-    (qkv_full, o_full, tok_full, gain_full) = refs[6:10]
-    (stage, tok_stage) = refs[10:12]
-    (zs, zr, cs, li, lo, xs, xr, ts, tr, tli, tlo, ls, lr, fs, fr, gs, gr, gl) = refs[12:]
+    (q_ref, k_ref, v_ref, o_ref, gate_ref, up_ref, down_ref, tok_ref, cot_ref, gain_ref) = refs[:10]
+    (qkv_full, o_full, mid_rows, down_rows, tok_full, cot_own, gain_full) = refs[10:17]
+    (stage, half_stage, tok_stage, cot_stage) = refs[17:21]
+    (zs, zr, cs, li, lo, xs, xr, ts, tr, tli, tlo, ls, lr, fs, fr) = refs[21:36]
+    (gs, gr, gl, os, orv, oi, hs, hr, hi, ho) = refs[36:]
     d, c, h, l = (lax.axis_index(name) for name in ("d", "c", "h", "l"))
     same = c == h
     apart = c != h
@@ -236,6 +244,27 @@
     def local_gains():
         return pltpu.make_async_copy(gain_ref, gain_full.at[d * 2 + c], gl)
 
+    half = gate_ref.shape[1] // 2
+    halves = ((gate_ref, mid_rows, 0), (up_ref, mid_rows, half), (down_ref, down_rows, 0))
+
+    def columns_of_core(j, of):
+        return halves[j][0].at[:, pl.ds(pl.multiple_of(of * half, half), half)]
+
+    def half_at(j, of):
+        return halves[j][1].at[rows_at(of, rows), pl.ds(halves[j][2], half)]
+
+    def half_to_core(j):
+        return remote(columns_of_core(j, 1 - c), half_at(j, c), hs.at[j], hr.at[j], c=1 - c)
+
+    def half_from_core(j):
+        return remote(half_at(j, 1 - c), half_at(j, 1 - c), hs.at[j], hr.at[j], c=1 - c)
+
+    def half_in(j):
+        return pltpu.make_async_copy(columns_of_core(j, c), half_stage.at[j], hi.at[j])
+
+    def half_out(j):
+        return pltpu.make_async_copy(half_stage.at[j], half_at(j, c), ho.at[j])
+
     local_gains().start()
 
     def start_weights(j):
@@ -250,8 +279,21 @@
         def _():
             trade_tokens(k).start()
 
+    def trade_cotangent():
+        return remote(cot_ref, cot_own, os, orv, c=h, h=c)
+
+    def cotangent_in():
+        return pltpu.make_async_copy(cot_ref, cot_stage, oi)
+
+    def cotangent_out():
+        return pltpu.make_async_copy(cot_stage, cot_own, oi)
+
     for step in ENTRY_START:
         {"w": start_weights, "t": start_tokens}[step[0]](int(step[1:]))
+
+    @pl.when(apart)
+    def _():
+        trade_cotangent().start()
 
     @pl.when(same)
     def _():
@@ -265,9 +307,18 @@
         for j in range(WEIGHTS):
             local_in(j).wait()
             local_out(j).start()
+        cotangent_in().start()
+        cotangent_in().wait()
+        cotangent_out().start()
 
     for step in range(1, 2 * nd):
         gains_to(step).start()
+    for j in range(3):
+        half_in(j).start()
+        half_to_core(j).start()
+    for j in range(3):
+        half_in(j).wait()
+        half_out(j).start()
 
     over_d = Spread(nd, d, block, xs, xr)
 
@@ -322,63 +373,92 @@
         gains_from(step).wait_recv()
         gains_to(step).wait_send()
     local_gains().wait()
+    for j in range(3):
+        half_from_core(j).wait_recv()
+        half_to_core(j).wait_send()
+        half_out(j).wait()
+
+    @pl.when(same)
+    def _():
+        cotangent_out().wait()
 
     @pl.when(apart)
     def _():
+        trade_cotangent().wait()
         for j in range(WEIGHTS):
             to_core(j).wait_send()
         for k in range(CHUNKS):
             trade_tokens(k).wait_send()
 
 
-def enter(q_weight, key_matrix, value_matrix, o_weight, tokens, gains):
+def enter(q_weight, k_weight, v_weight, o_weight, gate, up, down, tokens, cotangent, gains):
     nd, tl = lax.axis_size("d"), lax.axis_size("l")
     rows, q_cols = q_weight.shape
-    kv_cols = key_matrix.shape[1]
+    qkv_cols = q_cols + 2 * k_weight.shape[1]
     own, width = tokens.shape
-    hops = hop_count(nd)
+    half = gate.shape[1] // 2
     dma = pltpu.SemaphoreType.DMA
+    counts = (
+        (WEIGHTS,),
+        (WEIGHTS, 2),
+        (WEIGHTS,),
+        (WEIGHTS,),
+        (WEIGHTS,),
+        (WEIGHTS, hop_count(nd)),
+        (WEIGHTS, hop_count(nd)),
+        (CHUNKS,),
+        (CHUNKS,),
+        (),
+        (CHUNKS,),
+        ((tl - 1) * CHUNKS,),
+        ((tl - 1) * CHUNKS,),
+        (tl * CHUNKS,),
+        (tl * CHUNKS,),
+        (2 * nd - 1,),
+        (2 * nd - 1,),
+        (),
+        (),
+        (),
+        (),
+        (3,),
+        (3,),
+        (3,),
+        (3,),
+    )
+    anywhere = pl.BlockSpec(memory_space=pl.ANY)
+
+    def low(*shape):
+        return jax.ShapeDtypeStruct(shape, jnp.bfloat16)
+
     return pl.pallas_call(
         functools.partial(entry_kernel, nd, tl),
         name="entry",
         out_shape=(
-            jax.ShapeDtypeStruct((width, q_cols + 2 * kv_cols), jnp.bfloat16),
-            jax.ShapeDtypeStruct((width, o_weight.shape[1]), jnp.bfloat16),
-            jax.ShapeDtypeStruct((2 * tl * own, width), jnp.bfloat16),
+            low(width, qkv_cols),
+            low(width, o_weight.shape[1]),
+            low(2 * rows, 2 * half),
+            low(2 * rows, half),
+            low(2 * tl * own, width),
+            low(own, width),
             jax.ShapeDtypeStruct((2 * nd,) + gains.shape, jnp.float32),
         ),
-        in_specs=[pl.BlockSpec(memory_space=pl.ANY)] * 6,
-        out_specs=[pl.BlockSpec(memory_space=pl.ANY)] * 4,
+        in_specs=[anywhere] * 10,
+        out_specs=[anywhere] * 7,
         scratch_shapes=[
-            pltpu.VMEM((rows, q_cols + 2 * kv_cols + o_weight.shape[1]), jnp.bfloat16),
+            pltpu.VMEM((rows, qkv_cols + o_weight.shape[1]), jnp.bfloat16),
+            pltpu.VMEM((3, rows, half), jnp.bfloat16),
             pltpu.VMEM((own, width), jnp.bfloat16),
-            dma((WEIGHTS,)),
-            dma((WEIGHTS, 2)),
-            dma((WEIGHTS,)),
-            dma((WEIGHTS,)),
-            dma((WEIGHTS,)),
-            dma((WEIGHTS, hops)),
-            dma((WEIGHTS, hops)),
-            dma((CHUNKS,)),
-            dma((CHUNKS,)),
-            dma,
-            dma((CHUNKS,)),
-            dma(((tl - 1) * CHUNKS,)),
-            dma(((tl - 1) * CHUNKS,)),
-            dma((tl * CHUNKS,)),
-            dma((tl * CHUNKS,)),
-            dma((2 * nd - 1,)),
-            dma((2 * nd - 1,)),
-            dma,
-        ],
+            pltpu.VMEM((own, width), jnp.bfloat16),
+        ]
+        + [dma(count) if count else dma for count in counts],
         compiler_params=pltpu.CompilerParams(has_side_effects=True),
         cost_estimate=pl.CostEstimate(flops=0, bytes_accessed=250_000_000, transcendentals=0),
-    )(q_weight, key_matrix, value_matrix, o_weight, tokens, gains)
+    )(q_weight, k_weight, v_weight, o_weight, gate, up, down, tokens, cotangent, gains)
 
 
 PIECES = 6
 SUM_ORDER = (
-    "s0", "f0", "s1", "r0", "f1", "s2", "r1", "f2", "s3", "r2", "s4", "r3", "s5", "r4", "r5",
+    "s3", "s4", "s5", "f0", "r3", "s0", "f1", "r4", "r0", "s1", "f2", "r5", "r1", "s2", "r2",
     "a0", "a1", "a2",
 )
 
@@ -388,13 +468,13 @@
     aux = refs[1 : 1 + aux_count]
     refs = refs[1 + aux_count :]
     if carry_weights:
-        weight_rows, refs = refs[0], refs[1:]
+        weight_rows, here_rows, refs = refs[0], refs[1], refs[2:]
     outs = refs[:out_count]
     rest = refs[out_count:]
     if gather:
         full, rest = rest[0], rest[1:]
     if carry_weights:
-        weights, ws, wr, xs, xr, rest = rest[0], *rest[1:5], rest[5:]
+        weights, stage, ws, wr, xs, xr, hi, ho, rest = rest[0], *rest[1:8], rest[8:]
     if gather:
         finished, ls, lr, fs, fr, keep, rest = rest[0], *rest[1:6], rest[6:]
     mine, other, sums, arrivals, cs, cr, loc, ss, sr = rest
@@ -446,30 +526,47 @@
 
     if carry_weights:
         half = weight_rows.shape[0] // 2
-        piece = weight_rows.shape[1] // PIECES
+        far_pieces = PIECES // 2
+        piece = here_rows.shape[1] // far_pieces
 
         def block(j, row):
             return weights.at[rows_at(row, half), pl.ds(j * piece, piece)]
 
+        def given(j, row_part):
+            source = weight_rows if j < far_pieces else here_rows
+            return source.at[pl.ds(row_part * half, half), pl.ds(j % far_pieces * piece, piece)]
+
+        def held_here(j, row_part):
+            return block(j, d * 2 + row_part) if j < far_pieces else given(j, row_part)
+
         def from_far(j, row_part):
             return remote(
-                weight_rows.at[pl.ds(row_part * half, half), pl.ds(j * piece, piece)],
+                given(j, row_part),
                 block(j, d * 2 + row_part),
                 ws.at[j, row_part],
                 wr.at[j, row_part],
                 h=1 - h,
             )
 
-        over_d = Spread(nd, d, block, xs, xr)
+        def here_in():
+            return pltpu.make_async_copy(here_rows, stage, hi)
+
+        def here_out():
+            here = weights.at[rows_at(d, 2 * half), pl.ds(far_pieces * piece, far_pieces * piece)]
+            return pltpu.make_async_copy(stage, here, ho)
+
+        over_d = Spread(nd, d, block, xs, xr, held_here)
 
         def spread(j):
             for row_part in range(2):
-                from_far(j, row_part).wait_recv()
+                if j < far_pieces:
+                    from_far(j, row_part).wait_recv()
                 over_d.send(j, row_part)
 
-        for j in range(PIECES):
+        for j in range(far_pieces):
             for row_part in range(2):
                 from_far(j, row_part).start()
+        here_in().start()
 
     order = list(range(1, tl)) + [0]
     for index in order:
@@ -542,6 +639,8 @@
             "f": lambda k: finish(k, 0),
             "a": pass_across,
         }
+        here_in().wait()
+        here_out().start()
         for step in SUM_ORDER:
             steps[step[0]](int(step[1:]))
     else:
@@ -559,8 +658,10 @@
     if carry_weights:
         for j in range(PIECES):
             over_d.finish(j)
-            for row_part in range(2):
-                from_far(j, row_part).wait_send()
+            if j < far_pieces:
+                for row_part in range(2):
+                    from_far(j, row_part).wait_send()
+        here_out().wait()
     for k in range(CHUNKS):
         for index in range(tl):
             to_core(index, k).wait_send()
@@ -568,7 +669,7 @@
             along(step, k).wait_send()
 
 
-def exchange(collective_id, partial, aux, outs, epilogue, gather, weight_rows=None):
+def exchange(collective_id, partial, aux, outs, epilogue, gather, weight_rows=()):
     nd, tl = lax.axis_size("d"), lax.axis_size("l")
     total, width = partial.shape
     own = total // (2 * tl)
@@ -578,20 +679,21 @@
     out_shape = list(outs)
     out_specs = [vmem] * len(outs)
     scratch = []
-    given = ()
     if gather:
         out_shape.append(jax.ShapeDtypeStruct((total, width), jnp.bfloat16))
         out_specs.append(anywhere)
-    if weight_rows is not None:
-        given = (weight_rows,)
-        rows, cols = weight_rows.shape
-        out_shape.append(jax.ShapeDtypeStruct((nd * rows, cols), jnp.bfloat16))
+    if weight_rows:
+        rows, cols = weight_rows[1].shape
+        out_shape.append(jax.ShapeDtypeStruct((nd * rows, 2 * cols), jnp.bfloat16))
         out_specs.append(anywhere)
         scratch += [
+            pltpu.VMEM((rows, cols), jnp.bfloat16),
             dma((PIECES, 2)),
             dma((PIECES, 2)),
             dma((PIECES, hop_count(nd))),
             dma((PIECES, hop_count(nd))),
+            dma,
+            dma,
         ]
     if gather:
         scratch += [
@@ -615,10 +717,10 @@
     ]
     return pl.pallas_call(
         functools.partial(
-            exchange_kernel, nd, tl, epilogue, len(aux), len(outs), gather, bool(given)
+            exchange_kernel, nd, tl, epilogue, len(aux), len(outs), gather, bool(weight_rows)
         ),
         out_shape=tuple(out_shape),
-        in_specs=[anywhere] + [vmem] * len(aux) + [anywhere] * len(given),
+        in_specs=[anywhere] + [vmem] * len(aux) + [anywhere] * len(weight_rows),
         out_specs=out_specs,
         scratch_shapes=scratch,
         compiler_params=pltpu.CompilerParams(
@@ -627,7 +729,7 @@
         cost_estimate=pl.CostEstimate(
             flops=0, bytes_accessed=200_000_000 if gather else 110_000_000, transcendentals=0
         ),
-    )(partial, *aux, *given)
+    )(partial, *aux, *weight_rows)
 
 
 def gain_kernel(nd, tl, tiles, out, got, send_sem, recv_sem):
@@ -987,12 +1089,15 @@
     return lax.ppermute(values, ("c", "h"), [(0, 0), (1, 2), (2, 1), (3, 3)])
 
 
-def gather_tokens(own, *first):
+def gather_along(own):
     places = lax.axis_size("l")
-    moved = [lax.ppermute(own, "l", shift_perm(places, step)) for step in range(1, places)]
-    parts = [own] + [after(part, *first) for part in moved]
+    return [own] + [lax.ppermute(own, "l", shift_perm(places, step)) for step in range(1, places)]
+
+
+def gather_across(parts):
     half = jnp.concatenate(parts, axis=0)
-    return jnp.concatenate([half, lax.ppermute(half, "c", shift_perm(2, 1))], axis=0)
+    other = lax.ppermute(half, "c", shift_perm(2, 1))
+    return jnp.concatenate([half, other], axis=0)
 
 
 def scatter_tokens(partial, *first):
@@ -1014,16 +1119,6 @@
     return lax.optimization_barrier((value,) + others)[0]
 
 
-def core_halves(shard):
-    core = lax.axis_index("c")
-    half = shard.shape[-1] // 2
-    first, second = shard[..., :half], shard[..., half:]
-    mine = jnp.where(core == 0, first, second)
-    other = lax.ppermute(jnp.where(core == 0, second, first), "c", shift_perm(2, 1))
-    both = jnp.where(core == 0, jnp.stack([mine, other]), jnp.stack([other, mine]))
-    return jnp.moveaxis(both, 0, -3).reshape(shard.shape[:-2] + (2 * shard.shape[-2], half))
-
-
 def return_halves(near, far):
     core = lax.axis_index("c")
     far = lax.ppermute(far, "h", shift_perm(2, 1))
@@ -1056,16 +1151,16 @@
     return values[:, :half], values[:, half:]
 
 
-def scatter_weights(partial):
+def return_blocks(rows):
     core, upper = lax.axis_index("c"), lax.axis_index("h")
-    rows = sum_over_d(partial)
     half = rows.shape[0] // 2
     first, second = rows[:half], rows[half:]
     mine = jnp.where(core == 0, first, second)
     other = lax.ppermute(jnp.where(core == 0, second, first), "c", shift_perm(2, 1))
     same = core == upper
-    far = lax.ppermute(jnp.where(same, other, mine), "h", shift_perm(2, 1))
-    return jnp.where(same, mine, other).astype(jnp.float32) + far.astype(jnp.float32)
+    sent = jnp.where(same, other, mine)
+    far = lax.ppermute(sent, "h", shift_perm(2, 1))
+    return jnp.where(same, mine, other).astype(jnp.float32) + far.astype(jnp.float32), sent
 
 
 def per_device(
@@ -1091,12 +1186,6 @@
     q_cols, kv_cols, ff_cols = q_weight.shape[2], key_matrix.shape[2], gate_weight.shape[2]
     half_cols = ff_cols // 2
 
-    gate_half = core_halves(gate_weight[0])
-    up_half = core_halves(up_weight[0])
-    mid_rows = jnp.concatenate([gate_half, up_half], axis=1)
-    down_rows = core_halves(down_weight[0])
-    down_near = lax.all_gather(down_rows, "d", axis=0, tiled=True)
-
     cut = attn_gain.shape[1]
     head_cut = q_gain.shape[1]
     gains = jnp.concatenate([attn_gain[0], mlp_gain[0], q_gain[0], k_gain[0]]).astype(jnp.float32)
@@ -1112,12 +1201,23 @@
     row_index = (order[:, None] * own_rows + jnp.arange(own_rows, dtype=jnp.int32)[None, :]).reshape(-1)
     labels = labels.reshape(2 * places, own_rows)[order].reshape(-1)
     cosine, sine, first_row = rotary_tables(labels, row_index)
-    qkv_full, o_full, group, gains = enter(
-        q_weight[0], key_matrix[0], value_matrix[0], o_weight[0], after(tokens, mid_rows), gains
-    )
-    mid_near = lax.all_gather(after(mid_rows, group), "d", axis=0, tiled=True)
-    down_far = lax.ppermute(after(down_rows, group), "h", shift_perm(2, 1))
-    cotangent = trade(after(cotangent, group))
+    qkv_full, o_full, mid_rows, down_rows, group, cotangent, gains = enter(
+        q_weight[0],
+        key_matrix[0],
+        value_matrix[0],
+        o_weight[0],
+        gate_weight[0],
+        up_weight[0],
+        down_weight[0],
+        after(tokens, cosine, sine, first_row),
+        cotangent,
+        gains,
+    )
+    mid_near = lax.all_gather(mid_rows, "d", axis=0, tiled=True)
+    down_near = lax.all_gather(down_rows, "d", axis=0, tiled=True)
+    up_far = lax.ppermute(mid_rows[:, half_cols:], "h", shift_perm(2, 1))
+    down_far = lax.ppermute(down_rows, "h", shift_perm(2, 1))
+    grad_half = gather_along(cotangent)
     gains = gains.reshape(gains.shape[0], -1)
     attn_scale = gains[:, :cut].reshape(-1)
     mlp_scale = gains[:, cut : 2 * cut].reshape(-1)
@@ -1132,7 +1232,8 @@
     query_reduced, key_reduced, value_reduced, attended, totals = attention(
         qkv, tables, order, head_count, kv_heads
     )
-    down_far = lax.all_gather(after(down_far, attended), "d", axis=0, tiled=True)
+
+    grad_rows = gather_across([grad_half[0]] + [after(part, attended) for part in grad_half[1:]])
 
     def whole(values):
         return jax.ShapeDtypeStruct((own_rows, width), values)
@@ -1145,9 +1246,9 @@
         (whole(jnp.float32),),
         middle_rows,
         True,
-        mid_rows,
-    )
-    cotangent = after(cotangent, normed_mid)
+        (mid_rows, after(up_far, attended)),
+    )
+    down_far = lax.all_gather(after(down_far, normed_mid), "d", axis=0, tiled=True)
 
     mid = jnp.dot(normed_mid, mid_near, preferred_element_type=jnp.float32)
     gate_near, up_near = split(mid)
@@ -1155,7 +1256,6 @@
     mid = jnp.dot(normed_mid, mid_far, preferred_element_type=jnp.float32)
     gate_far, up_far = split(mid)
     hidden_far = swiglu(gate_far, up_far).astype(jnp.bfloat16)
-    grad_rows = gather_tokens(cotangent, hidden_near, hidden_far)
     down_partial = jnp.concatenate(
         [
             contract_rows(grad_rows, hidden_near).astype(jnp.bfloat16),
@@ -1192,7 +1292,9 @@
     mid_grad_near = contract_rows(normed_mid, after(mid_back_near, grad_rows)).astype(jnp.bfloat16)
     mid_sum_near = sum_over_d(mid_grad_near)
 
-    grad_rows = after(grad_rows, mid_grad_near)
+    hidden_near = after(hidden_near, mid_grad_near)
+    branch = contract_cols(hidden_near, down_near) + contract_cols(hidden_far, down_far)
+    grad_rows = after(grad_rows, branch)
     out_grad = jnp.dot(grad_rows, o_full, preferred_element_type=jnp.float32).astype(jnp.bfloat16)
     o_wgrad = contract_rows(grad_rows, attended)
     query_back, key_back, value_back, q_gain_grad, k_gain_grad = attention_pull(
@@ -1206,9 +1308,10 @@
     )
     qkv_back = jnp.concatenate([query_back, key_back, value_back], axis=1)
     qkv_grad = contract_rows(normed, qkv_back).astype(jnp.bfloat16)
-    attn_grad = scatter_weights(
-        after(jnp.concatenate([qkv_grad, o_wgrad.astype(jnp.bfloat16)], axis=1), mid_sum_far)
-    )
+    attn_partial = jnp.concatenate([qkv_grad, o_wgrad.astype(jnp.bfloat16)], axis=1)
+    attn_rows = sum_over_d(after(attn_partial, mid_sum_far))
+    branch = scatter_tokens(branch, qkv_grad)
+    activations = trade((middle + branch).astype(jnp.bfloat16))
     gradient, moved, attn_gain_grad = exchange(
         3,
         contract_cols(after(qkv_back, qkv_grad), qkv_full).astype(jnp.bfloat16),
@@ -1217,21 +1320,6 @@
         stream_pull_rows,
         False,
     )
-    moved = trade(moved)
-    gradient = jnp.where(core == lax.axis_index("h"), gradient, moved.astype(jnp.float32))
-
-    hidden_near = after(hidden_near, attn_gain_grad)
-    branch = scatter_tokens(
-        contract_cols(hidden_near, down_near) + contract_cols(hidden_far, down_far)
-    )
-    activations = trade((middle + branch).astype(jnp.bfloat16))
-
-    split_at = down_rows.shape[1]
-    down_grad = columns_of(*return_halves(down_grads[:, :split_at], down_grads[:, split_at:]))
-    mine, other = return_halves(mid_sum_near, mid_sum_far)
-    gate_grad = columns_of(mine[:, :half_cols], other[:, :half_cols])
-    up_grad = columns_of(mine[:, half_cols:], other[:, half_cols:])
-
     devices = gains.shape[0]
     sums = jnp.concatenate(
         [
@@ -1242,6 +1330,18 @@
     )
     sums = jnp.pad(sums, ((0, 0), (0, 1024 - sums.shape[1]))).reshape(devices, 8, 128)
     sums = gain_total(sums).reshape(1, -1)
+    moved = trade(moved)
+    gradient = jnp.where(core == lax.axis_index("h"), gradient, moved.astype(jnp.float32))
+
+
+    attn_grad, attn_sent = return_blocks(after(attn_rows, attn_gain_grad))
+    activations = after(activations, attn_sent)
+    mid_sum_near = after(mid_sum_near, attn_sent)
+    split_at = down_rows.shape[1]
+    down_grad = columns_of(*return_halves(down_grads[:, :split_at], down_grads[:, split_at:]))
+    mine, other = return_halves(mid_sum_near, mid_sum_far)
+    gate_grad = columns_of(mine[:, :half_cols], other[:, :half_cols])
+    up_grad = columns_of(mine[:, half_cols:], other[:, half_cols:])
 
     return (
         activations,

time: 870 us -> 837 us (0.962)
  waiting for transfers between devices: 200 us -> 169 us
    ppermute x2, waiting for transfers between devices: 138 us -> 104 us  [return_halves(): far = lax.ppermute(far, 'h', shift_perm(2, 1))]
    pallas_call x3, Pallas kernels: 197 us -> 179 us  [exchange(): pl.pallas_call(functools.partial(exchange_kernel, nd, tl, epilogue, len(a...]
    ppermute x8 -> x6, waiting for transfers between devices: 47 us -> 63.7 us  [the longest x1 27 us: gather_along(): lax.ppermute(own, 'l', shift_perm(places, step))]
    pallas_call x1, Pallas kernels: 80.3 us -> 95 us  [enter(): pl.pallas_call(functools.partial(entry_kernel, nd, tl), name='entry', out...]
    pallas_call x1, Pallas kernels: 21.9 us -> 34.9 us  [gain_total(): pl.pallas_call(functools.partial(gain_kernel, nd, tl), name='gain_total',...]
    all_gather x1, waiting for transfers between devices: 10.2 us -> 0.02 us  [per_device(): down_near = lax.all_gather(down_rows, 'd', axis=0, tiled=True)]
    unnamed x149 -> x128, local copies, waits for them, and re-layouts: 33.9 us -> 34.5 us
  transfers between devices with their start and end apart: 25 -> 22, of which waited for: 9 -> 5; matrix products, arithmetic and copies ran while one was open for 28% -> 28% of each run, Pallas kernels for 32% -> 32%
where the time goes in v7:
time: 837 us; the launch traced here: 831 us
  Pallas kernels  363 us (43%)
  waiting for transfers between devices  169 us (20%)
  matrix products  154 us (18%)
  local copies, waits for them, and re-layouts  59.5 us (7%)
  other arithmetic  47.7 us (6%)
  starting transfers between devices  23.3 us (3%)
  between operations  15.3 us (2%)
    pallas_call x3, Pallas kernels, exchange(): pl.pallas_call(functools.partial(exchange_kernel, nd, tl, epilogue, len(a...  179 us
    ppermute x2, waiting for transfers between devices, return_halves(): far = lax.ppermute(far, 'h', shift_perm(2, 1))  104 us
    pallas_call x1, Pallas kernels, enter(): pl.pallas_call(functools.partial(entry_kernel, nd, tl), name='entry', out...  95 us
    dot_general x6, matrix products, contract_cols(): lax.dot_general(left, right, (((1,), (1,)), ((), ())), preferred_element_...  53.7 us
    dot_general x6, matrix products, contract_rows(): lax.dot_general(left, right, (((0,), (0,)), ((), ())), preferred_element_...  45.8 us
    pallas_call x1, Pallas kernels, gain_total(): pl.pallas_call(functools.partial(gain_kernel, nd, tl), name='gain_total',...  34.9 us
    unnamed x128, local copies, waits for them, and re-layouts  34.5 us
    pallas_call x1, Pallas kernels, attention_pull(): pl.pallas_call(functools.partial(attention_pull_kernel, blocks, repeat),...  34 us
  transfers between devices with their start and end apart: 22, of which 5 were waited for; matrix products, arithmetic and copies ran while one was open for 28% of the time, Pallas kernels for 32%

profile of v7, /device:TPU:0, one launch (start us, length us, event | category | flops | bytes accessed | tf_op | source)
XLA Modules:
  0.0 831.3 jit_solution(18013239062694152775)
XLA Ops:
  7.2 1.3 collective-permute-start
  12.6 2.1 fusion.16
  15.2 95.0 %entry.1 = (bf16[2048,1024]{1,0:T(8,128)(2,1)}, bf16[2048,512]{1,0:T(8,128)(2,1)}, bf16[512,1536]{1,0:T(8,128)(2,1)}, bf16[512,768]{1,0:T(8,128)(2,1)}, bf16[115...) custom-call(bf16[256,512]{1,0:T(8,128)(2,1)} %bitcast.100, bf16[256,256]{1,0:T(8,128)(2,1)} %bitcast.102, ...), custom_call_target="tpu_custom_call" | custom-call | bytes 250000000 | tf_op jit(solution)/shard_map/entry/pallas_call | solution.py:433
  110.9 2.3 slice.115
  114.0 3.0 collective-permute-start.1
  117.0 1.3 slice.113.refs_1_
  118.4 4.2 fusion
  123.3 9.1 %fusion.14.refs_0_.refs_1_.refs_2_ = f32[1152,1024]{1,0:T(8,128)} fusion(bf16[2048,1024]{1,0:T(8,128)(2,1)} %get-tuple-element.57, bf16[1152,2048]{1,0:T(8,128)(2,1)S(1)} %copy-done.21, f32[2048]{0:T(1024)S(1)} %bitcast.110, f32[1152]{0:T(1024)S(1)} %add_rsqrt_fusion), kind=kOutput, calls=%fused_computation.53 | convolution fusion | flops 4841275392 | bytes 13644288 | tf_op jit(solution)/shard_map/dot_general | solution.py:1230
  132.5 20.1 %attention.1 = (bf16[1152,512]{1,0:T(8,128)(2,1)}, bf16[1152,256]{1,0:T(8,128)(2,1)S(1)}, bf16[1152,256]{1,0:T(8,128)(2,1)S(1)}, bf16[1152,512]{1,0:T(8,128)(2,1)}, f32[1152,256]{1,0:T(8,128)}) custom-call(s32[4]{0:T(128)S(1)} %get-tuple-element.135.order_ref, f32[1152,1024]{1,0:T(8,128)} %fusion.14.refs_0_.refs_1_.refs_2_, ...), custom_call_target="tpu_custom_call" | custom-call | flops 2717908992 | bytes 60000000 | tf_op jit(solution)/shard_map/attention/pallas_call | solution.py:939
  152.6 6.0 convolution_convert_fusion.3.refs_0_
  158.7 10.2 %collective-permute-done.1.refs_4_ = bf16[512,768]{1,0:T(8,128)(2,1)} collective-permute-done((bf16[512,768]{1,0:T(8,128)(2,1)}, bf16[512,768]{1,0:T(8,128)(2,1)}, u32[]{:S(2)}, u32[]{:S(2)}) %collective-permute-start.1) | collective-permute-done | bytes 786464 | tf_op jit(solution)/shard_map/ppermute | solution.py:1218
  168.8 89.4 %shard_map.237 = (f32[288,2048]{1,0:T(8,128)S(1)}, bf16[1152,2048]{1,0:T(8,128)(2,1)S(1)}, bf16[2048,1536]{1,0:T(8,128)(2,1)}) custom-call(bf16[1152,2048]{1,0:T(8,128)(2,1)} %convolution_convert_fusion.3.refs_0_, bf16[288,2048]{1,0:T(8,128)(2,1)S(1)} %slice.113.refs_1_, f32[1,2048]{1,0:T(1,128)S(1)} %bitcast.90, bf16[512,1536]{1,0:T(8,128)(2,1)S(1)} %copy-done.1, ...), custom_call_target="tpu_custom_call" | custom-call | bytes 200000000 | tf_op jit(solution)/shard_map/pallas_call | solution.py:718
  258.3 1.5 copy-done.2
  259.7 2.2 copy-done.13
  263.4 27.0 %collective-permute-done.2 = bf16[288,2048]{1,0:T(8,128)(2,1)} collective-permute-done((bf16[288,2048]{1,0:T(8,128)(2,1)S(1)}, bf16[288,2048]{1,0:T(8,128)(2,1)}, u32[]{:S(2)}, u32[]{:S(2)}) %collective-permute-start.2) | collective-permute-done | bytes 1179680 | tf_op jit(solution)/shard_map/ppermute | solution.py:1094
  290.5 1.5 pad_maximum_fusion.4
  292.0 9.7 %fusion.35 = f32[1152,1536]{1,0:T(8,128)S(1)} fusion(bf16[1152,2048]{1,0:T(8,128)(2,1)S(1)} %copy-done.14, bf16[2048,1536]{1,0:T(8,128)(2,1)} %get-tuple-element.66), kind=kOutput, calls=%fused_computation.122 | convolution fusion | flops 7247757312 | bytes 18087936 | tf_op jit(solution)/shard_map/dot_general | solution.py:1256
  302.8 1.8 copy-done.23
  304.7 2.0 constant_dynamic-update-slice_fusion.1
  307.0 2.2 copy-done.35
  309.1 5.8 convolution_convert_fusion.5
  314.9 11.3 %fusion.34 = f32[1152,1536]{1,0:T(8,128)S(1)} fusion(bf16[1152,2048]{1,0:T(8,128)(2,1)} %copy-done.13, bf16[2048,1536]{1,0:T(8,128)(2,1)} %all-gather.4.cloned.1.call-done), kind=kOutput, calls=%fused_computation.121 | convolution fusion | flops 7247757312 | bytes 18087936 | tf_op jit(solution)/shard_map/dot_general | solution.py:1253
  327.3 2.5 copy-done.22
  331.1 4.8 convolution_convert_fusion.6
  335.9 3.7 pad_maximum_fusion
  339.7 10.2 %fusion.8 = (bf16[1152,768]{1,0:T(8,128)(2,1)S(1)}, bf16[1152,768]{1,0:T(8,128)(2,1)S(1)}) fusion(f32[1152,1536]{1,0:T(8,128)} %copy-done.23, bf16[1152,2048]{1,0:T(8,128)(2,1)} %copy-done.35, bf16[2048,768]{1,0:T(8,128)(2,1)} %all-gather.8.cloned.1.call-done), kind=kOutput, calls=%fused_computation.24 | convolution fusion | flops 3636264960 | bytes 18481152 | tf_op jit(solution)/shard_map/dot_general | solution.py:1270
  351.7 12.7 %convolution_convert_fusion.2 = bf16[2048,1536]{0,1:T(8,128)(2,1)} fusion(bf16[1152,2048]{1,0:T(8,128)(2,1)} %copy-done.13, bf16[1152,768]{1,0:T(8,128)(2,1)S(1)} %get-tuple-element.137, bf16[1152,768]{1,0:T(8,128)(2,1)S(1)} %get-tuple-element.136), kind=kOutput, calls=%fused_computation.10 | convolution fusion | flops 7257980928 | bytes 14548992 | tf_op jit(solution)/shard_map/dot_general | solution.py:47
  365.0 10.2 %fusion.5 = (bf16[1152,768]{1,0:T(8,128)(2,1)S(1)}, bf16[1152,768]{1,0:T(8,128)(2,1)S(1)}) fusion(f32[1152,1536]{1,0:T(8,128)} %copy-done.22, bf16[1152,2048]{1,0:T(8,128)(2,1)} %copy-done.35, bf16[2048,768]{1,0:T(8,128)(2,1)} %all-gather.6.cloned.1.call-done), kind=kOutput, calls=%fused_computation.21 | convolution fusion | flops 3636264960 | bytes 18481152 | tf_op jit(solution)/shard_map/dot_general | solution.py:1270
  376.4 12.3 %fusion.30 = f32[1152,2048]{1,0:T(8,128)} fusion(bf16[2048,1536]{1,0:T(8,128)(2,1)} %all-gather.4.cloned.1.call-done, bf16[1152,768]{1,0:T(8,128)(2,1)S(1)} %get-tuple-element.139, bf16[1152,768]{1,0:T(8,128)(2,1)S(1)} %get-tuple-element.138), kind=kOutput, calls=%fused_computation.117 | convolution fusion | flops 7254835200 | bytes 19267584 | tf_op jit(solution)/shard_map/dot_general | solution.py:53
  388.7 13.4 %add_convert_fusion.refs_0_ = bf16[1152,2048]{1,0:T(8,128)(2,1)} fusion(f32[1152,2048]{1,0:T(8,128)} %fusion.30, bf16[2048,1536]{1,0:T(8,128)(2,1)} %get-tuple-element.66, bf16[1152,768]{1,0:T(8,128)(2,1)S(1)} %copy-done.50, bf16[1152,768]{1,0:T(8,128)(2,1)S(1)} %copy-done.48), kind=kOutput, calls=%fused_computation.6 | convolution fusion | flops 7259553792 | bytes 23986176 | tf_op jit(solution)/shard_map/dot_general | solution.py:53
  402.1 57.2 %shard_map.238 = (f32[288,2048]{1,0:T(8,128)S(1)}, f32[1,2048]{1,0:T(1,128)S(1)}, bf16[1152,2048]{1,0:T(8,128)(2,1)S(1)}) custom-call(bf16[1152,2048]{1,0:T(8,128)(2,1)} %add_convert_fusion.refs_0_, f32[288,2048]{1,0:T(8,128)S(1)} %copy-done.3, bf16[288,2048]{1,0:T(8,128)(2,1)S(1)} %copy-done, f32[1,2048]{1,0:T(1,128)S(1)} %bitcast.91), custom_call_target="tpu_custom_call" | custom-call | bytes 200000000 | tf_op jit(solution)/shard_map/pallas_call | solution.py:718
  459.4 3.2 pad_maximum_fusion.2
  462.6 10.3 %convolution_convert_fusion.1 = bf16[2048,1536]{0,1:T(8,128)(2,1)} fusion(bf16[1152,2048]{1,0:T(8,128)(2,1)S(1)} %bitcast.94, bf16[1152,1536]{1,0:T(8,128)(2,1)S(1)} %pad_maximum_fusion.2), kind=kOutput, calls=%fused_computation.9 | convolution fusion | flops 7250903040 | bytes 14548992 | tf_op jit(solution)/shard_map/dot_general | solution.py:47
  472.9 6.4 fusion.36
  479.4 6.8 convolution_add_fusion
  486.2 3.6 convolution_convert_fusion.8.refs_11_
  489.8 34.0 %attention_pull.1 = (bf16[1152,512]{1,0:T(8,128)(2,1)}, bf16[1152,256]{1,0:T(8,128)(2,1)}, bf16[1152,256]{1,0:T(8,128)(2,1)}, f32[8,128]{1,0:T(8,128)}, f32[8,128]{1,0:T(8,128)}) custom-call(s32[4]{0:T(128)} %copy-done.12, f32[1152,1024]{1,0:T(8,128)} %fusion.14.refs_0_.refs_1_.refs_2_, f32[1152,1024]{1,0:T(8,128)} %fusion.14.refs_0_.refs_1_.refs_2_, ...), custom_call_target="tpu_custom_call" | custom-call | flops 6794772480 | bytes 120000000 | tf_op jit(solution)/shard_map/attention_pull/pallas_call | solution.py:1045
  523.9 1.6 constant_dynamic-update-slice_fusion.5
  526.7 3.2 convolution_convert_fusion.7
  529.9 9.1 %convolution_convert_fusion.4 = bf16[2048,1024]{0,1:T(8,128)(2,1)S(1)} fusion(bf16[1152,1024]{1,0:T(8,128)(2,1)S(1)} %constant_dynamic-update-slice_fusion.3, bf16[1152,2048]{1,0:T(8,128)(2,1)} %get-tuple-element.55, f32[2048]{0:T(1024)S(1)} %bitcast.111, f32[1152]{0:T(1024)S(1)} %copy-done.42), kind=kOutput, calls=%fused_computation.18 | convolution fusion | flops 4843372544 | bytes 11284992 | tf_op jit(solution)/shard_map/dot_general | solution.py:47
  539.0 3.4 pad_maximum_fusion.1
  543.3 4.3 slice.248
  547.8 8.8 %convolution_convert_fusion.refs_0_ = bf16[1152,2048]{1,0:T(8,128)(2,1)S(1)} fusion(bf16[1152,1024]{1,0:T(8,128)(2,1)S(1)} %copy-done.33, bf16[2048,1024]{1,0:T(8,128)(2,1)} %get-tuple-element.57), kind=kOutput, calls=%fused_computation.8 | convolution fusion | flops 4834197504 | bytes 11272192 | tf_op jit(solution)/shard_map/dot_general | solution.py:53
  556.6 32.0 %shard_map.239 = (f32[288,2048]{1,0:T(8,128)S(1)}, bf16[288,2048]{1,0:T(8,128)(2,1)}, f32[1,2048]{1,0:T(1,128)S(1)}) custom-call(bf16[1152,2048]{1,0:T(8,128)(2,1)S(1)} %convolution_convert_fusion.refs_0_, bf16[288,2048]{1,0:T(8,128)(2,1)S(1)} %slice.113.refs_1_, f32[288,2048]{1,0:T(8,128)S(1)} %copy-done.7, f32[1,2048]{1,0:T(1,128)S(1)} %bitcast.92), custom_call_target="tpu_custom_call" | custom-call | bytes 110000000 | tf_op jit(solution)/shard_map/pallas_call | solution.py:718
  588.6 1.9 collective-permute-start.9
  591.7 6.6 slice_add_fusion
  598.3 2.9 slice.249
  601.2 1.4 collective-permute-start.6
  612.3 34.9 %gain_total.1 = f32[8,128]{1,0:T(8,128)} custom-call(f32[8,8,128]{2,1,0:T(8,128)} %bitcast.104), custom_call_target="tpu_custom_call" | custom-call | bytes 40000000 | tf_op jit(solution)/shard_map/gain_total/pallas_call | solution.py:777
  651.2 1.7 convert_select_fusion
  652.9 2.9 collective-permute-start.11
  655.8 62.8 %collective-permute-done.13 = bf16[512,768]{0,1:T(8,128)(2,1)S(1)} collective-permute-done((bf16[512,768]{0,1:T(8,128)(2,1)S(1)}, bf16[512,768]{0,1:T(8,128)(2,1)S(1)}, u32[]{:S(2)}, u32[]{:S(2)}) %collective-permute-start.13) | collective-permute-done | bytes 786464 | tf_op jit(solution)/shard_map/ppermute | solution.py:1124
  720.2 2.3 broadcast_select_fusion.1
  723.0 3.6 fusion.12
  726.5 10.4 %collective-permute-start.7 = (bf16[288,2048]{1,0:T(8,128)(2,1)}, bf16[288,2048]{1,0:T(8,128)(2,1)}, u32[]{:S(2)}, u32[]{:S(2)}) collective-permute-start(bf16[288,2048]{1,0:T(8,128)(2,1)} %fusion.12), channel_id=1, source_target_pairs={{0,0},{2,4},{4,2},{6,6},{1,1},{3,5},{5,3},{7,7},{8,8},{10,12},{12,... | collective-permute-start | bytes 3538952 | tf_op jit(solution)/shard_map/ppermute | solution.py:1089
  737.2 1.6 copy.69
  738.8 2.1 broadcast_select_fusion.2
  740.9 41.0 %collective-permute-done.11 = bf16[512,1536]{0,1:T(8,128)(2,1)} collective-permute-done((bf16[512,1536]{0,1:T(8,128)(2,1)}, bf16[512,1536]{0,1:T(8,128)(2,1)}, u32[]{:S(2)}, u32[]{:S(2)}) %collective-permute-start.11) | collective-permute-done | bytes 1572896 | tf_op jit(solution)/shard_map/ppermute | solution.py:1124
  781.9 2.3 convert_add_fusion
  784.7 26.5 %collective-permute-done.10 = bf16[256,1536]{0,1:T(8,128)(2,1)S(1)} collective-permute-done((bf16[256,1536]{0,1:T(8,128)(2,1)}, bf16[256,1536]{0,1:T(8,128)(2,1)S(1)}, u32[]{:S(2)}, u32[]{:S(2)}) %collective-permute-start.10) | collective-permute-done | bytes 786464 | tf_op jit(solution)/shard_map/ppermute | solution.py:1162
  813.8 1.6 copy.68
  815.6 1.6 copy.67
  817.2 2.0 copy.63
  821.9 2.4 copy.88
  (211 shorter events, 40.9 us)
Async XLA Ops:
  7.2 307.7 %all-gather.4.cloned.1.call-start = ((), (), s32[]{:S(2)}) async-start(), calls=%async_computation.4 | async-start | bytes 7864320 | tf_op jit(solution)/shard_map/all_gather | solution.py:1216
  7.2 4.4 collective-permute-start
  8.7 123.7 %copy-start.12 = (s32[4]{0:T(128)}, s32[4]{0:T(128)S(1)}, u32[]{:S(2)}) copy-start(s32[4]{0:T(128)S(1)} %get-tuple-element.135.order_ref) | copy-start | bytes 52
  15.2 117.3 %copy-start.8 = (f32[1152,128]{1,0:T(8,128)}, f32[1152,128]{1,0:T(8,128)S(1)}, u32[]{:S(2)}) copy-start(f32[1152,128]{1,0:T(8,128)S(1)} %get-tuple-element.162.refs_3_.refs_2_) | copy-start | bytes 1769476
  15.2 117.3 %copy-start.9 = (f32[1152,128]{1,0:T(8,128)}, f32[1152,128]{1,0:T(8,128)S(1)}, u32[]{:S(2)}) copy-start(f32[1152,128]{1,0:T(8,128)S(1)} %get-tuple-element.163.refs_4_.refs_3_) | copy-start | bytes 1769476
  110.3 229.4 %all-gather.8.cloned.1.call-start = ((), (), s32[]{:S(2)}) async-start(), calls=%async_computation.6 | async-start | bytes 3932160 | tf_op jit(solution)/shard_map/all_gather | solution.py:1251
  110.8 21.7 %copy-start.5 = (s32[1152,1]{1,0:T(8,128)}, s32[1152,1]{1,0:T(8,128)S(1)}, u32[]{:S(2)}) copy-start(s32[1152,1]{1,0:T(8,128)S(1)} %copy.55.refs_7_.refs_6_) | copy-start | bytes 13828
  113.8 8.9 %copy-start.39 = (f32[1,2,8,128]{3,1,2,0:T(2,128)}, f32[1,2,8,128]{3,1,2,0:T(2,128)S(1)}, u32[]{:S(2)}) copy-start(f32[1,2,8,128]{3,1,2,0:T(2,128)S(1)} %copy.75) | copy-start | bytes 24580
  113.9 18.6 %copy-start.10 = (f32[1,128]{1,0:T(1,128)}, f32[1,128]{1,0:T(1,128)S(1)}, u32[]{:S(2)}) copy-start(f32[1,128]{1,0:T(1,128)S(1)} %reshape_reshape.11.refs_5_.refs_4_) | copy-start | bytes 1540
  114.0 18.5 %copy-start.11 = (f32[1,128]{1,0:T(1,128)}, f32[1,128]{1,0:T(1,128)S(1)}, u32[]{:S(2)}) copy-start(f32[1,128]{1,0:T(1,128)S(1)} %reshape_reshape.12.refs_6_.refs_5_) | copy-start | bytes 1540
  114.0 54.8 %collective-permute-start.1 = (bf16[512,768]{1,0:T(8,128)(2,1)}, bf16[512,768]{1,0:T(8,128)(2,1)}, u32[]{:S(2)}, u32[]{:S(2)}) collective-permute-start(bf16[512,768]{1,0:T(8,128)(2,1)} %slice.115), channel_id=1, source_target_pairs={{2,0},{0,2},{3,1},{1,3},{6,4},{4,6},{7,5},{5,7},{10,8},{8,10},{11,... | collective-permute-start | bytes 2359304 | tf_op jit(solution)/shard_map/ppermute | solution.py:1218
  118.3 5.0 copy-start.21
  118.4 143.6 %collective-permute-start.4 = (bf16[512,768]{1,0:T(8,128)(2,1)}, bf16[512,768]{1,0:T(8,128)(2,1)}, u32[]{:S(2)}, u32[]{:S(2)}) collective-permute-start(bf16[512,768]{1,0:T(8,128)(2,1)} %get-tuple-element.68), channel_id=1, source_target_pairs={{2,0},{0,2},{3,1},{1,3},{6,4},{4,6},{7,5},{5,7},{10,8},{8,10},{11,... | collective-permute-start | bytes 2359304 | tf_op jit(solution)/shard_map/ppermute | solution.py:1219
  122.7 9.8 %copy-start.41 = (f32[1152]{0:T(1024)}, f32[1152]{0:T(1024)S(1)}, u32[]{:S(2)}) copy-start(f32[1152]{0:T(1024)S(1)} %add_rsqrt_fusion) | copy-start | bytes 13828
  132.5 20.1 %copy-start.44 = (bf16[2048,512]{1,0:T(8,128)(2,1)S(1)}, bf16[2048,512]{1,0:T(8,128)(2,1)}, u32[]{:S(2)}) copy-start(bf16[2048,512]{1,0:T(8,128)(2,1)} %get-tuple-element.59) | copy-start | bytes 6291460
  152.6 6.1 copy-start.16
  152.6 6.1 copy-start.17
  152.6 16.2 %copy-start.1 = (bf16[512,1536]{1,0:T(8,128)(2,1)S(1)}, bf16[512,1536]{1,0:T(8,128)(2,1)}, u32[]{:S(2)}) copy-start(bf16[512,1536]{1,0:T(8,128)(2,1)} %get-tuple-element.60.refs_3_) | copy-start | bytes 4718596
  168.8 93.2 %copy-start = (bf16[288,2048]{1,0:T(8,128)(2,1)S(1)}, bf16[288,2048]{1,0:T(8,128)(2,1)}, u32[]{:S(2)}) copy-start(bf16[288,2048]{1,0:T(8,128)(2,1)} %get-tuple-element.64.refs_2_) | copy-start | bytes 3538948
  262.0 103.0 %all-gather.6.cloned.1.call-start = ((), (), s32[]{:S(2)}) async-start(), calls=%async_computation.5 | async-start | bytes 3932160 | tf_op jit(solution)/shard_map/all_gather | solution.py:1217
  262.0 28.4 %collective-permute-start.2 = (bf16[288,2048]{1,0:T(8,128)(2,1)S(1)}, bf16[288,2048]{1,0:T(8,128)(2,1)}, u32[]{:S(2)}, u32[]{:S(2)}) collective-permute-start(bf16[288,2048]{1,0:T(8,128)(2,1)S(1)} %copy-done), channel_id=1, source_target_pairs={{1,0},{0,1},{3,2},{2,3},{5,4},{4,5},{7,6},{6,7},{9,8},{8,9},{11,10... | collective-permute-start | bytes 3538952 | tf_op jit(solution)/shard_map/ppermute | solution.py:1094
  262.7 279.7 %reduce-scatter.5.cloned.1.call-start = ((), (), s32[]{:S(2)}) async-start(), calls=%async_computation.7 | async-start | bytes 7864320 | tf_op jit(solution)/shard_map/reduce_scatter | solution.py:1142
  263.3 28.7 %copy-start.14 = (bf16[1152,2048]{1,0:T(8,128)(2,1)S(1)}, bf16[1152,2048]{1,0:T(8,128)(2,1)}, u32[]{:S(2)}) copy-start(bf16[1152,2048]{1,0:T(8,128)(2,1)} %copy-done.13) | copy-start | bytes 14155780
  291.9 14.7 %collective-permute-start.3 = (bf16[576,2048]{1,0:T(8,128)(2,1)S(1)}, bf16[576,2048]{1,0:T(8,128)(2,1)S(1)}, u32[]{:S(2)}, u32[]{:S(2)}) collective-permute-start(bf16[576,2048]{1,0:T(8,128)(2,1)S(1)} %pad_maximum_fusion.4), channel_id=1, source_target_pairs={{4,0},{0,4},{5,1},{1,5},{6,2},{2,6},{7,3},{3,7},{12,8},{8,12},{13,... | collective-permute-start | bytes 7077896 | tf_op jit(solution)/shard_map/ppermute | solution.py:1099
  326.2 3.6 copy-start.22
  326.2 4.9 copy-start.36
  331.1 4.8 copy-start.29
  331.1 4.8 copy-start.24
  364.4 284.2 %reduce-scatter.11.cloned.1.call-start = ((), (), s32[]{:S(2)}) async-start(), calls=%async_computation.10 | async-start | bytes 7864320 | tf_op jit(solution)/shard_map/reduce_scatter | solution.py:1142
  365.0 355.2 %reduce-scatter.7.cloned.1.call-start = ((), (), s32[]{:S(2)}) async-start(), calls=%async_computation.8 | async-start | bytes 7864320 | tf_op jit(solution)/shard_map/reduce_scatter | solution.py:1142
  376.4 12.3 %copy-start.48 = (bf16[1152,768]{1,0:T(8,128)(2,1)S(1)}, bf16[1152,768]{1,0:T(8,128)(2,1)}, u32[]{:S(2)}) copy-start(bf16[1152,768]{1,0:T(8,128)(2,1)} %copy-done.47) | copy-start | bytes 5308420
  376.4 12.3 %copy-start.50 = (bf16[1152,768]{1,0:T(8,128)(2,1)S(1)}, bf16[1152,768]{1,0:T(8,128)(2,1)}, u32[]{:S(2)}) copy-start(bf16[1152,768]{1,0:T(8,128)(2,1)} %copy-done.49) | copy-start | bytes 5308420
  376.4 86.2 %slice-start = ((s8[4718592]{0:T(1024)(128)(4,1)}), s8[4194304]{0:T(1024)(128)(4,1)S(1)}, s32[]{:S(2)}) async-start(s8[4718592]{0:T(1024)(128)(4,1)} %bitcast.93), calls=%async_computation.11 | async-start | bytes 8388608
  388.7 13.4 %copy-start.3 = (f32[288,2048]{1,0:T(8,128)S(1)}, f32[288,2048]{1,0:T(8,128)}, u32[]{:S(2)}) copy-start(f32[288,2048]{1,0:T(8,128)} %copy-done.2) | copy-start | bytes 7077892
  388.7 73.9 %slice-start.1 = ((s8[4718592]{0:T(1024)(128)(4,1)}), s8[524288]{0:T(1024)(128)(4,1)S(1)}, s32[]{:S(2)}) async-start(s8[4718592]{0:T(1024)(128)(4,1)} %bitcast.93), calls=%async_computation.12 | async-start | bytes 1048576
  459.4 3.2 copy-start.6
  459.4 3.2 copy-start.15
  472.9 6.5 copy-start.28
  472.9 6.5 copy-start.43
  472.9 13.3 %slice-start.2 = ((s8[4718592]{0:T(1024)(128)(4,1)}), s8[4194304]{0:T(1024)(128)(4,1)S(1)}, s32[]{:S(2)}) async-start(s8[4718592]{0:T(1024)(128)(4,1)} %bitcast.95), calls=%async_computation.13 | async-start | bytes 8388608
  479.4 6.8 slice-start.3
  479.4 6.8 copy-start.45
  526.7 3.2 copy-start.32
  526.7 3.2 copy-start.40
  526.7 3.2 copy-start.42
  542.5 198.4 %reduce-scatter.9.cloned.1.call-start = ((), (), s32[]{:S(2)}) async-start(), calls=%async_computation.9 | async-start | bytes 7864320 | tf_op jit(solution)/shard_map/reduce_scatter | solution.py:1142
  543.2 4.6 copy-start.37
  543.3 4.6 copy-start.33
  547.5 44.2 %collective-permute-start.5 = (bf16[576,2048]{1,0:T(8,128)(2,1)}, bf16[576,2048]{1,0:T(8,128)(2,1)}, u32[]{:S(2)}, u32[]{:S(2)}) collective-permute-start(bf16[576,2048]{1,0:T(8,128)(2,1)} %slice.248), channel_id=1, source_target_pairs={{4,0},{0,4},{5,1},{1,5},{6,2},{2,6},{7,3},{3,7},{12,8},{8,12},{13,... | collective-permute-start | bytes 7077896 | tf_op jit(solution)/shard_map/ppermute | solution.py:1107
  547.8 8.8 %copy-start.7 = (f32[288,2048]{1,0:T(8,128)S(1)}, f32[288,2048]{1,0:T(8,128)}, u32[]{:S(2)}) copy-start(f32[288,2048]{1,0:T(8,128)} %copy-done.6) | copy-start | bytes 7077892
  588.6 62.7 %collective-permute-start.9 = (bf16[288,2048]{1,0:T(8,128)(2,1)}, bf16[288,2048]{1,0:T(8,128)(2,1)S(1)}, u32[]{:S(2)}, u32[]{:S(2)}) collective-permute-start(bf16[288,2048]{1,0:T(8,128)(2,1)} %get-tuple-element.90), channel_id=1, source_target_pairs={{0,0},{2,4},{4,2},{6,6},{1,1},{3,5},{5,3},{7,7},{8,8},{10,12},{12,... | collective-permute-start | bytes 3538952 | tf_op jit(solution)/shard_map/ppermute | solution.py:1089
  601.2 51.7 %collective-permute-start.6 = (bf16[288,2048]{1,0:T(8,128)(2,1)}, bf16[288,2048]{1,0:T(8,128)(2,1)}, u32[]{:S(2)}, u32[]{:S(2)}) collective-permute-start(bf16[288,2048]{1,0:T(8,128)(2,1)} %slice.249), channel_id=1, source_target_pairs={{1,0},{0,1},{3,2},{2,3},{5,4},{4,5},{7,6},{6,7},{9,8},{8,9},{11,10... | collective-permute-start | bytes 3538952 | tf_op jit(solution)/shard_map/ppermute | solution.py:1112
  648.5 70.1 %copy-start.30 = (bf16[512,1536]{0,1:T(8,128)(2,1)S(1)}, bf16[512,1536]{0,1:T(8,128)(2,1)}, u32[]{:S(2)}) copy-start(bf16[512,1536]{0,1:T(8,128)(2,1)} %reduce-scatter.11.cloned.1.call-done) | copy-start | bytes 4718596
  649.8 68.8 %collective-permute-start.13 = (bf16[512,768]{0,1:T(8,128)(2,1)S(1)}, bf16[512,768]{0,1:T(8,128)(2,1)S(1)}, u32[]{:S(2)}, u32[]{:S(2)}) collective-permute-start(bf16[512,768]{0,1:T(8,128)(2,1)S(1)} %slice.175), channel_id=1, source_target_pairs={{2,0},{0,2},{3,1},{1,3},{6,4},{4,6},{7,5},{5,7},{10,8},{8,10},{11,... | collective-permute-start | bytes 2359304 | tf_op jit(solution)/shard_map/ppermute | solution.py:1124
  652.9 70.0 %copy-start.4 = (f32[288,2048]{1,0:T(8,128)S(1)}, f32[288,2048]{1,0:T(8,128)}, u32[]{:S(2)}) copy-start(f32[288,2048]{1,0:T(8,128)} %copy-done.2) | copy-start | bytes 7077892
  652.9 129.0 %collective-permute-start.11 = (bf16[512,1536]{0,1:T(8,128)(2,1)}, bf16[512,1536]{0,1:T(8,128)(2,1)}, u32[]{:S(2)}, u32[]{:S(2)}) collective-permute-start(bf16[512,1536]{0,1:T(8,128)(2,1)} %reduce-scatter.5.cloned.1.call-done), channel_id=1, source_target_pairs={{2,0},{0,2},{3,1},{1,3},{6,4},{4,6},{7,5},{5,7},{10,8},{8,10},{11,... | collective-permute-start | bytes 4718600 | tf_op jit(solution)/shard_map/ppermute | solution.py:1124
  720.0 16.9 %collective-permute-start.14 = (bf16[256,768]{0,1:T(8,128)(2,1)S(1)}, bf16[256,768]{0,1:T(8,128)(2,1)S(1)}, u32[]{:S(2)}, u32[]{:S(2)}) collective-permute-start(bf16[256,768]{0,1:T(8,128)(2,1)S(1)} %select_convert_fusion.1), channel_id=1, source_target_pairs={{4,0},{0,4},{5,1},{1,5},{6,2},{2,6},{7,3},{3,7},{12,8},{8,12},{13,... | collective-permute-start | bytes 1179656 | tf_op jit(solution)/shard_map/ppermute | solution.py:1130
  722.5 14.4 %copy-start.20 = (f32[512,768]{0,1:T(8,128)S(1)}, f32[512,768]{0,1:T(8,128)}, u32[]{:S(2)}) copy-start(f32[512,768]{0,1:T(8,128)} %copy-done.19) | copy-start | bytes 4718596
  722.5 16.3 %collective-permute-start.8 = (bf16[256,1536]{0,1:T(8,128)(2,1)}, bf16[256,1536]{0,1:T(8,128)(2,1)}, u32[]{:S(2)}, u32[]{:S(2)}) collective-permute-start(bf16[256,1536]{0,1:T(8,128)(2,1)} %broadcast_select_fusion.1), channel_id=1, source_target_pairs={{4,0},{0,4},{5,1},{1,5},{6,2},{2,6},{7,3},{3,7},{12,8},{8,12},{13,... | collective-permute-start | bytes 2359304 | tf_op jit(solution)/shard_map/ppermute | solution.py:1159
  726.5 57.9 %collective-permute-start.7 = (bf16[288,2048]{1,0:T(8,128)(2,1)}, bf16[288,2048]{1,0:T(8,128)(2,1)}, u32[]{:S(2)}, u32[]{:S(2)}) collective-permute-start(bf16[288,2048]{1,0:T(8,128)(2,1)} %fusion.12), channel_id=1, source_target_pairs={{0,0},{2,4},{4,2},{6,6},{1,1},{3,5},{5,3},{7,7},{8,8},{10,12},{12,... | collective-permute-start | bytes 3538952 | tf_op jit(solution)/shard_map/ppermute | solution.py:1089
  740.9 70.3 %collective-permute-start.10 = (bf16[256,1536]{0,1:T(8,128)(2,1)}, bf16[256,1536]{0,1:T(8,128)(2,1)S(1)}, u32[]{:S(2)}, u32[]{:S(2)}) collective-permute-start(bf16[256,1536]{0,1:T(8,128)(2,1)} %broadcast_select_fusion.2), channel_id=1, source_target_pairs={{2,0},{0,2},{3,1},{1,3},{6,4},{4,6},{7,5},{5,7},{10,8},{8,10},{11,... | collective-permute-start | bytes 2359304 | tf_op jit(solution)/shard_map/ppermute | solution.py:1162
  784.4 28.9 %collective-permute-start.12 = (bf16[256,1536]{0,1:T(8,128)(2,1)S(1)}, bf16[256,1536]{0,1:T(8,128)(2,1)S(1)}, u32[]{:S(2)}, u32[]{:S(2)}) collective-permute-start(bf16[256,1536]{0,1:T(8,128)(2,1)S(1)} %select_convert_fusion), channel_id=1, source_target_pairs={{4,0},{0,4},{5,1},{1,5},{6,2},{2,6},{7,3},{3,7},{12,8},{8,12},{13,... | collective-permute-start | bytes 2359304 | tf_op jit(solution)/shard_map/ppermute | solution.py:1130
  815.5 3.7 copy-start.25
  815.6 4.7 copy-start.31
  (13 other events, 26.8 us)
Sparse Core Ops, SparseCore 0:
  110.4 78.8 all-gather.3
  262.1 42.8 all-gather.7
  306.9 43.8 all-gather.5
  364.5 69.6 reduce-scatter.4
  437.0 70.0 reduce-scatter.10
  542.6 69.5 reduce-scatter.6
  615.2 70.7 reduce-scatter.8

commit v8 on v7

--- a/solution.py
+++ b/solution.py
@@ -463,10 +463,78 @@
 )
 
 
-def exchange_kernel(nd, tl, epilogue, aux_count, out_count, gather, carry_weights, *refs):
+class Job:
+    def __init__(self, inputs, shape, tiles, made):
+        self.inputs, self.shape, self.tiles, self.made = inputs, shape, tiles, made
+
+    def scratch(self):
+        dma = pltpu.SemaphoreType.DMA
+        return [pltpu.VMEM(value.shape, value.dtype) for value in self.inputs] + [
+            pltpu.VMEM(self.shape, jnp.bfloat16),
+            dma((len(self.inputs),)),
+            dma((self.tiles,)),
+        ]
+
+
+class RunningJob:
+    def __init__(self, job, given, result, scratch):
+        self.job, self.given, self.result = job, given, result
+        *self.held, self.product, self.in_sem, self.out_sem = scratch
+        self.rows = job.shape[0] // job.tiles
+
+    def copy_in(self, at):
+        return pltpu.make_async_copy(self.given[at], self.held[at], self.in_sem.at[at])
+
+    def copy_out(self, i):
+        rows = rows_at(i, self.rows)
+        return pltpu.make_async_copy(
+            self.product.at[rows], self.result.at[rows], self.out_sem.at[i]
+        )
+
+    def fetch(self):
+        for at in range(len(self.given)):
+            self.copy_in(at).start()
+
+    def run(self):
+        for at in range(len(self.given)):
+            self.copy_in(at).wait()
+
+        def one(i, carry):
+            self.product[rows_at(i, self.rows), :] = self.job.made(self.held, i, self.rows)
+            self.copy_out(i).start()
+            return carry
+
+        lax.fori_loop(0, self.job.tiles, one, 0)
+
+    def finish(self):
+        for i in range(self.job.tiles):
+            self.copy_out(i).wait()
+
+
+def weight_grad_tile(held, i, rows):
+    left, right = held
+    return contract_rows(left[:, rows_at(i, rows)], right[...]).astype(jnp.bfloat16)
+
+
+def down_tile(held, i, rows):
+    near, far, down_near, down_far = held
+    at = rows_at(i, rows)
+    return (
+        contract_cols(near[at, :], down_near[...]) + contract_cols(far[at, :], down_far[...])
+    ).astype(jnp.bfloat16)
+
+
+def exchange_kernel(
+    nd, tl, epilogue, aux_count, out_count, gather, carry_weights, jobs, last, *refs
+):
     partial = refs[0]
     aux = refs[1 : 1 + aux_count]
     refs = refs[1 + aux_count :]
+    job_given = []
+    for job in jobs:
+        count = len(job.inputs)
+        job_given.append(refs[:count])
+        refs = refs[count:]
     if carry_weights:
         weight_rows, here_rows, refs = refs[0], refs[1], refs[2:]
     outs = refs[:out_count]
@@ -475,6 +543,15 @@
         full, rest = rest[0], rest[1:]
     if carry_weights:
         weights, stage, ws, wr, xs, xr, hi, ho, rest = rest[0], *rest[1:8], rest[8:]
+    job_results, rest = rest[: len(jobs)], rest[len(jobs) :]
+    running = []
+    for job, given, result in zip(jobs, job_given, job_results):
+        count = len(job.inputs) + 3
+        running.append(RunningJob(job, given, result, rest[:count]))
+        rest = rest[count:]
+    if last:
+        low, back, gain_acc, tiles, got, ts, tr, gs, gr = rest[:9]
+        rest = rest[9:]
     if gather:
         finished, ls, lr, fs, fr, keep, rest = rest[0], *rest[1:6], rest[6:]
     mine, other, sums, arrivals, cs, cr, loc, ss, sr = rest
@@ -483,22 +560,17 @@
     own = arrivals.shape[0] // (tl - 1)
     chunk = own // CHUNKS
 
-    barrier = pltpu.get_barrier_semaphore()
-    pl.semaphore_signal(barrier, inc=1, device_id={"c": 1 - c}, device_id_type=MESH)
-    for step in range(1, tl):
-        pl.semaphore_signal(
-            barrier, inc=1, device_id={"l": lax.rem(l + step, tl)}, device_id_type=MESH
-        )
-    partners = tl
-    if carry_weights:
-        pl.semaphore_signal(barrier, inc=1, device_id={"h": 1 - h}, device_id_type=MESH)
-        partners += 1
-        for step in range(1, nd):
-            pl.semaphore_signal(
-                barrier, inc=1, device_id={"d": lax.rem(d + step, nd)}, device_id_type=MESH
-            )
-        partners += nd - 1
-    pl.semaphore_wait(barrier, partners)
+    def greet():
+        barrier = pltpu.get_barrier_semaphore()
+        peers = [{"c": 1 - c}] + [{"l": lax.rem(l + step, tl)} for step in range(1, tl)]
+        if carry_weights:
+            peers += [{"h": 1 - h}] + [{"d": lax.rem(d + step, nd)} for step in range(1, nd)]
+        for peer in peers:
+            pl.semaphore_signal(barrier, inc=1, device_id=peer, device_id_type=MESH)
+        pl.semaphore_wait(barrier, len(peers))
+
+    if not last:
+        greet()
 
     def part(base, k):
         return rows_at(base * CHUNKS + k, chunk)
@@ -589,6 +661,58 @@
 
         lax.fori_loop(0, CHUNKS, pass_on, 0)
 
+    for job in running:
+        job.fetch()
+    if running:
+        running[0].run()
+
+    if last:
+        apart = c != h
+        count = 4 * nd * tl
+        me = ((d * 2 + c) * 2 + h) * tl + l
+
+        def to_owner(k):
+            return remote(low.at[part(0, k)], back.at[part(0, k)], ts.at[k], tr.at[k], c=h, h=c)
+
+        def gains_to(step):
+            place = lax.rem(me + step, count)
+            row = place // (2 * tl)
+            return remote(
+                tiles.at[row],
+                got.at[step - 1],
+                gs.at[step - 1],
+                gr.at[step - 1],
+                d=row // 2,
+                c=lax.rem(row, 2),
+                h=lax.rem(place // tl, 2),
+                l=lax.rem(place, tl),
+            )
+
+        def start_gains(step, carry):
+            gains_to(step).start()
+            return carry
+
+        def add_gains(step, total):
+            gains_to(step).wait_recv()
+            return total + got[step - 1]
+
+        def drain_gains(step, carry):
+            gains_to(step).wait_send()
+            return carry
+
+        def send_gains():
+            cut = gain_acc.shape[1] // (2 * nd)
+            lines = cut // 128
+            tiles[...] = jnp.zeros_like(tiles)
+            for row in range(2 * nd):
+                for line in range(lines):
+                    at = slice(row * cut + line * 128, row * cut + (line + 1) * 128)
+                    tiles[row, line : line + 1, :] = gain_acc[:, at]
+                    tiles[row, lines + line : lines + line + 1, :] = aux[3][:, at]
+                tiles[row, 2 * lines : 2 * lines + 1, :] = aux[4][0:1, :]
+                tiles[row, 2 * lines + 1 : 2 * lines + 2, :] = aux[5][0:1, :]
+            lax.fori_loop(1, count, start_gains, 0)
+
     def gathered(index, k):
         return full.at[part(index, k)]
 
@@ -618,7 +742,14 @@
         for step in range(1, tl):
             along(step, k).wait_recv()
             total = total + arrivals[part(step - 1, k), :].astype(jnp.float32)
-        row = epilogue(total, part(0, k), k, aux, outs)
+        kept = (outs[0], low, gain_acc) if last else outs
+        row = epilogue(total, part(0, k), k, aux[:3], kept)
+        if last:
+
+            @pl.when(apart)
+            def _():
+                to_owner(k).start()
+
         if gather:
             finished[part(0, k), :] = row
             keep_own(k).start()
@@ -645,9 +776,24 @@
             steps[step[0]](int(step[1:]))
     else:
         lax.fori_loop(0, CHUNKS, finish, 0)
+        for job in running[1:]:
+            job.run()
         if gather:
             for k in range(CHUNKS):
                 pass_across(k)
+    if last:
+        send_gains()
+
+        @pl.when(apart)
+        def _():
+            for k in range(CHUNKS):
+                to_owner(k).wait()
+                outs[0][part(0, k), :] = back[part(0, k), :].astype(jnp.float32)
+
+        outs[1][...] = lax.fori_loop(1, count, add_gains, tiles[d * 2 + c])
+        lax.fori_loop(1, count, drain_gains, 0)
+    for job in running:
+        job.finish()
     if gather:
         for k in range(CHUNKS):
             keep_own(k).wait()
@@ -669,7 +815,9 @@
             along(step, k).wait_send()
 
 
-def exchange(collective_id, partial, aux, outs, epilogue, gather, weight_rows=()):
+def exchange(
+    collective_id, partial, aux, outs, epilogue, gather, weight_rows=(), jobs=(), last=False
+):
     nd, tl = lax.axis_size("d"), lax.axis_size("l")
     total, width = partial.shape
     own = total // (2 * tl)
@@ -679,6 +827,7 @@
     out_shape = list(outs)
     out_specs = [vmem] * len(outs)
     scratch = []
+    given = tuple(value for job in jobs for value in job.inputs)
     if gather:
         out_shape.append(jax.ShapeDtypeStruct((total, width), jnp.bfloat16))
         out_specs.append(anywhere)
@@ -694,6 +843,23 @@
             dma((PIECES, hop_count(nd))),
             dma,
             dma,
+        ]
+    for job in jobs:
+        out_shape.append(jax.ShapeDtypeStruct(job.shape, jnp.bfloat16))
+        out_specs.append(anywhere)
+        scratch += job.scratch()
+    if last:
+        others = 4 * nd * tl - 1
+        scratch += [
+            pltpu.VMEM((own, width), jnp.bfloat16),
+            pltpu.VMEM((own, width), jnp.bfloat16),
+            pltpu.VMEM((1, width), jnp.float32),
+            pltpu.VMEM((2 * nd, 8, 128), jnp.float32),
+            pltpu.VMEM((others, 8, 128), jnp.float32),
+            dma((CHUNKS,)),
+            dma((CHUNKS,)),
+            dma((others,)),
+            dma((others,)),
         ]
     if gather:
         scratch += [
@@ -717,77 +883,28 @@
     ]
     return pl.pallas_call(
         functools.partial(
-            exchange_kernel, nd, tl, epilogue, len(aux), len(outs), gather, bool(weight_rows)
+            exchange_kernel,
+            nd,
+            tl,
+            epilogue,
+            len(aux),
+            len(outs),
+            gather,
+            bool(weight_rows),
+            jobs,
+            last,
         ),
         out_shape=tuple(out_shape),
-        in_specs=[anywhere] + [vmem] * len(aux) + [anywhere] * len(weight_rows),
+        in_specs=[anywhere] + [vmem] * len(aux) + [anywhere] * (len(given) + len(weight_rows)),
         out_specs=out_specs,
         scratch_shapes=scratch,
         compiler_params=pltpu.CompilerParams(
-            has_side_effects=True, collective_id=collective_id, vmem_limit_bytes=40 << 20
+            has_side_effects=True, collective_id=collective_id, vmem_limit_bytes=60 << 20
         ),
         cost_estimate=pl.CostEstimate(
             flops=0, bytes_accessed=200_000_000 if gather else 110_000_000, transcendentals=0
         ),
-    )(partial, *aux, *weight_rows)
-
-
-def gain_kernel(nd, tl, tiles, out, got, send_sem, recv_sem):
-    d, c, h, l = (lax.axis_index(name) for name in ("d", "c", "h", "l"))
-    count = 4 * nd * tl
-    me = ((d * 2 + c) * 2 + h) * tl + l
-
-    def to(step):
-        place = lax.rem(me + step, count)
-        to_l = lax.rem(place, tl)
-        to_h = lax.rem(place // tl, 2)
-        row = place // (2 * tl)
-        return remote(
-            tiles.at[row],
-            got.at[step - 1],
-            send_sem.at[step - 1],
-            recv_sem.at[step - 1],
-            d=row // 2,
-            c=lax.rem(row, 2),
-            h=to_h,
-            l=to_l,
-        )
-
-    def start(step, carry):
-        to(step).start()
-        return carry
-
-    def add(step, total):
-        to(step).wait_recv()
-        return total + got[step - 1]
-
-    def drain(step, carry):
-        to(step).wait_send()
-        return carry
-
-    lax.fori_loop(1, count, start, 0)
-    out[...] = lax.fori_loop(1, count, add, tiles[d * 2 + c])
-    lax.fori_loop(1, count, drain, 0)
-
-
-def gain_total(tiles):
-    nd, tl = lax.axis_size("d"), lax.axis_size("l")
-    others = 4 * nd * tl - 1
-    vmem = pl.BlockSpec(memory_space=pltpu.VMEM)
-    return pl.pallas_call(
-        functools.partial(gain_kernel, nd, tl),
-        name="gain_total",
-        out_shape=jax.ShapeDtypeStruct(tiles.shape[1:], jnp.float32),
-        in_specs=[vmem],
-        out_specs=vmem,
-        scratch_shapes=[
-            pltpu.VMEM((others,) + tiles.shape[1:], jnp.float32),
-            pltpu.SemaphoreType.DMA((others,)),
-            pltpu.SemaphoreType.DMA((others,)),
-        ],
-        compiler_params=pltpu.CompilerParams(has_side_effects=True),
-        cost_estimate=pl.CostEstimate(flops=0, bytes_accessed=40_000_000, transcendentals=0),
-    )(tiles)
+    )(partial, *aux, *given, *weight_rows)
 
 
 def middle_rows(total, rows, k, aux, outs):
@@ -1044,7 +1161,6 @@
     own, tile = rows // blocks, key_tile(rows)
     return pl.pallas_call(
         functools.partial(attention_pull_kernel, blocks, repeat),
-        name="attention_pull",
         out_shape=(
             jax.ShapeDtypeStruct((rows, wide), jnp.bfloat16),
             jax.ShapeDtypeStruct((rows, narrow), jnp.bfloat16),
@@ -1256,15 +1372,11 @@
     mid = jnp.dot(normed_mid, mid_far, preferred_element_type=jnp.float32)
     gate_far, up_far = split(mid)
     hidden_far = swiglu(gate_far, up_far).astype(jnp.bfloat16)
-    down_partial = jnp.concatenate(
-        [
-            contract_rows(grad_rows, hidden_near).astype(jnp.bfloat16),
-            contract_rows(grad_rows, hidden_far).astype(jnp.bfloat16),
-        ],
-        axis=1,
-    )
-    down_grads = sum_over_d(down_partial)
-    grad_rows = after(grad_rows, down_partial)
+    down_grad_far = contract_rows(grad_rows, hidden_far).astype(jnp.bfloat16)
+    down_sum_far = sum_over_d(down_grad_far)
+    down_grad_near = contract_rows(grad_rows, hidden_near).astype(jnp.bfloat16)
+    down_sum_near = sum_over_d(down_grad_near)
+    grad_rows = after(grad_rows, down_grad_near, down_grad_far)
 
     def hidden_pull(gate, up, down):
         hidden_grad = jnp.dot(grad_rows, down, preferred_element_type=jnp.float32)
@@ -1278,23 +1390,22 @@
     mid_back_far = hidden_pull(gate_far, up_far, down_far)
     mid_grad_far = contract_rows(normed_mid, mid_back_far).astype(jnp.bfloat16)
     mid_sum_far = sum_over_d(mid_grad_far)
-    normed_grad = (contract_cols(mid_back_near, mid_near) + contract_cols(mid_back_far, mid_far)).astype(
-        jnp.bfloat16
-    )
-    gradient, mlp_gain_grad, grad_rows = exchange(
+    normed_grad = contract_cols(mid_back_near, mid_near) + contract_cols(mid_back_far, mid_far)
+    normed_grad = normed_grad.astype(jnp.bfloat16)
+    gradient, mlp_gain_grad, grad_rows, mid_grad_near, branch = exchange(
         2,
         after(normed_grad, mid_grad_far),
         (middle, cotangent, as_row(mlp_scale)),
         (whole(jnp.float32), gain_sum),
         middle_pull_rows,
         True,
-    )
-    mid_grad_near = contract_rows(normed_mid, after(mid_back_near, grad_rows)).astype(jnp.bfloat16)
+        jobs=(
+            Job((normed_mid, mid_back_near), mid_near.shape, 8, weight_grad_tile),
+            Job((hidden_near, hidden_far, down_near, down_far), normed_mid.shape, 4, down_tile),
+        ),
+    )
     mid_sum_near = sum_over_d(mid_grad_near)
 
-    hidden_near = after(hidden_near, mid_grad_near)
-    branch = contract_cols(hidden_near, down_near) + contract_cols(hidden_far, down_far)
-    grad_rows = after(grad_rows, branch)
     out_grad = jnp.dot(grad_rows, o_full, preferred_element_type=jnp.float32).astype(jnp.bfloat16)
     o_wgrad = contract_rows(grad_rows, attended)
     query_back, key_back, value_back, q_gain_grad, k_gain_grad = attention_pull(
@@ -1312,33 +1423,25 @@
     attn_rows = sum_over_d(after(attn_partial, mid_sum_far))
     branch = scatter_tokens(branch, qkv_grad)
     activations = trade((middle + branch).astype(jnp.bfloat16))
-    gradient, moved, attn_gain_grad = exchange(
-        3,
+    gradient, sums = exchange(
+        None,
         contract_cols(after(qkv_back, qkv_grad), qkv_full).astype(jnp.bfloat16),
-        (stream, gradient, as_row(attn_scale)),
-        (whole(jnp.float32), whole(jnp.bfloat16), gain_sum),
+        (stream, gradient, as_row(attn_scale), mlp_gain_grad, q_gain_grad, k_gain_grad),
+        (whole(jnp.float32), jax.ShapeDtypeStruct((8, 128), jnp.float32)),
         stream_pull_rows,
         False,
-    )
-    devices = gains.shape[0]
-    sums = jnp.concatenate(
-        [
-            part.reshape(devices, -1)
-            for part in (attn_gain_grad[0], mlp_gain_grad[0], q_gain_grad[0], k_gain_grad[0])
-        ],
-        axis=1,
-    )
-    sums = jnp.pad(sums, ((0, 0), (0, 1024 - sums.shape[1]))).reshape(devices, 8, 128)
-    sums = gain_total(sums).reshape(1, -1)
-    moved = trade(moved)
-    gradient = jnp.where(core == lax.axis_index("h"), gradient, moved.astype(jnp.float32))
-
-
-    attn_grad, attn_sent = return_blocks(after(attn_rows, attn_gain_grad))
+        last=True,
+    )
+    lines = cut // 128
+    head_at = (lax.axis_index("d") * 2 + core) * head_cut
+
+    def head_gain(line):
+        return lax.dynamic_slice(sums[line], (head_at,), (head_cut,))[None]
+
+    attn_grad, attn_sent = return_blocks(after(attn_rows, sums))
     activations = after(activations, attn_sent)
     mid_sum_near = after(mid_sum_near, attn_sent)
-    split_at = down_rows.shape[1]
-    down_grad = columns_of(*return_halves(down_grads[:, :split_at], down_grads[:, split_at:]))
+    down_grad = columns_of(*return_halves(down_sum_near, down_sum_far))
     mine, other = return_halves(mid_sum_near, mid_sum_far)
     gate_grad = columns_of(mine[:, :half_cols], other[:, :half_cols])
     up_grad = columns_of(mine[:, half_cols:], other[:, half_cols:])
@@ -1346,14 +1449,14 @@
     return (
         activations,
         gradient,
-        sums[:, :cut],
+        sums[:lines].reshape(1, cut),
         attn_grad[None, :, :q_cols],
         attn_grad[None, :, q_cols : q_cols + kv_cols],
         attn_grad[None, :, q_cols + kv_cols : q_cols + 2 * kv_cols],
         attn_grad[None, :, q_cols + 2 * kv_cols :],
-        sums[:, 2 * cut : 2 * cut + head_cut],
-        sums[:, 2 * cut + head_cut : 2 * cut + 2 * head_cut],
-        sums[:, cut : 2 * cut],
+        head_gain(2 * lines),
+        head_gain(2 * lines + 1),
+        sums[lines : 2 * lines].reshape(1, cut),
         gate_grad[None],
         up_grad[None],
         down_grad[None],

time: 837 us -> 783 us (0.935)
  waiting for transfers between devices: 169 us -> 130 us
  Pallas kernels: 363 us -> 388 us
  local copies, waits for them, and re-layouts: 59.5 us -> 36.9 us
  matrix products: 154 us -> 133 us
  starting transfers between devices: 23.3 us -> 39.2 us
  other arithmetic: 47.7 us -> 36 us
    pallas_call x3, Pallas kernels: 179 us -> 238 us  [exchange(): pl.pallas_call(functools.partial(exchange_kernel, nd, tl, epilogue, len(a...]
    ppermute x2, waiting for transfers between devices: 104 us -> 66 us  [return_halves(): far = lax.ppermute(far, 'h', shift_perm(2, 1))]
    pallas_call x1 -> x0, Pallas kernels: 34.9 us -> none  [gain_total(): pl.pallas_call(functools.partial(gain_kernel, nd, tl), name='gain_total',...]
    ppermute x1, waiting for transfers between devices: 26.5 us -> 8.3 us  [return_blocks(): far = lax.ppermute(sent, 'h', shift_perm(2, 1))]
    ppermute x2, starting transfers between devices: 0.14 us -> 18.2 us  [return_halves(): other = lax.ppermute(sent, 'c', shift_perm(2, 1)).astype(jnp.float32)]
    dot_general x6 -> x4, matrix products: 53.7 us -> 37.1 us  [contract_cols(): lax.dot_general(left, right, (((1,), (1,)), ((), ())), preferred_element_...]
    reduce_scatter x4 -> x5, waiting for transfers between devices: 0.03 us -> 13 us  [sum_over_d(): lax.psum_scatter(partial.astype(jnp.bfloat16), 'd', scatter_dimension=0,...]
    unnamed x128 -> x97, local copies, waits for them, and re-layouts: 34.5 us -> 23.3 us
  transfers between devices with their start and end apart: 22 -> 22, of which waited for: 5 -> 6; matrix products, arithmetic and copies ran while one was open for 28% -> 23% of each run, Pallas kernels for 32% -> 38%
where the time goes in v8:
time: 783 us; the launch traced here: 778 us
  Pallas kernels  388 us (50%)
  matrix products  133 us (17%)
  waiting for transfers between devices  130 us (17%)
  starting transfers between devices  39.2 us (5%)
  local copies, waits for them, and re-layouts  36.9 us (5%)
  other arithmetic  36 us (5%)
  between operations  15.1 us (2%)
    pallas_call x3, Pallas kernels, exchange(): pl.pallas_call(functools.partial(exchange_kernel, nd, tl, epilogue, len(a...  238 us
    pallas_call x1, Pallas kernels, enter(): pl.pallas_call(functools.partial(entry_kernel, nd, tl), name='entry', out...  95 us
    ppermute x2, waiting for transfers between devices, return_halves(): far = lax.ppermute(far, 'h', shift_perm(2, 1))  66 us
    dot_general x5, matrix products, contract_rows(): lax.dot_general(left, right, (((0,), (0,)), ((), ())), preferred_element_...  37.6 us
    dot_general x4, matrix products, contract_cols(): lax.dot_general(left, right, (((1,), (1,)), ((), ())), preferred_element_...  37.1 us
    pallas_call x1, Pallas kernels, attention_pull(): pl.pallas_call(functools.partial(attention_pull_kernel, blocks, repeat),...  34.3 us
    ppermute x1, waiting for transfers between devices, gather_along(): lax.ppermute(own, 'l', shift_perm(places, step))  27.3 us
    unnamed x97, local copies, waits for them, and re-layouts  23.3 us
  transfers between devices with their start and end apart: 22, of which 6 were waited for; matrix products, arithmetic and copies ran while one was open for 23% of the time, Pallas kernels for 38%

profile of v8, /device:TPU:0, one launch (start us, length us, event | category | flops | bytes accessed | tf_op | source)
XLA Modules:
  0.0 777.9 jit_solution(13915187294941019167)
XLA Ops:
  7.2 1.3 collective-permute-start
  10.2 1.3 fusion.25.refs_9_
  12.7 2.1 fusion.16
  15.2 95.0 %entry.1 = (bf16[2048,1024]{1,0:T(8,128)(2,1)}, bf16[2048,512]{1,0:T(8,128)(2,1)}, bf16[512,1536]{1,0:T(8,128)(2,1)}, bf16[512,768]{1,0:T(8,128)(2,1)}, bf16[115...) custom-call(bf16[256,512]{1,0:T(8,128)(2,1)} %bitcast.85, bf16[256,256]{1,0:T(8,128)(2,1)} %bitcast.87, ...), custom_call_target="tpu_custom_call" | custom-call | bytes 250000000 | tf_op jit(solution)/shard_map/entry/pallas_call | solution.py:433
  111.1 2.3 slice.102
  114.9 2.9 collective-permute-start.1
  117.9 2.6 slice.100.refs_1_
  120.5 4.1 fusion
  124.7 9.2 %fusion.14.refs_0_.refs_1_.refs_2_ = f32[1152,1024]{1,0:T(8,128)} fusion(bf16[2048,1024]{1,0:T(8,128)(2,1)} %get-tuple-element.55, bf16[1152,2048]{1,0:T(8,128)(2,1)S(1)} %copy-done.12, f32[2048]{0:T(1024)S(1)} %bitcast.95, f32[1152]{0:T(1024)S(1)} %add_rsqrt_fusion), kind=kOutput, calls=%fused_computation.48 | convolution fusion | flops 4841275392 | bytes 13644288 | tf_op jit(solution)/shard_map/dot_general | solution.py:1346
  134.0 20.2 %attention.1 = (bf16[1152,512]{1,0:T(8,128)(2,1)}, bf16[1152,256]{1,0:T(8,128)(2,1)S(1)}, bf16[1152,256]{1,0:T(8,128)(2,1)S(1)}, bf16[1152,512]{1,0:T(8,128)(2,1)}, f32[1152,256]{1,0:T(8,128)}) custom-call(s32[4]{0:T(128)S(1)} %get-tuple-element.92.order_ref, f32[1152,1024]{1,0:T(8,128)} %fusion.14.refs_0_.refs_1_.refs_2_, ...), custom_call_target="tpu_custom_call" | custom-call | flops 2717908992 | bytes 60000000 | tf_op jit(solution)/shard_map/attention/pallas_call | solution.py:1056
  154.2 6.1 convolution_convert_fusion.2.refs_0_
  160.3 9.3 %collective-permute-done.1.refs_4_ = bf16[512,768]{1,0:T(8,128)(2,1)S(1)} collective-permute-done((bf16[512,768]{1,0:T(8,128)(2,1)}, bf16[512,768]{1,0:T(8,128)(2,1)S(1)}, u32[]{:S(2)}, u32[]{:S(2)}) %collective-permute-start.1) | collective-permute-done | bytes 786464 | tf_op jit(solution)/shard_map/ppermute | solution.py:1334
  169.5 0.9 copy-done.21
  170.4 90.3 %shard_map.237 = (f32[288,2048]{1,0:T(8,128)}, bf16[1152,2048]{1,0:T(8,128)(2,1)}, bf16[2048,1536]{1,0:T(8,128)(2,1)}) custom-call(bf16[1152,2048]{1,0:T(8,128)(2,1)} %convolution_convert_fusion.2.refs_0_, bf16[288,2048]{1,0:T(8,128)(2,1)} %slice.100.refs_1_, f32[1,2048]{1,0:T(1,128)} %bitcast.91, bf16[512,1536]{1,0:T(8,128)(2,1)} %get-tuple-element.58.refs_3_, ...), custom_call_target="tpu_custom_call" | custom-call | bytes 200000000 | tf_op jit(solution)/shard_map/pallas_call | solution.py:884
  261.8 27.3 %collective-permute-done.2 = bf16[288,2048]{1,0:T(8,128)(2,1)S(1)} collective-permute-done((bf16[288,2048]{1,0:T(8,128)(2,1)S(1)}, bf16[288,2048]{1,0:T(8,128)(2,1)S(1)}, u32[]{:S(2)}, u32[]{:S(2)}) %collective-permute-start.2) | collective-permute-done | bytes 1179680 | tf_op jit(solution)/shard_map/ppermute | solution.py:1210
  289.4 9.7 %fusion.34 = f32[1152,1536]{1,0:T(8,128)S(1)} fusion(bf16[1152,2048]{1,0:T(8,128)(2,1)S(1)} %copy-done.17, bf16[2048,1536]{1,0:T(8,128)(2,1)} %get-tuple-element.64), kind=kOutput, calls=%fused_computation.111 | convolution fusion | flops 7247757312 | bytes 18087936 | tf_op jit(solution)/shard_map/dot_general | solution.py:1372
  299.1 1.1 multiply_convert_fusion.2.refs_7_
  300.1 1.8 copy-done.16
  303.2 2.2 copy-done.27
  305.5 5.8 convolution_convert_fusion.4
  311.3 11.8 %fusion.33 = f32[1152,1536]{1,0:T(8,128)S(1)} fusion(bf16[1152,2048]{1,0:T(8,128)(2,1)} %get-tuple-element.63.refs_4_, bf16[2048,1536]{1,0:T(8,128)(2,1)} %all-gather.4.cloned.1.call-done), kind=kOutput, calls=%fused_computation.110 | convolution fusion | flops 7247757312 | bytes 18087936 | tf_op jit(solution)/shard_map/dot_general | solution.py:1369
  323.1 1.1 multiply_convert_fusion.3.refs_6_
  324.2 2.5 copy-done.15
  326.6 1.3 copy-done.28
  328.0 6.1 convolution_convert_fusion.5
  334.1 10.2 %fusion.8 = (bf16[1152,768]{1,0:T(8,128)(2,1)S(1)}, bf16[1152,768]{1,0:T(8,128)(2,1)S(1)}) fusion(f32[1152,1536]{1,0:T(8,128)} %copy-done.16, bf16[1152,2048]{1,0:T(8,128)(2,1)} %copy-done.27, bf16[2048,768]{1,0:T(8,128)(2,1)} %all-gather.8.cloned.1.call-done.refs_9_), kind=kOutput, calls=%fused_computation.20 | convolution fusion | flops 3636264960 | bytes 18481152 | tf_op jit(solution)/shard_map/dot_general | solution.py:1382
  344.2 12.8 %convolution_convert_fusion.1 = bf16[2048,1536]{1,0:T(8,128)(2,1)} fusion(bf16[1152,2048]{1,0:T(8,128)(2,1)} %get-tuple-element.63.refs_4_, bf16[1152,768]{1,0:T(8,128)(2,1)S(1)} %get-tuple-element.94, bf16[1152,768]{1,0:T(8,128)(2,1)S(1)} %get-tuple-element.93), kind=kOutput, calls=%fused_computation.8 | convolution fusion | flops 7257980928 | bytes 14548992 | tf_op jit(solution)/shard_map/dot_general | solution.py:47
  358.3 11.3 %fusion.5 = (bf16[1152,768]{1,0:T(8,128)(2,1)S(1)}, bf16[1152,768]{1,0:T(8,128)(2,1)S(1)}) fusion(f32[1152,1536]{1,0:T(8,128)} %copy-done.15, bf16[1152,2048]{1,0:T(8,128)(2,1)} %copy-done.27, bf16[2048,768]{1,0:T(8,128)(2,1)} %all-gather.6.cloned.1.call-done.refs_8_), kind=kOutput, calls=%fused_computation.17 | convolution fusion | flops 3636264960 | bytes 18481152 | tf_op jit(solution)/shard_map/dot_general | solution.py:1382
  369.7 12.9 %fusion.29 = f32[1152,2048]{1,0:T(8,128)} fusion(bf16[2048,1536]{1,0:T(8,128)(2,1)} %all-gather.4.cloned.1.call-done, bf16[1152,768]{1,0:T(8,128)(2,1)S(1)} %get-tuple-element.96, bf16[1152,768]{1,0:T(8,128)(2,1)S(1)} %get-tuple-element.95), kind=kOutput, calls=%fused_computation.106 | convolution fusion | flops 7254835200 | bytes 19267584 | tf_op jit(solution)/shard_map/dot_general | solution.py:53
  382.6 11.4 %add_convert_fusion.refs_0_ = bf16[1152,2048]{1,0:T(8,128)(2,1)} fusion(f32[1152,2048]{1,0:T(8,128)} %fusion.29, bf16[2048,1536]{1,0:T(8,128)(2,1)S(1)} %bitcast.102, bf16[1152,768]{1,0:T(8,128)(2,1)S(1)} %get-tuple-element.94, bf16[1152,768]{1,0:T(8,128)(2,1)S(1)} %get-tuple-element.93), kind=kOutput, calls=%fused_computation.6 | convolution fusion | flops 7259553792 | bytes 23986176 | tf_op jit(solution)/shard_map/dot_general | solution.py:53
  393.9 2.1 pad_maximum_fusion.1.refs_5_
  396.0 61.2 %shard_map.238 = (f32[288,2048]{1,0:T(8,128)}, f32[1,2048]{1,0:T(1,128)}, bf16[1152,2048]{1,0:T(8,128)(2,1)}, bf16[2048,1536]{1,0:T(8,128)(2,1)}, bf16[1152,2048]{1,0:T(8,128)(2,1)}) custom-call(bf16[1152,2048]{1,0:T(8,128)(2,1)} %add_convert_fusion.refs_0_, f32[288,2048]{1,0:T(8,128)} %get-tuple-element.60.refs_1_, ...), custom_call_target="tpu_custom_call" | custom-call | bytes 200000000 | tf_op jit(solution)/shard_map/pallas_call | solution.py:884
  457.2 6.0 convolution_convert_fusion.7.refs_11_
  463.2 34.3 %shard_map.239 = (bf16[1152,512]{1,0:T(8,128)(2,1)}, bf16[1152,256]{1,0:T(8,128)(2,1)}, bf16[1152,256]{1,0:T(8,128)(2,1)}, f32[8,128]{1,0:T(8,128)}, f32[8,128]{1,0:T(8,128)}) custom-call(s32[4]{0:T(128)} %copy-done.5, f32[1152,1024]{1,0:T(8,128)} %fusion.14.refs_0_.refs_1_.refs_2_, f32[1152,1024]{1,0:T(8,128)} %fusion.14.refs_0_.refs_1_.refs_2_, ...), custom_call_target="tpu_custom_call" | custom-call | flops 6794772480 | bytes 120000000 | tf_op jit(solution)/shard_map/pallas_call | solution.py:1162
  497.5 1.6 constant_dynamic-update-slice_fusion.5
  499.1 1.5 constant_dynamic-update-slice_fusion.4
  500.7 6.4 convolution_convert_fusion.6
  507.2 6.5 convolution_convert_fusion.3
  513.7 3.2 pad_maximum_fusion
  517.7 1.8 slice.108
  520.5 3.7 collective-permute-done.5
  524.3 3.3 convert_add_fusion
  527.6 2.6 copy-done.8
  530.4 6.8 convolution_convert_fusion.refs_0_
  537.2 86.7 %shard_map.240 = (f32[288,2048]{1,0:T(8,128)}, f32[8,128]{1,0:T(8,128)}) custom-call(bf16[1152,2048]{1,0:T(8,128)(2,1)} %convolution_convert_fusion.refs_0_, bf16[288,2048]{1,0:T(8,128)(2,1)} %slice.100.refs_1_, f32[288,2048]{1,0:T(8,128)} %get-tuple-element.81.refs_2_, f32[1,2048]{1,0:T(1,128)} %bitcast.93, f32[1,2048]{1,0:T(1,128)} %get-tuple-element.82.refs_4_, ...), custom_call_target="tpu_custom_call" | custom-call | bytes 110000000 | tf_op jit(solution)/shard_map/pallas_call | solution.py:884
  625.8 1.3 fusion.31
  628.0 1.5 convert_add_fusion.2
  629.7 4.0 collective-permute-start.10
  633.7 1.6 broadcast_select_fusion.1
  635.9 3.3 fusion.12
  639.2 10.7 %collective-permute-start.7 = (bf16[288,2048]{1,0:T(8,128)(2,1)}, bf16[288,2048]{1,0:T(8,128)(2,1)}, u32[]{:S(2)}, u32[]{:S(2)}) collective-permute-start(bf16[288,2048]{1,0:T(8,128)(2,1)} %fusion.12), channel_id=1, source_target_pairs={{0,0},{2,4},{4,2},{6,6},{1,1},{3,5},{5,3},{7,7},{8,8},{10,12},{12,... | collective-permute-start | bytes 3538952 | tf_op jit(solution)/shard_map/ppermute | solution.py:1205
  649.9 1.1 convert_select_fusion.1
  651.1 1.3 maximum_bitcast_fusion.2
  652.4 0.9 copy-done.18
  653.5 13.0 %reduce-scatter.10.cloned.1.call-done = bf16[512,1536]{1,0:T(8,128)(2,1)} async-done(((bf16[2048,1536]{1,0:T(8,128)(2,1)}), bf16[512,1536]{1,0:T(8,128)(2,1)}) %reduce-scatter.10.cloned.1.call-update) | async-done | bytes 1572880 | tf_op jit(solution)/shard_map/reduce_scatter | solution.py:1258
  666.5 66.0 %collective-permute-done.10 = bf16[512,1536]{1,0:T(8,128)(2,1)} collective-permute-done((bf16[512,1536]{1,0:T(8,128)(2,1)}, bf16[512,1536]{1,0:T(8,128)(2,1)}, u32[]{:S(2)}, u32[]{:S(2)}) %collective-permute-start.10) | collective-permute-done | bytes 1572896 | tf_op jit(solution)/shard_map/ppermute | solution.py:1240
  732.5 2.3 convert_add_fusion.1
  735.0 18.1 %collective-permute-start.11 = (bf16[256,1536]{1,0:T(8,128)(2,1)S(1)}, bf16[256,1536]{1,0:T(8,128)(2,1)S(1)}, u32[]{:S(2)}, u32[]{:S(2)}) collective-permute-start(bf16[256,1536]{1,0:T(8,128)(2,1)S(1)} %select_convert_fusion), channel_id=1, source_target_pairs={{4,0},{0,4},{5,1},{1,5},{6,2},{2,6},{7,3},{3,7},{12,8},{8,12},{13,... | collective-permute-start | bytes 2359304 | tf_op jit(solution)/shard_map/ppermute | solution.py:1246
  753.3 8.3 %collective-permute-done.9 = bf16[256,1536]{1,0:T(8,128)(2,1)S(1)} collective-permute-done((bf16[256,1536]{1,0:T(8,128)(2,1)S(1)}, bf16[256,1536]{1,0:T(8,128)(2,1)S(1)}, u32[]{:S(2)}, u32[]{:S(2)}) %collective-permute-start.9) | collective-permute-done | bytes 786464 | tf_op jit(solution)/shard_map/ppermute | solution.py:1278
  762.8 1.0 slice_bitcast_fusion
  764.3 1.4 maximum_bitcast_fusion.1
  765.7 1.4 maximum_bitcast_fusion
  767.0 2.4 copy.65
  769.5 1.4 copy.66
  (166 shorter events, 17.0 us)
Async XLA Ops:
  7.2 304.1 %all-gather.4.cloned.1.call-start = ((), (), s32[]{:S(2)}) async-start(), calls=%async_computation.5 | async-start | bytes 7864320 | tf_op jit(solution)/shard_map/all_gather | solution.py:1332
  7.2 4.4 collective-permute-start
  10.1 123.8 %copy-start.5 = (s32[4]{0:T(128)}, s32[4]{0:T(128)S(1)}, u32[]{:S(2)}) copy-start(s32[4]{0:T(128)S(1)} %get-tuple-element.92.order_ref) | copy-start | bytes 52
  15.2 118.7 %copy-start.1 = (f32[1152,128]{1,0:T(8,128)}, f32[1152,128]{1,0:T(8,128)S(1)}, u32[]{:S(2)}) copy-start(f32[1152,128]{1,0:T(8,128)S(1)} %get-tuple-element.119.refs_3_.refs_2_) | copy-start | bytes 1769476
  15.2 118.7 %copy-start.2 = (f32[1152,128]{1,0:T(8,128)}, f32[1152,128]{1,0:T(8,128)S(1)}, u32[]{:S(2)}) copy-start(f32[1152,128]{1,0:T(8,128)S(1)} %get-tuple-element.120.refs_4_.refs_3_) | copy-start | bytes 1769476
  110.2 3.2 copy-start.30
  110.2 7.6 copy-start.22
  110.3 223.8 %all-gather.8.cloned.1.call-start = ((), (), s32[]{:S(2)}) async-start(), calls=%async_computation.7 | async-start | bytes 3932160 | tf_op jit(solution)/shard_map/all_gather | solution.py:1367
  111.1 22.8 %copy-start = (s32[1152,1]{1,0:T(8,128)}, s32[1152,1]{1,0:T(8,128)S(1)}, u32[]{:S(2)}) copy-start(s32[1152,1]{1,0:T(8,128)S(1)} %copy.41.refs_7_.refs_6_) | copy-start | bytes 13828
  113.6 20.4 %copy-start.3 = (f32[1,128]{1,0:T(1,128)}, f32[1,128]{1,0:T(1,128)S(1)}, u32[]{:S(2)}) copy-start(f32[1,128]{1,0:T(1,128)S(1)} %reshape_reshape.12.refs_6_.refs_5_) | copy-start | bytes 1540
  113.6 20.3 %copy-start.4 = (f32[1,128]{1,0:T(1,128)}, f32[1,128]{1,0:T(1,128)S(1)}, u32[]{:S(2)}) copy-start(f32[1,128]{1,0:T(1,128)S(1)} %reshape_reshape.11.refs_5_.refs_4_) | copy-start | bytes 1540
  114.9 9.8 %copy-start.31 = (f32[1,2,8,128]{3,1,2,0:T(2,128)}, f32[1,2,8,128]{3,1,2,0:T(2,128)S(1)}, u32[]{:S(2)}) copy-start(f32[1,2,8,128]{3,1,2,0:T(2,128)S(1)} %copy.54) | copy-start | bytes 24580
  114.9 54.7 %collective-permute-start.1 = (bf16[512,768]{1,0:T(8,128)(2,1)}, bf16[512,768]{1,0:T(8,128)(2,1)S(1)}, u32[]{:S(2)}, u32[]{:S(2)}) collective-permute-start(bf16[512,768]{1,0:T(8,128)(2,1)} %slice.102), channel_id=1, source_target_pairs={{2,0},{0,2},{3,1},{1,3},{6,4},{4,6},{7,5},{5,7},{10,8},{8,10},{11,... | collective-permute-start | bytes 2359304 | tf_op jit(solution)/shard_map/ppermute | solution.py:1334
  117.8 142.9 %collective-permute-start.4 = (bf16[512,768]{1,0:T(8,128)(2,1)S(1)}, bf16[512,768]{1,0:T(8,128)(2,1)}, u32[]{:S(2)}, u32[]{:S(2)}) collective-permute-start(bf16[512,768]{1,0:T(8,128)(2,1)S(1)} %copy-done.22), channel_id=1, source_target_pairs={{2,0},{0,2},{3,1},{1,3},{6,4},{4,6},{7,5},{5,7},{10,8},{8,10},{11,... | collective-permute-start | bytes 2359304 | tf_op jit(solution)/shard_map/ppermute | solution.py:1335
  117.9 6.8 copy-start.12
  124.7 9.2 %copy-start.33 = (f32[1152]{0:T(1024)}, f32[1152]{0:T(1024)S(1)}, u32[]{:S(2)}) copy-start(f32[1152]{0:T(1024)S(1)} %add_rsqrt_fusion) | copy-start | bytes 13828
  133.9 20.3 %copy-start.36 = (bf16[2048,512]{1,0:T(8,128)(2,1)S(1)}, bf16[2048,512]{1,0:T(8,128)(2,1)}, u32[]{:S(2)}) copy-start(bf16[2048,512]{1,0:T(8,128)(2,1)} %get-tuple-element.57) | copy-start | bytes 6291460
  154.2 6.1 copy-start.6
  154.2 6.1 copy-start.7
  170.4 90.4 %copy-start.10 = (bf16[288,2048]{1,0:T(8,128)(2,1)S(1)}, bf16[288,2048]{1,0:T(8,128)(2,1)}, u32[]{:S(2)}) copy-start(bf16[288,2048]{1,0:T(8,128)(2,1)} %get-tuple-element.61.refs_2_) | copy-start | bytes 3538948
  260.7 97.5 %all-gather.6.cloned.1.call-start = ((), (), s32[]{:S(2)}) async-start(), calls=%async_computation.6 | async-start | bytes 3932160 | tf_op jit(solution)/shard_map/all_gather | solution.py:1333
  260.8 28.3 %collective-permute-start.2 = (bf16[288,2048]{1,0:T(8,128)(2,1)S(1)}, bf16[288,2048]{1,0:T(8,128)(2,1)S(1)}, u32[]{:S(2)}, u32[]{:S(2)}) collective-permute-start(bf16[288,2048]{1,0:T(8,128)(2,1)S(1)} %copy-done.10), channel_id=1, source_target_pairs={{1,0},{0,1},{3,2},{2,3},{5,4},{4,5},{7,6},{6,7},{9,8},{8,9},{11,10... | collective-permute-start | bytes 3538952 | tf_op jit(solution)/shard_map/ppermute | solution.py:1210
  261.5 255.4 %reduce-scatter.6.cloned.1.call-start = ((), (), s32[]{:S(2)}) async-start(), calls=%async_computation.8 | async-start | bytes 7864320 | tf_op jit(solution)/shard_map/reduce_scatter | solution.py:1258
  261.7 27.7 %copy-start.17 = (bf16[1152,2048]{1,0:T(8,128)(2,1)S(1)}, bf16[1152,2048]{1,0:T(8,128)(2,1)}, u32[]{:S(2)}) copy-start(bf16[1152,2048]{1,0:T(8,128)(2,1)} %get-tuple-element.63.refs_4_) | copy-start | bytes 14155780
  289.3 12.8 %collective-permute-start.3 = (bf16[576,2048]{1,0:T(8,128)(2,1)S(1)}, bf16[576,2048]{1,0:T(8,128)(2,1)S(1)}, u32[]{:S(2)}, u32[]{:S(2)}) collective-permute-start(bf16[576,2048]{1,0:T(8,128)(2,1)S(1)} %pad_maximum_fusion.3), channel_id=1, source_target_pairs={{4,0},{0,4},{5,1},{1,5},{6,2},{2,6},{7,3},{3,7},{12,8},{8,12},{13,... | collective-permute-start | bytes 7077896 | tf_op jit(solution)/shard_map/ppermute | solution.py:1215
  299.0 2.9 copy-start.16
  302.0 1.2 copy-start.13
  303.2 2.2 copy-start.27
  323.1 3.6 copy-start.15
  323.1 4.9 copy-start.28
  328.0 6.1 copy-start.14
  357.1 163.4 %reduce-scatter.14.cloned.1.call-start = ((), (), s32[]{:S(2)}) async-start(), calls=%async_computation.12 | async-start | bytes 3932160 | tf_op jit(solution)/shard_map/reduce_scatter | solution.py:1258
  357.7 270.4 %reduce-scatter.12.cloned.1.call-start = ((), (), s32[]{:S(2)}) async-start(), calls=%async_computation.11 | async-start | bytes 3932160 | tf_op jit(solution)/shard_map/reduce_scatter | solution.py:1258
  358.2 275.5 %reduce-scatter.8.cloned.1.call-start = ((), (), s32[]{:S(2)}) async-start(), calls=%async_computation.9 | async-start | bytes 7864320 | tf_op jit(solution)/shard_map/reduce_scatter | solution.py:1258
  358.3 24.3 %slice-start.2 = ((s8[6291456]{0:T(1024)(128)(4,1)}), s8[4194304]{0:T(1024)(128)(4,1)S(1)}, s32[]{:S(2)}) async-start(s8[6291456]{0:T(1024)(128)(4,1)} %bitcast.101), calls=%async_computation.15 | async-start | bytes 8388608
  369.7 12.9 %slice-start.3 = ((s8[6291456]{0:T(1024)(128)(4,1)}), s8[2097152]{0:T(1024)(128)(4,1)S(1)}, s32[]{:S(2)}) async-start(s8[6291456]{0:T(1024)(128)(4,1)} %bitcast.101), calls=%async_computation.16 | async-start | bytes 4194304
  396.0 61.2 %copy-start.37 = (bf16[2048,512]{1,0:T(8,128)(2,1)S(1)}, bf16[2048,512]{1,0:T(8,128)(2,1)}, u32[]{:S(2)}) copy-start(bf16[2048,512]{1,0:T(8,128)(2,1)} %get-tuple-element.57) | copy-start | bytes 6291460
  463.2 44.0 %slice-start = ((s8[4718592]{0:T(1024)(128)(4,1)}), s8[524288]{0:T(1024)(128)(4,1)S(1)}, s32[]{:S(2)}) async-start(s8[4718592]{0:T(1024)(128)(4,1)} %bitcast.80), calls=%async_computation.13 | async-start | bytes 1048576
  497.5 3.1 copy-start.26
  497.5 3.2 copy-start.38
  497.5 9.7 %slice-start.1 = ((s8[4718592]{0:T(1024)(128)(4,1)}), s8[4194304]{0:T(1024)(128)(4,1)S(1)}, s32[]{:S(2)}) async-start(s8[4718592]{0:T(1024)(128)(4,1)} %bitcast.80), calls=%async_computation.14 | async-start | bytes 8388608
  500.7 6.5 copy-start.24
  500.7 6.5 copy-start.32
  500.7 6.5 copy-start.34
  516.9 149.5 %reduce-scatter.10.cloned.1.call-start = ((), (), s32[]{:S(2)}) async-start(), calls=%async_computation.10 | async-start | bytes 7864320 | tf_op jit(solution)/shard_map/reduce_scatter | solution.py:1258
  517.7 2.2 copy-start.29
  519.5 4.7 collective-permute-start.5
  520.5 9.9 %copy-start.25 = (bf16[1152,1024]{1,0:T(8,128)(2,1)S(1)}, bf16[1152,1024]{1,0:T(8,128)(2,1)}, u32[]{:S(2)}) copy-start(bf16[1152,1024]{1,0:T(8,128)(2,1)} %copy-done.24) | copy-start | bytes 7077892
  520.5 9.9 %copy-start.35 = (bf16[2048,1024]{1,0:T(8,128)(2,1)S(1)}, bf16[2048,1024]{1,0:T(8,128)(2,1)}, u32[]{:S(2)}) copy-start(bf16[2048,1024]{1,0:T(8,128)(2,1)} %get-tuple-element.55) | copy-start | bytes 12582916
  520.5 106.6 %collective-permute-start.12 = (bf16[512,768]{1,0:T(8,128)(2,1)}, bf16[512,768]{1,0:T(8,128)(2,1)S(1)}, u32[]{:S(2)}, u32[]{:S(2)}) collective-permute-start(bf16[512,768]{1,0:T(8,128)(2,1)} %reduce-scatter.14.cloned.1.call-done), channel_id=1, source_target_pairs={{2,0},{0,2},{3,1},{1,3},{6,4},{4,6},{7,5},{5,7},{10,8},{8,10},{11,... | collective-permute-start | bytes 2359304 | tf_op jit(solution)/shard_map/ppermute | solution.py:1240
  527.6 2.6 copy-start.8
  530.4 96.8 %collective-permute-start.6 = (bf16[288,2048]{1,0:T(8,128)(2,1)S(1)}, bf16[288,2048]{1,0:T(8,128)(2,1)S(1)}, u32[]{:S(2)}, u32[]{:S(2)}) collective-permute-start(bf16[288,2048]{1,0:T(8,128)(2,1)S(1)} %slice.219), channel_id=1, source_target_pairs={{1,0},{0,1},{3,2},{2,3},{5,4},{4,5},{7,6},{6,7},{9,8},{8,9},{11,10... | collective-permute-start | bytes 3538952 | tf_op jit(solution)/shard_map/ppermute | solution.py:1228
  627.1 0.9 copy-start.23
  629.6 20.3 %collective-permute-start.13 = (bf16[256,768]{1,0:T(8,128)(2,1)S(1)}, bf16[256,768]{1,0:T(8,128)(2,1)}, u32[]{:S(2)}, u32[]{:S(2)}) collective-permute-start(bf16[256,768]{1,0:T(8,128)(2,1)S(1)} %select_convert_fusion.1), channel_id=1, source_target_pairs={{4,0},{0,4},{5,1},{1,5},{6,2},{2,6},{7,3},{3,7},{12,8},{8,12},{13,... | collective-permute-start | bytes 1179656 | tf_op jit(solution)/shard_map/ppermute | solution.py:1246
  629.7 102.8 %collective-permute-start.10 = (bf16[512,1536]{1,0:T(8,128)(2,1)}, bf16[512,1536]{1,0:T(8,128)(2,1)}, u32[]{:S(2)}, u32[]{:S(2)}) collective-permute-start(bf16[512,1536]{1,0:T(8,128)(2,1)} %reduce-scatter.6.cloned.1.call-done), channel_id=1, source_target_pairs={{2,0},{0,2},{3,1},{1,3},{6,4},{4,6},{7,5},{5,7},{10,8},{8,10},{11,... | collective-permute-start | bytes 4718600 | tf_op jit(solution)/shard_map/ppermute | solution.py:1240
  633.7 2.1 copy-start.11
  635.3 17.0 %collective-permute-start.8 = (bf16[256,1536]{1,0:T(8,128)(2,1)S(1)}, bf16[256,1536]{1,0:T(8,128)(2,1)S(1)}, u32[]{:S(2)}, u32[]{:S(2)}) collective-permute-start(bf16[256,1536]{1,0:T(8,128)(2,1)S(1)} %broadcast_select_fusion.1), channel_id=1, source_target_pairs={{4,0},{0,4},{5,1},{1,5},{6,2},{2,6},{7,3},{3,7},{12,8},{8,12},{13,... | collective-permute-start | bytes 2359304 | tf_op jit(solution)/shard_map/ppermute | solution.py:1275
  639.2 14.1 %copy-start.9 = (bf16[512,1536]{1,0:T(8,128)(2,1)S(1)}, bf16[512,1536]{1,0:T(8,128)(2,1)}, u32[]{:S(2)}) copy-start(bf16[512,1536]{1,0:T(8,128)(2,1)} %reduce-scatter.8.cloned.1.call-done) | copy-start | bytes 4718596
  639.2 95.8 %collective-permute-start.7 = (bf16[288,2048]{1,0:T(8,128)(2,1)}, bf16[288,2048]{1,0:T(8,128)(2,1)}, u32[]{:S(2)}, u32[]{:S(2)}) collective-permute-start(bf16[288,2048]{1,0:T(8,128)(2,1)} %fusion.12), channel_id=1, source_target_pairs={{0,0},{2,4},{4,2},{6,6},{1,1},{3,5},{5,3},{7,7},{8,8},{10,12},{12,... | collective-permute-start | bytes 3538952 | tf_op jit(solution)/shard_map/ppermute | solution.py:1205
  652.4 0.9 copy-start.18
  653.4 108.2 %collective-permute-start.9 = (bf16[256,1536]{1,0:T(8,128)(2,1)S(1)}, bf16[256,1536]{1,0:T(8,128)(2,1)S(1)}, u32[]{:S(2)}, u32[]{:S(2)}) collective-permute-start(bf16[256,1536]{1,0:T(8,128)(2,1)S(1)} %broadcast_select_fusion.2), channel_id=1, source_target_pairs={{2,0},{0,2},{3,1},{1,3},{6,4},{4,6},{7,5},{5,7},{10,8},{8,10},{11,... | collective-permute-start | bytes 2359304 | tf_op jit(solution)/shard_map/ppermute | solution.py:1278
  734.8 26.8 %copy-start.19 = (bf16[256,1536]{1,0:T(8,128)(2,1)S(1)}, bf16[256,1536]{1,0:T(8,128)(2,1)}, u32[]{:S(2)}) copy-start(bf16[256,1536]{1,0:T(8,128)(2,1)} %copy-done.18) | copy-start | bytes 2359300
  735.0 28.9 %collective-permute-start.11 = (bf16[256,1536]{1,0:T(8,128)(2,1)S(1)}, bf16[256,1536]{1,0:T(8,128)(2,1)S(1)}, u32[]{:S(2)}, u32[]{:S(2)}) collective-permute-start(bf16[256,1536]{1,0:T(8,128)(2,1)S(1)} %select_convert_fusion), channel_id=1, source_target_pairs={{4,0},{0,4},{5,1},{1,5},{6,2},{2,6},{7,3},{3,7},{12,8},{8,12},{13,... | collective-permute-start | bytes 2359304 | tf_op jit(solution)/shard_map/ppermute | solution.py:1246
  765.7 3.8 copy-start.20
  (1 other events, 0.9 us)
Sparse Core Ops, SparseCore 0:
  110.4 75.8 all-gather.3
  260.9 42.7 all-gather.7
  305.5 43.8 all-gather.5
  357.2 68.5 reduce-scatter.5
  428.6 43.8 reduce-scatter.13
  475.4 43.8 reduce-scatter.11
  522.3 70.0 reduce-scatter.7
  595.3 71.0 reduce-scatter.9

commit v9 on v8

--- a/solution.py
+++ b/solution.py
@@ -457,10 +457,170 @@
 
 
 PIECES = 6
+RETURN_AHEAD = 2
+RETURN_ORDER = (
+    "m0", "w2", "f0", "m1", "w3", "f1", "h0", "m2", "w4", "f2", "g0", "h1", "m3", "w5", "h2", "m4",
+    "h3", "m5", "h4", "h5",
+)
 SUM_ORDER = (
     "s3", "s4", "s5", "f0", "r3", "s0", "f1", "r4", "r0", "s1", "f2", "r5", "r1", "s2", "r2",
     "a0", "a1", "a2",
 )
+
+
+class Return:
+    def __init__(self, nd, pieces, out, scratch):
+        self.nd, self.pieces, self.out = nd, pieces, out
+        self.held, self.first, self.mixed, self.second, self.sums, self.parts = scratch[:6]
+        (self.load, self.fs, self.fr, self.ss, self.sr, self.ps, self.pr) = scratch[6:]
+        self.d, self.c, self.h = (lax.axis_index(name) for name in ("d", "c", "h"))
+        self.rows = out.shape[0]
+        d = self.d
+        if nd == 4:
+            side_x = d + 1 - 2 * lax.rem(d, 2)
+            side_y = d + 2 - 4 * (d // 2)
+            corner = side_x + side_y - d
+            self.blocks = ((d, 0), (side_y, 0), (d, 1), (side_x, 1))
+            self.sends = (
+                (side_x, 0, side_x),
+                (corner, 0, side_x),
+                (side_y, 1, side_y),
+                (corner, 1, side_y),
+            )
+            self.mixes = ((1, side_y), (3, side_x))
+        else:
+            self.blocks = ((d, 0), (d, 1))
+            self.sends = tuple(
+                (lax.rem(d + step, nd), part, lax.rem(d + step, nd))
+                for step in range(1, nd)
+                for part in range(2)
+            )
+            self.mixes = ()
+
+    @staticmethod
+    def scratch(nd, count, rows, cols):
+        dma = pltpu.SemaphoreType.DMA
+        blocks, sends, mixes = (4, 4, 2) if nd == 4 else (2, 2 * (nd - 1), 1)
+
+        def buffer(number):
+            return pltpu.VMEM((count, number, rows, cols), jnp.bfloat16)
+
+        return [
+            buffer(blocks),
+            buffer(sends),
+            buffer(mixes),
+            buffer(mixes),
+            buffer(2),
+            buffer(2),
+            dma((count, blocks)),
+            dma((count, sends)),
+            dma((count, sends)),
+            dma((count, mixes)),
+            dma((count, mixes)),
+            dma((count, 2)),
+            dma((count, 2)),
+        ]
+
+    def source(self, j, of, part):
+        ref, start = self.pieces[j]
+        cols = self.held.shape[3]
+        return ref.at[rows_at(of * 2 + part, self.rows), pl.ds(start, cols)]
+
+    def loading(self, j, at):
+        return pltpu.make_async_copy(
+            self.source(j, *self.blocks[at]), self.held.at[j, at], self.load.at[j, at]
+        )
+
+    def sending(self, j, at):
+        of, part, to = self.sends[at]
+        return remote(
+            self.source(j, of, part), self.first.at[j, at], self.fs.at[j, at], self.fr.at[j, at], d=to
+        )
+
+    def mixing(self, j, at):
+        return remote(
+            self.mixed.at[j, at],
+            self.second.at[j, at],
+            self.ss.at[j, at],
+            self.sr.at[j, at],
+            d=self.mixes[at][1],
+        )
+
+    def handing(self, j, part):
+        return remote(
+            self.sums.at[j, part],
+            self.parts.at[j, self.h],
+            self.ps.at[j, part],
+            self.pr.at[j, self.h],
+            c=part,
+            h=self.c,
+        )
+
+    def stays(self, part):
+        return jnp.logical_and(self.c == part, self.h == self.c)
+
+    def start(self, j):
+        for at in range(len(self.sends)):
+            self.sending(j, at).start()
+        for at in range(len(self.blocks)):
+            self.loading(j, at).start()
+
+    def value(self, ref, j, at):
+        return ref[j, at].astype(jnp.float32)
+
+    def mix(self, j):
+        for at, (block, _) in enumerate(self.mixes):
+            self.loading(j, block).wait()
+            self.sending(j, block).wait_recv()
+            total = self.value(self.held, j, block) + self.value(self.first, j, block)
+            self.mixed[j, at] = total.astype(jnp.bfloat16)
+            self.mixing(j, at).start()
+
+    def hand(self, j):
+        for part in range(2):
+            own = 2 * part if self.mixes else part
+            self.loading(j, own).wait()
+            total = self.value(self.held, j, own)
+            for at in [own] if self.mixes else range(part, len(self.sends), 2):
+                self.sending(j, at).wait_recv()
+                total = total + self.value(self.first, j, at)
+            if self.mixes:
+                self.mixing(j, part).wait_recv()
+                total = total + self.value(self.second, j, part)
+            self.sums[j, part] = total.astype(jnp.bfloat16)
+
+            @pl.when(self.stays(part))
+            def _():
+                self.parts[j, self.h] = self.sums[j, part]
+
+            @pl.when(jnp.logical_not(self.stays(part)))
+            def _():
+                self.handing(j, part).start()
+
+    def arriving(self, j, of_h):
+        return remote(
+            self.parts.at[j, of_h], self.parts.at[j, of_h], self.ps.at[j, 0], self.pr.at[j, of_h], h=1 - self.h
+        )
+
+    def finish(self, j):
+        for of_h in range(2):
+
+            @pl.when(jnp.logical_not(jnp.logical_and(self.c == self.h, self.h == of_h)))
+            def _():
+                self.arriving(j, of_h).wait_recv()
+
+        cols = self.held.shape[3]
+        total = self.value(self.parts, j, 0) + self.value(self.parts, j, 1)
+        self.out[:, j * cols : (j + 1) * cols] = total
+        for at in range(len(self.sends)):
+            self.sending(j, at).wait_send()
+        for at in range(len(self.mixes)):
+            self.mixing(j, at).wait_send()
+        for part in range(2):
+
+            @pl.when(jnp.logical_not(self.stays(part)))
+            def _():
+                self.handing(j, part).wait_send()
 
 
 class Job:
@@ -537,6 +697,7 @@
         refs = refs[count:]
     if carry_weights:
         weight_rows, here_rows, refs = refs[0], refs[1], refs[2:]
+    gradients, refs = refs[:last], refs[last:]
     outs = refs[:out_count]
     rest = refs[out_count:]
     if gather:
@@ -551,7 +712,12 @@
         rest = rest[count:]
     if last:
         low, back, gain_acc, tiles, got, ts, tr, gs, gr = rest[:9]
-        rest = rest[9:]
+        returned, rest = rest[9:22], rest[22:]
+        cols = returned[0].shape[3]
+        pieces = [
+            (array, start) for array in gradients for start in range(0, array.shape[1], cols)
+        ]
+        back_home = Return(nd, pieces, outs[2], returned)
     if gather:
         finished, ls, lr, fs, fr, keep, rest = rest[0], *rest[1:6], rest[6:]
     mine, other, sums, arrivals, cs, cr, loc, ss, sr = rest
@@ -645,6 +811,10 @@
         for k in range(CHUNKS):
             to_core(index, k).start()
             local(index, k).start()
+
+    if last:
+        for j in range(RETURN_AHEAD):
+            back_home.start(j)
 
     def both(index, k):
         local(index, k).wait()
@@ -700,7 +870,7 @@
             gains_to(step).wait_send()
             return carry
 
-        def send_gains():
+        def send_gains(_):
             cut = gain_acc.shape[1] // (2 * nd)
             lines = cut // 128
             tiles[...] = jnp.zeros_like(tiles)
@@ -774,6 +944,16 @@
         here_out().start()
         for step in SUM_ORDER:
             steps[step[0]](int(step[1:]))
+    elif last:
+        steps = {
+            "w": back_home.start,
+            "m": back_home.mix,
+            "h": back_home.hand,
+            "f": lambda k: finish(k, 0),
+            "g": send_gains,
+        }
+        for step in RETURN_ORDER:
+            steps[step[0]](int(step[1:]))
     else:
         lax.fori_loop(0, CHUNKS, finish, 0)
         for job in running[1:]:
@@ -782,8 +962,6 @@
             for k in range(CHUNKS):
                 pass_across(k)
     if last:
-        send_gains()
-
         @pl.when(apart)
         def _():
             for k in range(CHUNKS):
@@ -792,6 +970,8 @@
 
         outs[1][...] = lax.fori_loop(1, count, add_gains, tiles[d * 2 + c])
         lax.fori_loop(1, count, drain_gains, 0)
+        for j in range(len(pieces)):
+            back_home.finish(j)
     for job in running:
         job.finish()
     if gather:
@@ -815,9 +995,7 @@
             along(step, k).wait_send()
 
 
-def exchange(
-    collective_id, partial, aux, outs, epilogue, gather, weight_rows=(), jobs=(), last=False
-):
+def exchange(collective_id, partial, aux, outs, epilogue, gather, weight_rows=(), jobs=(), last=()):
     nd, tl = lax.axis_size("d"), lax.axis_size("l")
     total, width = partial.shape
     own = total // (2 * tl)
@@ -861,6 +1039,9 @@
             dma((others,)),
             dma((others,)),
         ]
+        cols = min(array.shape[1] for array in last) // 2
+        count = sum(array.shape[1] for array in last) // cols
+        scratch += Return.scratch(nd, count, outs[2].shape[0], cols)
     if gather:
         scratch += [
             pltpu.VMEM((own, width), jnp.bfloat16),
@@ -892,10 +1073,10 @@
             gather,
             bool(weight_rows),
             jobs,
-            last,
+            len(last),
         ),
         out_shape=tuple(out_shape),
-        in_specs=[anywhere] + [vmem] * len(aux) + [anywhere] * (len(given) + len(weight_rows)),
+        in_specs=[anywhere] + [vmem] * len(aux) + [anywhere] * (len(given) + len(weight_rows) + len(last)),
         out_specs=out_specs,
         scratch_shapes=scratch,
         compiler_params=pltpu.CompilerParams(
@@ -904,7 +1085,7 @@
         cost_estimate=pl.CostEstimate(
             flops=0, bytes_accessed=200_000_000 if gather else 110_000_000, transcendentals=0
         ),
-    )(partial, *aux, *given, *weight_rows)
+    )(partial, *aux, *given, *weight_rows, *last)
 
 
 def middle_rows(total, rows, k, aux, outs):
@@ -1267,18 +1448,6 @@
     return values[:, :half], values[:, half:]
 
 
-def return_blocks(rows):
-    core, upper = lax.axis_index("c"), lax.axis_index("h")
-    half = rows.shape[0] // 2
-    first, second = rows[:half], rows[half:]
-    mine = jnp.where(core == 0, first, second)
-    other = lax.ppermute(jnp.where(core == 0, second, first), "c", shift_perm(2, 1))
-    same = core == upper
-    sent = jnp.where(same, other, mine)
-    far = lax.ppermute(sent, "h", shift_perm(2, 1))
-    return jnp.where(same, mine, other).astype(jnp.float32) + far.astype(jnp.float32), sent
-
-
 def per_device(
     tokens,
     segment_ids,
@@ -1419,18 +1588,21 @@
     )
     qkv_back = jnp.concatenate([query_back, key_back, value_back], axis=1)
     qkv_grad = contract_rows(normed, qkv_back).astype(jnp.bfloat16)
-    attn_partial = jnp.concatenate([qkv_grad, o_wgrad.astype(jnp.bfloat16)], axis=1)
-    attn_rows = sum_over_d(after(attn_partial, mid_sum_far))
+    o_wgrad = o_wgrad.astype(jnp.bfloat16)
     branch = scatter_tokens(branch, qkv_grad)
     activations = trade((middle + branch).astype(jnp.bfloat16))
-    gradient, sums = exchange(
+    gradient, sums, attn_grad = exchange(
         None,
         contract_cols(after(qkv_back, qkv_grad), qkv_full).astype(jnp.bfloat16),
         (stream, gradient, as_row(attn_scale), mlp_gain_grad, q_gain_grad, k_gain_grad),
-        (whole(jnp.float32), jax.ShapeDtypeStruct((8, 128), jnp.float32)),
+        (
+            whole(jnp.float32),
+            jax.ShapeDtypeStruct((8, 128), jnp.float32),
+            jax.ShapeDtypeStruct((q_weight.shape[1], 2 * q_cols + 2 * kv_cols), jnp.float32),
+        ),
         stream_pull_rows,
         False,
-        last=True,
+        last=(qkv_grad, o_wgrad),
     )
     lines = cut // 128
     head_at = (lax.axis_index("d") * 2 + core) * head_cut
@@ -1438,9 +1610,8 @@
     def head_gain(line):
         return lax.dynamic_slice(sums[line], (head_at,), (head_cut,))[None]
 
-    attn_grad, attn_sent = return_blocks(after(attn_rows, sums))
-    activations = after(activations, attn_sent)
-    mid_sum_near = after(mid_sum_near, attn_sent)
+    mid_sum_near = after(mid_sum_near, sums)
+    down_sum_near = after(down_sum_near, sums)
     down_grad = columns_of(*return_halves(down_sum_near, down_sum_far))
     mine, other = return_halves(mid_sum_near, mid_sum_far)
     gate_grad = columns_of(mine[:, :half_cols], other[:, :half_cols])

time: 783 us -> 797 us (1.018)
  Pallas kernels: 388 us -> 417 us
  starting transfers between devices: 39.2 us -> 24.6 us
  waiting for transfers between devices: 130 us -> 141 us
    ppermute x2, waiting for transfers between devices: 66 us -> 102 us  [return_halves(): far = lax.ppermute(far, 'h', shift_perm(2, 1))]
    pallas_call x3, Pallas kernels: 238 us -> 267 us  [exchange(): pl.pallas_call(functools.partial(exchange_kernel, nd, tl, epilogue, len(a...]
    reduce_scatter x5 -> x4, waiting for transfers between devices: 13 us -> 0.03 us  [sum_over_d(): lax.psum_scatter(partial.astype(jnp.bfloat16), 'd', scatter_dimension=0,...]
    ppermute x2, starting transfers between devices: 12.1 us -> 3.4 us  [trade(): return lax.ppermute(values, ('c', 'h'), [(0, 0), (1, 2), (2, 1), (3, 3)])]
    ppermute x2 -> x0, waiting for transfers between devices: 8.3 us -> none  [the longest x1 8.3 us: return_blocks(): far = lax.ppermute(sent, 'h', shift_perm(2, 1))]
    unnamed x97 -> x93, local copies, waits for them, and re-layouts: 23.3 us -> 19.6 us
  transfers between devices with their start and end apart: 22 -> 19, of which waited for: 6 -> 5; matrix products, arithmetic and copies ran while one was open for 23% -> 22% of each run, Pallas kernels for 38% -> 41%
where the time goes in v9:
time: 797 us; the launch traced here: 793 us
  Pallas kernels  417 us (52%)
  waiting for transfers between devices  141 us (18%)
  matrix products  131 us (16%)
  local copies, waits for them, and re-layouts  35.3 us (4%)
  other arithmetic  29.1 us (4%)
  starting transfers between devices  24.6 us (3%)
  between operations  15.3 us (2%)
    pallas_call x3, Pallas kernels, exchange(): pl.pallas_call(functools.partial(exchange_kernel, nd, tl, epilogue, len(a...  267 us
    ppermute x2, waiting for transfers between devices, return_halves(): far = lax.ppermute(far, 'h', shift_perm(2, 1))  102 us
    pallas_call x1, Pallas kernels, enter(): pl.pallas_call(functools.partial(entry_kernel, nd, tl), name='entry', out...  95 us
    dot_general x5, matrix products, contract_rows(): lax.dot_general(left, right, (((0,), (0,)), ((), ())), preferred_element_...  36.7 us
    dot_general x4, matrix products, contract_cols(): lax.dot_general(left, right, (((1,), (1,)), ((), ())), preferred_element_...  36.2 us
    pallas_call x1, Pallas kernels, attention_pull(): pl.pallas_call(functools.partial(attention_pull_kernel, blocks, repeat),...  34.3 us
    ppermute x1, waiting for transfers between devices, gather_along(): lax.ppermute(own, 'l', shift_perm(places, step))  27.2 us
    dot_general x2, matrix products, hidden_pull(): hidden_grad = jnp.dot(grad_rows, down, preferred_element_type=jnp.float32)  20.8 us
  transfers between devices with their start and end apart: 19, of which 5 were waited for; matrix products, arithmetic and copies ran while one was open for 22% of the time, Pallas kernels for 41%

profile of v9, /device:TPU:0, one launch (start us, length us, event | category | flops | bytes accessed | tf_op | source)
XLA Modules:
  0.0 792.7 jit_solution(6346684660640761131)
XLA Ops:
  7.2 1.3 collective-permute-start
  8.6 0.7 reduce.1
  10.2 1.3 fusion.25.refs_9_
  12.7 2.1 fusion.16
  15.2 95.0 %entry.1 = (bf16[2048,1024]{1,0:T(8,128)(2,1)}, bf16[2048,512]{1,0:T(8,128)(2,1)}, bf16[512,1536]{1,0:T(8,128)(2,1)}, bf16[512,768]{1,0:T(8,128)(2,1)}, bf16[115...) custom-call(bf16[256,512]{1,0:T(8,128)(2,1)} %bitcast.87, bf16[256,256]{1,0:T(8,128)(2,1)} %bitcast.89, ...), custom_call_target="tpu_custom_call" | custom-call | bytes 250000000 | tf_op jit(solution)/shard_map/entry/pallas_call | solution.py:433
  110.8 2.3 slice.96
  114.5 2.9 collective-permute-start.1
  117.6 2.6 slice.94.refs_1_
  120.1 4.0 fusion
  124.2 9.2 %fusion.14.refs_0_.refs_1_.refs_2_ = f32[1152,1024]{1,0:T(8,128)} fusion(bf16[2048,1024]{1,0:T(8,128)(2,1)} %get-tuple-element.54, bf16[1152,2048]{1,0:T(8,128)(2,1)S(1)} %copy-done.11, f32[2048]{0:T(1024)S(1)} %bitcast.97, f32[1152]{0:T(1024)S(1)} %add_rsqrt_fusion), kind=kOutput, calls=%fused_computation.46 | convolution fusion | flops 4841275392 | bytes 13644288 | tf_op jit(solution)/shard_map/dot_general | solution.py:1515
  133.4 20.2 %attention.1 = (bf16[1152,512]{1,0:T(8,128)(2,1)}, bf16[1152,256]{1,0:T(8,128)(2,1)S(1)}, bf16[1152,256]{1,0:T(8,128)(2,1)S(1)}, bf16[1152,512]{1,0:T(8,128)(2,1)}, f32[1152,256]{1,0:T(8,128)}) custom-call(s32[4]{0:T(128)S(1)} %get-tuple-element.90.order_ref, f32[1152,1024]{1,0:T(8,128)} %fusion.14.refs_0_.refs_1_.refs_2_, ...), custom_call_target="tpu_custom_call" | custom-call | flops 2717908992 | bytes 60000000 | tf_op jit(solution)/shard_map/attention/pallas_call | solution.py:1237
  153.7 6.1 convolution_convert_fusion.2.refs_0_
  159.7 9.5 %collective-permute-done.1.refs_4_ = bf16[512,768]{1,0:T(8,128)(2,1)S(1)} collective-permute-done((bf16[512,768]{1,0:T(8,128)(2,1)}, bf16[512,768]{1,0:T(8,128)(2,1)S(1)}, u32[]{:S(2)}, u32[]{:S(2)}) %collective-permute-start.1) | collective-permute-done | bytes 786464 | tf_op jit(solution)/shard_map/ppermute | solution.py:1503
  169.2 0.9 copy-done.19
  170.1 90.3 %shard_map.237 = (f32[288,2048]{1,0:T(8,128)}, bf16[1152,2048]{1,0:T(8,128)(2,1)}, bf16[2048,1536]{1,0:T(8,128)(2,1)}) custom-call(bf16[1152,2048]{1,0:T(8,128)(2,1)} %convolution_convert_fusion.2.refs_0_, bf16[288,2048]{1,0:T(8,128)(2,1)} %slice.94.refs_1_, f32[1,2048]{1,0:T(1,128)} %bitcast.93, bf16[512,1536]{1,0:T(8,128)(2,1)} %get-tuple-element.57.refs_3_, ...), custom_call_target="tpu_custom_call" | custom-call | bytes 200000000 | tf_op jit(solution)/shard_map/pallas_call | solution.py:1065
  261.6 27.2 %collective-permute-done.2 = bf16[288,2048]{1,0:T(8,128)(2,1)S(1)} collective-permute-done((bf16[288,2048]{1,0:T(8,128)(2,1)S(1)}, bf16[288,2048]{1,0:T(8,128)(2,1)S(1)}, u32[]{:S(2)}, u32[]{:S(2)}) %collective-permute-start.2) | collective-permute-done | bytes 1179680 | tf_op jit(solution)/shard_map/ppermute | solution.py:1391
  289.1 9.7 %fusion.34 = f32[1152,1536]{1,0:T(8,128)S(1)} fusion(bf16[1152,2048]{1,0:T(8,128)(2,1)S(1)} %copy-done.16, bf16[2048,1536]{1,0:T(8,128)(2,1)} %get-tuple-element.63), kind=kOutput, calls=%fused_computation.106 | convolution fusion | flops 7247757312 | bytes 18087936 | tf_op jit(solution)/shard_map/dot_general | solution.py:1541
  298.7 1.1 multiply_convert_fusion.2.refs_7_
  299.8 1.8 copy-done.15
  302.1 0.8 copy-done.12
  302.9 2.2 copy-done.22
  305.1 5.8 convolution_convert_fusion.4
  311.5 11.7 %fusion.33 = f32[1152,1536]{1,0:T(8,128)S(1)} fusion(bf16[1152,2048]{1,0:T(8,128)(2,1)} %get-tuple-element.62.refs_4_, bf16[2048,1536]{1,0:T(8,128)(2,1)} %all-gather.4.cloned.1.call-done), kind=kOutput, calls=%fused_computation.105 | convolution fusion | flops 7247757312 | bytes 18087936 | tf_op jit(solution)/shard_map/dot_general | solution.py:1538
  323.2 1.1 multiply_convert_fusion.3.refs_6_
  324.3 2.5 copy-done.14
  326.8 1.3 copy-done.23
  328.1 5.9 convolution_convert_fusion.5
  334.0 10.2 %fusion.8 = (bf16[1152,768]{1,0:T(8,128)(2,1)S(1)}, bf16[1152,768]{1,0:T(8,128)(2,1)S(1)}) fusion(f32[1152,1536]{1,0:T(8,128)} %copy-done.15, bf16[1152,2048]{1,0:T(8,128)(2,1)} %copy-done.22, bf16[2048,768]{1,0:T(8,128)(2,1)} %all-gather.8.cloned.1.call-done.refs_9_), kind=kOutput, calls=%fused_computation.19 | convolution fusion | flops 3636264960 | bytes 18481152 | tf_op jit(solution)/shard_map/dot_general | solution.py:1551
  344.1 13.0 %convolution_convert_fusion.1 = bf16[2048,1536]{1,0:T(8,128)(2,1)} fusion(bf16[1152,2048]{1,0:T(8,128)(2,1)} %get-tuple-element.62.refs_4_, bf16[1152,768]{1,0:T(8,128)(2,1)S(1)} %get-tuple-element.92, bf16[1152,768]{1,0:T(8,128)(2,1)S(1)} %get-tuple-element.91), kind=kOutput, calls=%fused_computation.8 | convolution fusion | flops 7257980928 | bytes 14548992 | tf_op jit(solution)/shard_map/dot_general | solution.py:47
  357.8 10.6 %fusion.5 = (bf16[1152,768]{1,0:T(8,128)(2,1)S(1)}, bf16[1152,768]{1,0:T(8,128)(2,1)S(1)}) fusion(f32[1152,1536]{1,0:T(8,128)} %copy-done.14, bf16[1152,2048]{1,0:T(8,128)(2,1)} %copy-done.22, bf16[2048,768]{1,0:T(8,128)(2,1)} %all-gather.6.cloned.1.call-done.refs_8_), kind=kOutput, calls=%fused_computation.16 | convolution fusion | flops 3636264960 | bytes 18481152 | tf_op jit(solution)/shard_map/dot_general | solution.py:1551
  368.5 12.3 %fusion.29 = f32[1152,2048]{1,0:T(8,128)} fusion(bf16[2048,1536]{1,0:T(8,128)(2,1)} %all-gather.4.cloned.1.call-done, bf16[1152,768]{1,0:T(8,128)(2,1)S(1)} %get-tuple-element.94, bf16[1152,768]{1,0:T(8,128)(2,1)S(1)} %get-tuple-element.93), kind=kOutput, calls=%fused_computation.101 | convolution fusion | flops 7254835200 | bytes 19267584 | tf_op jit(solution)/shard_map/dot_general | solution.py:53
  380.7 11.1 %add_convert_fusion.refs_0_ = bf16[1152,2048]{1,0:T(8,128)(2,1)} fusion(f32[1152,2048]{1,0:T(8,128)} %fusion.29, bf16[2048,1536]{1,0:T(8,128)(2,1)S(1)} %bitcast.104, bf16[1152,768]{1,0:T(8,128)(2,1)S(1)} %get-tuple-element.92, bf16[1152,768]{1,0:T(8,128)(2,1)S(1)} %get-tuple-element.91), kind=kOutput, calls=%fused_computation.6 | convolution fusion | flops 7259553792 | bytes 23986176 | tf_op jit(solution)/shard_map/dot_general | solution.py:53
  391.8 2.1 pad_maximum_fusion.refs_5_
  393.9 61.3 %shard_map.238 = (f32[288,2048]{1,0:T(8,128)}, f32[1,2048]{1,0:T(1,128)}, bf16[1152,2048]{1,0:T(8,128)(2,1)}, bf16[2048,1536]{1,0:T(8,128)(2,1)}, bf16[1152,2048]{1,0:T(8,128)(2,1)}) custom-call(bf16[1152,2048]{1,0:T(8,128)(2,1)} %add_convert_fusion.refs_0_, f32[288,2048]{1,0:T(8,128)} %get-tuple-element.59.refs_1_, ...), custom_call_target="tpu_custom_call" | custom-call | bytes 200000000 | tf_op jit(solution)/shard_map/pallas_call | solution.py:1065
  456.5 1.9 slice.102
  458.9 6.9 convolution_convert_fusion.7.refs_11_
  465.8 34.3 %shard_map.239 = (bf16[1152,512]{1,0:T(8,128)(2,1)}, bf16[1152,256]{1,0:T(8,128)(2,1)}, bf16[1152,256]{1,0:T(8,128)(2,1)}, f32[8,128]{1,0:T(8,128)}, f32[8,128]{1,0:T(8,128)}) custom-call(s32[4]{0:T(128)} %copy-done.5, f32[1152,1024]{1,0:T(8,128)} %fusion.14.refs_0_.refs_1_.refs_2_, f32[1152,1024]{1,0:T(8,128)} %fusion.14.refs_0_.refs_1_.refs_2_, ...), custom_call_target="tpu_custom_call" | custom-call | flops 6794772480 | bytes 120000000 | tf_op jit(solution)/shard_map/pallas_call | solution.py:1343
  500.2 1.5 constant_dynamic-update-slice_fusion.5
  501.7 1.1 constant_dynamic-update-slice_fusion.4
  503.0 7.9 convolution_convert_fusion.3.refs_7_
  510.9 2.8 convert_add_fusion
  513.7 2.2 copy-done.8
  515.9 1.2 slice.195
  517.7 6.8 convolution_convert_fusion.refs_0_
  524.5 4.1 convolution_convert_fusion.6.refs_8_
  528.7 115.3 %shard_map.240 = (f32[288,2048]{1,0:T(8,128)}, f32[8,128]{1,0:T(8,128)}, f32[256,1536]{1,0:T(8,128)}) custom-call(bf16[1152,2048]{1,0:T(8,128)(2,1)} %convolution_convert_fusion.refs_0_, bf16[288,2048]{1,0:T(8,128)(2,1)} %slice.94.refs_1_, f32[288,2048]{1,0:T(8,128)} %get-tuple-element.79.refs_2_, f32[1,2048]{1,0:T(1,128)} %bitcast.95, ...), custom_call_target="tpu_custom_call" | custom-call | bytes 110000000 | tf_op jit(solution)/shard_map/pallas_call | solution.py:1065
  643.9 1.3 fusion.31
  645.3 1.9 slice_bitcast_fusion.2
  647.1 0.9 collective-permute-start.10
  648.0 2.0 collective-permute-start.8
  650.0 3.3 fusion.12
  653.3 2.0 collective-permute-start.7
  655.4 0.8 fusion.32
  656.1 72.9 %collective-permute-done.10 = bf16[512,768]{1,0:T(8,128)(2,1)} collective-permute-done((bf16[512,768]{1,0:T(8,128)(2,1)}, bf16[512,768]{1,0:T(8,128)(2,1)}, u32[]{:S(2)}, u32[]{:S(2)}) %collective-permute-start.10) | collective-permute-done | bytes 786464 | tf_op jit(solution)/shard_map/ppermute | solution.py:1421
  729.0 1.5 convert_add_fusion.2
  732.0 1.0 slice_bitcast_fusion
  733.2 29.5 %collective-permute-done.8 = bf16[512,1536]{1,0:T(8,128)(2,1)} collective-permute-done((bf16[512,1536]{1,0:T(8,128)(2,1)}, bf16[512,1536]{1,0:T(8,128)(2,1)}, u32[]{:S(2)}, u32[]{:S(2)}) %collective-permute-start.8) | collective-permute-done | bytes 1572896 | tf_op jit(solution)/shard_map/ppermute | solution.py:1421
  762.7 2.3 convert_add_fusion.1
  765.2 12.6 %collective-permute-start.9 = (bf16[256,1536]{1,0:T(8,128)(2,1)S(1)}, bf16[256,1536]{1,0:T(8,128)(2,1)S(1)}, u32[]{:S(2)}, u32[]{:S(2)}) collective-permute-start(bf16[256,1536]{1,0:T(8,128)(2,1)S(1)} %select_convert_fusion), channel_id=1, source_target_pairs={{4,0},{0,4},{5,1},{1,5},{6,2},{2,6},{7,3},{3,7},{12,8},{8,12},{13,... | collective-permute-start | bytes 2359304 | tf_op jit(solution)/shard_map/ppermute | solution.py:1427
  777.8 1.4 maximum_bitcast_fusion.2
  780.2 1.4 maximum_bitcast_fusion.1
  781.6 1.4 maximum_bitcast_fusion
  782.9 1.0 copy.57
  783.9 1.4 copy.58
  (153 shorter events, 12.7 us)
Async XLA Ops:
  7.2 304.3 %all-gather.4.cloned.1.call-start = ((), (), s32[]{:S(2)}) async-start(), calls=%async_computation.4 | async-start | bytes 7864320 | tf_op jit(solution)/shard_map/all_gather | solution.py:1501
  7.2 4.4 collective-permute-start
  10.1 123.2 %copy-start.5 = (s32[4]{0:T(128)}, s32[4]{0:T(128)S(1)}, u32[]{:S(2)}) copy-start(s32[4]{0:T(128)S(1)} %get-tuple-element.90.order_ref) | copy-start | bytes 52
  15.2 118.2 %copy-start.1 = (f32[1152,128]{1,0:T(8,128)}, f32[1152,128]{1,0:T(8,128)S(1)}, u32[]{:S(2)}) copy-start(f32[1152,128]{1,0:T(8,128)S(1)} %get-tuple-element.117.refs_3_.refs_2_) | copy-start | bytes 1769476
  15.2 118.2 %copy-start.2 = (f32[1152,128]{1,0:T(8,128)}, f32[1152,128]{1,0:T(8,128)S(1)}, u32[]{:S(2)}) copy-start(f32[1152,128]{1,0:T(8,128)S(1)} %get-tuple-element.118.refs_4_.refs_3_) | copy-start | bytes 1769476
  110.2 2.9 copy-start.25
  110.2 7.3 copy-start.20
  110.3 223.7 %all-gather.8.cloned.1.call-start = ((), (), s32[]{:S(2)}) async-start(), calls=%async_computation.6 | async-start | bytes 3932160 | tf_op jit(solution)/shard_map/all_gather | solution.py:1536
  110.8 22.6 %copy-start = (s32[1152,1]{1,0:T(8,128)}, s32[1152,1]{1,0:T(8,128)S(1)}, u32[]{:S(2)}) copy-start(s32[1152,1]{1,0:T(8,128)S(1)} %copy.37.refs_7_.refs_6_) | copy-start | bytes 13828
  113.2 20.2 %copy-start.3 = (f32[1,128]{1,0:T(1,128)}, f32[1,128]{1,0:T(1,128)S(1)}, u32[]{:S(2)}) copy-start(f32[1,128]{1,0:T(1,128)S(1)} %reshape_reshape.12.refs_6_.refs_5_) | copy-start | bytes 1540
  113.3 20.1 %copy-start.4 = (f32[1,128]{1,0:T(1,128)}, f32[1,128]{1,0:T(1,128)S(1)}, u32[]{:S(2)}) copy-start(f32[1,128]{1,0:T(1,128)S(1)} %reshape_reshape.11.refs_5_.refs_4_) | copy-start | bytes 1540
  114.5 9.6 %copy-start.26 = (f32[1,2,8,128]{3,1,2,0:T(2,128)}, f32[1,2,8,128]{3,1,2,0:T(2,128)S(1)}, u32[]{:S(2)}) copy-start(f32[1,2,8,128]{3,1,2,0:T(2,128)S(1)} %copy.46) | copy-start | bytes 24580
  114.5 54.7 %collective-permute-start.1 = (bf16[512,768]{1,0:T(8,128)(2,1)}, bf16[512,768]{1,0:T(8,128)(2,1)S(1)}, u32[]{:S(2)}, u32[]{:S(2)}) collective-permute-start(bf16[512,768]{1,0:T(8,128)(2,1)} %slice.96), channel_id=1, source_target_pairs={{2,0},{0,2},{3,1},{1,3},{6,4},{4,6},{7,5},{5,7},{10,8},{8,10},{11,... | collective-permute-start | bytes 2359304 | tf_op jit(solution)/shard_map/ppermute | solution.py:1503
  117.5 142.9 %collective-permute-start.4 = (bf16[512,768]{1,0:T(8,128)(2,1)S(1)}, bf16[512,768]{1,0:T(8,128)(2,1)}, u32[]{:S(2)}, u32[]{:S(2)}) collective-permute-start(bf16[512,768]{1,0:T(8,128)(2,1)S(1)} %copy-done.20), channel_id=1, source_target_pairs={{2,0},{0,2},{3,1},{1,3},{6,4},{4,6},{7,5},{5,7},{10,8},{8,10},{11,... | collective-permute-start | bytes 2359304 | tf_op jit(solution)/shard_map/ppermute | solution.py:1504
  117.6 6.6 copy-start.11
  124.1 9.2 %copy-start.28 = (f32[1152]{0:T(1024)}, f32[1152]{0:T(1024)S(1)}, u32[]{:S(2)}) copy-start(f32[1152]{0:T(1024)S(1)} %add_rsqrt_fusion) | copy-start | bytes 13828
  133.4 20.3 %copy-start.31 = (bf16[2048,512]{1,0:T(8,128)(2,1)S(1)}, bf16[2048,512]{1,0:T(8,128)(2,1)}, u32[]{:S(2)}) copy-start(bf16[2048,512]{1,0:T(8,128)(2,1)} %get-tuple-element.56) | copy-start | bytes 6291460
  153.7 6.1 copy-start.6
  153.7 6.1 copy-start.7
  169.2 0.9 copy-start.19
  170.1 90.4 %copy-start.9 = (bf16[288,2048]{1,0:T(8,128)(2,1)S(1)}, bf16[288,2048]{1,0:T(8,128)(2,1)}, u32[]{:S(2)}) copy-start(bf16[288,2048]{1,0:T(8,128)(2,1)} %get-tuple-element.60.refs_2_) | copy-start | bytes 3538948
  260.4 97.4 %all-gather.6.cloned.1.call-start = ((), (), s32[]{:S(2)}) async-start(), calls=%async_computation.5 | async-start | bytes 3932160 | tf_op jit(solution)/shard_map/all_gather | solution.py:1502
  260.5 28.3 %collective-permute-start.2 = (bf16[288,2048]{1,0:T(8,128)(2,1)S(1)}, bf16[288,2048]{1,0:T(8,128)(2,1)S(1)}, u32[]{:S(2)}, u32[]{:S(2)}) collective-permute-start(bf16[288,2048]{1,0:T(8,128)(2,1)S(1)} %copy-done.9), channel_id=1, source_target_pairs={{1,0},{0,1},{3,2},{2,3},{5,4},{4,5},{7,6},{6,7},{9,8},{8,9},{11,10... | collective-permute-start | bytes 3538952 | tf_op jit(solution)/shard_map/ppermute | solution.py:1391
  261.2 385.9 %reduce-scatter.11.cloned.1.call-start = ((), (), s32[]{:S(2)}) async-start(), calls=%async_computation.10 | async-start | bytes 3932160 | tf_op jit(solution)/shard_map/reduce_scatter | solution.py:1439
  261.5 27.6 %copy-start.16 = (bf16[1152,2048]{1,0:T(8,128)(2,1)S(1)}, bf16[1152,2048]{1,0:T(8,128)(2,1)}, u32[]{:S(2)}) copy-start(bf16[1152,2048]{1,0:T(8,128)(2,1)} %get-tuple-element.62.refs_4_) | copy-start | bytes 14155780
  289.0 12.8 %collective-permute-start.3 = (bf16[576,2048]{1,0:T(8,128)(2,1)S(1)}, bf16[576,2048]{1,0:T(8,128)(2,1)S(1)}, u32[]{:S(2)}, u32[]{:S(2)}) collective-permute-start(bf16[576,2048]{1,0:T(8,128)(2,1)S(1)} %pad_maximum_fusion.2), channel_id=1, source_target_pairs={{4,0},{0,4},{5,1},{1,5},{6,2},{2,6},{7,3},{3,7},{12,8},{8,12},{13,... | collective-permute-start | bytes 7077896 | tf_op jit(solution)/shard_map/ppermute | solution.py:1396
  298.7 2.9 copy-start.15
  301.7 1.2 copy-start.12
  302.9 2.2 copy-start.22
  311.0 337.1 %reduce-scatter.7.cloned.1.call-start = ((), (), s32[]{:S(2)}) async-start(), calls=%async_computation.8 | async-start | bytes 7864320 | tf_op jit(solution)/shard_map/reduce_scatter | solution.py:1439
  323.2 3.6 copy-start.14
  323.2 4.9 copy-start.23
  328.1 5.9 copy-start.13
  357.2 299.0 %reduce-scatter.9.cloned.1.call-start = ((), (), s32[]{:S(2)}) async-start(), calls=%async_computation.9 | async-start | bytes 3932160 | tf_op jit(solution)/shard_map/reduce_scatter | solution.py:1439
  357.7 375.5 %reduce-scatter.5.cloned.1.call-start = ((), (), s32[]{:S(2)}) async-start(), calls=%async_computation.7 | async-start | bytes 7864320 | tf_op jit(solution)/shard_map/reduce_scatter | solution.py:1439
  357.8 22.9 %slice-start.4 = ((s8[6291456]{0:T(1024)(128)(4,1)}), s8[4194304]{0:T(1024)(128)(4,1)S(1)}, s32[]{:S(2)}) async-start(s8[6291456]{0:T(1024)(128)(4,1)} %bitcast.103), calls=%async_computation.15 | async-start | bytes 8388608
  368.4 12.3 %slice-start.5 = ((s8[6291456]{0:T(1024)(128)(4,1)}), s8[2097152]{0:T(1024)(128)(4,1)S(1)}, s32[]{:S(2)}) async-start(s8[6291456]{0:T(1024)(128)(4,1)} %bitcast.103), calls=%async_computation.16 | async-start | bytes 4194304
  455.2 0.7 copy-start.24
  458.5 52.4 %collective-permute-start.5 = (bf16[576,2048]{1,0:T(8,128)(2,1)S(1)}, bf16[576,2048]{1,0:T(8,128)(2,1)}, u32[]{:S(2)}, u32[]{:S(2)}) collective-permute-start(bf16[576,2048]{1,0:T(8,128)(2,1)S(1)} %slice.102), channel_id=1, source_target_pairs={{4,0},{0,4},{5,1},{1,5},{6,2},{2,6},{7,3},{3,7},{12,8},{8,12},{13,... | collective-permute-start | bytes 7077896 | tf_op jit(solution)/shard_map/ppermute | solution.py:1404
  458.9 44.0 %slice-start = ((s8[4718592]{0:T(1024)(128)(4,1)}), s8[4194304]{0:T(1024)(128)(4,1)S(1)}, s32[]{:S(2)}) async-start(s8[4718592]{0:T(1024)(128)(4,1)} %bitcast.80), calls=%async_computation.11 | async-start | bytes 8388608
  465.8 37.1 %slice-start.1 = ((s8[4718592]{0:T(1024)(128)(4,1)}), s8[524288]{0:T(1024)(128)(4,1)S(1)}, s32[]{:S(2)}) async-start(s8[4718592]{0:T(1024)(128)(4,1)} %bitcast.80), calls=%async_computation.12 | async-start | bytes 1048576
  500.2 2.7 copy-start.21
  500.2 2.8 copy-start.27
  500.2 2.8 copy-start.29
  502.9 8.1 %slice-start.2 = ((s8[4718592]{0:T(1024)(128)(4,1)}), s8[4194304]{0:T(1024)(128)(4,1)S(1)}, s32[]{:S(2)}) async-start(s8[4718592]{0:T(1024)(128)(4,1)} %bitcast.82), calls=%async_computation.13 | async-start | bytes 8388608
  503.0 7.9 slice-start.3
  510.9 6.8 copy-start.30
  513.7 2.2 copy-start.8
  515.9 8.6 %slice-start.6 = ((s8[4718592]{0:T(1024)(128)(4,1)}), s8[524288]{0:T(1024)(128)(4,1)S(1)}, s32[]{:S(2)}) async-start(s8[4718592]{0:T(1024)(128)(4,1)} %bitcast.105), calls=%async_computation.17 | async-start | bytes 1048576
  517.1 7.4 slice-start.7
  517.1 7.4 copy-start.32
  517.1 130.9 %collective-permute-start.6 = (bf16[288,2048]{1,0:T(8,128)(2,1)}, bf16[288,2048]{1,0:T(8,128)(2,1)S(1)}, u32[]{:S(2)}, u32[]{:S(2)}) collective-permute-start(bf16[288,2048]{1,0:T(8,128)(2,1)} %slice.195), channel_id=1, source_target_pairs={{1,0},{0,1},{3,2},{2,3},{5,4},{4,5},{7,6},{6,7},{9,8},{8,9},{11,10... | collective-permute-start | bytes 3538952 | tf_op jit(solution)/shard_map/ppermute | solution.py:1409
  528.7 121.4 %copy-start.10 = (f32[288,2048]{1,0:T(8,128)S(1)}, f32[288,2048]{1,0:T(8,128)}, u32[]{:S(2)}) copy-start(f32[288,2048]{1,0:T(8,128)} %get-tuple-element.59.refs_1_) | copy-start | bytes 7077892
  647.1 81.9 %collective-permute-start.10 = (bf16[512,768]{1,0:T(8,128)(2,1)}, bf16[512,768]{1,0:T(8,128)(2,1)}, u32[]{:S(2)}, u32[]{:S(2)}) collective-permute-start(bf16[512,768]{1,0:T(8,128)(2,1)} %reduce-scatter.11.cloned.1.call-done), channel_id=1, source_target_pairs={{2,0},{0,2},{3,1},{1,3},{6,4},{4,6},{7,5},{5,7},{10,8},{8,10},{11,... | collective-permute-start | bytes 2359304 | tf_op jit(solution)/shard_map/ppermute | solution.py:1421
  648.0 114.7 %collective-permute-start.8 = (bf16[512,1536]{1,0:T(8,128)(2,1)}, bf16[512,1536]{1,0:T(8,128)(2,1)}, u32[]{:S(2)}, u32[]{:S(2)}) collective-permute-start(bf16[512,1536]{1,0:T(8,128)(2,1)} %reduce-scatter.7.cloned.1.call-done), channel_id=1, source_target_pairs={{2,0},{0,2},{3,1},{1,3},{6,4},{4,6},{7,5},{5,7},{10,8},{8,10},{11,... | collective-permute-start | bytes 4718600 | tf_op jit(solution)/shard_map/ppermute | solution.py:1421
  653.3 78.7 %copy-start.18 = (f32[256,1536]{1,0:T(8,128)S(1)}, f32[256,1536]{1,0:T(8,128)}, u32[]{:S(2)}) copy-start(f32[256,1536]{1,0:T(8,128)} %get-tuple-element.85) | copy-start | bytes 4718596
  653.3 79.8 %collective-permute-start.7 = (bf16[288,2048]{1,0:T(8,128)(2,1)}, bf16[288,2048]{1,0:T(8,128)(2,1)S(1)}, u32[]{:S(2)}, u32[]{:S(2)}) collective-permute-start(bf16[288,2048]{1,0:T(8,128)(2,1)} %fusion.12), channel_id=1, source_target_pairs={{0,0},{2,4},{4,2},{6,6},{1,1},{3,5},{5,3},{7,7},{8,8},{10,12},{12,... | collective-permute-start | bytes 3538952 | tf_op jit(solution)/shard_map/ppermute | solution.py:1386
  730.6 2.4 collective-permute-start.11
  765.2 14.5 %collective-permute-start.9 = (bf16[256,1536]{1,0:T(8,128)(2,1)S(1)}, bf16[256,1536]{1,0:T(8,128)(2,1)S(1)}, u32[]{:S(2)}, u32[]{:S(2)}) collective-permute-start(bf16[256,1536]{1,0:T(8,128)(2,1)S(1)} %select_convert_fusion), channel_id=1, source_target_pairs={{4,0},{0,4},{5,1},{1,5},{6,2},{2,6},{7,3},{3,7},{12,8},{8,12},{13,... | collective-permute-start | bytes 2359304 | tf_op jit(solution)/shard_map/ppermute | solution.py:1427
  781.6 2.4 copy-start.17
Sparse Core Ops, SparseCore 0:
  110.4 76.1 all-gather.3
  260.6 42.7 all-gather.7
  305.2 43.8 all-gather.5
  351.9 43.8 reduce-scatter.10
  398.7 70.0 reduce-scatter.6
  471.6 43.8 reduce-scatter.8
  518.5 111.1 reduce-scatter.4

commit v10 on v9

--- a/solution.py
+++ b/solution.py
@@ -1,4 +1,5 @@
 import functools
+import math
 
 import jax
 import jax.numpy as jnp
@@ -833,8 +834,8 @@
 
     for job in running:
         job.fetch()
-    if running:
-        running[0].run()
+    for job in running[:-1]:
+        job.run()
 
     if last:
         apart = c != h
@@ -956,7 +957,7 @@
             steps[step[0]](int(step[1:]))
     else:
         lax.fori_loop(0, CHUNKS, finish, 0)
-        for job in running[1:]:
+        for job in running[-1:]:
             job.run()
         if gather:
             for k in range(CHUNKS):
@@ -1163,7 +1164,7 @@
     acc, den = refs[13:]
     rows = q.shape[0] // blocks
     tile = key_tile(q.shape[0])
-    scale = HEAD_WIDTH**-0.5
+    scale = HEAD_WIDTH**-0.5 * math.log2(math.e)
 
     def rotated(values, gain, at):
         scaled = values * head_norm(values) * gain
@@ -1192,7 +1193,7 @@
             for r in range(repeat):
                 head = slice(r * HEAD_WIDTH, (r + 1) * HEAD_WIDTH)
                 scores = dot_last(qr[at, head], kr[keys, :]) * scale
-                weights = jnp.where(mask, jnp.exp(scores), 0.0)
+                weights = jnp.where(mask, jnp.exp2(scores), 0.0)
                 den[r] += jnp.sum(weights, axis=-1, keepdims=True)
                 acc[r] += jnp.dot(
                     weights.astype(jnp.bfloat16), vb[keys, :], preferred_element_type=jnp.float32
@@ -1262,9 +1263,9 @@
 
 
 def attention_pull_kernel(blocks, repeat, order_ref, *refs):
-    q, k, cosine, sine, q_gain, k_gain, first, qr, kr, vb, total, grad = refs[:12]
-    dq, dk, dv, dq_gain, dk_gain = refs[12:17]
-    shares, share_grads, dq_acc, dk_acc, dv_acc, inner_sum = refs[17:]
+    q, k, cosine, sine, q_gain, k_gain, first, qr, kr, vb, total, out, grad = refs[:13]
+    dq, dk, dv, dq_gain, dk_gain = refs[13:18]
+    dq_acc, dk_acc, dv_acc = refs[18:]
     rows = q.shape[0] // blocks
     tile = key_tile(q.shape[0])
     scale = HEAD_WIDTH**-0.5
@@ -1289,35 +1290,31 @@
         row0 = order_ref[i] * rows
         tiles = (row0 + rows + tile - 1) // tile
         dq_acc[...] = jnp.zeros_like(dq_acc)
-        inner_sum[...] = jnp.zeros_like(inner_sum)
-
-        def first_pass(t, inner):
+        heads = [slice(r * HEAD_WIDTH, (r + 1) * HEAD_WIDTH) for r in range(repeat)]
+        inner = [
+            jnp.sum(
+                grad[at, head].astype(jnp.float32) * out[at, head].astype(jnp.float32),
+                axis=-1,
+                keepdims=True,
+            )
+            for head in heads
+        ]
+        inverse = [1.0 / total[at, r : r + 1] for r in range(repeat)]
+
+        def over_keys(t, carry):
             keys = rows_at(t, tile)
             mask = tile_mask(first[at, :], t * tile, tile, row0, rows)
-            for r in range(repeat):
-                head = slice(r * HEAD_WIDTH, (r + 1) * HEAD_WIDTH)
-                scores = dot_last(qr[at, head], kr[keys, :]) * scale
-                share = jnp.where(mask, jnp.exp(scores), 0.0) * (1.0 / total[at, r : r + 1])
+            for r, head in enumerate(heads):
+                scores = dot_last(qr[at, head], kr[keys, :]) * (scale * math.log2(math.e))
+                share = jnp.where(mask, jnp.exp2(scores), 0.0) * inverse[r]
                 share_grad = dot_last(grad[at, head], vb[keys, :])
-                inner_sum[r] += jnp.sum(share * share_grad, axis=-1, keepdims=True)
-                shares[t, r] = share
-                share_grads[t, r] = share_grad
-            return inner
-
-        lax.fori_loop(0, tiles, first_pass, 0)
-
-        def second_pass(t, inner):
-            keys = rows_at(t, tile)
-            for r in range(repeat):
-                head = slice(r * HEAD_WIDTH, (r + 1) * HEAD_WIDTH)
-                share = shares[t, r]
-                score_grad = (share * (share_grads[t, r] - inner_sum[r])).astype(jnp.bfloat16)
+                score_grad = (share * (share_grad - inner[r])).astype(jnp.bfloat16)
                 dq_acc[r] += jnp.dot(score_grad, kr[keys, :], preferred_element_type=jnp.float32)
                 dk_acc[keys, :] += contract_rows(score_grad, qr[at, head])
                 dv_acc[keys, :] += contract_rows(share.astype(jnp.bfloat16), grad[at, head])
-            return inner
-
-        lax.fori_loop(0, tiles, second_pass, 0)
+            return carry
+
+        lax.fori_loop(0, tiles, over_keys, 0)
         for r in range(repeat):
             head = slice(r * HEAD_WIDTH, (r + 1) * HEAD_WIDTH)
             dq[at, head] = pull(q[at, head], q_gain[...], dq_acc[r] * scale, at, dq_gain)
@@ -1339,7 +1336,7 @@
     blocks = order.shape[0]
     repeat, columns, fixed, raw, table_specs = attention_specs(rows, q_heads, kv_heads)
     wide, narrow = q_heads * HEAD_WIDTH, kv_heads * HEAD_WIDTH
-    own, tile = rows // blocks, key_tile(rows)
+    own = rows // blocks
     return pl.pallas_call(
         functools.partial(attention_pull_kernel, blocks, repeat),
         out_shape=(
@@ -1354,7 +1351,7 @@
             grid=(kv_heads,),
             in_specs=raw[:2]
             + table_specs
-            + [columns(repeat), columns(1), columns(1), columns(1), columns(repeat)],
+            + [columns(repeat), columns(1), columns(1), columns(1), columns(repeat), columns(repeat)],
             out_specs=[
                 columns(repeat),
                 columns(1),
@@ -1363,12 +1360,9 @@
                 fixed(8, HEAD_WIDTH),
             ],
             scratch_shapes=[
-                pltpu.VMEM((rows // tile, repeat, own, tile), jnp.float32),
-                pltpu.VMEM((rows // tile, repeat, own, tile), jnp.float32),
                 pltpu.VMEM((repeat, own, HEAD_WIDTH), jnp.float32),
                 pltpu.VMEM((rows, HEAD_WIDTH), jnp.float32),
                 pltpu.VMEM((rows, HEAD_WIDTH), jnp.float32),
-                pltpu.VMEM((repeat, own, 1), jnp.float32),
             ],
         ),
         compiler_params=pltpu.CompilerParams(vmem_limit_bytes=56 << 20),
@@ -1501,7 +1495,6 @@
     mid_near = lax.all_gather(mid_rows, "d", axis=0, tiled=True)
     down_near = lax.all_gather(down_rows, "d", axis=0, tiled=True)
     up_far = lax.ppermute(mid_rows[:, half_cols:], "h", shift_perm(2, 1))
-    down_far = lax.ppermute(down_rows, "h", shift_perm(2, 1))
     grad_half = gather_along(cotangent)
     gains = gains.reshape(gains.shape[0], -1)
     attn_scale = gains[:, :cut].reshape(-1)
@@ -1513,12 +1506,12 @@
     normed = rms_scale(group.astype(jnp.float32), attn_scale).astype(jnp.bfloat16)
     head_count, kv_heads = q_cols // HEAD_WIDTH, kv_cols // HEAD_WIDTH
     qkv = jnp.dot(normed, qkv_full, preferred_element_type=jnp.float32)
+    down_far = lax.ppermute(after(down_rows, qkv), "h", shift_perm(2, 1))
     tables = (cosine, sine, as_row(q_scale), as_row(k_scale), first_row)
     query_reduced, key_reduced, value_reduced, attended, totals = attention(
         qkv, tables, order, head_count, kv_heads
     )
 
-    grad_rows = gather_across([grad_half[0]] + [after(part, attended) for part in grad_half[1:]])
 
     def whole(values):
         return jax.ShapeDtypeStruct((own_rows, width), values)
@@ -1533,6 +1526,7 @@
         True,
         (mid_rows, after(up_far, attended)),
     )
+    grad_rows = gather_across([grad_half[0]] + [after(part, normed_mid) for part in grad_half[1:]])
     down_far = lax.all_gather(after(down_far, normed_mid), "d", axis=0, tiled=True)
 
     mid = jnp.dot(normed_mid, mid_near, preferred_element_type=jnp.float32)
@@ -1543,9 +1537,7 @@
     hidden_far = swiglu(gate_far, up_far).astype(jnp.bfloat16)
     down_grad_far = contract_rows(grad_rows, hidden_far).astype(jnp.bfloat16)
     down_sum_far = sum_over_d(down_grad_far)
-    down_grad_near = contract_rows(grad_rows, hidden_near).astype(jnp.bfloat16)
-    down_sum_near = sum_over_d(down_grad_near)
-    grad_rows = after(grad_rows, down_grad_near, down_grad_far)
+    grad_rows = after(grad_rows, down_grad_far, hidden_near)
 
     def hidden_pull(gate, up, down):
         hidden_grad = jnp.dot(grad_rows, down, preferred_element_type=jnp.float32)
@@ -1561,7 +1553,7 @@
     mid_sum_far = sum_over_d(mid_grad_far)
     normed_grad = contract_cols(mid_back_near, mid_near) + contract_cols(mid_back_far, mid_far)
     normed_grad = normed_grad.astype(jnp.bfloat16)
-    gradient, mlp_gain_grad, grad_rows, mid_grad_near, branch = exchange(
+    gradient, mlp_gain_grad, grad_rows, mid_grad_near, down_grad_near, branch = exchange(
         2,
         after(normed_grad, mid_grad_far),
         (middle, cotangent, as_row(mlp_scale)),
@@ -1570,9 +1562,11 @@
         True,
         jobs=(
             Job((normed_mid, mid_back_near), mid_near.shape, 8, weight_grad_tile),
+            Job((grad_rows, hidden_near), down_near.shape, 8, weight_grad_tile),
             Job((hidden_near, hidden_far, down_near, down_far), normed_mid.shape, 4, down_tile),
         ),
     )
+    down_sum_near = sum_over_d(down_grad_near)
     mid_sum_near = sum_over_d(mid_grad_near)
 
     out_grad = jnp.dot(grad_rows, o_full, preferred_element_type=jnp.float32).astype(jnp.bfloat16)
@@ -1581,7 +1575,7 @@
         qkv,
         tables,
         order,
-        (query_reduced, key_reduced, value_reduced, totals),
+        (query_reduced, key_reduced, value_reduced, totals, attended),
         out_grad,
         head_count,
         kv_heads,

time: 797 us -> 791 us (level)
    dot_general x5 -> x4, matrix products: 36.7 us -> 30.4 us  [contract_rows(): lax.dot_general(left, right, (((0,), (0,)), ((), ())), preferred_element_...]
    unnamed x93 -> x89, local copies, waits for them, and re-layouts: 19.6 us -> 17.8 us
  transfers between devices with their start and end apart: 19 -> 19, of which waited for: 5 -> 5; matrix products, arithmetic and copies ran while one was open for 22% -> 21% of each run, Pallas kernels for 41% -> 41%
where the time goes in v10:
time: 791 us; the launch traced here: 786 us
  Pallas kernels  415 us (52%)
  waiting for transfers between devices  142 us (18%)
  matrix products  125 us (16%)
  local copies, waits for them, and re-layouts  33.5 us (4%)
  other arithmetic  30.7 us (4%)
  starting transfers between devices  24.5 us (3%)
  between operations  15.2 us (2%)
    pallas_call x3, Pallas kernels, exchange(): pl.pallas_call(functools.partial(exchange_kernel, nd, tl, epilogue, len(a...  268 us
    ppermute x2, waiting for transfers between devices, return_halves(): far = lax.ppermute(far, 'h', shift_perm(2, 1))  103 us
    pallas_call x1, Pallas kernels, enter(): pl.pallas_call(functools.partial(entry_kernel, nd, tl), name='entry', out...  95 us
    dot_general x4, matrix products, contract_cols(): lax.dot_general(left, right, (((1,), (1,)), ((), ())), preferred_element_...  35.9 us
    pallas_call x1, Pallas kernels, attention_pull(): pl.pallas_call(functools.partial(attention_pull_kernel, blocks, repeat),...  32.6 us
    dot_general x4, matrix products, contract_rows(): lax.dot_general(left, right, (((0,), (0,)), ((), ())), preferred_element_...  30.4 us
    ppermute x1, waiting for transfers between devices, gather_along(): lax.ppermute(own, 'l', shift_perm(places, step))  27.2 us
    dot_general x2, matrix products, hidden_pull(): hidden_grad = jnp.dot(grad_rows, down, preferred_element_type=jnp.float32)  21 us
  transfers between devices with their start and end apart: 19, of which 5 were waited for; matrix products, arithmetic and copies ran while one was open for 21% of the time, Pallas kernels for 41%

profile of v10, /device:TPU:0, one launch (start us, length us, event | category | flops | bytes accessed | tf_op | source)
XLA Modules:
  0.0 786.1 jit_solution(7447365389908030043)
XLA Ops:
  7.2 1.3 collective-permute-start
  8.6 0.7 reduce.1
  9.3 0.7 reduce.2
  10.2 1.3 fusion.25.refs_9_
  12.7 2.1 fusion.16
  15.2 95.0 %entry.1 = (bf16[2048,1024]{1,0:T(8,128)(2,1)}, bf16[2048,512]{1,0:T(8,128)(2,1)}, bf16[512,1536]{1,0:T(8,128)(2,1)}, bf16[512,768]{1,0:T(8,128)(2,1)}, bf16[115...) custom-call(bf16[256,512]{1,0:T(8,128)(2,1)} %bitcast.85, bf16[256,256]{1,0:T(8,128)(2,1)} %bitcast.87, ...), custom_call_target="tpu_custom_call" | custom-call | bytes 250000000 | tf_op jit(solution)/shard_map/entry/pallas_call | solution.py:434
  110.8 2.3 slice.96
  114.5 2.9 collective-permute-start.1
  117.5 2.6 slice.94.refs_1_
  120.0 4.0 fusion
  124.1 9.3 %fusion.14.refs_0_.refs_1_.refs_2_ = f32[1152,1024]{1,0:T(8,128)} fusion(bf16[2048,1024]{1,0:T(8,128)(2,1)} %get-tuple-element.56, bf16[1152,2048]{1,0:T(8,128)(2,1)S(1)} %copy-done.12, f32[2048]{0:T(1024)S(1)} %bitcast.95, f32[1152]{0:T(1024)S(1)} %add_rsqrt_fusion), kind=kOutput, calls=%fused_computation.45 | convolution fusion | flops 4841275392 | bytes 13644288 | tf_op jit(solution)/shard_map/dot_general | solution.py:1508
  133.4 19.9 %attention.1 = (bf16[1152,512]{1,0:T(8,128)(2,1)}, bf16[1152,256]{1,0:T(8,128)(2,1)S(1)}, bf16[1152,256]{1,0:T(8,128)(2,1)S(1)}, bf16[1152,512]{1,0:T(8,128)(2,1)}, f32[1152,256]{1,0:T(8,128)}) custom-call(s32[4]{0:T(128)S(1)} %get-tuple-element.94.order_ref, f32[1152,1024]{1,0:T(8,128)} %fusion.14.refs_0_.refs_1_.refs_2_, ...), custom_call_target="tpu_custom_call" | custom-call | flops 2717908992 | bytes 60000000 | tf_op jit(solution)/shard_map/attention/pallas_call | solution.py:1238
  153.4 6.1 convolution_convert_fusion.2.refs_0_
  159.4 9.8 %collective-permute-done.1.refs_4_ = bf16[512,768]{1,0:T(8,128)(2,1)S(1)} collective-permute-done((bf16[512,768]{1,0:T(8,128)(2,1)}, bf16[512,768]{1,0:T(8,128)(2,1)S(1)}, u32[]{:S(2)}, u32[]{:S(2)}) %collective-permute-start.1) | collective-permute-done | bytes 786464 | tf_op jit(solution)/shard_map/ppermute | solution.py:1497
  169.2 0.9 copy-done.19
  170.1 90.4 %shard_map.237 = (f32[288,2048]{1,0:T(8,128)}, bf16[1152,2048]{1,0:T(8,128)(2,1)}, bf16[2048,1536]{1,0:T(8,128)(2,1)}) custom-call(bf16[1152,2048]{1,0:T(8,128)(2,1)} %convolution_convert_fusion.2.refs_0_, bf16[288,2048]{1,0:T(8,128)(2,1)} %slice.94.refs_1_, f32[1,2048]{1,0:T(1,128)} %bitcast.91, bf16[512,1536]{1,0:T(8,128)(2,1)} %get-tuple-element.59.refs_3_, ...), custom_call_target="tpu_custom_call" | custom-call | bytes 200000000 | tf_op jit(solution)/shard_map/pallas_call | solution.py:1066
  261.6 27.2 %collective-permute-done.2 = bf16[288,2048]{1,0:T(8,128)(2,1)S(1)} collective-permute-done((bf16[288,2048]{1,0:T(8,128)(2,1)S(1)}, bf16[288,2048]{1,0:T(8,128)(2,1)S(1)}, u32[]{:S(2)}, u32[]{:S(2)}) %collective-permute-start.2) | collective-permute-done | bytes 1179680 | tf_op jit(solution)/shard_map/ppermute | solution.py:1385
  289.1 9.7 %fusion.33 = f32[1152,1536]{1,0:T(8,128)S(1)} fusion(bf16[1152,2048]{1,0:T(8,128)(2,1)S(1)} %copy-done.16, bf16[2048,1536]{1,0:T(8,128)(2,1)} %get-tuple-element.65), kind=kOutput, calls=%fused_computation.104 | convolution fusion | flops 7247757312 | bytes 18087936 | tf_op jit(solution)/shard_map/dot_general | solution.py:1535
  298.8 1.1 multiply_convert_fusion.3.refs_9_
  299.9 1.7 copy-done.13
  302.0 0.8 copy-done.15
  302.8 2.1 copy-done.11
  304.9 5.9 convolution_convert_fusion.4
  311.3 11.7 %fusion.34 = f32[1152,1536]{1,0:T(8,128)S(1)} fusion(bf16[1152,2048]{1,0:T(8,128)(2,1)} %get-tuple-element.63.refs_4_, bf16[2048,1536]{1,0:T(8,128)(2,1)} %all-gather.4.cloned.1.call-done), kind=kOutput, calls=%fused_computation.105 | convolution fusion | flops 7247757312 | bytes 18087936 | tf_op jit(solution)/shard_map/dot_general | solution.py:1532
  323.1 2.9 copy-done.14
  326.0 2.3 multiply_convert_fusion.2.refs_7_.refs_8_
  328.3 10.7 %fusion.8 = (bf16[1152,768]{1,0:T(8,128)(2,1)S(1)}, bf16[1152,768]{1,0:T(8,128)(2,1)S(1)}) fusion(f32[1152,1536]{1,0:T(8,128)} %copy-done.13, bf16[1152,2048]{1,0:T(8,128)(2,1)} %copy-done.11, bf16[2048,768]{1,0:T(8,128)(2,1)} %all-gather.8.cloned.1.call-done.refs_11_), kind=kOutput, calls=%fused_computation.19 | convolution fusion | flops 3636264960 | bytes 18481152 | tf_op jit(solution)/shard_map/dot_general | solution.py:1543
  339.0 12.8 %convolution_convert_fusion.1 = bf16[2048,1536]{1,0:T(8,128)(2,1)} fusion(bf16[1152,2048]{1,0:T(8,128)(2,1)} %get-tuple-element.63.refs_4_, bf16[1152,768]{1,0:T(8,128)(2,1)S(1)} %get-tuple-element.96, bf16[1152,768]{1,0:T(8,128)(2,1)S(1)} %get-tuple-element.95), kind=kOutput, calls=%fused_computation.8 | convolution fusion | flops 7257980928 | bytes 14548992 | tf_op jit(solution)/shard_map/dot_general | solution.py:48
  352.0 10.3 %fusion.5 = (bf16[1152,768]{1,0:T(8,128)(2,1)S(1)}, bf16[1152,768]{1,0:T(8,128)(2,1)S(1)}) fusion(f32[1152,1536]{1,0:T(8,128)} %copy-done.14, bf16[1152,2048]{1,0:T(8,128)(2,1)} %copy-done.11, bf16[2048,768]{1,0:T(8,128)(2,1)} %all-gather.6.cloned.1.call-done.refs_10_), kind=kOutput, calls=%fused_computation.16 | convolution fusion | flops 3636264960 | bytes 18481152 | tf_op jit(solution)/shard_map/dot_general | solution.py:1543
  362.3 12.0 %fusion.29 = f32[1152,2048]{1,0:T(8,128)} fusion(bf16[2048,1536]{1,0:T(8,128)(2,1)} %all-gather.4.cloned.1.call-done, bf16[1152,768]{1,0:T(8,128)(2,1)S(1)} %get-tuple-element.98, bf16[1152,768]{1,0:T(8,128)(2,1)S(1)} %get-tuple-element.97), kind=kOutput, calls=%fused_computation.100 | convolution fusion | flops 7254835200 | bytes 19267584 | tf_op jit(solution)/shard_map/dot_general | solution.py:54
  374.3 11.1 %add_convert_fusion.refs_0_ = bf16[1152,2048]{1,0:T(8,128)(2,1)} fusion(f32[1152,2048]{1,0:T(8,128)} %fusion.29, bf16[2048,1536]{1,0:T(8,128)(2,1)S(1)} %bitcast.102, bf16[1152,768]{1,0:T(8,128)(2,1)S(1)} %get-tuple-element.96, bf16[1152,768]{1,0:T(8,128)(2,1)S(1)} %get-tuple-element.95), kind=kOutput, calls=%fused_computation.6 | convolution fusion | flops 7259553792 | bytes 23986176 | tf_op jit(solution)/shard_map/dot_general | solution.py:54
  385.4 2.1 pad_maximum_fusion.refs_5_
  387.5 61.4 %shard_map.238 = (f32[288,2048]{1,0:T(8,128)}, f32[1,2048]{1,0:T(1,128)}, bf16[1152,2048]{1,0:T(8,128)(2,1)}, bf16[2048,1536]{1,0:T(8,128)(2,1)}, bf16[2048,768]{1,0:T(8,128)(2,1)}, /*index=5*/bf16[1152,2048]{1,0:T(8,128)(2,1)}) custom-call(bf16[1152,2048]{1,0:T(8,128)(2,1)} %add_convert_fusion.refs_0_, f32[288,2048]{1,0:T(8,128)} %get-tuple-element.61.refs_1_, ...), custom_call_target="tpu_custom_call" | custom-call | bytes 200000000 | tf_op jit(solution)/shard_map/pallas_call | solution.py:1066
  448.9 0.7 reduce-scatter.5.cloned.1.call-update
  450.3 1.9 slice.102
  452.6 6.8 convolution_convert_fusion.6.refs_12_
  459.4 32.6 %shard_map.239 = (bf16[1152,512]{1,0:T(8,128)(2,1)}, bf16[1152,256]{1,0:T(8,128)(2,1)}, bf16[1152,256]{1,0:T(8,128)(2,1)}, f32[8,128]{1,0:T(8,128)}, f32[8,128]{1,0:T(8,128)}) custom-call(s32[4]{0:T(128)} %copy-done.5, f32[1152,1024]{1,0:T(8,128)} %fusion.14.refs_0_.refs_1_.refs_2_, f32[1152,1024]{1,0:T(8,128)} %fusion.14.refs_0_.refs_1_.refs_2_, ...), custom_call_target="tpu_custom_call" | custom-call | flops 6794772480 | bytes 120000000 | tf_op jit(solution)/shard_map/pallas_call | solution.py:1340
  492.1 1.5 constant_dynamic-update-slice_fusion.5
  493.6 1.2 constant_dynamic-update-slice_fusion.4
  494.9 7.6 convolution_convert_fusion.3.refs_7_
  502.6 3.2 convert_add_fusion
  505.8 2.1 copy-done.8
  508.0 1.2 slice.195
  509.6 6.8 convolution_convert_fusion.refs_0_
  516.4 4.1 convolution_convert_fusion.5.refs_8_
  520.5 115.9 %shard_map.240 = (f32[288,2048]{1,0:T(8,128)}, f32[8,128]{1,0:T(8,128)}, f32[256,1536]{1,0:T(8,128)}) custom-call(bf16[1152,2048]{1,0:T(8,128)(2,1)} %convolution_convert_fusion.refs_0_, bf16[288,2048]{1,0:T(8,128)(2,1)} %slice.94.refs_1_, f32[288,2048]{1,0:T(8,128)} %get-tuple-element.82.refs_2_, f32[1,2048]{1,0:T(1,128)} %bitcast.93, ...), custom_call_target="tpu_custom_call" | custom-call | bytes 110000000 | tf_op jit(solution)/shard_map/pallas_call | solution.py:1066
  636.4 1.3 fusion.31
  637.7 1.9 slice_bitcast_fusion.2
  639.6 0.9 collective-permute-start.10
  640.5 2.0 collective-permute-start.8
  642.5 3.3 fusion.12
  645.8 2.0 collective-permute-start.7
  647.8 0.8 fusion.32
  648.6 73.9 %collective-permute-done.10 = bf16[512,768]{1,0:T(8,128)(2,1)} collective-permute-done((bf16[512,768]{1,0:T(8,128)(2,1)}, bf16[512,768]{1,0:T(8,128)(2,1)}, u32[]{:S(2)}, u32[]{:S(2)}) %collective-permute-start.10) | collective-permute-done | bytes 786464 | tf_op jit(solution)/shard_map/ppermute | solution.py:1415
  722.5 1.5 convert_add_fusion.2
  725.5 1.0 slice_bitcast_fusion
  726.7 29.5 %collective-permute-done.8 = bf16[512,1536]{1,0:T(8,128)(2,1)} collective-permute-done((bf16[512,1536]{1,0:T(8,128)(2,1)}, bf16[512,1536]{1,0:T(8,128)(2,1)}, u32[]{:S(2)}, u32[]{:S(2)}) %collective-permute-start.8) | collective-permute-done | bytes 1572896 | tf_op jit(solution)/shard_map/ppermute | solution.py:1415
  756.2 2.3 convert_add_fusion.1
  758.7 12.6 %collective-permute-start.9 = (bf16[256,1536]{1,0:T(8,128)(2,1)S(1)}, bf16[256,1536]{1,0:T(8,128)(2,1)S(1)}, u32[]{:S(2)}, u32[]{:S(2)}) collective-permute-start(bf16[256,1536]{1,0:T(8,128)(2,1)S(1)} %select_convert_fusion), channel_id=1, source_target_pairs={{4,0},{0,4},{5,1},{1,5},{6,2},{2,6},{7,3},{3,7},{12,8},{8,12},{13,... | collective-permute-start | bytes 2359304 | tf_op jit(solution)/shard_map/ppermute | solution.py:1421
  771.3 1.4 maximum_bitcast_fusion.2
  773.7 1.4 maximum_bitcast_fusion.1
  775.1 1.4 maximum_bitcast_fusion
  776.4 1.0 copy.57
  777.4 1.4 copy.58
  (148 shorter events, 10.7 us)
Async XLA Ops:
  7.2 304.1 %all-gather.4.cloned.1.call-start = ((), (), s32[]{:S(2)}) async-start(), calls=%async_computation.4 | async-start | bytes 7864320 | tf_op jit(solution)/shard_map/all_gather | solution.py:1495
  7.2 4.4 collective-permute-start
  10.1 123.3 %copy-start.5 = (s32[4]{0:T(128)}, s32[4]{0:T(128)S(1)}, u32[]{:S(2)}) copy-start(s32[4]{0:T(128)S(1)} %get-tuple-element.94.order_ref) | copy-start | bytes 52
  15.2 118.2 %copy-start.1 = (f32[1152,128]{1,0:T(8,128)}, f32[1152,128]{1,0:T(8,128)S(1)}, u32[]{:S(2)}) copy-start(f32[1152,128]{1,0:T(8,128)S(1)} %get-tuple-element.121.refs_3_.refs_2_) | copy-start | bytes 1769476
  15.2 118.2 %copy-start.2 = (f32[1152,128]{1,0:T(8,128)}, f32[1152,128]{1,0:T(8,128)S(1)}, u32[]{:S(2)}) copy-start(f32[1152,128]{1,0:T(8,128)S(1)} %get-tuple-element.122.refs_4_.refs_3_) | copy-start | bytes 1769476
  110.2 2.8 copy-start.23
  110.3 218.0 %all-gather.8.cloned.1.call-start = ((), (), s32[]{:S(2)}) async-start(), calls=%async_computation.6 | async-start | bytes 3932160 | tf_op jit(solution)/shard_map/all_gather | solution.py:1530
  110.8 22.6 %copy-start = (s32[1152,1]{1,0:T(8,128)}, s32[1152,1]{1,0:T(8,128)S(1)}, u32[]{:S(2)}) copy-start(s32[1152,1]{1,0:T(8,128)S(1)} %copy.37.refs_7_.refs_6_) | copy-start | bytes 13828
  113.2 20.2 %copy-start.3 = (f32[1,128]{1,0:T(1,128)}, f32[1,128]{1,0:T(1,128)S(1)}, u32[]{:S(2)}) copy-start(f32[1,128]{1,0:T(1,128)S(1)} %reshape_reshape.12.refs_6_.refs_5_) | copy-start | bytes 1540
  113.3 20.1 %copy-start.4 = (f32[1,128]{1,0:T(1,128)}, f32[1,128]{1,0:T(1,128)S(1)}, u32[]{:S(2)}) copy-start(f32[1,128]{1,0:T(1,128)S(1)} %reshape_reshape.11.refs_5_.refs_4_) | copy-start | bytes 1540
  114.5 9.5 %copy-start.24 = (f32[1,2,8,128]{3,1,2,0:T(2,128)}, f32[1,2,8,128]{3,1,2,0:T(2,128)S(1)}, u32[]{:S(2)}) copy-start(f32[1,2,8,128]{3,1,2,0:T(2,128)S(1)} %copy.46) | copy-start | bytes 24580
  114.5 54.7 %collective-permute-start.1 = (bf16[512,768]{1,0:T(8,128)(2,1)}, bf16[512,768]{1,0:T(8,128)(2,1)S(1)}, u32[]{:S(2)}, u32[]{:S(2)}) collective-permute-start(bf16[512,768]{1,0:T(8,128)(2,1)} %slice.96), channel_id=1, source_target_pairs={{2,0},{0,2},{3,1},{1,3},{6,4},{4,6},{7,5},{5,7},{10,8},{8,10},{11,... | collective-permute-start | bytes 2359304 | tf_op jit(solution)/shard_map/ppermute | solution.py:1497
  117.5 6.6 copy-start.12
  124.0 9.3 %copy-start.26 = (f32[1152]{0:T(1024)}, f32[1152]{0:T(1024)S(1)}, u32[]{:S(2)}) copy-start(f32[1152]{0:T(1024)S(1)} %add_rsqrt_fusion) | copy-start | bytes 13828
  124.0 9.3 %copy-start.20 = (bf16[512,768]{1,0:T(8,128)(2,1)S(1)}, bf16[512,768]{1,0:T(8,128)(2,1)}, u32[]{:S(2)}) copy-start(bf16[512,768]{1,0:T(8,128)(2,1)} %get-tuple-element.68) | copy-start | bytes 2359300
  133.3 127.1 %collective-permute-start.4 = (bf16[512,768]{1,0:T(8,128)(2,1)S(1)}, bf16[512,768]{1,0:T(8,128)(2,1)}, u32[]{:S(2)}, u32[]{:S(2)}) collective-permute-start(bf16[512,768]{1,0:T(8,128)(2,1)S(1)} %copy-done.20), channel_id=1, source_target_pairs={{2,0},{0,2},{3,1},{1,3},{6,4},{4,6},{7,5},{5,7},{10,8},{8,10},{11,... | collective-permute-start | bytes 2359304 | tf_op jit(solution)/shard_map/ppermute | solution.py:1509
  133.4 19.9 %copy-start.29 = (bf16[2048,512]{1,0:T(8,128)(2,1)S(1)}, bf16[2048,512]{1,0:T(8,128)(2,1)}, u32[]{:S(2)}) copy-start(bf16[2048,512]{1,0:T(8,128)(2,1)} %get-tuple-element.58) | copy-start | bytes 6291460
  153.4 6.1 copy-start.6
  153.4 6.1 copy-start.7
  169.2 0.9 copy-start.19
  170.1 90.5 %copy-start.9 = (bf16[288,2048]{1,0:T(8,128)(2,1)S(1)}, bf16[288,2048]{1,0:T(8,128)(2,1)}, u32[]{:S(2)}) copy-start(bf16[288,2048]{1,0:T(8,128)(2,1)} %get-tuple-element.62.refs_2_) | copy-start | bytes 3538948
  260.5 91.5 %all-gather.6.cloned.1.call-start = ((), (), s32[]{:S(2)}) async-start(), calls=%async_computation.5 | async-start | bytes 3932160 | tf_op jit(solution)/shard_map/all_gather | solution.py:1496
  260.5 28.3 %collective-permute-start.2 = (bf16[288,2048]{1,0:T(8,128)(2,1)S(1)}, bf16[288,2048]{1,0:T(8,128)(2,1)S(1)}, u32[]{:S(2)}, u32[]{:S(2)}) collective-permute-start(bf16[288,2048]{1,0:T(8,128)(2,1)S(1)} %copy-done.9), channel_id=1, source_target_pairs={{1,0},{0,1},{3,2},{2,3},{5,4},{4,5},{7,6},{6,7},{9,8},{8,9},{11,10... | collective-permute-start | bytes 3538952 | tf_op jit(solution)/shard_map/ppermute | solution.py:1385
  261.2 378.4 %reduce-scatter.11.cloned.1.call-start = ((), (), s32[]{:S(2)}) async-start(), calls=%async_computation.10 | async-start | bytes 3932160 | tf_op jit(solution)/shard_map/reduce_scatter | solution.py:1433
  261.5 27.6 %copy-start.16 = (bf16[1152,2048]{1,0:T(8,128)(2,1)S(1)}, bf16[1152,2048]{1,0:T(8,128)(2,1)}, u32[]{:S(2)}) copy-start(bf16[1152,2048]{1,0:T(8,128)(2,1)} %get-tuple-element.63.refs_4_) | copy-start | bytes 14155780
  289.0 12.7 %collective-permute-start.3 = (bf16[576,2048]{1,0:T(8,128)(2,1)S(1)}, bf16[576,2048]{1,0:T(8,128)(2,1)S(1)}, u32[]{:S(2)}, u32[]{:S(2)}) collective-permute-start(bf16[576,2048]{1,0:T(8,128)(2,1)S(1)} %pad_maximum_fusion.2), channel_id=1, source_target_pairs={{4,0},{0,4},{5,1},{1,5},{6,2},{2,6},{7,3},{3,7},{12,8},{8,12},{13,... | collective-permute-start | bytes 7077896 | tf_op jit(solution)/shard_map/ppermute | solution.py:1390
  298.8 2.8 copy-start.13
  301.6 1.2 copy-start.15
  302.8 2.1 copy-start.11
  310.8 329.7 %reduce-scatter.7.cloned.1.call-start = ((), (), s32[]{:S(2)}) async-start(), calls=%async_computation.8 | async-start | bytes 7864320 | tf_op jit(solution)/shard_map/reduce_scatter | solution.py:1433
  323.0 2.9 copy-start.14
  351.7 296.8 %reduce-scatter.9.cloned.1.call-start = ((), (), s32[]{:S(2)}) async-start(), calls=%async_computation.9 | async-start | bytes 3932160 | tf_op jit(solution)/shard_map/reduce_scatter | solution.py:1433
  352.0 22.3 %slice-start.4 = ((s8[6291456]{0:T(1024)(128)(4,1)}), s8[4194304]{0:T(1024)(128)(4,1)S(1)}, s32[]{:S(2)}) async-start(s8[6291456]{0:T(1024)(128)(4,1)} %bitcast.101), calls=%async_computation.15 | async-start | bytes 8388608
  362.3 12.0 %slice-start.5 = ((s8[6291456]{0:T(1024)(128)(4,1)}), s8[2097152]{0:T(1024)(128)(4,1)S(1)}, s32[]{:S(2)}) async-start(s8[6291456]{0:T(1024)(128)(4,1)} %bitcast.101), calls=%async_computation.16 | async-start | bytes 4194304
  448.9 0.8 copy-start.22
  448.9 277.9 %reduce-scatter.5.cloned.1.call-start = ((), (), s32[]{:S(2)}) async-start(), calls=%async_computation.7 | async-start | bytes 7864320 | tf_op jit(solution)/shard_map/reduce_scatter | solution.py:1433
  452.2 50.4 %collective-permute-start.5 = (bf16[576,2048]{1,0:T(8,128)(2,1)S(1)}, bf16[576,2048]{1,0:T(8,128)(2,1)}, u32[]{:S(2)}, u32[]{:S(2)}) collective-permute-start(bf16[576,2048]{1,0:T(8,128)(2,1)S(1)} %slice.102), channel_id=1, source_target_pairs={{4,0},{0,4},{5,1},{1,5},{6,2},{2,6},{7,3},{3,7},{12,8},{8,12},{13,... | collective-permute-start | bytes 7077896 | tf_op jit(solution)/shard_map/ppermute | solution.py:1398
  452.6 42.2 %slice-start = ((s8[4718592]{0:T(1024)(128)(4,1)}), s8[4194304]{0:T(1024)(128)(4,1)S(1)}, s32[]{:S(2)}) async-start(s8[4718592]{0:T(1024)(128)(4,1)} %bitcast.78), calls=%async_computation.11 | async-start | bytes 8388608
  459.4 35.4 %slice-start.1 = ((s8[4718592]{0:T(1024)(128)(4,1)}), s8[524288]{0:T(1024)(128)(4,1)S(1)}, s32[]{:S(2)}) async-start(s8[4718592]{0:T(1024)(128)(4,1)} %bitcast.78), calls=%async_computation.12 | async-start | bytes 1048576
  492.0 2.7 copy-start.21
  492.1 2.8 copy-start.25
  492.1 2.8 copy-start.27
  494.8 7.8 slice-start.2
  494.9 7.7 slice-start.3
  502.6 7.0 copy-start.28
  505.8 2.2 copy-start.8
  508.0 8.4 %slice-start.6 = ((s8[4718592]{0:T(1024)(128)(4,1)}), s8[524288]{0:T(1024)(128)(4,1)S(1)}, s32[]{:S(2)}) async-start(s8[4718592]{0:T(1024)(128)(4,1)} %bitcast.103), calls=%async_computation.17 | async-start | bytes 1048576
  509.2 7.2 slice-start.7
  509.2 7.2 copy-start.30
  509.2 131.3 %collective-permute-start.6 = (bf16[288,2048]{1,0:T(8,128)(2,1)}, bf16[288,2048]{1,0:T(8,128)(2,1)S(1)}, u32[]{:S(2)}, u32[]{:S(2)}) collective-permute-start(bf16[288,2048]{1,0:T(8,128)(2,1)} %slice.195), channel_id=1, source_target_pairs={{1,0},{0,1},{3,2},{2,3},{5,4},{4,5},{7,6},{6,7},{9,8},{8,9},{11,10... | collective-permute-start | bytes 3538952 | tf_op jit(solution)/shard_map/ppermute | solution.py:1403
  520.5 122.0 %copy-start.10 = (f32[288,2048]{1,0:T(8,128)S(1)}, f32[288,2048]{1,0:T(8,128)}, u32[]{:S(2)}) copy-start(f32[288,2048]{1,0:T(8,128)} %get-tuple-element.61.refs_1_) | copy-start | bytes 7077892
  639.6 83.0 %collective-permute-start.10 = (bf16[512,768]{1,0:T(8,128)(2,1)}, bf16[512,768]{1,0:T(8,128)(2,1)}, u32[]{:S(2)}, u32[]{:S(2)}) collective-permute-start(bf16[512,768]{1,0:T(8,128)(2,1)} %reduce-scatter.11.cloned.1.call-done), channel_id=1, source_target_pairs={{2,0},{0,2},{3,1},{1,3},{6,4},{4,6},{7,5},{5,7},{10,8},{8,10},{11,... | collective-permute-start | bytes 2359304 | tf_op jit(solution)/shard_map/ppermute | solution.py:1415
  640.5 115.7 %collective-permute-start.8 = (bf16[512,1536]{1,0:T(8,128)(2,1)}, bf16[512,1536]{1,0:T(8,128)(2,1)}, u32[]{:S(2)}, u32[]{:S(2)}) collective-permute-start(bf16[512,1536]{1,0:T(8,128)(2,1)} %reduce-scatter.7.cloned.1.call-done), channel_id=1, source_target_pairs={{2,0},{0,2},{3,1},{1,3},{6,4},{4,6},{7,5},{5,7},{10,8},{8,10},{11,... | collective-permute-start | bytes 4718600 | tf_op jit(solution)/shard_map/ppermute | solution.py:1415
  645.8 79.8 %copy-start.18 = (f32[256,1536]{1,0:T(8,128)S(1)}, f32[256,1536]{1,0:T(8,128)}, u32[]{:S(2)}) copy-start(f32[256,1536]{1,0:T(8,128)} %get-tuple-element.88) | copy-start | bytes 4718596
  645.8 80.8 %collective-permute-start.7 = (bf16[288,2048]{1,0:T(8,128)(2,1)}, bf16[288,2048]{1,0:T(8,128)(2,1)S(1)}, u32[]{:S(2)}, u32[]{:S(2)}) collective-permute-start(bf16[288,2048]{1,0:T(8,128)(2,1)} %fusion.12), channel_id=1, source_target_pairs={{0,0},{2,4},{4,2},{6,6},{1,1},{3,5},{5,3},{7,7},{8,8},{10,12},{12,... | collective-permute-start | bytes 3538952 | tf_op jit(solution)/shard_map/ppermute | solution.py:1380
  724.1 2.4 collective-permute-start.11
  758.7 14.5 %collective-permute-start.9 = (bf16[256,1536]{1,0:T(8,128)(2,1)S(1)}, bf16[256,1536]{1,0:T(8,128)(2,1)S(1)}, u32[]{:S(2)}, u32[]{:S(2)}) collective-permute-start(bf16[256,1536]{1,0:T(8,128)(2,1)S(1)} %select_convert_fusion), channel_id=1, source_target_pairs={{4,0},{0,4},{5,1},{1,5},{6,2},{2,6},{7,3},{3,7},{12,8},{8,12},{13,... | collective-permute-start | bytes 2359304 | tf_op jit(solution)/shard_map/ppermute | solution.py:1421
  775.1 2.4 copy-start.17
Sparse Core Ops, SparseCore 0:
  110.4 76.1 all-gather.3
  260.6 42.7 all-gather.7
  305.3 43.8 all-gather.5
  352.0 43.8 reduce-scatter.10
  398.8 70.0 reduce-scatter.6
  471.7 43.8 reduce-scatter.8
  518.6 112.8 reduce-scatter.4

commit v11 on v10

--- a/solution.py
+++ b/solution.py
@@ -459,24 +459,27 @@
 
 PIECES = 6
 RETURN_AHEAD = 2
+ROW_CHUNK = 48
 RETURN_ORDER = (
-    "m0", "w2", "f0", "m1", "w3", "f1", "h0", "m2", "w4", "f2", "g0", "h1", "m3", "w5", "h2", "m4",
-    "h3", "m5", "h4", "h5",
+    "m0", "w2", "f0", "f1", "m1", "w3", "f2", "f3", "h0", "m2", "w4", "f4", "f5", "g0", "h1", "m3",
+    "w5", "h2", "m4", "h3", "m5", "h4", "h5",
 )
 SUM_ORDER = (
-    "s3", "s4", "s5", "f0", "r3", "s0", "f1", "r4", "r0", "s1", "f2", "r5", "r1", "s2", "r2",
-    "a0", "a1", "a2",
+    "s3", "s4", "s5", "f0", "f1", "r3", "s0", "f2", "f3", "r4", "r0", "s1", "f4", "f5", "r5", "r1",
+    "s2", "r2", "a0", "a1", "a2", "a3", "a4", "a5",
 )
 
 
 class Return:
-    def __init__(self, nd, pieces, out, scratch):
-        self.nd, self.pieces, self.out = nd, pieces, out
+    def __init__(self, nd, pieces, outs, scratch):
+        self.nd, self.pieces = nd, pieces
         self.held, self.first, self.mixed, self.second, self.sums, self.parts = scratch[:6]
         (self.load, self.fs, self.fr, self.ss, self.sr, self.ps, self.pr) = scratch[6:]
         self.d, self.c, self.h = (lax.axis_index(name) for name in ("d", "c", "h"))
-        self.rows = out.shape[0]
+        self.rows = outs[0].shape[0]
         d = self.d
+        cols = self.first.shape[3]
+        self.places = [(out, start) for out in outs for start in range(0, out.shape[1], cols)]
         if nd == 4:
             side_x = d + 1 - 2 * lax.rem(d, 2)
             side_y = d + 2 - 4 * (d // 2)
@@ -610,9 +613,10 @@
             def _():
                 self.arriving(j, of_h).wait_recv()
 
-        cols = self.held.shape[3]
-        total = self.value(self.parts, j, 0) + self.value(self.parts, j, 1)
-        self.out[:, j * cols : (j + 1) * cols] = total
+        out, start = self.places[j]
+        out[:, start : start + self.first.shape[3]] = self.value(self.parts, j, 0) + self.value(
+            self.parts, j, 1
+        )
         for at in range(len(self.sends)):
             self.sending(j, at).wait_send()
         for at in range(len(self.mixes)):
@@ -718,14 +722,15 @@
         pieces = [
             (array, start) for array in gradients for start in range(0, array.shape[1], cols)
         ]
-        back_home = Return(nd, pieces, outs[2], returned)
+        back_home = Return(nd, pieces, outs[2:], returned)
     if gather:
         finished, ls, lr, fs, fr, keep, rest = rest[0], *rest[1:6], rest[6:]
     mine, other, sums, arrivals, cs, cr, loc, ss, sr = rest
     c, l = lax.axis_index("c"), lax.axis_index("l")
     d, h = lax.axis_index("d"), lax.axis_index("h")
     own = arrivals.shape[0] // (tl - 1)
-    chunk = own // CHUNKS
+    chunk = ROW_CHUNK
+    chunks = own // chunk
 
     def greet():
         barrier = pltpu.get_barrier_semaphore()
@@ -740,21 +745,21 @@
         greet()
 
     def part(base, k):
-        return rows_at(base * CHUNKS + k, chunk)
+        return rows_at(base * chunks + k, chunk)
 
     def to_core(index, k):
-        at = index * CHUNKS + k
+        at = index * chunks + k
         return remote(
             partial.at[part(tl + index, k)], other.at[part(index, k)], cs.at[at], cr.at[at], c=1 - c
         )
 
     def local(index, k):
         return pltpu.make_async_copy(
-            partial.at[part(index, k)], mine.at[part(index, k)], loc.at[index * CHUNKS + k]
+            partial.at[part(index, k)], mine.at[part(index, k)], loc.at[index * chunks + k]
         )
 
     def along(step, k):
-        at = (step - 1) * CHUNKS + k
+        at = (step - 1) * chunks + k
         return remote(
             sums.at[part(step - 1, k)],
             arrivals.at[part(step - 1, k)],
@@ -809,7 +814,7 @@
 
     order = list(range(1, tl)) + [0]
     for index in order:
-        for k in range(CHUNKS):
+        for k in range(chunks):
             to_core(index, k).start()
             local(index, k).start()
 
@@ -830,7 +835,7 @@
             along(step, k).start()
             return carry
 
-        lax.fori_loop(0, CHUNKS, pass_on, 0)
+        lax.fori_loop(0, chunks, pass_on, 0)
 
     for job in running:
         job.fetch()
@@ -894,18 +899,18 @@
         return remote(
             finished.at[part(0, k)],
             gathered(tl - step, k),
-            ls.at[(step - 1) * CHUNKS + k],
-            lr.at[(tl - step - 1) * CHUNKS + k],
+            ls.at[(step - 1) * chunks + k],
+            lr.at[(tl - step - 1) * chunks + k],
             l=lax.rem(l + step, tl),
         )
 
     def from_along(index, k):
-        at = (index - 1) * CHUNKS + k
+        at = (index - 1) * chunks + k
         return remote(gathered(index, k), gathered(index, k), ls.at[at], lr.at[at], l=l)
 
     def across(index, k):
         source = finished.at[part(0, k)] if index == 0 else gathered(index, k)
-        at = index * CHUNKS + k
+        at = index * chunks + k
         return remote(source, gathered(tl + index, k), fs.at[at], fr.at[at], c=1 - c)
 
     def finish(k, carry):
@@ -944,6 +949,8 @@
         here_in().wait()
         here_out().start()
         for step in SUM_ORDER:
+            if step[0] in "fa" and int(step[1:]) >= chunks:
+                continue
             steps[step[0]](int(step[1:]))
     elif last:
         steps = {
@@ -954,18 +961,20 @@
             "g": send_gains,
         }
         for step in RETURN_ORDER:
+            if step[0] == "f" and int(step[1:]) >= chunks:
+                continue
             steps[step[0]](int(step[1:]))
     else:
-        lax.fori_loop(0, CHUNKS, finish, 0)
+        lax.fori_loop(0, chunks, finish, 0)
         for job in running[-1:]:
             job.run()
         if gather:
-            for k in range(CHUNKS):
+            for k in range(chunks):
                 pass_across(k)
     if last:
         @pl.when(apart)
         def _():
-            for k in range(CHUNKS):
+            for k in range(chunks):
                 to_owner(k).wait()
                 outs[0][part(0, k), :] = back[part(0, k), :].astype(jnp.float32)
 
@@ -976,7 +985,7 @@
     for job in running:
         job.finish()
     if gather:
-        for k in range(CHUNKS):
+        for k in range(chunks):
             keep_own(k).wait()
             for index in range(tl):
                 across(index, k).wait()
@@ -989,7 +998,7 @@
                 for row_part in range(2):
                     from_far(j, row_part).wait_send()
         here_out().wait()
-    for k in range(CHUNKS):
+    for k in range(chunks):
         for index in range(tl):
             to_core(index, k).wait_send()
         for step in range(1, tl):
@@ -1000,6 +1009,7 @@
     nd, tl = lax.axis_size("d"), lax.axis_size("l")
     total, width = partial.shape
     own = total // (2 * tl)
+    chunks = own // ROW_CHUNK
     dma = pltpu.SemaphoreType.DMA
     vmem = pl.BlockSpec(memory_space=pltpu.VMEM)
     anywhere = pl.BlockSpec(memory_space=pl.ANY)
@@ -1035,8 +1045,8 @@
             pltpu.VMEM((1, width), jnp.float32),
             pltpu.VMEM((2 * nd, 8, 128), jnp.float32),
             pltpu.VMEM((others, 8, 128), jnp.float32),
-            dma((CHUNKS,)),
-            dma((CHUNKS,)),
+            dma((chunks,)),
+            dma((chunks,)),
             dma((others,)),
             dma((others,)),
         ]
@@ -1046,22 +1056,22 @@
     if gather:
         scratch += [
             pltpu.VMEM((own, width), jnp.bfloat16),
-            dma(((tl - 1) * CHUNKS,)),
-            dma(((tl - 1) * CHUNKS,)),
-            dma((tl * CHUNKS,)),
-            dma((tl * CHUNKS,)),
-            dma((CHUNKS,)),
+            dma(((tl - 1) * chunks,)),
+            dma(((tl - 1) * chunks,)),
+            dma((tl * chunks,)),
+            dma((tl * chunks,)),
+            dma((chunks,)),
         ]
     scratch += [
         pltpu.VMEM((tl * own, width), jnp.bfloat16),
         pltpu.VMEM((tl * own, width), jnp.bfloat16),
         pltpu.VMEM(((tl - 1) * own, width), jnp.bfloat16),
         pltpu.VMEM(((tl - 1) * own, width), jnp.bfloat16),
-        dma((tl * CHUNKS,)),
-        dma((tl * CHUNKS,)),
-        dma((tl * CHUNKS,)),
-        dma(((tl - 1) * CHUNKS,)),
-        dma(((tl - 1) * CHUNKS,)),
+        dma((tl * chunks,)),
+        dma((tl * chunks,)),
+        dma((tl * chunks,)),
+        dma(((tl - 1) * chunks,)),
+        dma(((tl - 1) * chunks,)),
     ]
     return pl.pallas_call(
         functools.partial(
@@ -1585,14 +1595,17 @@
     o_wgrad = o_wgrad.astype(jnp.bfloat16)
     branch = scatter_tokens(branch, qkv_grad)
     activations = trade((middle + branch).astype(jnp.bfloat16))
-    gradient, sums, attn_grad = exchange(
+    gradient, sums, *attn_grads = exchange(
         None,
         contract_cols(after(qkv_back, qkv_grad), qkv_full).astype(jnp.bfloat16),
         (stream, gradient, as_row(attn_scale), mlp_gain_grad, q_gain_grad, k_gain_grad),
         (
             whole(jnp.float32),
             jax.ShapeDtypeStruct((8, 128), jnp.float32),
-            jax.ShapeDtypeStruct((q_weight.shape[1], 2 * q_cols + 2 * kv_cols), jnp.float32),
+        )
+        + tuple(
+            jax.ShapeDtypeStruct((q_weight.shape[1], cols), jnp.float32)
+            for cols in (q_cols, kv_cols, kv_cols, q_cols)
         ),
         stream_pull_rows,
         False,
@@ -1615,10 +1628,7 @@
         activations,
         gradient,
         sums[:lines].reshape(1, cut),
-        attn_grad[None, :, :q_cols],
-        attn_grad[None, :, q_cols : q_cols + kv_cols],
-        attn_grad[None, :, q_cols + kv_cols : q_cols + 2 * kv_cols],
-        attn_grad[None, :, q_cols + 2 * kv_cols :],
+        *(array[None] for array in attn_grads),
         head_gain(2 * lines),
         head_gain(2 * lines + 1),
         sums[lines : 2 * lines].reshape(1, cut),

time: 791 us -> 791 us (level)
    unnamed x89 -> x101, local copies, waits for them, and re-layouts: 17.8 us -> 20.9 us
where the time goes in v11:
time: 791 us; the launch traced here: 786 us
  Pallas kernels  415 us (52%)
  waiting for transfers between devices  144 us (18%)
  matrix products  125 us (16%)
  local copies, waits for them, and re-layouts  32.2 us (4%)
  other arithmetic  30.7 us (4%)
  starting transfers between devices  24.5 us (3%)
  between operations  15.3 us (2%)
    pallas_call x3, Pallas kernels, exchange(): pl.pallas_call(functools.partial(exchange_kernel, nd, tl, epilogue, len(a...  268 us
    ppermute x2, waiting for transfers between devices, return_halves(): far = lax.ppermute(far, 'h', shift_perm(2, 1))  105 us
    pallas_call x1, Pallas kernels, enter(): pl.pallas_call(functools.partial(entry_kernel, nd, tl), name='entry', out...  95 us
    dot_general x4, matrix products, contract_cols(): lax.dot_general(left, right, (((1,), (1,)), ((), ())), preferred_element_...  36.1 us
    pallas_call x1, Pallas kernels, attention_pull(): pl.pallas_call(functools.partial(attention_pull_kernel, blocks, repeat),...  32.5 us
    dot_general x4, matrix products, contract_rows(): lax.dot_general(left, right, (((0,), (0,)), ((), ())), preferred_element_...  30.5 us
    ppermute x1, waiting for transfers between devices, gather_along(): lax.ppermute(own, 'l', shift_perm(places, step))  27.2 us
    dot_general x2, matrix products, hidden_pull(): hidden_grad = jnp.dot(grad_rows, down, preferred_element_type=jnp.float32)  21 us
  transfers between devices with their start and end apart: 19, of which 5 were waited for; matrix products, arithmetic and copies ran while one was open for 21% of the time, Pallas kernels for 41%

profile of v11, /device:TPU:0, one launch (start us, length us, event | category | flops | bytes accessed | tf_op | source)
XLA Modules:
  0.0 786.2 jit_solution(7058128370629009699)
XLA Ops:
  7.2 1.3 collective-permute-start
  8.6 0.7 reduce.1
  9.3 0.7 reduce.2
  10.2 1.3 fusion.25.refs_9_
  12.7 2.1 fusion.16
  15.2 95.0 %entry.1 = (bf16[2048,1024]{1,0:T(8,128)(2,1)}, bf16[2048,512]{1,0:T(8,128)(2,1)}, bf16[512,1536]{1,0:T(8,128)(2,1)}, bf16[512,768]{1,0:T(8,128)(2,1)}, bf16[115...) custom-call(bf16[256,512]{1,0:T(8,128)(2,1)} %bitcast.83, bf16[256,256]{1,0:T(8,128)(2,1)} %bitcast.87, ...), custom_call_target="tpu_custom_call" | custom-call | bytes 250000000 | tf_op jit(solution)/shard_map/entry/pallas_call | solution.py:434
  110.8 2.3 slice.84
  114.5 2.9 collective-permute-start.1
  117.5 2.6 slice.82.refs_1_
  120.0 4.0 fusion
  124.1 9.3 %fusion.14.refs_0_.refs_1_.refs_2_ = f32[1152,1024]{1,0:T(8,128)} fusion(bf16[2048,1024]{1,0:T(8,128)(2,1)} %get-tuple-element.59, bf16[1152,2048]{1,0:T(8,128)(2,1)S(1)} %copy-done.12, f32[2048]{0:T(1024)S(1)} %bitcast.95, f32[1152]{0:T(1024)S(1)} %add_rsqrt_fusion), kind=kOutput, calls=%fused_computation.45 | convolution fusion | flops 4841275392 | bytes 13644288 | tf_op jit(solution)/shard_map/dot_general | solution.py:1518
  133.4 19.9 %attention.1 = (bf16[1152,512]{1,0:T(8,128)(2,1)}, bf16[1152,256]{1,0:T(8,128)(2,1)S(1)}, bf16[1152,256]{1,0:T(8,128)(2,1)S(1)}, bf16[1152,512]{1,0:T(8,128)(2,1)}, f32[1152,256]{1,0:T(8,128)}) custom-call(s32[4]{0:T(128)S(1)} %get-tuple-element.100.order_ref, f32[1152,1024]{1,0:T(8,128)} %fusion.14.refs_0_.refs_1_.refs_2_, ...), custom_call_target="tpu_custom_call" | custom-call | flops 2717908992 | bytes 60000000 | tf_op jit(solution)/shard_map/attention/pallas_call | solution.py:1248
  153.4 6.1 convolution_convert_fusion.2.refs_0_
  159.4 9.8 %collective-permute-done.1.refs_4_ = bf16[512,768]{1,0:T(8,128)(2,1)S(1)} collective-permute-done((bf16[512,768]{1,0:T(8,128)(2,1)}, bf16[512,768]{1,0:T(8,128)(2,1)S(1)}, u32[]{:S(2)}, u32[]{:S(2)}) %collective-permute-start.1) | collective-permute-done | bytes 786464 | tf_op jit(solution)/shard_map/ppermute | solution.py:1507
  169.2 0.9 copy-done.18
  170.1 90.2 %shard_map.237 = (f32[288,2048]{1,0:T(8,128)}, bf16[1152,2048]{1,0:T(8,128)(2,1)}, bf16[2048,1536]{1,0:T(8,128)(2,1)}) custom-call(bf16[1152,2048]{1,0:T(8,128)(2,1)} %convolution_convert_fusion.2.refs_0_, bf16[288,2048]{1,0:T(8,128)(2,1)} %slice.82.refs_1_, f32[1,2048]{1,0:T(1,128)} %bitcast.91, bf16[512,1536]{1,0:T(8,128)(2,1)} %get-tuple-element.62.refs_3_, ...), custom_call_target="tpu_custom_call" | custom-call | bytes 200000000 | tf_op jit(solution)/shard_map/pallas_call | solution.py:1076
  261.5 27.2 %collective-permute-done.2 = bf16[288,2048]{1,0:T(8,128)(2,1)S(1)} collective-permute-done((bf16[288,2048]{1,0:T(8,128)(2,1)S(1)}, bf16[288,2048]{1,0:T(8,128)(2,1)S(1)}, u32[]{:S(2)}, u32[]{:S(2)}) %collective-permute-start.2) | collective-permute-done | bytes 1179680 | tf_op jit(solution)/shard_map/ppermute | solution.py:1395
  288.9 9.8 %fusion.33 = f32[1152,1536]{1,0:T(8,128)S(1)} fusion(bf16[1152,2048]{1,0:T(8,128)(2,1)S(1)} %copy-done.16, bf16[2048,1536]{1,0:T(8,128)(2,1)} %get-tuple-element.68), kind=kOutput, calls=%fused_computation.100 | convolution fusion | flops 7247757312 | bytes 18087936 | tf_op jit(solution)/shard_map/dot_general | solution.py:1545
  298.7 1.1 multiply_convert_fusion.3.refs_9_
  299.8 1.7 copy-done.13
  301.9 0.9 copy-done.15
  302.8 2.1 copy-done.11
  304.9 5.9 convolution_convert_fusion.4
  311.3 11.7 %fusion.34 = f32[1152,1536]{1,0:T(8,128)S(1)} fusion(bf16[1152,2048]{1,0:T(8,128)(2,1)} %get-tuple-element.66.refs_4_, bf16[2048,1536]{1,0:T(8,128)(2,1)} %all-gather.4.cloned.1.call-done), kind=kOutput, calls=%fused_computation.101 | convolution fusion | flops 7247757312 | bytes 18087936 | tf_op jit(solution)/shard_map/dot_general | solution.py:1542
  323.0 2.9 copy-done.14
  326.0 2.3 multiply_convert_fusion.2.refs_7_.refs_8_
  328.3 10.7 %fusion.8 = (bf16[1152,768]{1,0:T(8,128)(2,1)S(1)}, bf16[1152,768]{1,0:T(8,128)(2,1)S(1)}) fusion(f32[1152,1536]{1,0:T(8,128)} %copy-done.13, bf16[1152,2048]{1,0:T(8,128)(2,1)} %copy-done.11, bf16[2048,768]{1,0:T(8,128)(2,1)} %all-gather.8.cloned.1.call-done.refs_11_), kind=kOutput, calls=%fused_computation.19 | convolution fusion | flops 3636264960 | bytes 18481152 | tf_op jit(solution)/shard_map/dot_general | solution.py:1553
  338.9 12.7 %convolution_convert_fusion.1 = bf16[2048,1536]{1,0:T(8,128)(2,1)} fusion(bf16[1152,2048]{1,0:T(8,128)(2,1)} %get-tuple-element.66.refs_4_, bf16[1152,768]{1,0:T(8,128)(2,1)S(1)} %get-tuple-element.102, bf16[1152,768]{1,0:T(8,128)(2,1)S(1)} %get-tuple-element.101), kind=kOutput, calls=%fused_computation.8 | convolution fusion | flops 7257980928 | bytes 14548992 | tf_op jit(solution)/shard_map/dot_general | solution.py:48
  352.0 10.3 %fusion.5 = (bf16[1152,768]{1,0:T(8,128)(2,1)S(1)}, bf16[1152,768]{1,0:T(8,128)(2,1)S(1)}) fusion(f32[1152,1536]{1,0:T(8,128)} %copy-done.14, bf16[1152,2048]{1,0:T(8,128)(2,1)} %copy-done.11, bf16[2048,768]{1,0:T(8,128)(2,1)} %all-gather.6.cloned.1.call-done.refs_10_), kind=kOutput, calls=%fused_computation.16 | convolution fusion | flops 3636264960 | bytes 18481152 | tf_op jit(solution)/shard_map/dot_general | solution.py:1553
  362.3 12.1 %fusion.29 = f32[1152,2048]{1,0:T(8,128)} fusion(bf16[2048,1536]{1,0:T(8,128)(2,1)} %all-gather.4.cloned.1.call-done, bf16[1152,768]{1,0:T(8,128)(2,1)S(1)} %get-tuple-element.104, bf16[1152,768]{1,0:T(8,128)(2,1)S(1)} %get-tuple-element.103), kind=kOutput, calls=%fused_computation.96 | convolution fusion | flops 7254835200 | bytes 19267584 | tf_op jit(solution)/shard_map/dot_general | solution.py:54
  374.4 11.1 %add_convert_fusion.refs_0_ = bf16[1152,2048]{1,0:T(8,128)(2,1)} fusion(f32[1152,2048]{1,0:T(8,128)} %fusion.29, bf16[2048,1536]{1,0:T(8,128)(2,1)S(1)} %bitcast.102, bf16[1152,768]{1,0:T(8,128)(2,1)S(1)} %get-tuple-element.102, bf16[1152,768]{1,0:T(8,128)(2,1)S(1)} %get-tuple-element.101), kind=kOutput, calls=%fused_computation.6 | convolution fusion | flops 7259553792 | bytes 23986176 | tf_op jit(solution)/shard_map/dot_general | solution.py:54
  385.4 2.1 pad_maximum_fusion.refs_5_
  387.5 61.2 %shard_map.238 = (f32[288,2048]{1,0:T(8,128)}, f32[1,2048]{1,0:T(1,128)}, bf16[1152,2048]{1,0:T(8,128)(2,1)}, bf16[2048,1536]{1,0:T(8,128)(2,1)}, bf16[2048,768]{1,0:T(8,128)(2,1)}, /*index=5*/bf16[1152,2048]{1,0:T(8,128)(2,1)}) custom-call(bf16[1152,2048]{1,0:T(8,128)(2,1)} %add_convert_fusion.refs_0_, f32[288,2048]{1,0:T(8,128)} %get-tuple-element.64.refs_1_, ...), custom_call_target="tpu_custom_call" | custom-call | bytes 200000000 | tf_op jit(solution)/shard_map/pallas_call | solution.py:1076
  448.8 0.7 reduce-scatter.5.cloned.1.call-update
  450.1 1.9 slice.90
  452.5 6.8 convolution_convert_fusion.6.refs_12_
  459.3 32.5 %shard_map.239 = (bf16[1152,512]{1,0:T(8,128)(2,1)}, bf16[1152,256]{1,0:T(8,128)(2,1)}, bf16[1152,256]{1,0:T(8,128)(2,1)}, f32[8,128]{1,0:T(8,128)}, f32[8,128]{1,0:T(8,128)}) custom-call(s32[4]{0:T(128)} %copy-done.5, f32[1152,1024]{1,0:T(8,128)} %fusion.14.refs_0_.refs_1_.refs_2_, f32[1152,1024]{1,0:T(8,128)} %fusion.14.refs_0_.refs_1_.refs_2_, ...), custom_call_target="tpu_custom_call" | custom-call | flops 6794772480 | bytes 120000000 | tf_op jit(solution)/shard_map/pallas_call | solution.py:1350
  491.8 1.5 constant_dynamic-update-slice_fusion.5
  493.3 1.1 constant_dynamic-update-slice_fusion.4
  494.7 7.8 convolution_convert_fusion.3.refs_7_
  502.5 3.2 convert_add_fusion
  505.7 2.2 copy-done.8
  507.8 1.2 slice.175
  509.4 4.1 convolution_convert_fusion.5.refs_8_
  513.5 6.9 convolution_convert_fusion.refs_0_
  520.4 116.1 %shard_map.240 = (f32[288,2048]{1,0:T(8,128)}, f32[8,128]{1,0:T(8,128)}, f32[256,512]{1,0:T(8,128)}, f32[256,256]{1,0:T(8,128)}, f32[256,256]{1,0:T(8,128)}, /*index=5*/f32[256,512]{1,0:T(8,128)}) custom-call(bf16[1152,2048]{1,0:T(8,128)(2,1)} %convolution_convert_fusion.refs_0_, bf16[288,2048]{1,0:T(8,128)(2,1)} %slice.82.refs_1_, ...), custom_call_target="tpu_custom_call" | custom-call | bytes 110000000 | tf_op jit(solution)/shard_map/pallas_call | solution.py:1076
  636.6 1.0 collective-permute-start.10
  637.6 2.0 collective-permute-start.8
  639.6 3.3 fusion.12
  642.9 1.9 collective-permute-start.7
  644.8 74.8 %collective-permute-done.10 = bf16[512,768]{1,0:T(8,128)(2,1)} collective-permute-done((bf16[512,768]{1,0:T(8,128)(2,1)}, bf16[512,768]{1,0:T(8,128)(2,1)}, u32[]{:S(2)}, u32[]{:S(2)}) %collective-permute-start.10) | collective-permute-done | bytes 786464 | tf_op jit(solution)/shard_map/ppermute | solution.py:1425
  719.6 1.5 convert_add_fusion.2
  723.3 30.0 %collective-permute-done.8 = bf16[512,1536]{1,0:T(8,128)(2,1)} collective-permute-done((bf16[512,1536]{1,0:T(8,128)(2,1)}, bf16[512,1536]{1,0:T(8,128)(2,1)}, u32[]{:S(2)}, u32[]{:S(2)}) %collective-permute-start.8) | collective-permute-done | bytes 1572896 | tf_op jit(solution)/shard_map/ppermute | solution.py:1425
  753.3 2.3 convert_add_fusion.1
  755.8 12.6 %collective-permute-start.9 = (bf16[256,1536]{1,0:T(8,128)(2,1)S(1)}, bf16[256,1536]{1,0:T(8,128)(2,1)S(1)}, u32[]{:S(2)}, u32[]{:S(2)}) collective-permute-start(bf16[256,1536]{1,0:T(8,128)(2,1)S(1)} %select_convert_fusion), channel_id=1, source_target_pairs={{4,0},{0,4},{5,1},{1,5},{6,2},{2,6},{7,3},{3,7},{12,8},{8,12},{13,... | collective-permute-start | bytes 2359304 | tf_op jit(solution)/shard_map/ppermute | solution.py:1431
  768.4 1.4 maximum_bitcast_fusion.2
  770.8 1.4 maximum_bitcast_fusion.1
  772.1 1.4 maximum_bitcast_fusion
  773.5 1.0 copy.61
  774.5 1.4 copy.62
  775.9 0.8 copy.63
  776.7 0.7 copy.64
  777.4 0.7 copy.65
  778.1 0.8 copy.66
  (158 shorter events, 11.3 us)
Async XLA Ops:
  7.2 304.1 %all-gather.4.cloned.1.call-start = ((), (), s32[]{:S(2)}) async-start(), calls=%async_computation.4 | async-start | bytes 7864320 | tf_op jit(solution)/shard_map/all_gather | solution.py:1505
  7.2 4.4 collective-permute-start
  10.1 123.2 %copy-start.5 = (s32[4]{0:T(128)}, s32[4]{0:T(128)S(1)}, u32[]{:S(2)}) copy-start(s32[4]{0:T(128)S(1)} %get-tuple-element.100.order_ref) | copy-start | bytes 52
  15.2 118.2 %copy-start.1 = (f32[1152,128]{1,0:T(8,128)}, f32[1152,128]{1,0:T(8,128)S(1)}, u32[]{:S(2)}) copy-start(f32[1152,128]{1,0:T(8,128)S(1)} %get-tuple-element.123.refs_3_.refs_2_) | copy-start | bytes 1769476
  15.2 118.2 %copy-start.2 = (f32[1152,128]{1,0:T(8,128)}, f32[1152,128]{1,0:T(8,128)S(1)}, u32[]{:S(2)}) copy-start(f32[1152,128]{1,0:T(8,128)S(1)} %get-tuple-element.124.refs_4_.refs_3_) | copy-start | bytes 1769476
  110.2 2.8 copy-start.26
  110.3 218.0 %all-gather.8.cloned.1.call-start = ((), (), s32[]{:S(2)}) async-start(), calls=%async_computation.6 | async-start | bytes 3932160 | tf_op jit(solution)/shard_map/all_gather | solution.py:1540
  110.8 22.6 %copy-start = (s32[1152,1]{1,0:T(8,128)}, s32[1152,1]{1,0:T(8,128)S(1)}, u32[]{:S(2)}) copy-start(s32[1152,1]{1,0:T(8,128)S(1)} %copy.37.refs_7_.refs_6_) | copy-start | bytes 13828
  113.2 20.2 %copy-start.3 = (f32[1,128]{1,0:T(1,128)}, f32[1,128]{1,0:T(1,128)S(1)}, u32[]{:S(2)}) copy-start(f32[1,128]{1,0:T(1,128)S(1)} %reshape_reshape.12.refs_6_.refs_5_) | copy-start | bytes 1540
  113.3 20.1 %copy-start.4 = (f32[1,128]{1,0:T(1,128)}, f32[1,128]{1,0:T(1,128)S(1)}, u32[]{:S(2)}) copy-start(f32[1,128]{1,0:T(1,128)S(1)} %reshape_reshape.11.refs_5_.refs_4_) | copy-start | bytes 1540
  114.5 9.5 %copy-start.27 = (f32[1,2,8,128]{3,1,2,0:T(2,128)}, f32[1,2,8,128]{3,1,2,0:T(2,128)S(1)}, u32[]{:S(2)}) copy-start(f32[1,2,8,128]{3,1,2,0:T(2,128)S(1)} %copy.46) | copy-start | bytes 24580
  114.5 54.7 %collective-permute-start.1 = (bf16[512,768]{1,0:T(8,128)(2,1)}, bf16[512,768]{1,0:T(8,128)(2,1)S(1)}, u32[]{:S(2)}, u32[]{:S(2)}) collective-permute-start(bf16[512,768]{1,0:T(8,128)(2,1)} %slice.84), channel_id=1, source_target_pairs={{2,0},{0,2},{3,1},{1,3},{6,4},{4,6},{7,5},{5,7},{10,8},{8,10},{11,... | collective-permute-start | bytes 2359304 | tf_op jit(solution)/shard_map/ppermute | solution.py:1507
  117.5 6.6 copy-start.12
  124.0 9.3 %copy-start.29 = (f32[1152]{0:T(1024)}, f32[1152]{0:T(1024)S(1)}, u32[]{:S(2)}) copy-start(f32[1152]{0:T(1024)S(1)} %add_rsqrt_fusion) | copy-start | bytes 13828
  124.0 9.3 %copy-start.19 = (bf16[512,768]{1,0:T(8,128)(2,1)S(1)}, bf16[512,768]{1,0:T(8,128)(2,1)}, u32[]{:S(2)}) copy-start(bf16[512,768]{1,0:T(8,128)(2,1)} %get-tuple-element.71) | copy-start | bytes 2359300
  133.3 127.0 %collective-permute-start.4 = (bf16[512,768]{1,0:T(8,128)(2,1)S(1)}, bf16[512,768]{1,0:T(8,128)(2,1)}, u32[]{:S(2)}, u32[]{:S(2)}) collective-permute-start(bf16[512,768]{1,0:T(8,128)(2,1)S(1)} %copy-done.19), channel_id=1, source_target_pairs={{2,0},{0,2},{3,1},{1,3},{6,4},{4,6},{7,5},{5,7},{10,8},{8,10},{11,... | collective-permute-start | bytes 2359304 | tf_op jit(solution)/shard_map/ppermute | solution.py:1519
  133.4 19.9 %copy-start.33 = (bf16[2048,512]{1,0:T(8,128)(2,1)S(1)}, bf16[2048,512]{1,0:T(8,128)(2,1)}, u32[]{:S(2)}) copy-start(bf16[2048,512]{1,0:T(8,128)(2,1)} %get-tuple-element.61) | copy-start | bytes 6291460
  153.3 6.1 copy-start.6
  153.4 6.1 copy-start.7
  169.2 0.9 copy-start.18
  170.1 90.3 %copy-start.9 = (bf16[288,2048]{1,0:T(8,128)(2,1)S(1)}, bf16[288,2048]{1,0:T(8,128)(2,1)}, u32[]{:S(2)}) copy-start(bf16[288,2048]{1,0:T(8,128)(2,1)} %get-tuple-element.65.refs_2_) | copy-start | bytes 3538948
  260.3 91.6 %all-gather.6.cloned.1.call-start = ((), (), s32[]{:S(2)}) async-start(), calls=%async_computation.5 | async-start | bytes 3932160 | tf_op jit(solution)/shard_map/all_gather | solution.py:1506
  260.4 28.3 %collective-permute-start.2 = (bf16[288,2048]{1,0:T(8,128)(2,1)S(1)}, bf16[288,2048]{1,0:T(8,128)(2,1)S(1)}, u32[]{:S(2)}, u32[]{:S(2)}) collective-permute-start(bf16[288,2048]{1,0:T(8,128)(2,1)S(1)} %copy-done.9), channel_id=1, source_target_pairs={{1,0},{0,1},{3,2},{2,3},{5,4},{4,5},{7,6},{6,7},{9,8},{8,9},{11,10... | collective-permute-start | bytes 3538952 | tf_op jit(solution)/shard_map/ppermute | solution.py:1395
  261.1 375.5 %reduce-scatter.11.cloned.1.call-start = ((), (), s32[]{:S(2)}) async-start(), calls=%async_computation.10 | async-start | bytes 3932160 | tf_op jit(solution)/shard_map/reduce_scatter | solution.py:1443
  261.4 27.6 %copy-start.16 = (bf16[1152,2048]{1,0:T(8,128)(2,1)S(1)}, bf16[1152,2048]{1,0:T(8,128)(2,1)}, u32[]{:S(2)}) copy-start(bf16[1152,2048]{1,0:T(8,128)(2,1)} %get-tuple-element.66.refs_4_) | copy-start | bytes 14155780
  288.9 12.8 %collective-permute-start.3 = (bf16[576,2048]{1,0:T(8,128)(2,1)S(1)}, bf16[576,2048]{1,0:T(8,128)(2,1)S(1)}, u32[]{:S(2)}, u32[]{:S(2)}) collective-permute-start(bf16[576,2048]{1,0:T(8,128)(2,1)S(1)} %pad_maximum_fusion.2), channel_id=1, source_target_pairs={{4,0},{0,4},{5,1},{1,5},{6,2},{2,6},{7,3},{3,7},{12,8},{8,12},{13,... | collective-permute-start | bytes 7077896 | tf_op jit(solution)/shard_map/ppermute | solution.py:1400
  298.7 2.8 copy-start.13
  301.5 1.3 copy-start.15
  302.8 2.1 copy-start.11
  310.8 326.8 %reduce-scatter.7.cloned.1.call-start = ((), (), s32[]{:S(2)}) async-start(), calls=%async_computation.8 | async-start | bytes 7864320 | tf_op jit(solution)/shard_map/reduce_scatter | solution.py:1443
  323.0 2.9 copy-start.14
  351.7 293.1 %reduce-scatter.9.cloned.1.call-start = ((), (), s32[]{:S(2)}) async-start(), calls=%async_computation.9 | async-start | bytes 3932160 | tf_op jit(solution)/shard_map/reduce_scatter | solution.py:1443
  352.0 22.4 %slice-start.4 = ((s8[6291456]{0:T(1024)(128)(4,1)}), s8[4194304]{0:T(1024)(128)(4,1)S(1)}, s32[]{:S(2)}) async-start(s8[6291456]{0:T(1024)(128)(4,1)} %bitcast.101), calls=%async_computation.15 | async-start | bytes 8388608
  362.3 12.1 %slice-start.5 = ((s8[6291456]{0:T(1024)(128)(4,1)}), s8[2097152]{0:T(1024)(128)(4,1)S(1)}, s32[]{:S(2)}) async-start(s8[6291456]{0:T(1024)(128)(4,1)} %bitcast.101), calls=%async_computation.16 | async-start | bytes 4194304
  448.7 0.8 copy-start.25
  448.7 274.6 %reduce-scatter.5.cloned.1.call-start = ((), (), s32[]{:S(2)}) async-start(), calls=%async_computation.7 | async-start | bytes 7864320 | tf_op jit(solution)/shard_map/reduce_scatter | solution.py:1443
  452.1 50.4 %collective-permute-start.5 = (bf16[576,2048]{1,0:T(8,128)(2,1)S(1)}, bf16[576,2048]{1,0:T(8,128)(2,1)}, u32[]{:S(2)}, u32[]{:S(2)}) collective-permute-start(bf16[576,2048]{1,0:T(8,128)(2,1)S(1)} %slice.90), channel_id=1, source_target_pairs={{4,0},{0,4},{5,1},{1,5},{6,2},{2,6},{7,3},{3,7},{12,8},{8,12},{13,... | collective-permute-start | bytes 7077896 | tf_op jit(solution)/shard_map/ppermute | solution.py:1408
  452.5 42.1 %slice-start = ((s8[4718592]{0:T(1024)(128)(4,1)}), s8[4194304]{0:T(1024)(128)(4,1)S(1)}, s32[]{:S(2)}) async-start(s8[4718592]{0:T(1024)(128)(4,1)} %bitcast.74), calls=%async_computation.11 | async-start | bytes 8388608
  459.3 35.3 %slice-start.1 = ((s8[4718592]{0:T(1024)(128)(4,1)}), s8[524288]{0:T(1024)(128)(4,1)S(1)}, s32[]{:S(2)}) async-start(s8[4718592]{0:T(1024)(128)(4,1)} %bitcast.74), calls=%async_computation.12 | async-start | bytes 1048576
  491.8 2.7 copy-start.20
  491.8 2.8 copy-start.28
  491.8 2.8 copy-start.30
  494.5 7.9 %slice-start.2 = ((s8[4718592]{0:T(1024)(128)(4,1)}), s8[4194304]{0:T(1024)(128)(4,1)S(1)}, s32[]{:S(2)}) async-start(s8[4718592]{0:T(1024)(128)(4,1)} %bitcast.76), calls=%async_computation.13 | async-start | bytes 8388608
  494.5 14.9 %slice-start.6 = ((s8[4718592]{0:T(1024)(128)(4,1)}), s8[4194304]{0:T(1024)(128)(4,1)S(1)}, s32[]{:S(2)}) async-start(s8[4718592]{0:T(1024)(128)(4,1)} %bitcast.103), calls=%async_computation.17 | async-start | bytes 8388608
  494.7 7.8 slice-start.3
  494.7 14.8 %slice-start.7 = ((s8[4718592]{0:T(1024)(128)(4,1)}), s8[524288]{0:T(1024)(128)(4,1)S(1)}, s32[]{:S(2)}) async-start(s8[4718592]{0:T(1024)(128)(4,1)} %bitcast.103), calls=%async_computation.18 | async-start | bytes 1048576
  502.4 7.0 copy-start.34
  505.7 2.2 copy-start.8
  509.0 4.5 copy-start.32
  509.0 128.6 %collective-permute-start.6 = (bf16[288,2048]{1,0:T(8,128)(2,1)}, bf16[288,2048]{1,0:T(8,128)(2,1)S(1)}, u32[]{:S(2)}, u32[]{:S(2)}) collective-permute-start(bf16[288,2048]{1,0:T(8,128)(2,1)} %slice.175), channel_id=1, source_target_pairs={{1,0},{0,1},{3,2},{2,3},{5,4},{4,5},{7,6},{6,7},{9,8},{8,9},{11,10... | collective-permute-start | bytes 3538952 | tf_op jit(solution)/shard_map/ppermute | solution.py:1413
  520.4 119.2 %copy-start.10 = (f32[288,2048]{1,0:T(8,128)S(1)}, f32[288,2048]{1,0:T(8,128)}, u32[]{:S(2)}) copy-start(f32[288,2048]{1,0:T(8,128)} %get-tuple-element.64.refs_1_) | copy-start | bytes 7077892
  636.5 8.2 %copy-start.31 = (f32[8,128]{1,0:T(8,128)S(1)}, f32[8,128]{1,0:T(8,128)}, u32[]{:S(2)}) copy-start(f32[8,128]{1,0:T(8,128)} %get-tuple-element.90) | copy-start | bytes 12292
  636.6 83.0 %collective-permute-start.10 = (bf16[512,768]{1,0:T(8,128)(2,1)}, bf16[512,768]{1,0:T(8,128)(2,1)}, u32[]{:S(2)}, u32[]{:S(2)}) collective-permute-start(bf16[512,768]{1,0:T(8,128)(2,1)} %reduce-scatter.11.cloned.1.call-done), channel_id=1, source_target_pairs={{2,0},{0,2},{3,1},{1,3},{6,4},{4,6},{7,5},{5,7},{10,8},{8,10},{11,... | collective-permute-start | bytes 2359304 | tf_op jit(solution)/shard_map/ppermute | solution.py:1425
  637.6 115.7 %collective-permute-start.8 = (bf16[512,1536]{1,0:T(8,128)(2,1)}, bf16[512,1536]{1,0:T(8,128)(2,1)}, u32[]{:S(2)}, u32[]{:S(2)}) collective-permute-start(bf16[512,1536]{1,0:T(8,128)(2,1)} %reduce-scatter.7.cloned.1.call-done), channel_id=1, source_target_pairs={{2,0},{0,2},{3,1},{1,3},{6,4},{4,6},{7,5},{5,7},{10,8},{8,10},{11,... | collective-permute-start | bytes 4718600 | tf_op jit(solution)/shard_map/ppermute | solution.py:1425
  642.9 80.3 %collective-permute-start.7 = (bf16[288,2048]{1,0:T(8,128)(2,1)}, bf16[288,2048]{1,0:T(8,128)(2,1)S(1)}, u32[]{:S(2)}, u32[]{:S(2)}) collective-permute-start(bf16[288,2048]{1,0:T(8,128)(2,1)} %fusion.12), channel_id=1, source_target_pairs={{0,0},{2,4},{4,2},{6,6},{1,1},{3,5},{5,3},{7,7},{8,8},{10,12},{12,... | collective-permute-start | bytes 3538952 | tf_op jit(solution)/shard_map/ppermute | solution.py:1390
  721.2 2.0 collective-permute-start.11
  755.8 14.5 %collective-permute-start.9 = (bf16[256,1536]{1,0:T(8,128)(2,1)S(1)}, bf16[256,1536]{1,0:T(8,128)(2,1)S(1)}, u32[]{:S(2)}, u32[]{:S(2)}) collective-permute-start(bf16[256,1536]{1,0:T(8,128)(2,1)S(1)} %select_convert_fusion), channel_id=1, source_target_pairs={{4,0},{0,4},{5,1},{1,5},{6,2},{2,6},{7,3},{3,7},{12,8},{8,12},{13,... | collective-permute-start | bytes 2359304 | tf_op jit(solution)/shard_map/ppermute | solution.py:1431
  772.1 2.4 copy-start.17
  773.5 2.4 copy-start.22
  773.5 3.2 copy-start.24
  774.5 2.9 copy-start.23
  774.5 3.6 copy-start.21
Sparse Core Ops, SparseCore 0:
  110.4 76.1 all-gather.3
  260.4 42.7 all-gather.7
  305.1 43.8 all-gather.5
  351.8 43.8 reduce-scatter.10
  398.6 70.0 reduce-scatter.6
  471.5 43.8 reduce-scatter.8
  518.4 112.8 reduce-scatter.4
